TPU v7x, 32 devices: a whole 2x2x4 slice. The times are simulated.
32 devices in a mesh: row: 4 (over y, x), col: 8 (over z, core).
Axes of the slice: x: 2, y: 2, z: 4, core: 2. Of those that a mesh axis runs over, the one named last changes fastest.
Arguments:
- layer_input: bfloat16 [8192, 2048], P(('col', 'row')), may hold values from -6 to 6
- cotangent: bfloat16 [8192, 2048], P(('col', 'row')), may hold values from -6 to 6
- expert_index: int32 [8192, 8], P(('col', 'row')), may hold values from 0 to 63, all different within a row; in each aligned block of 256 rows (0 to 255, 256 to 511, ...) at most 36 rows name the same one
- attention_gain: bfloat16 [2048], P('col'), may hold values from 0.5 to 1.5
- query_gain: bfloat16 [2048], P(('row', 'col')), may hold values from 0.5 to 1.5
- key_gain: bfloat16 [2048], P(('row', 'col')), may hold values from 0.5 to 1.5
- query_weight: bfloat16 [2048, 2048], P('col', 'row'), may hold values from -1 to 1
- key_weight: bfloat16 [2048, 2048], P('col', 'row'), may hold values from -1 to 1
- value_weight: bfloat16 [2048, 2048], P('col', 'row'), may hold values from -0.125 to 0.125
- output_weight: bfloat16 [2048, 2048], P('row', 'col'), may hold values from -1 to 1
- feed_gain: bfloat16 [2048], P('col'), may hold values from 0.5 to 1.5
- router_weight: bfloat16 [2048, 64], P('col'), may hold values from -1 to 1
- gate_weight: bfloat16 [64, 2048, 1024], P('col', None, 'row'), may hold values from -0.125 to 0.125
- up_weight: bfloat16 [64, 2048, 1024], P('col', None, 'row'), may hold values from -0.125 to 0.125
- down_weight: bfloat16 [64, 1024, 2048], P('col', 'row'), may hold values from -1.5 to 1.5
Outputs:
- layer_output: float32 [8192, 2048], P(('col', 'row'))
- input_grad: float32 [8192, 2048], P(('col', 'row'))
- grad_attention_gain: float32 [2048], P('col')
- grad_query_gain: float32 [2048], P(('row', 'col'))
- grad_key_gain: float32 [2048], P(('row', 'col'))
- grad_query_weight: float32 [2048, 2048], P('col', 'row')
- grad_key_weight: float32 [2048, 2048], P('col', 'row')
- grad_value_weight: float32 [2048, 2048], P('col', 'row')
- grad_output_weight: float32 [2048, 2048], P('row', 'col')
- grad_feed_gain: float32 [2048], P('col')
- grad_router_weight: float32 [2048, 64], P('col')
- grad_gate_weight: float32 [64, 2048, 1024], P('col', None, 'row')
- grad_up_weight: float32 [64, 2048, 1024], P('col', None, 'row')
- grad_down_weight: float32 [64, 1024, 2048], P('col', 'row')
Inputs may be any that keep to these rules, and one draw needn't show every extreme that they name: `expert_index`: each row names 8 different experts; among the rows of one device no expert is named more than 36 times, and one expert is named exactly 36 times on some device.
All inputs are finite; a program needn't handle non-finite values.
Results may differ from a plain program's by a relative error of at most 0.022.
Values may be sent and summed in bfloat16 or wider, within the bound.
A program may use at most 448 MiB of HBM per device.

v0:
```python
import jax
import jax.numpy as jnp
from jax import lax
from jax.sharding import PartitionSpec as P

HD = 128
CAP = 36


EPS = 1e-05
THETA = 10000.0
MASKED = -1e30


def wide_dot(left, right):
    return jnp.dot(left, right, preferred_element_type=jnp.float32)


def inner_rows(left, right):
    return lax.dot_general(
        left, right, (((0,), (0,)), ((), ())), preferred_element_type=jnp.float32
    )


def outer_cols(left, right):
    return lax.dot_general(
        left, right, (((1,), (1,)), ((), ())), preferred_element_type=jnp.float32
    )


def rms_scale(field):
    return lax.rsqrt(jnp.mean(field * field, axis=-1, keepdims=True) + EPS)


def rope_tables(length):
    half_size = HD // 2
    freqs = THETA ** (-(jnp.arange(half_size, dtype=jnp.float32) * 2.0) / HD)
    angles = jnp.arange(length, dtype=jnp.float32)[:, None] * freqs[None, :]
    cosine = jnp.concatenate([jnp.cos(angles), jnp.cos(angles)], axis=-1)[:, None, :]
    sine_table = jnp.concatenate([jnp.sin(angles), jnp.sin(angles)], axis=-1)[:, None, :]
    return (cosine, sine_table)


def rotate(field, cosine, sine_table):
    half_size = field.shape[-1] // 2
    turned = jnp.concatenate([-field[..., half_size:], field[..., :half_size]], axis=-1)
    return field * cosine + turned * sine_table


def unrotate(gradient, cosine, sine_table):
    half_size = gradient.shape[-1] // 2
    moved = gradient * sine_table
    back_turned = jnp.concatenate([moved[..., half_size:], -moved[..., :half_size]], axis=-1)
    return gradient * cosine + back_turned


def expert_back(
    expert_rows, expert_grads, gate_in, up_in, activated_rows, gate_mat, up_mat, down_mat
):
    sigmoid_val = jax.nn.sigmoid(gate_in)
    silu_val = gate_in * sigmoid_val
    grad_act = outer_cols(expert_grads, down_mat)
    grad_up = (grad_act * silu_val).astype(jnp.bfloat16)
    grad_gate = (grad_act * up_in * sigmoid_val * (1.0 + gate_in * (1.0 - sigmoid_val))).astype(
        jnp.bfloat16
    )
    grad_down_mat = inner_rows(activated_rows, expert_grads)
    grad_gate_mat = inner_rows(expert_rows, grad_gate)
    grad_up_mat = inner_rows(expert_rows, grad_up)
    grad_rows_val = outer_cols(grad_gate, gate_mat) + outer_cols(grad_up, up_mat)
    return (grad_rows_val.astype(jnp.bfloat16), grad_gate_mat, grad_up_mat, grad_down_mat)


def local(
    layer_input,
    cotangent,
    expert_index,
    attention_gain,
    query_gain,
    key_gain,
    query_weight,
    key_weight,
    value_weight,
    output_weight,
    feed_gain,
    router_weight,
    gate_weight,
    up_weight,
    down_weight,
):
    tokens = layer_input.shape[0]
    rows_count = lax.axis_size("row")
    (
        attention_full,
        query_scale_w,
        key_scale_w,
        query_full,
        key_full,
        value_full,
        output_full,
        feed_full,
        router_full,
    ) = (
        lax.all_gather(attention_gain, "col", axis=0, tiled=True),
        lax.all_gather(query_gain, "col", axis=0, tiled=True),
        lax.all_gather(key_gain, "col", axis=0, tiled=True),
        lax.all_gather(query_weight, "col", axis=0, tiled=True),
        lax.all_gather(key_weight, "col", axis=0, tiled=True),
        lax.all_gather(value_weight, "col", axis=0, tiled=True),
        lax.all_gather(output_weight, "col", axis=1, tiled=True),
        lax.all_gather(feed_gain, "col", axis=0, tiled=True),
        lax.all_gather(router_weight, "col", axis=0, tiled=True),
    )
    sequence = lax.all_gather(layer_input, "row", axis=0, tiled=True)
    length = sequence.shape[0]
    model_width = sequence.shape[1]
    local_width = query_full.shape[1]
    local_heads = local_width // HD
    seq_float = sequence.astype(jnp.float32)
    seq_scale = rms_scale(seq_float)
    attention_float = attention_full.astype(jnp.float32)
    normed = (seq_float * seq_scale * attention_float).astype(jnp.bfloat16)
    query_raw = wide_dot(normed, query_full)
    key_raw = wide_dot(normed, key_full)
    value_heads = wide_dot(normed, value_full).astype(jnp.bfloat16).reshape(length, local_heads, HD)
    query_total, key_total = lax.psum(
        (jnp.sum(query_raw * query_raw, axis=-1), jnp.sum(key_raw * key_raw, axis=-1)), "row"
    )
    query_rs = lax.rsqrt(query_total / model_width + EPS)[:, None]
    key_rs = lax.rsqrt(key_total / model_width + EPS)[:, None]
    query_gain_f = query_scale_w.astype(jnp.float32)
    key_gain_f = key_scale_w.astype(jnp.float32)
    cosine, sine_table = rope_tables(length)
    queries = rotate(
        (query_raw * query_rs * query_gain_f).reshape(length, local_heads, HD), cosine, sine_table
    ).astype(jnp.bfloat16)
    keys_rotated = rotate(
        (key_raw * key_rs * key_gain_f).reshape(length, local_heads, HD), cosine, sine_table
    ).astype(jnp.bfloat16)
    block_rows = min(512, length)
    starts = jnp.arange(length // block_rows, dtype=jnp.int32) * block_rows
    key_position = jnp.arange(length, dtype=jnp.int32)
    score_scale = HD ** (-0.5)

    def block_scores(offset):
        query_rows = lax.dynamic_slice_in_dim(queries, offset, block_rows, 0)
        scores = (
            jnp.einsum("qhd,khd->hqk", query_rows, keys_rotated, preferred_element_type=jnp.float32)
            * score_scale
        )
        query_position = offset + jnp.arange(block_rows, dtype=jnp.int32)
        allowed = query_position[:, None] >= key_position[None, :]
        return (query_rows, jnp.where(allowed[None, :, :], scores, MASKED))

    def forward_block(offset):
        query_rows, scores = block_scores(offset)
        row_top = jnp.max(scores, axis=-1, keepdims=True)
        exponent = jnp.exp(scores - row_top)
        row_total = jnp.sum(exponent, axis=-1, keepdims=True)
        weights = (exponent / row_total).astype(jnp.bfloat16)
        mixed_block = jnp.einsum(
            "hqk,khd->qhd", weights, value_heads, preferred_element_type=jnp.float32
        )
        return (mixed_block, (row_top + jnp.log(row_total))[..., 0])

    mixed_blocks, lse_blocks = lax.map(forward_block, starts)
    mixed_heads = mixed_blocks.reshape(length, local_width).astype(jnp.bfloat16)
    lse_all = jnp.moveaxis(lse_blocks, 0, 1).reshape(local_heads, length)
    branch = lax.psum_scatter(
        wide_dot(mixed_heads, output_full), "row", scatter_dimension=0, tiled=True
    )
    hidden = layer_input.astype(jnp.float32) + branch
    feed_scale = rms_scale(hidden)
    feed_float = feed_full.astype(jnp.float32)
    feed_normed = (hidden * feed_scale * feed_float).astype(jnp.bfloat16)
    logits = wide_dot(feed_normed, router_full)
    logit_top = jnp.max(logits, axis=-1, keepdims=True)
    logit_exp = jnp.exp(logits - logit_top)
    router_probs = logit_exp / jnp.sum(logit_exp, axis=-1, keepdims=True)
    experts = router_full.shape[1]
    top_count = expert_index.shape[1]
    flat_index = expert_index.reshape(-1)
    onehot = (flat_index[:, None] == jnp.arange(experts, dtype=jnp.int32)[None, :]).astype(
        jnp.int32
    )
    running = jnp.cumsum(onehot, axis=0, dtype=jnp.int32) - 1
    slot_rank = jnp.sum(running * onehot, axis=-1, dtype=jnp.int32)
    slot_index = flat_index * CAP + slot_rank
    pick_table = onehot.astype(jnp.float32).reshape(tokens, top_count, experts)
    gate_probs = jnp.einsum("tje,te->tj", pick_table, router_probs)
    entries = jnp.arange(tokens * top_count, dtype=jnp.int32)
    slot_source = (
        jnp.full((experts * CAP,), tokens * top_count, jnp.int32).at[slot_index].set(entries)
    )
    padded = jnp.concatenate([feed_normed, jnp.zeros((1, model_width), jnp.bfloat16)], axis=0)
    outgoing = padded[slot_source // top_count].reshape(experts, CAP, model_width)
    incoming = lax.all_to_all(outgoing, "col", split_axis=0, concat_axis=1, tiled=True)

    def expert_weights():
        return (
            lax.all_gather(gate_weight, "row", axis=2, tiled=True),
            lax.all_gather(up_weight, "row", axis=2, tiled=True),
            lax.all_gather(down_weight, "row", axis=1, tiled=True),
        )

    gate_full, up_full, down_full = expert_weights()
    gate_val = jnp.einsum("erd,edf->erf", incoming, gate_full, preferred_element_type=jnp.float32)
    up_val = jnp.einsum("erd,edf->erf", incoming, up_full, preferred_element_type=jnp.float32)
    activated = (jax.nn.silu(gate_val) * up_val).astype(jnp.bfloat16)
    expert_out = jnp.einsum(
        "erf,efd->erd", activated, down_full, preferred_element_type=jnp.float32
    ).astype(jnp.bfloat16)
    returned = lax.all_to_all(expert_out, "col", split_axis=1, concat_axis=0, tiled=True)
    picked = (
        returned.reshape(experts * CAP, model_width)[slot_index]
        .reshape(tokens, top_count, model_width)
        .astype(jnp.float32)
    )
    mixture = jnp.einsum("tj,tjd->td", gate_probs, picked)
    layer_output = hidden + mixture
    grad_out = cotangent.astype(jnp.float32)
    grad_gates = jnp.einsum("td,tjd->tj", grad_out, picked)
    grad_picked = (
        (gate_probs[:, :, None] * grad_out[:, None, :])
        .astype(jnp.bfloat16)
        .reshape(tokens * top_count, model_width)
    )
    grad_padded = jnp.concatenate([grad_picked, jnp.zeros((1, model_width), jnp.bfloat16)], axis=0)
    outgoing_grad = grad_padded[slot_source].reshape(experts, CAP, model_width)
    incoming_grad = lax.all_to_all(outgoing_grad, "col", split_axis=0, concat_axis=1, tiled=True)
    gate_full, up_full, down_full = expert_weights()
    grad_rows_all, gate_terms, up_terms, down_terms = jax.vmap(expert_back)(
        incoming, incoming_grad, gate_val, up_val, activated, gate_full, up_full, down_full
    )
    grad_gate_weight = lax.psum_scatter(
        gate_terms.astype(jnp.bfloat16), "row", scatter_dimension=2, tiled=True
    ).astype(jnp.float32)
    grad_up_weight = lax.psum_scatter(
        up_terms.astype(jnp.bfloat16), "row", scatter_dimension=2, tiled=True
    ).astype(jnp.float32)
    grad_down_weight = lax.psum_scatter(
        down_terms.astype(jnp.bfloat16), "row", scatter_dimension=1, tiled=True
    ).astype(jnp.float32)
    returned_grad = lax.all_to_all(grad_rows_all, "col", split_axis=1, concat_axis=0, tiled=True)
    grad_slots = (
        returned_grad.reshape(experts * CAP, model_width)[slot_index]
        .reshape(tokens, top_count, model_width)
        .astype(jnp.float32)
    )
    grad_feed = jnp.sum(grad_slots, axis=1)
    grad_probs = jnp.einsum("tj,tje->te", grad_gates, pick_table)
    grad_logits = (
        router_probs * (grad_probs - jnp.sum(router_probs * grad_probs, axis=-1, keepdims=True))
    ).astype(jnp.bfloat16)
    router_grad = inner_rows(feed_normed, grad_logits)
    grad_feed = grad_feed + outer_cols(grad_logits, router_full)
    feed_gain_term = jnp.sum(grad_feed * hidden * feed_scale, axis=0)
    feed_weighted = grad_feed * feed_float
    grad_hidden = (
        grad_out
        + feed_scale * feed_weighted
        - hidden * feed_scale**3 * jnp.mean(feed_weighted * hidden, axis=-1, keepdims=True)
    )
    grad_branch = lax.all_gather(grad_hidden.astype(jnp.bfloat16), "row", axis=0, tiled=True)
    output_grad = inner_rows(mixed_heads, grad_branch)
    grad_mixed = (
        outer_cols(grad_branch, output_full).astype(jnp.bfloat16).reshape(length, local_heads, HD)
    )

    def backward_block(carry, offset):
        grad_keys, grad_values = carry
        query_rows, scores = block_scores(offset)
        lse_rows = lax.dynamic_slice_in_dim(lse_all, offset, block_rows, 1)
        probs_block = jnp.exp(scores - lse_rows[:, :, None])
        weights_low = probs_block.astype(jnp.bfloat16)
        grad_rows_out = lax.dynamic_slice_in_dim(grad_mixed, offset, block_rows, 0)
        grad_weights = jnp.einsum(
            "qhd,khd->hqk", grad_rows_out, value_heads, preferred_element_type=jnp.float32
        )
        grad_values = grad_values + jnp.einsum(
            "hqk,qhd->khd", weights_low, grad_rows_out, preferred_element_type=jnp.float32
        )
        delta_rows = jnp.sum(probs_block * grad_weights, axis=-1, keepdims=True)
        grad_scores = (probs_block * (grad_weights - delta_rows)).astype(jnp.bfloat16)
        grad_query_block = (
            jnp.einsum(
                "hqk,khd->qhd", grad_scores, keys_rotated, preferred_element_type=jnp.float32
            )
            * score_scale
        )
        grad_keys = (
            grad_keys
            + jnp.einsum(
                "hqk,qhd->khd", grad_scores, query_rows, preferred_element_type=jnp.float32
            )
            * score_scale
        )
        return ((grad_keys, grad_values), grad_query_block)

    zero_heads = jnp.zeros((length, local_heads, HD), jnp.float32)
    (grad_keys, grad_values), grad_query_blocks = lax.scan(
        backward_block, (zero_heads, zero_heads), starts
    )
    grad_queries = grad_query_blocks.reshape(length, local_heads, HD)
    grad_query_normed = unrotate(grad_queries, cosine, sine_table).reshape(length, local_width)
    grad_key_normed = unrotate(grad_keys, cosine, sine_table).reshape(length, local_width)
    grad_value_low = grad_values.reshape(length, local_width).astype(jnp.bfloat16)
    query_weighted = grad_query_normed * query_gain_f
    key_weighted = grad_key_normed * key_gain_f
    query_gain_term = jnp.sum(grad_query_normed * query_raw * query_rs, axis=0)
    key_gain_term = jnp.sum(grad_key_normed * key_raw * key_rs, axis=0)
    query_inner, key_inner, feed_gain_total, router_total = (
        lax.psum(jnp.sum(query_weighted * query_raw, axis=-1).astype(jnp.bfloat16), "row").astype(
            jnp.float32
        ),
        lax.psum(jnp.sum(key_weighted * key_raw, axis=-1).astype(jnp.bfloat16), "row").astype(
            jnp.float32
        ),
        lax.psum(feed_gain_term.astype(jnp.bfloat16), "row").astype(jnp.float32),
        lax.psum(router_grad.astype(jnp.bfloat16), "row").astype(jnp.float32),
    )
    grad_query_raw = (
        query_rs * query_weighted - query_raw * query_rs**3 * (query_inner / model_width)[:, None]
    ).astype(jnp.bfloat16)
    grad_key_raw = (
        key_rs * key_weighted - key_raw * key_rs**3 * (key_inner / model_width)[:, None]
    ).astype(jnp.bfloat16)
    query_grad = inner_rows(normed, grad_query_raw)
    key_grad = inner_rows(normed, grad_key_raw)
    value_grad = inner_rows(normed, grad_value_low)
    grad_normed = (
        outer_cols(grad_query_raw, query_full)
        + outer_cols(grad_key_raw, key_full)
        + outer_cols(grad_value_low, value_full)
    )
    attention_weighted = grad_normed * attention_float
    grad_seq_part = seq_scale * attention_weighted - seq_float * seq_scale**3 * jnp.mean(
        attention_weighted * seq_float, axis=-1, keepdims=True
    )
    attention_gain_term = jnp.sum(grad_normed * seq_float * seq_scale, axis=0)
    stacked = jnp.concatenate(
        [
            grad_seq_part.reshape(rows_count, tokens, model_width),
            jnp.broadcast_to(attention_gain_term[None, None, :], (rows_count, 1, model_width)),
        ],
        axis=1,
    ).reshape(rows_count * (tokens + 1), model_width)
    summed = lax.psum_scatter(
        stacked.astype(jnp.bfloat16), "row", scatter_dimension=0, tiled=True
    ).astype(jnp.float32)
    input_grad = grad_hidden + summed[:tokens]
    attention_gain_total = summed[tokens]
    (
        grad_attention_gain,
        grad_query_gain,
        grad_key_gain,
        grad_query_weight,
        grad_key_weight,
        grad_value_weight,
        grad_output_weight,
        grad_feed_gain,
        grad_router_weight,
    ) = (
        lax.psum_scatter(
            attention_gain_total.astype(jnp.bfloat16), "col", scatter_dimension=0, tiled=True
        ).astype(jnp.float32),
        lax.psum_scatter(
            query_gain_term.astype(jnp.bfloat16), "col", scatter_dimension=0, tiled=True
        ).astype(jnp.float32),
        lax.psum_scatter(
            key_gain_term.astype(jnp.bfloat16), "col", scatter_dimension=0, tiled=True
        ).astype(jnp.float32),
        lax.psum_scatter(
            query_grad.astype(jnp.bfloat16), "col", scatter_dimension=0, tiled=True
        ).astype(jnp.float32),
        lax.psum_scatter(
            key_grad.astype(jnp.bfloat16), "col", scatter_dimension=0, tiled=True
        ).astype(jnp.float32),
        lax.psum_scatter(
            value_grad.astype(jnp.bfloat16), "col", scatter_dimension=0, tiled=True
        ).astype(jnp.float32),
        lax.psum_scatter(
            output_grad.astype(jnp.bfloat16), "col", scatter_dimension=1, tiled=True
        ).astype(jnp.float32),
        lax.psum_scatter(
            feed_gain_total.astype(jnp.bfloat16), "col", scatter_dimension=0, tiled=True
        ).astype(jnp.float32),
        lax.psum_scatter(
            router_total.astype(jnp.bfloat16), "col", scatter_dimension=0, tiled=True
        ).astype(jnp.float32),
    )
    return (
        layer_output,
        input_grad,
        grad_attention_gain,
        grad_query_gain,
        grad_key_gain,
        grad_query_weight,
        grad_key_weight,
        grad_value_weight,
        grad_output_weight,
        grad_feed_gain,
        grad_router_weight,
        grad_gate_weight,
        grad_up_weight,
        grad_down_weight,
    )


def solution(mesh):
    placed = (
        P(("col", "row"), None),
        P(("col", "row"), None),
        P(("col", "row"), None),
        P("col"),
        P(("row", "col")),
        P(("row", "col")),
        P("col", "row"),
        P("col", "row"),
        P("col", "row"),
        P("row", "col"),
        P("col"),
        P("col", None),
        P("col", None, "row"),
        P("col", None, "row"),
        P("col", "row", None),
    )
    return jax.shard_map(
        local,
        mesh=mesh,
        in_specs=placed,
        out_specs=(
            P(("col", "row"), None),
            P(("col", "row"), None),
            P("col"),
            P(("row", "col")),
            P(("row", "col")),
            P("col", "row"),
            P("col", "row"),
            P("col", "row"),
            P("row", "col"),
            P("col"),
            P("col", None),
            P("col", None, "row"),
            P("col", None, "row"),
            P("col", "row", None),
        ),
        check_vma=False,
    )
```

profile of v0, /device:TPU:0, one launch (start us, length us, event | category | flops | bytes accessed | tf_op | source)
XLA Modules:
  0.0 3113.1 jit_solution(16195248210804608851)
XLA Ops:
  47.5 17.8 all-gather.12.cloned.1.call-done
  69.0 27.1 all-gather.14.cloned.1.call-done
  101.4 24.9 all-gather.16.cloned.1.call-done
  169.1 23.4 while.30
  218.6 18.1 reduce-window.6
  261.1 28.7 reduce-scatter.10.cloned.1.call-done
  312.1 23.1 gather_fusion.2
  376.3 205.9 %all-to-all-done.2 = bf16[64,36,2048]{2,1,0:T(8,128)(2,1)} async-done(((bf16[64,36,2048]{2,1,0:T(8,128)(2,1)}), bf16[64,36,2048]{2,1,0:T(8,128)(2,1)}, u32[]{:S(2)}, u32[]{:S(2)}) %all-to-all-start.2) | async-done | bytes 9437216 | tf_op jit(solution)/shard_map/all_to_all | solution.py:230
  604.4 211.9 %all-to-all-done = bf16[64,36,2048]{2,1,0:T(8,128)(2,1)} async-done(((bf16[64,36,2048]{2,1,0:T(8,128)(2,1)}), bf16[64,36,2048]{2,1,0:T(8,128)(2,1)}, u32[]{:S(2)}, u32[]{:S(2)}) %all-to-all-start) | async-done | bytes 9437216 | tf_op jit(solution)/shard_map/all_to_all | solution.py:197
  830.3 30.9 fusion.57
  861.2 26.8 all-gather.22.cloned.1.call-done
  888.0 32.5 %fusion.59 = f32[8,288,1024]{2,1,0:T(8,128)} fusion(bf16[8,2048,1024]{2,1,0:T(8,128)(2,1)} %all-gather.22.cloned.1.call-done, bf16[8,288,2048]{2,0,1:T(8,128)(2,1)} %bitcast.239), kind=kOutput, calls=%fused_computation.90 | convolution fusion | flops 9663676416 | bytes 52428800 | tf_op jit(solution)/shard_map/erd,edf->erf/dot_general | solution.py:207
  920.5 266.8 %all-gather.26.cloned.1.call-done = bf16[8,1024,2048]{2,1,0:T(8,128)(2,1)} async-done(((bf16[8,256,2048]{2,1,0:T(8,128)(2,1)}), bf16[8,1024,2048]{2,1,0:T(8,128)(2,1)}) %all-gather.26.cloned.1.call-update) | async-done | bytes 33554448 | tf_op jit(solution)/shard_map/all_gather | solution.py:203
  1187.3 68.1 %multiply_convert_fusion.1 = (bf16[8,288,1024]{2,1,0:T(8,128)(2,1)}, bf16[8,288,1024]{2,1,0:T(8,128)(2,1)}, bf16[8,288,1024]{2,1,0:T(8,128)(2,1)}) fusion(f32[8,288,1024]{2,1,0:T(8,128)} %fusion.59, f32[8,288,1024]{2,1,0:T(8,128)} %fusion.57, bf16[8,1024,2048]{2,1,0:T(8,128)(2,1)} %all-gather.26.cloned.1.call-done, bf16[8,288,2048]{2,0,1:T(8,128)(2,1)} %bitcast.242), kind=kOutput, calls=%fused_computation.64 | convolution fusion | flops 9699065856 | bytes 76021760 | tf_op jit(solution)/shard_map/vmap()/dot_general | solution.py:26
  1255.4 19.5 convolution_convert_fusion.3
  1292.8 21.7 fusion.122
  1314.6 23.3 add_convert_fusion
  1350.5 148.7 %all-to-all-done.1 = bf16[8,288,2048]{2,0,1:T(8,128)(2,1)} async-done(((bf16[8,288,2048]{2,0,1:T(8,128)(2,1)}), bf16[8,288,2048]{2,0,1:T(8,128)(2,1)}, u32[]{:S(2)}, u32[]{:S(2)}) %all-to-all-start.1) | async-done | bytes 9437216 | tf_op jit(solution)/shard_map/all_to_all | solution.py:213
  1531.9 21.3 gather_fusion.1
  1569.3 141.4 %all-to-all-done.3 = bf16[8,288,2048]{2,0,1:T(8,128)(2,1)} async-done(((bf16[8,288,2048]{2,0,1:T(8,128)(2,1)}), bf16[8,288,2048]{2,0,1:T(8,128)(2,1)}, u32[]{:S(2)}, u32[]{:S(2)}) %all-to-all-start.3) | async-done | bytes 9437216 | tf_op jit(solution)/shard_map/all_to_all | solution.py:244
  1737.9 21.6 gather_fusion.3
  1779.0 49.7 %all-gather.28.cloned.1.call-done = bf16[1024,2048]{1,0:T(8,128)(2,1)} async-done(((bf16[256,2048]{1,0:T(8,128)(2,1)}), bf16[1024,2048]{1,0:T(8,128)(2,1)}) %all-gather.28.cloned.1.call-update) | async-done | bytes 4194320 | tf_op jit(solution)/shard_map/all_gather | solution.py:264
  1834.9 50.5 %while.31 = (s32[]{:T(128)}, f32[1024,4,128]{0,2,1:T(8,128)S(1)}, f32[1024,4,128]{0,2,1:T(8,128)}, f32[2,512,4,128]{3,1,2,0:T(8,128)}, s32[2]{0:T(128)S(1)}, /*i...) while((s32[]{:T(128)}, f32[1024,4,128]{0,2,1:T(8,128)S(1)}, ...), condition=%wide.region_22.23_spmd.clone.clone, body=%wide.region_20.22_spmd.clone.sunk.clone | while | flops 2719218176 | bytes 180417440 | solution.py:301
  1991.0 55.6 %convolution_convert_fusion = bf16[8,1024,2048]{2,1,0:T(8,128)(2,1)} fusion(bf16[8,288,1024]{2,1,0:T(8,128)(2,1)} %get-tuple-element.288, bf16[8,288,2048]{2,0,1:T(8,128)(2,1)} %bitcast.243), kind=kOutput, calls=%fused_computation.52 | convolution fusion | flops 9680453632 | bytes 47710208 | tf_op jit(solution)/shard_map/vmap()/dot_general | solution.py:20
  2047.1 29.7 convolution_convert_fusion.2
  2076.8 29.8 convolution_convert_fusion.1
  2117.0 71.3 %all-reduce.16.cloned.1.call-done = bf16[1028,2048]{1,0:T(8,128)(2,1)} async-done(((bf16[1028,2048]{1,0:T(8,128)(2,1)}), bf16[1028,2048]{1,0:T(8,128)(2,1)}) %all-reduce.16.cloned.1.call-update) | async-done | bytes 4210704
  2189.0 28.6 all-reduce.10
  2221.8 17.9 all-reduce.12
  2245.6 266.2 %reduce-scatter.24.cloned.1.call-done = bf16[8,256,2048]{2,1,0:T(8,128)(2,1)} async-done(((bf16[8,1024,2048]{2,1,0:T(8,128)(2,1)}), bf16[8,256,2048]{2,1,0:T(8,128)(2,1)}) %reduce-scatter.24.cloned.1.call-update) | async-done | bytes 8388624 | tf_op jit(solution)/shard_map/reduce_scatter | solution.py:241
  2523.5 280.1 %reduce-scatter.20.cloned.1.call-done = bf16[8,2048,256]{2,1,0:T(8,128)(2,1)} async-done(((bf16[8,2048,1024]{2,1,0:T(8,128)(2,1)}), bf16[8,2048,256]{2,1,0:T(8,128)(2,1)}) %reduce-scatter.20.cloned.1.call-update) | async-done | bytes 8388624 | tf_op jit(solution)/shard_map/reduce_scatter | solution.py:235
  2814.8 280.6 %reduce-scatter.22.cloned.1.call-done = bf16[8,2048,256]{2,1,0:T(8,128)(2,1)} async-done(((bf16[8,2048,1024]{2,1,0:T(8,128)(2,1)}), bf16[8,2048,256]{2,1,0:T(8,128)(2,1)}) %reduce-scatter.22.cloned.1.call-update) | async-done | bytes 8388624 | tf_op jit(solution)/shard_map/reduce_scatter | solution.py:238
  (421 shorter events, 597.1 us)
Async XLA Ops:
  7.2 58.1 %all-gather.12.cloned.1.call-start = ((), (), s32[]{:S(2)}) async-start(), calls=%async_computation.13 | async-start | bytes 5242880 | tf_op jit(solution)/shard_map/all_gather | solution.py:114
  7.9 88.1 %all-gather.14.cloned.1.call-start = ((), (), s32[]{:S(2)}) async-start(), calls=%async_computation.14 | async-start | bytes 2359296 | tf_op jit(solution)/shard_map/all_gather | solution.py:107
  8.7 117.6 %all-gather.16.cloned.1.call-start = ((), (), s32[]{:S(2)}) async-start(), calls=%async_computation.15 | async-start | bytes 2359296 | tf_op jit(solution)/shard_map/all_gather | solution.py:108
  9.4 147.1 %all-gather.18.cloned.1.call-start = ((), (), s32[]{:S(2)}) async-start(), calls=%async_computation.16 | async-start | bytes 2359296 | tf_op jit(solution)/shard_map/all_gather | solution.py:109
  10.0 186.3 %all-gather.20.cloned.1.call-start = ((), (), s32[]{:S(2)}) async-start(), calls=%async_computation.17 | async-start | bytes 2359296 | tf_op jit(solution)/shard_map/all_gather | solution.py:110
  10.6 279.3 %reduce-scatter.10.cloned.1.call-start = ((), (), s32[]{:S(2)}) async-start(), calls=%async_computation.18 | async-start | bytes 10485760 | tf_op jit(solution)/shard_map/reduce_scatter | solution.py:169
  25.9 130.6 %copy-start.57 = (f32[8,1,256]{2,1,0:T(1,128)}, f32[8,1,256]{2,1,0:T(1,128)S(1)}, u32[]{:S(2)}) copy-start(f32[8,1,256]{2,1,0:T(1,128)S(1)} %convert_element_type.266) | copy-start | bytes 24580
  43.5 100.2 %copy-start.71 = (f32[512]{0:T(512)}, f32[512]{0:T(512)S(1)}, u32[]{:S(2)}) copy-start(f32[512]{0:T(512)S(1)} %convert_element_type.208) | copy-start | bytes 6148
  43.5 106.5 %copy-start.65 = (f32[512]{0:T(512)}, f32[512]{0:T(512)S(1)}, u32[]{:S(2)}) copy-start(f32[512]{0:T(512)S(1)} %convert_element_type.210) | copy-start | bytes 6148
  69.0 87.6 %copy-start.63 = (f32[1024]{0:T(1024)}, f32[1024]{0:T(1024)S(1)}, u32[]{:S(2)}) copy-start(f32[1024]{0:T(1024)S(1)} %get-tuple-element.305) | copy-start | bytes 12292
  204.0 626.3 %all-gather.24.cloned.1.call-start = ((), (), s32[]{:S(2)}) async-start(), calls=%async_computation.20 | async-start | bytes 41943040 | tf_op jit(solution)/shard_map/all_gather | solution.py:202
  204.8 683.3 %all-gather.22.cloned.1.call-start = ((), (), s32[]{:S(2)}) async-start(), calls=%async_computation.19 | async-start | bytes 41943040 | tf_op jit(solution)/shard_map/all_gather | solution.py:201
  205.6 981.8 %all-gather.26.cloned.1.call-start = ((), (), s32[]{:S(2)}) async-start(), calls=%async_computation.21 | async-start | bytes 41943040 | tf_op jit(solution)/shard_map/all_gather | solution.py:203
  206.4 87.6 %copy-start.44 = (s32[256,8]{1,0:T(8,128)}, s32[256,8]{1,0:T(8,128)S(1)}, u32[]{:S(2)}) copy-start(s32[256,8]{1,0:T(8,128)S(1)} %copy.91) | copy-start | bytes 24580
  348.2 234.0 %all-to-all-start.2 = ((bf16[64,36,2048]{2,1,0:T(8,128)(2,1)}), bf16[64,36,2048]{2,1,0:T(8,128)(2,1)}, u32[]{:S(2)}, u32[]{:S(2)}) async-start(bf16[64,36,2048]{2,1,0:T(8,128)(2,1)} %reshape.310), calls=%async_computation.3 | async-start | bytes 20971520 | tf_op jit(solution)/shard_map/all_to_all | solution.py:230
  582.2 234.1 %all-to-all-start = ((bf16[64,36,2048]{2,1,0:T(8,128)(2,1)}), bf16[64,36,2048]{2,1,0:T(8,128)(2,1)}, u32[]{:S(2)}, u32[]{:S(2)}) async-start(bf16[64,36,2048]{2,1,0:T(8,128)(2,1)} %reshape.307), calls=%async_computation.1 | async-start | bytes 20971520 | tf_op jit(solution)/shard_map/all_to_all | solution.py:197
  1287.4 211.8 %all-to-all-start.1 = ((bf16[8,288,2048]{2,0,1:T(8,128)(2,1)}), bf16[8,288,2048]{2,0,1:T(8,128)(2,1)}, u32[]{:S(2)}, u32[]{:S(2)}) async-start(bf16[8,288,2048]{2,0,1:T(8,128)(2,1)} %copy.101), calls=%async_computation.2 | async-start | bytes 18874368 | tf_op jit(solution)/shard_map/all_to_all | solution.py:213
  1350.5 154.0 %copy-start.70 = (s32[2048,1]{0,1:T(1,128)S(1)}, s32[2048,1]{0,1:T(1,128)}, u32[]{:S(2)}) copy-start(s32[2048,1]{0,1:T(1,128)} %copy-done.69) | copy-start | bytes 24580
  1499.2 211.5 %all-to-all-start.3 = ((bf16[8,288,2048]{2,0,1:T(8,128)(2,1)}), bf16[8,288,2048]{2,0,1:T(8,128)(2,1)}, u32[]{:S(2)}, u32[]{:S(2)}) async-start(bf16[8,288,2048]{2,0,1:T(8,128)(2,1)} %copy.106), calls=%async_computation.4 | async-start | bytes 18874368 | tf_op jit(solution)/shard_map/all_to_all | solution.py:244
  1504.3 324.4 %all-gather.28.cloned.1.call-start = ((), (), s32[]{:S(2)}) async-start(), calls=%async_computation.22 | async-start | bytes 5242880 | tf_op jit(solution)/shard_map/all_gather | solution.py:264
  1562.3 208.8 %copy-start.51 = (bf16[256,64]{0,1:T(8,128)(2,1)}, bf16[256,64]{0,1:T(8,128)(2,1)S(1)}, u32[]{:S(2)}) copy-start(bf16[256,64]{0,1:T(8,128)(2,1)S(1)} %fusion.98) | copy-start | bytes 98308
  1777.9 331.8 %reduce-scatter.14.cloned.1.call-start = ((), (), s32[]{:S(2)}) async-start(), calls=%async_computation.24 | async-start | bytes 2359296 | tf_op jit(solution)/shard_map/reduce_scatter | solution.py:376
  1934.1 177.5 %reduce-scatter.12.cloned.1.call-start = ((), (), s32[]{:S(2)}) async-start(), calls=%async_computation.23 | async-start | bytes 2359296 | tf_op jit(solution)/shard_map/reduce_scatter | solution.py:373
  1941.9 171.5 %reduce-scatter.18.cloned.1.call-start = ((), (), s32[]{:S(2)}) async-start(), calls=%async_computation.26 | async-start | bytes 2359296 | tf_op jit(solution)/shard_map/reduce_scatter | solution.py:382
  1947.8 167.3 %reduce-scatter.16.cloned.1.call-start = ((), (), s32[]{:S(2)}) async-start(), calls=%async_computation.25 | async-start | bytes 2359296 | tf_op jit(solution)/shard_map/reduce_scatter | solution.py:379
  1956.1 232.1 %all-reduce.16.cloned.1.call-start = ((), (), s32[]{:S(2)}) async-start(), calls=%async_computation.31 | async-start | bytes 8454144
  1988.5 233.3 %reduce-scatter.26.cloned.1.call-start = ((), (), s32[]{:S(2)}) async-start(), calls=%async_computation.30 | async-start | bytes 294912 | tf_op jit(solution)/shard_map/reduce_scatter | solution.py:388
  1990.7 521.1 %reduce-scatter.24.cloned.1.call-start = ((), (), s32[]{:S(2)}) async-start(), calls=%async_computation.29 | async-start | bytes 41943040 | tf_op jit(solution)/shard_map/reduce_scatter | solution.py:241
  2046.6 757.0 %reduce-scatter.20.cloned.1.call-start = ((), (), s32[]{:S(2)}) async-start(), calls=%async_computation.27 | async-start | bytes 41943040 | tf_op jit(solution)/shard_map/reduce_scatter | solution.py:235
  2076.8 1018.5 %reduce-scatter.22.cloned.1.call-start = ((), (), s32[]{:S(2)}) async-start(), calls=%async_computation.28 | async-start | bytes 41943040 | tf_op jit(solution)/shard_map/reduce_scatter | solution.py:238
  2106.6 82.4 %copy-start.77 = (bf16[2048]{0:T(1024)(128)(2,1)S(1)}, bf16[2048]{0:T(1024)(128)(2,1)}, u32[]{:S(2)}) copy-start(bf16[2048]{0:T(1024)(128)(2,1)} %get-tuple-element.225) | copy-start | bytes 12292
  2107.3 135.4 %copy-start.26 = (f32[256,2048]{1,0:T(8,128)S(1)}, f32[256,2048]{1,0:T(8,128)}, u32[]{:S(2)}) copy-start(f32[256,2048]{1,0:T(8,128)} %get-tuple-element.279) | copy-start | bytes 6291460
  (88 other events, 935.9 us)
Sparse Core Ops, SparseCore 0:
  9.9 55.3 all-gather.11
  66.9 29.0 all-gather.13
  97.6 28.5 all-gather.15
  127.7 28.5 all-gather.17
  157.8 30.3 all-gather.19
  204.1 85.6 reduce-scatter.9
  291.8 297.0 all-gather.23
  590.9 297.0 all-gather.21
  890.1 297.2 all-gather.25
  1778.1 50.6 all-gather.27
  1934.2 35.7 reduce-scatter.13
  1972.8 34.3 reduce-scatter.11
  2009.6 34.4 reduce-scatter.17
  2046.4 34.4 reduce-scatter.15
  2085.0 103.1 all-reduce.15
  2191.0 30.7 reduce-scatter.25
  2224.7 287.0 reduce-scatter.23
  2515.0 288.5 reduce-scatter.19
  2806.7 288.5 reduce-scatter.21
where the time goes:
time: 3120 us; the launch traced here: 3110 us
  waiting for transfers between devices  2060 us (66%)
  matrix products  450 us (14%)
  local copies, waits for them, and re-layouts  282 us (9%)
  other arithmetic  157 us (5%)
  blocking collectives  117 us (4%)
    reduce_scatter x1, waiting for transfers between devices, local(): lax.psum_scatter(up_terms.astype(jnp.bfloat16), 'row', scatter_dimension=...  281 us
    reduce_scatter x1, waiting for transfers between devices, local(): lax.psum_scatter(gate_terms.astype(jnp.bfloat16), 'row', scatter_dimensio...  280 us
    all_gather x1, waiting for transfers between devices, expert_weights(): lax.all_gather(down_weight, 'row', axis=1, tiled=True)  267 us
    reduce_scatter x1, waiting for transfers between devices, local(): lax.psum_scatter(down_terms.astype(jnp.bfloat16), 'row', scatter_dimensio...  266 us
    all_to_all x1, waiting for transfers between devices, local(): lax.all_to_all(outgoing, 'col', split_axis=0, concat_axis=1, tiled=True)  212 us
    all_to_all x1, waiting for transfers between devices, local(): lax.all_to_all(outgoing_grad, 'col', split_axis=0, concat_axis=1, tiled=T...  206 us
    all_to_all x1, waiting for transfers between devices, local(): lax.all_to_all(expert_out, 'col', split_axis=1, concat_axis=0, tiled=True)  149 us
    dot_general x8, matrix products, outer_cols(): lax.dot_general(left, right, (((1,), (1,)), ((), ())), preferred_element_...  144 us
  transfers between devices with their start and end apart: 23, of which 16 were waited for; matrix products, arithmetic and copies ran while one was open for 19% of the time, Pallas kernels for 0%

commit v1 on v0

--- a/solution.py
+++ b/solution.py
@@ -1,10 +1,13 @@
 import jax
 import jax.numpy as jnp
 from jax import lax
+from jax.experimental import pallas as pl
+from jax.experimental.pallas import tpu as pltpu
 from jax.sharding import PartitionSpec as P
 
 HD = 128
-CAP = 36
+SLOTS = 40
+BLOCK = 512
 
 
 EPS = 1e-05
@@ -54,21 +57,82 @@
     return gradient * cosine + back_turned
 
 
-def expert_back(
-    expert_rows, expert_grads, gate_in, up_in, activated_rows, gate_mat, up_mat, down_mat
-):
-    sigmoid_val = jax.nn.sigmoid(gate_in)
-    silu_val = gate_in * sigmoid_val
-    grad_act = outer_cols(expert_grads, down_mat)
-    grad_up = (grad_act * silu_val).astype(jnp.bfloat16)
-    grad_gate = (grad_act * up_in * sigmoid_val * (1.0 + gate_in * (1.0 - sigmoid_val))).astype(
-        jnp.bfloat16
-    )
-    grad_down_mat = inner_rows(activated_rows, expert_grads)
-    grad_gate_mat = inner_rows(expert_rows, grad_gate)
-    grad_up_mat = inner_rows(expert_rows, grad_up)
-    grad_rows_val = outer_cols(grad_gate, gate_mat) + outer_cols(grad_up, up_mat)
-    return (grad_rows_val.astype(jnp.bfloat16), grad_gate_mat, grad_up_mat, grad_down_mat)
+def dispatch_body(pick_ref, field_ref, rows_ref):
+    groups = rows_ref.shape[0]
+    first = wide_dot(pick_ref[0], field_ref[0]).reshape(groups, SLOTS, -1)
+    second = wide_dot(pick_ref[1], field_ref[1]).reshape(groups, SLOTS, -1)
+    rows_ref[...] = jnp.concatenate([first, second], axis=1).astype(jnp.bfloat16)
+
+
+def dispatch(pick, field):
+    ranks, width, tokens = pick.shape
+    groups, depth = width // SLOTS, field.shape[1]
+    return pl.pallas_call(
+        dispatch_body,
+        grid=(ranks // 2, depth // BLOCK),
+        in_specs=[
+            pl.BlockSpec((2, width, tokens), lambda i, k: (i, 0, 0)),
+            pl.BlockSpec((2, tokens, BLOCK), lambda i, k: (i, 0, k)),
+        ],
+        out_specs=pl.BlockSpec((groups, 2 * SLOTS, BLOCK), lambda i, k: (0, i, k)),
+        out_shape=jax.ShapeDtypeStruct((groups, ranks * SLOTS, depth), jnp.bfloat16),
+    )(pick, field.reshape(ranks, tokens, depth))
+
+
+def combine_body(spread_ref, rows_ref, field_ref):
+    rows = rows_ref[...].astype(jnp.float32)
+    width = rows.shape[0] * SLOTS
+    for side in range(2):
+        part = rows[:, side * SLOTS : (side + 1) * SLOTS].reshape(width, -1).astype(jnp.bfloat16)
+        field_ref[side] = wide_dot(spread_ref[side], part).astype(jnp.bfloat16)
+
+
+def combine(spread, rows):
+    ranks, tokens, width = spread.shape
+    groups, depth = width // SLOTS, rows.shape[2]
+    field = pl.pallas_call(
+        combine_body,
+        grid=(ranks // 2, depth // BLOCK),
+        in_specs=[
+            pl.BlockSpec((2, tokens, width), lambda i, k: (i, 0, 0)),
+            pl.BlockSpec((groups, 2 * SLOTS, BLOCK), lambda i, k: (0, i, k)),
+        ],
+        out_specs=pl.BlockSpec((2, tokens, BLOCK), lambda i, k: (i, 0, k)),
+        out_shape=jax.ShapeDtypeStruct((ranks, tokens, depth), jnp.bfloat16),
+    )(spread, rows)
+    return field.reshape(ranks * tokens, depth)
+
+
+def scatter_all(field):
+    part = lax.psum_scatter(field, "col", scatter_dimension=0, tiled=True)
+    return lax.psum_scatter(part, "row", scatter_dimension=0, tiled=True)
+
+
+def pieces_of(ranks, depth):
+    count = max(1, ranks // 32)
+    step = depth // count
+    return [(at, at + step) for at in range(0, depth, step)]
+
+
+def gather_rows(pick, field):
+    rows = []
+    for start, stop in pieces_of(pick.shape[0], field.shape[1]):
+        part = field[:, start:stop]
+        if rows:
+            part = lax.optimization_barrier((part, rows[-1]))[0]
+        whole = lax.all_gather(part, ("col", "row"), axis=0, tiled=True)
+        rows.append(dispatch(pick, whole))
+    return rows[0] if len(rows) == 1 else jnp.concatenate(rows, axis=2)
+
+
+def return_rows(spread, rows):
+    sums = []
+    for start, stop in pieces_of(spread.shape[0], rows.shape[2]):
+        part = rows[:, :, start:stop]
+        if sums:
+            part = lax.optimization_barrier((part, sums[-1]))[0]
+        sums.append(scatter_all(combine(spread, part)))
+    return sums[0] if len(sums) == 1 else jnp.concatenate(sums, axis=1)
 
 
 def local(
@@ -167,8 +231,8 @@
     mixed_heads = mixed_blocks.reshape(length, local_width).astype(jnp.bfloat16)
     lse_all = jnp.moveaxis(lse_blocks, 0, 1).reshape(local_heads, length)
     branch = lax.psum_scatter(
-        wide_dot(mixed_heads, output_full), "row", scatter_dimension=0, tiled=True
-    )
+        wide_dot(mixed_heads, output_full).astype(jnp.bfloat16), "row", scatter_dimension=0, tiled=True
+    ).astype(jnp.float32)
     hidden = layer_input.astype(jnp.float32) + branch
     feed_scale = rms_scale(hidden)
     feed_float = feed_full.astype(jnp.float32)
@@ -178,77 +242,73 @@
     logit_exp = jnp.exp(logits - logit_top)
     router_probs = logit_exp / jnp.sum(logit_exp, axis=-1, keepdims=True)
     experts = router_full.shape[1]
-    top_count = expert_index.shape[1]
-    flat_index = expert_index.reshape(-1)
-    onehot = (flat_index[:, None] == jnp.arange(experts, dtype=jnp.int32)[None, :]).astype(
-        jnp.int32
-    )
-    running = jnp.cumsum(onehot, axis=0, dtype=jnp.int32) - 1
-    slot_rank = jnp.sum(running * onehot, axis=-1, dtype=jnp.int32)
-    slot_index = flat_index * CAP + slot_rank
-    pick_table = onehot.astype(jnp.float32).reshape(tokens, top_count, experts)
-    gate_probs = jnp.einsum("tje,te->tj", pick_table, router_probs)
-    entries = jnp.arange(tokens * top_count, dtype=jnp.int32)
-    slot_source = (
-        jnp.full((experts * CAP,), tokens * top_count, jnp.int32).at[slot_index].set(entries)
-    )
-    padded = jnp.concatenate([feed_normed, jnp.zeros((1, model_width), jnp.bfloat16)], axis=0)
-    outgoing = padded[slot_source // top_count].reshape(experts, CAP, model_width)
-    incoming = lax.all_to_all(outgoing, "col", split_axis=0, concat_axis=1, tiled=True)
-
-    def expert_weights():
-        return (
-            lax.all_gather(gate_weight, "row", axis=2, tiled=True),
-            lax.all_gather(up_weight, "row", axis=2, tiled=True),
-            lax.all_gather(down_weight, "row", axis=1, tiled=True),
-        )
-
-    gate_full, up_full, down_full = expert_weights()
-    gate_val = jnp.einsum("erd,edf->erf", incoming, gate_full, preferred_element_type=jnp.float32)
-    up_val = jnp.einsum("erd,edf->erf", incoming, up_full, preferred_element_type=jnp.float32)
-    activated = (jax.nn.silu(gate_val) * up_val).astype(jnp.bfloat16)
-    expert_out = jnp.einsum(
-        "erf,efd->erd", activated, down_full, preferred_element_type=jnp.float32
-    ).astype(jnp.bfloat16)
-    returned = lax.all_to_all(expert_out, "col", split_axis=1, concat_axis=0, tiled=True)
-    picked = (
-        returned.reshape(experts * CAP, model_width)[slot_index]
-        .reshape(tokens, top_count, model_width)
-        .astype(jnp.float32)
-    )
-    mixture = jnp.einsum("tj,tjd->td", gate_probs, picked)
+    experts_local = gate_weight.shape[0]
+    ranks = lax.axis_size("col") * rows_count
+    gate_hits = expert_index[:, :, None] == jnp.arange(experts, dtype=jnp.int32)
+    gate_probs = jnp.sum(jnp.where(gate_hits, router_probs[:, None, :], 0.0), axis=-1)
+
+    index_all = lax.all_gather(expert_index, ("col", "row"), axis=0, tiled=True)
+    probs_all = lax.all_gather(gate_probs, ("col", "row"), axis=0, tiled=True)
+    own = (index_all - lax.axis_index("col") * experts_local).reshape(ranks, tokens, -1)
+    matches = own[..., None] == jnp.arange(experts_local, dtype=jnp.int32)
+    hit = jnp.sum(matches.astype(jnp.float32), axis=2)
+    earlier = jnp.tril(jnp.ones((tokens, tokens), jnp.bfloat16), -1)
+    rank = jnp.einsum(
+        "tu,sue->ste", earlier, hit.astype(jnp.bfloat16), preferred_element_type=jnp.float32
+    )
+    slot = jnp.where(hit > 0, rank, -1.0)
+    places = jnp.arange(SLOTS, dtype=jnp.float32)
+    slot_t = jnp.swapaxes(slot, 1, 2)
+    width = experts_local * SLOTS
+    pick = (slot_t[:, :, None, :] == places[None, None, :, None]).astype(jnp.bfloat16)
+    pick = pick.reshape(ranks, width, tokens)
+    spread = slot[:, :, :, None] == places
+    probs_own = jnp.sum(
+        jnp.where(matches, probs_all.reshape(ranks, tokens, -1, 1), 0.0), axis=2
+    )
+    spread_plain = spread.astype(jnp.bfloat16).reshape(ranks, tokens, width)
+    spread_probs = (
+        jnp.where(spread, probs_own[..., None], 0.0).astype(jnp.bfloat16).reshape(ranks, tokens, width)
+    )
+    row_probs = jnp.sum(jnp.where(spread, probs_own[..., None], 0.0), axis=1)
+    row_probs = jnp.swapaxes(row_probs, 0, 1).reshape(experts_local, ranks * SLOTS, 1)
+
+    expert_grads = gather_rows(pick, cotangent)
+    expert_rows = gather_rows(pick, feed_normed)
+    gate_val = jnp.einsum("erd,edf->erf", expert_rows, gate_weight, preferred_element_type=jnp.float32)
+    up_val = jnp.einsum("erd,edf->erf", expert_rows, up_weight, preferred_element_type=jnp.float32)
+    plain_act = jnp.einsum("erd,efd->erf", expert_grads, down_weight, preferred_element_type=jnp.float32)
+    sigmoid_val = jax.nn.sigmoid(gate_val)
+    silu_val = gate_val * sigmoid_val
+    activated = silu_val * up_val
+    grad_act = plain_act * row_probs
+    grad_up = (grad_act * silu_val).astype(jnp.bfloat16)
+    grad_gate = (
+        grad_act * up_val * sigmoid_val * (1.0 + gate_val * (1.0 - sigmoid_val))
+    ).astype(jnp.bfloat16)
+    row_gates = jnp.sum(activated * plain_act, axis=-1).reshape(experts_local, ranks, 1, SLOTS)
+    weighted_act = (activated * row_probs).astype(jnp.bfloat16)
+    activated = activated.astype(jnp.bfloat16)
+    own_gates = jnp.sum(jnp.where(spread, jnp.transpose(row_gates, (1, 2, 0, 3)), 0.0), axis=-1)
+    own_gates = lax.psum_scatter(
+        own_gates.reshape(-1, rows_count, tokens, experts_local), "row", scatter_dimension=1
+    )
+    grad_probs = lax.all_to_all(own_gates, "col", split_axis=0, concat_axis=2, tiled=True)[0]
+
+    back_rows = (
+        jnp.einsum("erf,edf->erd", grad_gate, gate_weight, preferred_element_type=jnp.float32)
+        + jnp.einsum("erf,edf->erd", grad_up, up_weight, preferred_element_type=jnp.float32)
+    ).astype(jnp.bfloat16)
+    grad_feed = return_rows(spread_plain, back_rows).astype(jnp.float32)
+    out_rows = jnp.einsum(
+        "erf,efd->erd", activated, down_weight, preferred_element_type=jnp.float32
+    ).astype(jnp.bfloat16)
+    mixture = return_rows(spread_probs, out_rows).astype(jnp.float32)
     layer_output = hidden + mixture
+    grad_gate_weight = jnp.einsum("erd,erf->edf", expert_rows, grad_gate, preferred_element_type=jnp.float32)
+    grad_up_weight = jnp.einsum("erd,erf->edf", expert_rows, grad_up, preferred_element_type=jnp.float32)
+    grad_down_weight = jnp.einsum("erf,erd->efd", weighted_act, expert_grads, preferred_element_type=jnp.float32)
     grad_out = cotangent.astype(jnp.float32)
-    grad_gates = jnp.einsum("td,tjd->tj", grad_out, picked)
-    grad_picked = (
-        (gate_probs[:, :, None] * grad_out[:, None, :])
-        .astype(jnp.bfloat16)
-        .reshape(tokens * top_count, model_width)
-    )
-    grad_padded = jnp.concatenate([grad_picked, jnp.zeros((1, model_width), jnp.bfloat16)], axis=0)
-    outgoing_grad = grad_padded[slot_source].reshape(experts, CAP, model_width)
-    incoming_grad = lax.all_to_all(outgoing_grad, "col", split_axis=0, concat_axis=1, tiled=True)
-    gate_full, up_full, down_full = expert_weights()
-    grad_rows_all, gate_terms, up_terms, down_terms = jax.vmap(expert_back)(
-        incoming, incoming_grad, gate_val, up_val, activated, gate_full, up_full, down_full
-    )
-    grad_gate_weight = lax.psum_scatter(
-        gate_terms.astype(jnp.bfloat16), "row", scatter_dimension=2, tiled=True
-    ).astype(jnp.float32)
-    grad_up_weight = lax.psum_scatter(
-        up_terms.astype(jnp.bfloat16), "row", scatter_dimension=2, tiled=True
-    ).astype(jnp.float32)
-    grad_down_weight = lax.psum_scatter(
-        down_terms.astype(jnp.bfloat16), "row", scatter_dimension=1, tiled=True
-    ).astype(jnp.float32)
-    returned_grad = lax.all_to_all(grad_rows_all, "col", split_axis=1, concat_axis=0, tiled=True)
-    grad_slots = (
-        returned_grad.reshape(experts * CAP, model_width)[slot_index]
-        .reshape(tokens, top_count, model_width)
-        .astype(jnp.float32)
-    )
-    grad_feed = jnp.sum(grad_slots, axis=1)
-    grad_probs = jnp.einsum("tj,tje->te", grad_gates, pick_table)
     grad_logits = (
         router_probs * (grad_probs - jnp.sum(router_probs * grad_probs, axis=-1, keepdims=True))
     ).astype(jnp.bfloat16)

time: 3120 us -> 2170 us (0.70)
  waiting for transfers between devices: 2060 us -> 1030 us
  Pallas kernels: 0 us -> 233 us
  local copies, waits for them, and re-layouts: 282 us -> 81.3 us
  blocking collectives: 117 us -> 274 us
  matrix products: 450 us -> 384 us
  other arithmetic: 157 us -> 122 us
    all_to_all x4 -> x0, waiting for transfers between devices: 708 us -> none  [the longest x1 212 us: local(): lax.all_to_all(outgoing, 'col', split_axis=0, concat_axis=1, tiled=True)]
    pallas_call x0 -> x4, Pallas kernels: none -> 233 us  [the longest x2 120 us: combine(): pl.pallas_call(combine_body, grid=(ranks // 2, depth // BLOCK), in_specs=...]
    all_gather x3 -> x2, waiting for transfers between devices: 294 us -> 93.8 us  [gather_rows(): whole = lax.all_gather(part, ('col', 'row'), axis=0, tiled=True)]
    reduce_scatter x4 -> x5, waiting for transfers between devices: 856 us -> 685 us  [the longest x2 542 us: scatter_all(): part = lax.psum_scatter(field, 'col', scatter_dimension=0, tiled=True)]
    dot_general x6 -> x10, matrix products: 99.2 us -> 267 us  [the longest x1 45.2 us: local(): jnp.einsum('erf,edf->erd', grad_up, up_weight, preferred_element_type=jnp...]
    all_gather x0 -> x2, blocking collectives: none -> 138 us  [the longest x1 71.2 us: local(): index_all = lax.all_gather(expert_index, ('col', 'row'), axis=0, tiled=True)]
    dot_general x8 -> x5, matrix products: 137 us -> 22.1 us  [inner_rows(): lax.dot_general(left, right, (((0,), (0,)), ((), ())), preferred_element_...]
    dot_general x8 -> x5, matrix products: 144 us -> 32.3 us  [outer_cols(): lax.dot_general(left, right, (((1,), (1,)), ((), ())), preferred_element_...]
  transfers between devices with their start and end apart: 23 -> 20, of which waited for: 16 -> 14; matrix products, arithmetic and copies ran while one was open for 19% -> 17% of each run, Pallas kernels for 0% -> 5%
where the time goes in v1:
time: 2170 us; the launch traced here: 2150 us
  waiting for transfers between devices  1030 us (47%)
  matrix products  384 us (18%)
  blocking collectives  274 us (13%)
  Pallas kernels  233 us (11%)
  other arithmetic  122 us (6%)
  local copies, waits for them, and re-layouts  81.3 us (4%)
    reduce_scatter x2, waiting for transfers between devices, scatter_all(): part = lax.psum_scatter(field, 'col', scatter_dimension=0, tiled=True)  542 us
    pallas_call x2, Pallas kernels, combine(): pl.pallas_call(combine_body, grid=(ranks // 2, depth // BLOCK), in_specs=...  120 us
    pallas_call x2, Pallas kernels, dispatch(): pl.pallas_call(dispatch_body, grid=(ranks // 2, depth // BLOCK), in_specs...  113 us
    unnamed x22, waiting for transfers between devices  96.8 us
    reduce_scatter x2, waiting for transfers between devices, scatter_all(): return lax.psum_scatter(part, 'row', scatter_dimension=0, tiled=True)  95.5 us
    all_gather x2, waiting for transfers between devices, gather_rows(): whole = lax.all_gather(part, ('col', 'row'), axis=0, tiled=True)  93.8 us
    all_gather x1, blocking collectives, local(): index_all = lax.all_gather(expert_index, ('col', 'row'), axis=0, tiled=True)  71.2 us
    all_gather x1, blocking collectives, local(): probs_all = lax.all_gather(gate_probs, ('col', 'row'), axis=0, tiled=True)  66.8 us
  transfers between devices with their start and end apart: 20, of which 14 were waited for; matrix products, arithmetic and copies ran while one was open for 17% of the time, Pallas kernels for 5%

profile of v1, /device:TPU:0, one launch (start us, length us, event | category | flops | bytes accessed | tf_op | source)
XLA Modules:
  0.0 2148.6 jit_solution(9300335369729344317)
XLA Ops:
  47.4 18.7 all-gather.11.cloned.1.call-done
  69.8 27.1 %all-gather.17.cloned.1.call-done = bf16[2048,512]{1,0:T(8,128)(2,1)} async-done(((bf16[256,512]{1,0:T(8,128)(2,1)}), bf16[2048,512]{1,0:T(8,128)(2,1)}) %all-gather.17.cloned.1.call-update) | async-done | bytes 2097168 | tf_op jit(solution)/shard_map/all_gather | solution.py:173
  102.9 24.2 %all-gather.15.cloned.1.call-done = bf16[2048,512]{1,0:T(8,128)(2,1)} async-done(((bf16[256,512]{1,0:T(8,128)(2,1)}), bf16[2048,512]{1,0:T(8,128)(2,1)}) %all-gather.15.cloned.1.call-update) | async-done | bytes 2097168 | tf_op jit(solution)/shard_map/all_gather | solution.py:172
  132.5 24.7 %all-gather.13.cloned.1.call-done = bf16[2048,512]{1,0:T(8,128)(2,1)} async-done(((bf16[256,512]{1,0:T(8,128)(2,1)}), bf16[2048,512]{1,0:T(8,128)(2,1)}) %all-gather.13.cloned.1.call-update) | async-done | bytes 2097168 | tf_op jit(solution)/shard_map/all_gather | solution.py:171
  192.9 24.2 %while.30 = (s32[]{:T(128)}, bf16[2,512,4,128]{3,1,2,0:T(8,128)(2,1)}, f32[2,4,512]{2,1,0:T(4,128)S(1)}, s32[2]{0:T(128)S(1)}, bf16[1024,4,128]{2,0,1:T(8,128)(2...) while((s32[]{:T(128)}, ...), condition=%wide.region_8.9_spmd.clone.clone, body=%wide.region_5.8_spmd.clone.sunk.clone | while | flops 1099430400 | bytes 39391432 | solution.py:230
  238.2 47.3 %reduce-scatter.12.cloned.1.call-done = bf16[256,2048]{1,0:T(8,128)(2,1)} async-done(((bf16[1024,2048]{1,0:T(8,128)(2,1)}), bf16[256,2048]{1,0:T(8,128)(2,1)}) %reduce-scatter.12.cloned.1.call-update) | async-done | bytes 1048592 | tf_op jit(solution)/shard_map/reduce_scatter | solution.py:233
  291.0 24.1 %all_gather.55 = bf16[2048,64]{0,1:T(8,128)(2,1)S(1)} all-gather(bf16[256,64]{0,1:T(8,128)(2,1)S(1)} %copy-done.61), channel_id=1, replica_groups=mesh['row'=4,'col'=8] {'col'}, dimensions={0}, use_global_device_ids=true | all-gather | bytes 294912 | tf_op jit(solution)/shard_map/all_gather | solution.py:176
  315.2 71.2 %all_gather.53 = s32[8192,8]{0,1:T(8,128)S(1)} all-gather(s32[256,8]{0,1:T(8,128)S(1)} %copy-done.62), channel_id=1, replica_groups=mesh['row'=4,'col'=8] {'col','row'}, dimensions={0}, use_global_device_ids=true | all-gather | bytes 270336 | tf_op jit(solution)/shard_map/all_gather | solution.py:250
  388.2 66.8 %all_gather.56 = f32[8192,8]{0,1:T(8,128)S(1)} all-gather(f32[256,8]{0,1:T(8,128)S(1)} %select_reduce_fusion.3), channel_id=1, replica_groups=mesh['row'=4,'col'=8] {'col','row'}, dimensions={0}, use_global_device_ids=true | all-gather | bytes 270336 | tf_op jit(solution)/shard_map/all_gather | solution.py:251
  487.3 56.8 %shard_map.256 = bf16[8,1280,2048]{2,1,0:T(8,128)(2,1)} custom-call(bf16[32,320,256]{2,1,0:T(8,128)(2,1)} %fusion.38.pick_ref, bf16[32,256,2048]{2,1,0:T(8,128)(2,1)} %bitcast.203), custom_call_target="tpu_custom_call" | custom-call | tf_op jit(solution)/shard_map/pallas_call | solution.py:70
  544.1 93.8 %all-gather.21.cloned.1.call-done = bf16[8192,2048]{1,0:T(8,128)(2,1)} async-done(((bf16[256,2048]{1,0:T(8,128)(2,1)}), bf16[8192,2048]{1,0:T(8,128)(2,1)}) %all-gather.21.cloned.1.call-update) | async-done | bytes 33554448 | tf_op jit(solution)/shard_map/all_gather | solution.py:123
  637.8 56.3 %shard_map.254 = bf16[8,1280,2048]{2,1,0:T(8,128)(2,1)} custom-call(bf16[32,320,256]{2,1,0:T(8,128)(2,1)} %fusion.38.pick_ref, bf16[32,256,2048]{2,1,0:T(8,128)(2,1)} %bitcast.204), custom_call_target="tpu_custom_call" | custom-call | tf_op jit(solution)/shard_map/pallas_call | solution.py:70
  694.1 24.8 %fusion.96 = f32[8,1280,256]{1,2,0:T(8,128)} fusion(bf16[8,1280,2048]{2,1,0:T(8,128)(2,1)} %shard_map.254, bf16[8,2048,256]{2,1,0:T(8,128)(2,1)} %param.32), kind=kOutput, calls=%fused_computation.194 | convolution fusion | flops 10737418240 | bytes 60817408 | tf_op jit(solution)/shard_map/erd,edf->erf/dot_general | solution.py:279
  718.9 24.8 %fusion.95 = f32[8,1280,256]{1,2,0:T(8,128)} fusion(bf16[8,1280,2048]{2,1,0:T(8,128)(2,1)} %shard_map.254, bf16[8,2048,256]{2,1,0:T(8,128)(2,1)} %param.31), kind=kOutput, calls=%fused_computation.193 | convolution fusion | flops 10737418240 | bytes 60817408 | tf_op jit(solution)/shard_map/erd,edf->erf/dot_general | solution.py:278
  743.8 29.6 %multiply_reduce_fusion.1 = (f32[8,1280]{1,0:T(8,128)S(1)}, f32[8,1280,256]{1,2,0:T(8,128)}) fusion(f32[8,1280,256]{1,2,0:T(8,128)} %fusion.96, f32[8,1280,256]{1,2,0:T(8,128)} %fusion.95, bf16[8,1280,2048]{2,1,0:T(8,128)(2,1)} %shard_map.256, bf16[8,256,2048]{2,1,0:T(8,128)(2,1)} %param.33), kind=kOutput, calls=%fused_computation.58 | convolution fusion | flops 10755758080 | bytes 81829888 | tf_op jit(solution)/shard_map/erd,efd->erf/dot_general | solution.py:280
  793.3 33.9 %fusion.97 = f32[8,1280,2048]{2,1,0:T(8,128)} fusion(bf16[8,1280,256]{1,2,0:T(8,128)(2,1)} %get-tuple-element.327, bf16[8,2048,256]{2,1,0:T(8,128)(2,1)} %param.31), kind=kOutput, calls=%fused_computation.195 | convolution fusion | flops 10737418240 | bytes 97517568 | tf_op jit(solution)/shard_map/erf,edf->erd/dot_general | solution.py:299
  827.2 45.2 %add_convert_fusion.rows_ref = bf16[8,1280,2048]{2,1,0:T(8,128)(2,1)} fusion(f32[8,1280,2048]{2,1,0:T(8,128)} %fusion.97, bf16[8,1280,256]{1,2,0:T(8,128)(2,1)} %get-tuple-element.326, bf16[8,2048,256]{2,1,0:T(8,128)(2,1)} %param.32), kind=kOutput, calls=%fused_computation.47 | convolution fusion | flops 10779361280 | bytes 139460608 | tf_op jit(solution)/shard_map/erf,edf->erd/dot_general | solution.py:300
  872.4 59.9 %shard_map.257 = bf16[32,256,2048]{2,1,0:T(8,128)(2,1)} custom-call(bf16[32,256,320]{2,1,0:T(8,128)(2,1)} %get-tuple-element.318.spread_ref, bf16[8,1280,2048]{2,1,0:T(8,128)(2,1)} %add_convert_fusion.rows_ref), custom_call_target="tpu_custom_call" | custom-call | tf_op jit(solution)/shard_map/pallas_call | solution.py:93
  952.0 27.4 %convolution_convert_fusion.rows_ref = bf16[8,1280,2048]{2,1,0:T(8,128)(2,1)} fusion(bf16[8,256,2048]{2,1,0:T(8,128)(2,1)} %param.33, f32[8,1280,256]{1,2,0:T(8,128)} %fusion.96, f32[8,1280,256]{1,2,0:T(8,128)} %fusion.95), kind=kOutput, calls=%fused_computation.48 | convolution fusion | flops 10774118400 | bytes 71303168 | tf_op jit(solution)/shard_map/erf,efd->erd/dot_general | solution.py:303
  979.4 60.2 %shard_map.255 = bf16[32,256,2048]{2,1,0:T(8,128)(2,1)} custom-call(bf16[32,256,320]{2,1,0:T(8,128)(2,1)} %select_convert_fusion.spread_ref, bf16[8,1280,2048]{2,1,0:T(8,128)(2,1)} %convolution_convert_fusion.rows_ref), custom_call_target="tpu_custom_call" | custom-call | tf_op jit(solution)/shard_map/pallas_call | solution.py:93
  1040.4 215.8 %reduce-scatter.18.cloned.1.call-done = bf16[1024,2048]{1,0:T(8,128)(2,1)} async-done(((bf16[8192,2048]{1,0:T(8,128)(2,1)}), bf16[1024,2048]{1,0:T(8,128)(2,1)}) %reduce-scatter.18.cloned.1.call-update) | async-done | bytes 4194320 | tf_op jit(solution)/shard_map/reduce_scatter | solution.py:107
  1256.3 326.2 %reduce-scatter.14.cloned.1.call-done = bf16[1024,2048]{1,0:T(8,128)(2,1)} async-done(((bf16[8192,2048]{1,0:T(8,128)(2,1)}), bf16[1024,2048]{1,0:T(8,128)(2,1)}) %reduce-scatter.14.cloned.1.call-update) | async-done | bytes 4194320 | tf_op jit(solution)/shard_map/reduce_scatter | solution.py:107
  1583.1 44.4 %all-reduce.16.cloned.1.call-done = f32[8,4,256,8]{2,3,1,0:T(8,128)} async-done(((f32[8,4,256,8]{2,3,1,0:T(8,128)}), f32[8,4,256,8]{2,3,1,0:T(8,128)}) %all-reduce.16.cloned.1.call-update) | async-done | bytes 262160
  1639.5 43.6 %reduce-scatter.20.cloned.1.call-done = bf16[256,2048]{1,0:T(8,128)(2,1)} async-done(((bf16[1024,2048]{1,0:T(8,128)(2,1)}), bf16[256,2048]{1,0:T(8,128)(2,1)}) %reduce-scatter.20.cloned.1.call-update) | async-done | bytes 1048592 | tf_op jit(solution)/shard_map/reduce_scatter | solution.py:108
  1687.2 51.9 %reduce-scatter.16.cloned.1.call-done = bf16[256,2048]{1,0:T(8,128)(2,1)} async-done(((bf16[1024,2048]{1,0:T(8,128)(2,1)}), bf16[256,2048]{1,0:T(8,128)(2,1)}) %reduce-scatter.16.cloned.1.call-update) | async-done | bytes 1048592 | tf_op jit(solution)/shard_map/reduce_scatter | solution.py:108
  1744.3 52.8 %all-gather.25.cloned.1.call-done = bf16[1024,2048]{1,0:T(8,128)(2,1)} async-done(((bf16[256,2048]{1,0:T(8,128)(2,1)}), bf16[1024,2048]{1,0:T(8,128)(2,1)}) %all-gather.25.cloned.1.call-update) | async-done | bytes 4194320 | tf_op jit(solution)/shard_map/all_gather | solution.py:324
  1809.7 42.2 %while.31 = (s32[]{:T(128)}, f32[1024,4,128]{0,2,1:T(8,128)S(1)}, f32[1024,4,128]{0,2,1:T(8,128)}, f32[2,512,4,128]{3,1,2,0:T(8,128)}, s32[2]{0:T(128)S(1)}, /*i...) while((s32[]{:T(128)}, f32[1024,4,128]{0,2,1:T(8,128)S(1)}, ...), condition=%wide.region_28.29_spmd.clone.clone, body=%wide.region_26.28_spmd.clone.sunk.clone | while | flops 2719218176 | bytes 109113680 | solution.py:361
  1915.2 25.8 %fusion.101 = f32[8,2048,256]{2,1,0:T(8,128)} fusion(bf16[8,1280,2048]{2,1,0:T(8,128)(2,1)} %shard_map.254, bf16[8,1280,256]{1,2,0:T(8,128)(2,1)} %get-tuple-element.326), kind=kOutput, calls=%fused_computation.199 | convolution fusion | flops 10737418240 | bytes 63963136 | tf_op jit(solution)/shard_map/erd,erf->edf/dot_general | solution.py:309
  1974.1 29.6 %fusion.48 = f32[8,256,2048]{2,1,0:T(8,128)} fusion(bf16[8,1280,2048]{2,1,0:T(8,128)(2,1)} %shard_map.256, f32[8,1280]{1,0:T(8,128)S(1)} %copy-done.44, f32[8,1280,256]{1,2,0:T(8,128)} %fusion.96, f32[8,1280,256]{1,2,0:T(8,128)} %fusion.95), kind=kOutput, calls=%fused_computation.77 | convolution fusion | flops 10755768320 | bytes 79732736 | tf_op jit(solution)/shard_map/erf,erd->efd/dot_general | solution.py:310
  2004.8 25.6 %fusion.100 = f32[8,2048,256]{2,1,0:T(8,128)} fusion(bf16[8,1280,2048]{2,1,0:T(8,128)(2,1)} %shard_map.254, bf16[8,1280,256]{1,2,0:T(8,128)(2,1)} %get-tuple-element.327), kind=kOutput, calls=%fused_computation.198 | convolution fusion | flops 10737418240 | bytes 63963136 | tf_op jit(solution)/shard_map/erd,erf->edf/dot_general | solution.py:308
  2037.8 47.9 %all-reduce.18.cloned.1.call-done = bf16[1028,2048]{1,0:T(8,128)(2,1)} async-done(((bf16[1028,2048]{1,0:T(8,128)(2,1)}), bf16[1028,2048]{1,0:T(8,128)(2,1)}) %all-reduce.18.cloned.1.call-update) | async-done | bytes 4210704
  2086.5 28.6 %all-reduce.9 = (bf16[2048]{0:T(1024)(128)(2,1)S(1)}, bf16[512]{0:T(512)(128)(2,1)S(1)}, bf16[512]{0:T(512)(128)(2,1)S(1)}, bf16[2048]{0:T(1024)(128)(2,1)S(1)}) all-reduce(bf16[2048]{0:T(1024)(128)(2,1)S(1)} %dynamic-slice_reduce_fusion, bf16[512]{0:T(512)(128)(2,1)S(1)} %get-tuple-element.263, ...), channel_id=9, replica_groups=mesh['row'=4,'col'=8] {'col'}, use_global_device_ids=true, to_apply=%region_36.37.clone | all-reduce | flops 5120 | bytes 20480
  (380 shorter events, 411.9 us)
Async XLA Ops:
  8.0 58.1 %all-gather.11.cloned.1.call-start = ((), (), s32[]{:S(2)}) async-start(), calls=%async_computation.11 | async-start | bytes 5242880 | tf_op jit(solution)/shard_map/all_gather | solution.py:178
  8.7 88.1 %all-gather.17.cloned.1.call-start = ((), (), s32[]{:S(2)}) async-start(), calls=%async_computation.14 | async-start | bytes 2359296 | tf_op jit(solution)/shard_map/all_gather | solution.py:173
  9.5 117.6 %all-gather.15.cloned.1.call-start = ((), (), s32[]{:S(2)}) async-start(), calls=%async_computation.13 | async-start | bytes 2359296 | tf_op jit(solution)/shard_map/all_gather | solution.py:172
  10.2 146.9 %all-gather.13.cloned.1.call-start = ((), (), s32[]{:S(2)}) async-start(), calls=%async_computation.12 | async-start | bytes 2359296 | tf_op jit(solution)/shard_map/all_gather | solution.py:171
  10.8 210.2 %all-gather.19.cloned.1.call-start = ((), (), s32[]{:S(2)}) async-start(), calls=%async_computation.15 | async-start | bytes 2359296 | tf_op jit(solution)/shard_map/all_gather | solution.py:174
  11.4 274.1 %reduce-scatter.12.cloned.1.call-start = ((), (), s32[]{:S(2)}) async-start(), calls=%async_computation.16 | async-start | bytes 5242880 | tf_op jit(solution)/shard_map/reduce_scatter | solution.py:233
  227.3 259.9 %all-gather.23.cloned.1.call-start = ((), (), s32[]{:S(2)}) async-start(), calls=%async_computation.20 | async-start | bytes 34603008 | tf_op jit(solution)/shard_map/all_gather | solution.py:123
  227.9 409.9 %all-gather.21.cloned.1.call-start = ((), (), s32[]{:S(2)}) async-start(), calls=%async_computation.17 | async-start | bytes 34603008 | tf_op jit(solution)/shard_map/all_gather | solution.py:123
  238.2 149.9 %copy-start.49 = (f32[8,1,256]{2,1,0:T(1,128)}, f32[8,1,256]{2,1,0:T(1,128)S(1)}, u32[]{:S(2)}) copy-start(f32[8,1,256]{2,1,0:T(1,128)S(1)} %convert_element_type.256) | copy-start | bytes 24580
  290.9 965.3 %reduce-scatter.18.cloned.1.call-start = ((), (), s32[]{:S(2)}) async-start(), calls=%async_computation.21 | async-start | bytes 37748736 | tf_op jit(solution)/shard_map/reduce_scatter | solution.py:107
  932.3 650.2 %reduce-scatter.14.cloned.1.call-start = ((), (), s32[]{:S(2)}) async-start(), calls=%async_computation.18 | async-start | bytes 37748736 | tf_op jit(solution)/shard_map/reduce_scatter | solution.py:107
  1039.6 587.9 %all-reduce.16.cloned.1.call-start = ((), (), s32[]{:S(2)}) async-start(), calls=%async_computation.29 | async-start | bytes 524288
  1040.4 642.7 %reduce-scatter.20.cloned.1.call-start = ((), (), s32[]{:S(2)}) async-start(), calls=%async_computation.22 | async-start | bytes 5242880 | tf_op jit(solution)/shard_map/reduce_scatter | solution.py:108
  1256.2 326.4 %copy-start.80 = (u32[32]{0:T(128)S(1)}, u32[32]{0:T(128)}, u32[]{:S(2)}) copy-start(u32[32]{0:T(128)} %constant.104) | copy-start | bytes 388
  1256.2 383.2 %copy-start.38 = (f32[256,64]{0,1:T(8,128)S(1)}, f32[256,64]{0,1:T(8,128)}, u32[]{:S(2)}) copy-start(f32[256,64]{0,1:T(8,128)} %copy-done.37) | copy-start | bytes 196612
  1256.2 383.2 %copy-start.66 = (f32[256]{0:T(256)S(1)}, f32[256]{0:T(256)}, u32[]{:S(2)}) copy-start(f32[256]{0:T(256)} %copy-done.65) | copy-start | bytes 3076
  1256.2 383.2 %copy-start.68 = (f32[256]{0:T(256)S(1)}, f32[256]{0:T(256)}, u32[]{:S(2)}) copy-start(f32[256]{0:T(256)} %copy-done.67) | copy-start | bytes 3076
  1256.2 426.9 %copy-start.17 = (bf16[256,2048]{1,0:T(8,128)(2,1)S(1)}, bf16[256,2048]{1,0:T(8,128)(2,1)}, u32[]{:S(2)}) copy-start(bf16[256,2048]{1,0:T(8,128)(2,1)} %param.19) | copy-start | bytes 3145732
  1256.2 426.9 %copy-start.20 = (bf16[256,2048]{1,0:T(8,128)(2,1)S(1)}, bf16[256,2048]{1,0:T(8,128)(2,1)}, u32[]{:S(2)}) copy-start(bf16[256,2048]{1,0:T(8,128)(2,1)} %reduce-scatter.12.cloned.1.call-done) | copy-start | bytes 3145732
  1256.2 426.9 %copy-start.40 = (bf16[2048,64]{0,1:T(8,128)(2,1)S(1)}, bf16[2048,64]{0,1:T(8,128)(2,1)}, u32[]{:S(2)}) copy-start(bf16[2048,64]{0,1:T(8,128)(2,1)} %copy-done.39) | copy-start | bytes 786436
  1256.2 426.9 %copy-start.50 = (f32[8,1,256]{2,1,0:T(1,128)S(1)}, f32[8,1,256]{2,1,0:T(1,128)}, u32[]{:S(2)}) copy-start(f32[8,1,256]{2,1,0:T(1,128)} %copy-done.49) | copy-start | bytes 24580
  1256.2 426.9 %copy-start.73 = (f32[256]{0:T(256)S(1)}, f32[256]{0:T(256)}, u32[]{:S(2)}) copy-start(f32[256]{0:T(256)} %copy-done.72) | copy-start | bytes 3076
  1256.3 482.8 %reduce-scatter.16.cloned.1.call-start = ((), (), s32[]{:S(2)}) async-start(), calls=%async_computation.19 | async-start | bytes 5242880 | tf_op jit(solution)/shard_map/reduce_scatter | solution.py:108
  1582.5 156.6 %copy-start.32 = (bf16[256,2048]{1,0:T(8,128)(2,1)S(1)}, bf16[256,2048]{1,0:T(8,128)(2,1)}, u32[]{:S(2)}) copy-start(bf16[256,2048]{1,0:T(8,128)(2,1)} %param.20) | copy-start | bytes 3145732
  1582.5 156.6 %copy-start.74 = (f32[256]{0:T(256)S(1)}, f32[256]{0:T(256)}, u32[]{:S(2)}) copy-start(f32[256]{0:T(256)} %get-tuple-element.347) | copy-start | bytes 3076
  1582.5 214.6 %all-gather.25.cloned.1.call-start = ((), (), s32[]{:S(2)}) async-start(), calls=%async_computation.23 | async-start | bytes 5242880 | tf_op jit(solution)/shard_map/all_gather | solution.py:324
  1744.2 286.2 %reduce-scatter.28.cloned.1.call-start = ((), (), s32[]{:S(2)}) async-start(), calls=%async_computation.27 | async-start | bytes 2359296 | tf_op jit(solution)/shard_map/reduce_scatter | solution.py:442
  1803.3 229.0 %reduce-scatter.26.cloned.1.call-start = ((), (), s32[]{:S(2)}) async-start(), calls=%async_computation.26 | async-start | bytes 2359296 | tf_op jit(solution)/shard_map/reduce_scatter | solution.py:439
  1861.2 173.0 %reduce-scatter.24.cloned.1.call-start = ((), (), s32[]{:S(2)}) async-start(), calls=%async_computation.25 | async-start | bytes 2359296 | tf_op jit(solution)/shard_map/reduce_scatter | solution.py:436
  1905.9 130.0 %reduce-scatter.22.cloned.1.call-start = ((), (), s32[]{:S(2)}) async-start(), calls=%async_computation.24 | async-start | bytes 2359296 | tf_op jit(solution)/shard_map/reduce_scatter | solution.py:433
  1915.1 170.6 %all-reduce.18.cloned.1.call-start = ((), (), s32[]{:S(2)}) async-start(), calls=%async_computation.30 | async-start | bytes 8454144
  1973.4 145.1 %reduce-scatter.30.cloned.1.call-start = ((), (), s32[]{:S(2)}) async-start(), calls=%async_computation.28 | async-start | bytes 294912 | tf_op jit(solution)/shard_map/reduce_scatter | solution.py:448
  (76 other events, 1816.5 us)
Sparse Core Ops, SparseCore 0:
  10.7 55.3 all-gather.10
  67.7 29.0 all-gather.16
  98.5 28.5 all-gather.14
  128.5 28.5 all-gather.12
  158.6 30.3 all-gather.18
  227.4 57.9 reduce-scatter.11
  932.4 323.6 reduce-scatter.17
  1258.5 323.8 reduce-scatter.13
  1586.2 41.2 all-reduce.15
  1630.4 52.6 reduce-scatter.19
  1686.3 52.6 reduce-scatter.15
  1744.3 52.6 all-gather.24
  1803.4 35.7 reduce-scatter.27
  1861.3 35.7 reduce-scatter.25
  1906.0 35.7 reduce-scatter.23
  1944.6 34.6 reduce-scatter.21
  1982.4 103.1 all-reduce.17
  2087.8 30.7 reduce-scatter.29
Sparse Core Ops, SparseCore 1:
  231.1 211.0 all-gather.22
  445.4 192.4 all-gather.20

commit v2 on v1

--- a/solution.py
+++ b/solution.py
@@ -1,3 +1,5 @@
+import functools
+
 import jax
 import jax.numpy as jnp
 from jax import lax
@@ -8,6 +10,8 @@
 HD = 128
 SLOTS = 40
 BLOCK = 512
+CHUNK = 256
+UNROLL = 4
 
 
 EPS = 1e-05
@@ -133,6 +137,477 @@
             part = lax.optimization_barrier((part, sums[-1]))[0]
         sums.append(scatter_all(combine(spread, part)))
     return sums[0] if len(sums) == 1 else jnp.concatenate(sums, axis=1)
+
+
+MESH = pl.DeviceIdType.MESH
+
+
+def seat():
+    r, c = lax.axis_index("row"), lax.axis_index("col")
+    y, x = r // 2, r % 2
+    z, core = c // 2, c % 2
+    first = y * (1 - core) + x * core
+    second = x * (1 - core) + y * core
+    return r, c, y, x, z, core, first, second
+
+
+def partners():
+    r, c, y, x, z, core, first, second = seat()
+    pair = (r, z * 2 + (1 - core))
+    flip_y = (1 - y) * 2 + x
+    flip_x = y * 2 + (1 - x)
+    along_first = (flip_y * (1 - core) + flip_x * core, c)
+    along_second = (flip_x * (1 - core) + flip_y * core, c)
+    up = [(r, ((z + k) % 4) * 2 + core) for k in range(1, 4)]
+    return pair, along_first, along_second, up
+
+
+RANKS = 32
+
+
+def nth(offset):
+    spot = (lax.axis_index("col") * 4 + lax.axis_index("row") + offset) % RANKS
+    return spot, (spot % 4, spot // 4)
+
+
+def meet():
+    barrier = pltpu.get_barrier_semaphore()
+
+    @pl.loop(1, RANKS)
+    def _(offset):
+        pl.semaphore_signal(barrier, inc=1, device_id=nth(offset)[1], device_id_type=MESH)
+
+    pl.semaphore_wait(barrier, RANKS - 1)
+
+
+def small_copy(src_of, small_all, small_send, small_recv, offset):
+    spot, device = nth(offset)
+    return send(
+        src_of(spot), small_all.at[nth(0)[0]], small_send.at[offset], small_recv.at[offset], device
+    )
+
+
+def row_of(core, first, second):
+    y = first * (1 - core) + second * core
+    x = second * (1 - core) + first * core
+    return y, x
+
+
+def send(src, dst, send_sem, recv_sem, device):
+    return pltpu.make_async_remote_copy(
+        src_ref=src, dst_ref=dst, send_sem=send_sem, recv_sem=recv_sem, device_id=device, device_id_type=MESH
+    )
+
+
+GSTEPS = 4
+
+
+def gather_body(own_ref, small_ref, all_ref, small_all, here_sem, small_here, small_send, small_recv, z_send, z_recv, g_send, g_recv, f_send, f_recv, p_send, p_recv):
+    r, c, y, x, z, core, first, second = seat()
+    pair, along_first, along_second, up = partners()
+    tokens = own_ref.shape[0]
+    step = tokens // GSTEPS
+
+    def rows(q):
+        return pl.ds(pl.multiple_of(q * step, step), step)
+
+    def place(zz, f, s, q):
+        yy, xx = row_of(core, f, s)
+        return all_ref.at[zz, core, yy, xx, rows(q)]
+
+    meet()
+    here = pltpu.make_async_copy(own_ref, all_ref.at[z, core, y, x], here_sem)
+    here.start()
+    small_local = pltpu.make_async_copy(small_ref, small_all.at[nth(0)[0]], small_here)
+    small_local.start()
+
+    def small(offset):
+        return small_copy(lambda spot: small_ref, small_all, small_send, small_recv, offset)
+
+    @pl.loop(1, RANKS)
+    def _(offset):
+        small(offset).start()
+
+    def z_copy(k, q):
+        return send(own_ref.at[rows(q)], place(z, first, second, q), z_send.at[k - 1, q], z_recv.at[k - 1, q], up[k - 1])
+
+    def g_copy(k, q, src):
+        zz = (z + 4 - k) % 4
+        return send(src, place(zz, first, second, q), g_send.at[k, q], g_recv.at[k, q], along_second)
+
+    def f_copy(k, s, q, src):
+        zz = (z + 4 - k) % 4
+        sec = second * (1 - s) + (1 - second) * s
+        return send(src, place(zz, first, sec, q), f_send.at[s, k, q], f_recv.at[s, k, q], along_first)
+
+    def p_copy(k, s, f, q, src):
+        zz = (z + 4 - k) % 4
+        sec = second * (1 - s) + (1 - second) * s
+        fir = first * (1 - f) + (1 - first) * f
+        return send(src, place(zz, fir, sec, q), p_send.at[f, s, k, q], p_recv.at[f, s, k, q], pair)
+
+    def out_of(k, s, f, q):
+        zz = (z + 4 - k) % 4
+        sec = second * (1 - s) + (1 - second) * s
+        fir = first * (1 - f) + (1 - first) * f
+        return place(zz, fir, sec, q)
+
+    @pl.loop(0, GSTEPS)
+    def _(q):
+        src = own_ref.at[rows(q)]
+        for k in (2, 1, 3):
+            z_copy(k, q).start()
+        g_copy(0, q, src).start()
+        f_copy(0, 0, q, src).start()
+        p_copy(0, 0, 0, q, src).start()
+
+    @pl.loop(0, GSTEPS)
+    def _(q):
+        for k in (1, 3, 2):
+            z_copy(k, q).wait_recv()
+            src = out_of(k, 0, 0, q)
+            g_copy(k, q, src).start()
+            f_copy(k, 0, q, src).start()
+            p_copy(k, 0, 0, q, src).start()
+        for k in (0, 1, 3, 2):
+            src = out_of(k, 1, 0, q)
+            g_copy(k, q, src).wait_recv()
+            f_copy(k, 1, q, src).start()
+            p_copy(k, 1, 0, q, src).start()
+        for k in (0, 1, 3, 2):
+            src = out_of(k, 0, 1, q)
+            f_copy(k, 0, q, src).wait_recv()
+            p_copy(k, 0, 1, q, src).start()
+
+    @pl.loop(0, GSTEPS)
+    def _(q):
+        for k in (0, 1, 3, 2):
+            src = out_of(k, 1, 1, q)
+            f_copy(k, 1, q, src).wait_recv()
+            p_copy(k, 1, 1, q, src).start()
+
+    here.wait()
+    small_local.wait()
+
+    @pl.loop(1, RANKS)
+    def _(offset):
+        small(offset).wait()
+
+    @pl.loop(0, GSTEPS)
+    def _(q):
+        for k in range(4):
+            src = own_ref.at[rows(q)]
+            if k:
+                z_copy(k, q).wait_send()
+            g_copy(k, q, src).wait_send()
+            for s in range(2):
+                f_copy(k, s, q, src).wait_send()
+                for f in range(2):
+                    p_copy(k, s, f, q, src).wait()
+
+
+def gather_near(own, small, collective_id):
+    tokens, depth = own.shape
+    dma = pltpu.SemaphoreType.DMA
+    out, small_out = pl.pallas_call(
+        gather_body,
+        out_shape=(
+            jax.ShapeDtypeStruct((4, 2, 2, 2, tokens, depth), own.dtype),
+            jax.ShapeDtypeStruct((RANKS, *small.shape), small.dtype),
+        ),
+        in_specs=[pl.BlockSpec(memory_space=pl.ANY)] * 2,
+        out_specs=[pl.BlockSpec(memory_space=pl.ANY)] * 2,
+        scratch_shapes=[
+            dma(()), dma(()), dma((RANKS,)), dma((RANKS,)),
+            dma((3, GSTEPS)), dma((3, GSTEPS)),
+            dma((4, GSTEPS)), dma((4, GSTEPS)),
+            dma((2, 4, GSTEPS)), dma((2, 4, GSTEPS)),
+            dma((2, 2, 4, GSTEPS)), dma((2, 2, 4, GSTEPS)),
+        ],
+        compiler_params=pltpu.CompilerParams(collective_id=collective_id, has_side_effects=True),
+    )(own, small)
+    return out.reshape(RANKS, tokens, depth), small_out
+
+
+RSTEPS = 8
+TILE = 16
+
+
+def reduce_body(part_ref, small_ref, out_ref, small_all, mine, pair_in, first_in, second_in, z_in, total,
+                load_sem, p_send, p_recv, f_send, f_recv, g_send, g_recv, z_send, z_recv, out_sem,
+                small_here, small_send, small_recv):
+    r, c, y, x, z, core, first, second = seat()
+    pair, along_first, along_second, up = partners()
+    tokens, depth = out_ref.shape
+    step = tokens // RSTEPS
+    other = 1 - core
+
+    def rows(q):
+        return pl.ds(pl.multiple_of(q * step, step), step)
+
+    meet()
+
+    small_local = pltpu.make_async_copy(small_ref.at[nth(0)[0]], small_all.at[nth(0)[0]], small_here)
+    small_local.start()
+
+    def small(offset):
+        return small_copy(lambda spot: small_ref.at[spot], small_all, small_send, small_recv, offset)
+
+    @pl.loop(1, RANKS)
+    def _(offset):
+        small(offset).start()
+
+    def load(f, s, q):
+        yy, xx = row_of(core, f, s)
+        return pltpu.make_async_copy(part_ref.at[:, core, yy, xx, rows(q)], mine.at[f, s, :, rows(q)], load_sem.at[f, s, q])
+
+    def give(f, s, q):
+        yy, xx = row_of(other, f, s)
+        return send(part_ref.at[:, other, yy, xx, rows(q)], pair_in.at[f, s, :, rows(q)],
+                    p_send.at[f, s, q], p_recv.at[f, s, q], pair)
+
+    def f_copy(s, q):
+        return send(mine.at[1 - first, s, :, rows(q)], first_in.at[s, :, rows(q)], f_send.at[s, q], f_recv.at[s, q], along_first)
+
+    def g_copy(q):
+        return send(mine.at[first, 1 - second, :, rows(q)], second_in.at[:, rows(q)], g_send.at[q], g_recv.at[q], along_second)
+
+    def z_copy(k, q):
+        return send(mine.at[first, second, (z + k) % 4, rows(q)], z_in.at[k - 1, rows(q)],
+                    z_send.at[k - 1, q], z_recv.at[k - 1, q], up[k - 1])
+
+    def order(me_first, me_second):
+        return [(1 - me_first, 1 - me_second), (1 - me_first, me_second), (me_first, 1 - me_second), (me_first, me_second)]
+
+    @pl.loop(0, RSTEPS)
+    def _(q):
+        for f, s in order(second, first):
+            give(f, s, q).start()
+        for f, s in order(first, second):
+            load(f, s, q).start()
+
+    def add_into(f, s, q, extra):
+        @pl.loop(0, 4 * (step // TILE))
+        def _(t):
+            zz, at = t // (step // TILE), t % (step // TILE)
+            here = pl.ds(pl.multiple_of(q * step + at * TILE, TILE), TILE)
+            value = mine[f, s, zz, here].astype(jnp.float32) + pair_in[f, s, zz, here].astype(jnp.float32)
+            for ref in extra:
+                value = value + ref[zz, here].astype(jnp.float32)
+            mine[f, s, zz, here] = value.astype(jnp.bfloat16)
+
+    def stage_first(q):
+        for s in (1 - second, second):
+            load(1 - first, s, q).wait()
+            give(1 - first, s, q).wait_recv()
+            add_into(1 - first, s, q, [])
+            f_copy(s, q).start()
+
+    def stage_second(q):
+        load(first, 1 - second, q).wait()
+        give(first, 1 - second, q).wait_recv()
+        f_copy(1 - second, q).wait_recv()
+        add_into(first, 1 - second, q, [first_in.at[1 - second]])
+        g_copy(q).start()
+
+    def stage_z(q):
+        load(first, second, q).wait()
+        give(first, second, q).wait_recv()
+        f_copy(second, q).wait_recv()
+        g_copy(q).wait_recv()
+        add_into(first, second, q, [first_in.at[second], second_in])
+        for k in (2, 1, 3):
+            z_copy(k, q).start()
+
+    def stage_out(q):
+        for k in (1, 3, 2):
+            z_copy(k, q).wait_recv()
+
+        @pl.loop(0, step // TILE)
+        def _(t):
+            here = pl.ds(pl.multiple_of(q * step + t * TILE, TILE), TILE)
+            value = mine[first, second, z, here].astype(jnp.float32)
+            for k in range(3):
+                value = value + z_in[k, here].astype(jnp.float32)
+            total[here] = value
+
+    LAG1, LAG2, LAG3 = 1, 2, 4
+
+    @pl.loop(0, RSTEPS + LAG3)
+    def _(q):
+        @pl.when(q < RSTEPS)
+        def _():
+            stage_first(q)
+
+        @pl.when((q >= LAG1) & (q < RSTEPS + LAG1))
+        def _():
+            stage_second(q - LAG1)
+
+        @pl.when((q >= LAG2) & (q < RSTEPS + LAG2))
+        def _():
+            stage_z(q - LAG2)
+
+        @pl.when(q >= LAG3)
+        def _():
+            stage_out(q - LAG3)
+
+    done = pltpu.make_async_copy(total, out_ref, out_sem)
+    done.start()
+
+    @pl.loop(0, RSTEPS)
+    def _(q):
+        for f in range(2):
+            for s in range(2):
+                give(f, s, q).wait_send()
+        for s in range(2):
+            f_copy(s, q).wait_send()
+        g_copy(q).wait_send()
+        for k in (1, 2, 3):
+            z_copy(k, q).wait_send()
+
+    small_local.wait()
+
+    @pl.loop(1, RANKS)
+    def _(offset):
+        small(offset).wait()
+
+    done.wait()
+
+
+def reduce_near(part, small, collective_id):
+    tokens, depth = part.shape[0] // RANKS, part.shape[1]
+    dma = pltpu.SemaphoreType.DMA
+    return pl.pallas_call(
+        reduce_body,
+        out_shape=(
+            jax.ShapeDtypeStruct((tokens, depth), jnp.float32),
+            jax.ShapeDtypeStruct(small.shape, small.dtype),
+        ),
+        in_specs=[pl.BlockSpec(memory_space=pl.ANY)] * 2,
+        out_specs=[pl.BlockSpec(memory_space=pl.ANY)] * 2,
+        scratch_shapes=[
+            pltpu.VMEM((2, 2, 4, tokens, depth), jnp.bfloat16),
+            pltpu.VMEM((2, 2, 4, tokens, depth), jnp.bfloat16),
+            pltpu.VMEM((2, 4, tokens, depth), jnp.bfloat16),
+            pltpu.VMEM((4, tokens, depth), jnp.bfloat16),
+            pltpu.VMEM((3, tokens, depth), jnp.bfloat16),
+            pltpu.VMEM((tokens, depth), jnp.float32),
+            dma((2, 2, RSTEPS)),
+            dma((2, 2, RSTEPS)), dma((2, 2, RSTEPS)),
+            dma((2, RSTEPS)), dma((2, RSTEPS)),
+            dma((RSTEPS,)), dma((RSTEPS,)),
+            dma((3, RSTEPS)), dma((3, RSTEPS)),
+            dma(()),
+            dma(()), dma((RANKS,)), dma((RANKS,)),
+        ],
+        compiler_params=pltpu.CompilerParams(
+            collective_id=collective_id, has_side_effects=True, vmem_limit_bytes=60 * 1024 * 1024
+        ),
+    )(part.reshape(4, 2, 2, 2, tokens, depth), small)
+
+
+def project_body(flipped, pick_ref, field_ref, *refs):
+    count = len(flipped)
+    weights, (rows_ref, *outs), sums = refs[:count], refs[count:2*count+1], refs[2*count+1:]
+    k = pl.program_id(0)
+    ranks = pick_ref.shape[0]
+    groups = rows_ref.shape[0]
+
+    @pl.loop(0, ranks // 2, unroll=UNROLL)
+    def _(i):
+        parts = [
+            wide_dot(pick_ref[2 * i + side], field_ref[2 * i + side]).reshape(groups, SLOTS, CHUNK)
+            for side in range(2)
+        ]
+        rows_ref[:, pl.ds(pl.multiple_of(i * 2 * SLOTS, 2 * SLOTS), 2 * SLOTS)] = jnp.concatenate(parts, axis=1).astype(jnp.bfloat16)
+
+    def project(e, first):
+        rows = rows_ref[e]
+        for weight, flip, total in zip(weights, flipped, sums):
+            term = outer_cols(rows, weight[e]) if flip else wide_dot(rows, weight[e])
+            if first: total[e] = term
+            else: total[e] += term
+
+    @pl.when(k == 0)
+    def _():
+        @pl.loop(0, groups)
+        def _(e):
+            project(e, True)
+
+    @pl.when(k > 0)
+    def _():
+        @pl.loop(0, groups)
+        def _(e):
+            project(e, False)
+
+    @pl.when(k == pl.num_programs(0) - 1)
+    def _():
+        for out, total in zip(outs, sums):
+            pltpu.sync_copy(total, out)
+
+def project(pick, field, weights, flipped):
+    ranks, width, tokens = pick.shape
+    groups, depth = width // SLOTS, field.shape[-1]
+    length = ranks * SLOTS
+    inner = weights[0].shape[1] if flipped[0] else weights[0].shape[2]
+    wspecs = [pl.BlockSpec((groups, inner, CHUNK), lambda k: (0, 0, k)) if f else pl.BlockSpec((groups, CHUNK, inner), lambda k: (0, k, 0)) for f in flipped]
+    flops = 2 * groups * length * depth * (tokens + inner * len(weights))
+    return pl.pallas_call(
+        functools.partial(project_body, flipped),
+        grid=(depth // CHUNK,),
+        in_specs=[
+            pl.BlockSpec((ranks, width, tokens), lambda k: (0, 0, 0), pipeline_mode=pl.Buffered(1)),
+            pl.BlockSpec((ranks, tokens, CHUNK), lambda k: (0, 0, k)),
+            *wspecs,
+        ],
+        out_specs=[pl.BlockSpec((groups, length, CHUNK), lambda k: (0, 0, k))] + [pl.BlockSpec(memory_space=pl.ANY)] * len(weights),
+        out_shape=[jax.ShapeDtypeStruct((groups, length, depth), jnp.bfloat16)]
+        + [jax.ShapeDtypeStruct((groups, length, inner), jnp.float32)] * len(weights),
+        scratch_shapes=[pltpu.VMEM((groups, length, inner), jnp.float32)] * len(weights),
+        compiler_params=pltpu.CompilerParams(vmem_limit_bytes=63 * 1024 * 1024),
+        cost_estimate=pl.CostEstimate(flops=flops, bytes_accessed=120 << 20, transcendentals=0),
+    )(pick, field.reshape(ranks, tokens, depth), *weights)
+
+
+def restore_body(flipped, spread_ref, *refs):
+    count = len(flipped)
+    lefts, weights, field_ref, rows = refs[:count], refs[count:2*count], refs[2*count], refs[2*count+1]
+    groups = rows.shape[0]
+    ranks = spread_ref.shape[0]
+
+    @pl.loop(0, groups)
+    def _(e):
+        total = None
+        for left, weight, flip in zip(lefts, weights, flipped):
+            term = outer_cols(left[e], weight[e]) if flip else wide_dot(left[e], weight[e])
+            total = term if total is None else total + term
+        rows[e] = total
+
+    @pl.loop(0, ranks, unroll=2*UNROLL)
+    def _(s):
+        part = rows[:, pl.ds(pl.multiple_of(s * SLOTS, SLOTS), SLOTS)].reshape(groups * SLOTS, CHUNK).astype(jnp.bfloat16)
+        field_ref[s] = wide_dot(spread_ref[s], part).astype(jnp.bfloat16)
+
+def restore(spread, lefts, weights, flipped):
+    ranks, tokens, width = spread.shape
+    groups = width // SLOTS
+    length = ranks * SLOTS
+    inner = lefts[0].shape[2]
+    depth = weights[0].shape[1] if flipped[0] else weights[0].shape[2]
+    wspecs = [pl.BlockSpec((groups, CHUNK, inner), lambda k: (0, k, 0)) if f else pl.BlockSpec((groups, inner, CHUNK), lambda k: (0, 0, k)) for f in flipped]
+    flops = 2 * groups * length * depth * (tokens + inner * len(weights))
+    field = pl.pallas_call(
+        functools.partial(restore_body, flipped),
+        grid=(depth // CHUNK,),
+        in_specs=[pl.BlockSpec((ranks, tokens, width), lambda k: (0, 0, 0), pipeline_mode=pl.Buffered(1))]
+        + [pl.BlockSpec((groups, length, inner), lambda k: (0, 0, 0), pipeline_mode=pl.Buffered(1))] * len(lefts) + wspecs,
+        out_specs=pl.BlockSpec((ranks, tokens, CHUNK), lambda k: (0, 0, k)),
+        out_shape=jax.ShapeDtypeStruct((ranks, tokens, depth), jnp.bfloat16),
+        scratch_shapes=[pltpu.VMEM((groups, length, CHUNK), jnp.float32)],
+        compiler_params=pltpu.CompilerParams(vmem_limit_bytes=63 * 1024 * 1024),
+        cost_estimate=pl.CostEstimate(flops=flops, bytes_accessed=60 << 20, transcendentals=0),
+    )(spread, *lefts, *weights)
+    return field.reshape(ranks * tokens, depth)
 
 
 def local(
@@ -247,8 +722,12 @@
     gate_hits = expert_index[:, :, None] == jnp.arange(experts, dtype=jnp.int32)
     gate_probs = jnp.sum(jnp.where(gate_hits, router_probs[:, None, :], 0.0), axis=-1)
 
-    index_all = lax.all_gather(expert_index, ("col", "row"), axis=0, tiled=True)
-    probs_all = lax.all_gather(gate_probs, ("col", "row"), axis=0, tiled=True)
+    near = rows_count == 4 and lax.axis_size("col") == 8
+    if near:
+        cotangent_all, index_all = gather_near(cotangent, expert_index.T, 1)
+        index_all = jnp.swapaxes(index_all, 1, 2)
+    else:
+        index_all = lax.all_gather(expert_index, ("col", "row"), axis=0, tiled=True)
     own = (index_all - lax.axis_index("col") * experts_local).reshape(ranks, tokens, -1)
     matches = own[..., None] == jnp.arange(experts_local, dtype=jnp.int32)
     hit = jnp.sum(matches.astype(jnp.float32), axis=2)
@@ -263,21 +742,34 @@
     pick = (slot_t[:, :, None, :] == places[None, None, :, None]).astype(jnp.bfloat16)
     pick = pick.reshape(ranks, width, tokens)
     spread = slot[:, :, :, None] == places
+    spread_plain = spread.astype(jnp.bfloat16).reshape(ranks, tokens, width)
+    if near:
+        expert_grads, plain_act = project(pick, cotangent_all, [down_weight], (True,))
+        feed_all, probs_all = gather_near(feed_normed, gate_probs.T, 2)
+        probs_all = jnp.swapaxes(probs_all, 1, 2)
+        expert_rows, gate_val, up_val = project(
+            pick, feed_all, [gate_weight, up_weight], (False, False)
+        )
+    else:
+        probs_all = lax.all_gather(gate_probs, ("col", "row"), axis=0, tiled=True)
+        expert_grads = gather_rows(pick, cotangent)
+        expert_rows = gather_rows(pick, feed_normed)
+        gate_val = jnp.einsum(
+            "erd,edf->erf", expert_rows, gate_weight, preferred_element_type=jnp.float32
+        )
+        up_val = jnp.einsum(
+            "erd,edf->erf", expert_rows, up_weight, preferred_element_type=jnp.float32
+        )
+        plain_act = jnp.einsum(
+            "erd,efd->erf", expert_grads, down_weight, preferred_element_type=jnp.float32
+        )
     probs_own = jnp.sum(
         jnp.where(matches, probs_all.reshape(ranks, tokens, -1, 1), 0.0), axis=2
     )
-    spread_plain = spread.astype(jnp.bfloat16).reshape(ranks, tokens, width)
-    spread_probs = (
-        jnp.where(spread, probs_own[..., None], 0.0).astype(jnp.bfloat16).reshape(ranks, tokens, width)
-    )
-    row_probs = jnp.sum(jnp.where(spread, probs_own[..., None], 0.0), axis=1)
+    weighted = jnp.where(spread, probs_own[..., None], 0.0)
+    spread_probs = weighted.astype(jnp.bfloat16).reshape(ranks, tokens, width)
+    row_probs = jnp.sum(weighted, axis=1)
     row_probs = jnp.swapaxes(row_probs, 0, 1).reshape(experts_local, ranks * SLOTS, 1)
-
-    expert_grads = gather_rows(pick, cotangent)
-    expert_rows = gather_rows(pick, feed_normed)
-    gate_val = jnp.einsum("erd,edf->erf", expert_rows, gate_weight, preferred_element_type=jnp.float32)
-    up_val = jnp.einsum("erd,edf->erf", expert_rows, up_weight, preferred_element_type=jnp.float32)
-    plain_act = jnp.einsum("erd,efd->erf", expert_grads, down_weight, preferred_element_type=jnp.float32)
     sigmoid_val = jax.nn.sigmoid(gate_val)
     silu_val = gate_val * sigmoid_val
     activated = silu_val * up_val
@@ -290,24 +782,40 @@
     weighted_act = (activated * row_probs).astype(jnp.bfloat16)
     activated = activated.astype(jnp.bfloat16)
     own_gates = jnp.sum(jnp.where(spread, jnp.transpose(row_gates, (1, 2, 0, 3)), 0.0), axis=-1)
-    own_gates = lax.psum_scatter(
-        own_gates.reshape(-1, rows_count, tokens, experts_local), "row", scatter_dimension=1
-    )
-    grad_probs = lax.all_to_all(own_gates, "col", split_axis=0, concat_axis=2, tiled=True)[0]
-
-    back_rows = (
-        jnp.einsum("erf,edf->erd", grad_gate, gate_weight, preferred_element_type=jnp.float32)
-        + jnp.einsum("erf,edf->erd", grad_up, up_weight, preferred_element_type=jnp.float32)
-    ).astype(jnp.bfloat16)
-    grad_feed = return_rows(spread_plain, back_rows).astype(jnp.float32)
-    out_rows = jnp.einsum(
-        "erf,efd->erd", activated, down_weight, preferred_element_type=jnp.float32
-    ).astype(jnp.bfloat16)
-    mixture = return_rows(spread_probs, out_rows).astype(jnp.float32)
+    if near:
+        own_gates = jnp.swapaxes(own_gates, 1, 2)
+        grad_feed_part = restore(
+            spread_plain, [grad_gate, grad_up], [gate_weight, up_weight], (True, True)
+        )
+        grad_feed, gates_in = reduce_near(grad_feed_part, own_gates, 3)
+        gates_in = jnp.sum(gates_in.reshape(-1, rows_count, experts_local, tokens), axis=1)
+        grad_probs = gates_in.reshape(experts, tokens).T
+        mixture_part = restore(spread_probs, [activated], [down_weight], (False,))
+        mixture = reduce_near(mixture_part, own_gates, 3)[0]
+    else:
+        own_gates = lax.psum_scatter(
+            own_gates.reshape(-1, rows_count, tokens, experts_local), "row", scatter_dimension=1
+        )
+        grad_probs = lax.all_to_all(own_gates, "col", split_axis=0, concat_axis=2, tiled=True)[0]
+        back_rows = (
+            jnp.einsum("erf,edf->erd", grad_gate, gate_weight, preferred_element_type=jnp.float32)
+            + jnp.einsum("erf,edf->erd", grad_up, up_weight, preferred_element_type=jnp.float32)
+        ).astype(jnp.bfloat16)
+        grad_feed = return_rows(spread_plain, back_rows).astype(jnp.float32)
+        out_rows = jnp.einsum(
+            "erf,efd->erd", activated, down_weight, preferred_element_type=jnp.float32
+        ).astype(jnp.bfloat16)
+        mixture = return_rows(spread_probs, out_rows).astype(jnp.float32)
     layer_output = hidden + mixture
-    grad_gate_weight = jnp.einsum("erd,erf->edf", expert_rows, grad_gate, preferred_element_type=jnp.float32)
-    grad_up_weight = jnp.einsum("erd,erf->edf", expert_rows, grad_up, preferred_element_type=jnp.float32)
-    grad_down_weight = jnp.einsum("erf,erd->efd", weighted_act, expert_grads, preferred_element_type=jnp.float32)
+    grad_gate_weight = jnp.einsum(
+        "erd,erf->edf", expert_rows, grad_gate, preferred_element_type=jnp.float32
+    )
+    grad_up_weight = jnp.einsum(
+        "erd,erf->edf", expert_rows, grad_up, preferred_element_type=jnp.float32
+    )
+    grad_down_weight = jnp.einsum(
+        "erf,erd->efd", weighted_act, expert_grads, preferred_element_type=jnp.float32
+    )
     grad_out = cotangent.astype(jnp.float32)
     grad_logits = (
         router_probs * (grad_probs - jnp.sum(router_probs * grad_probs, axis=-1, keepdims=True))

time: 2170 us -> 1710 us (0.79)
  waiting for transfers between devices: 1030 us -> 242 us
  Pallas kernels: 233 us -> 896 us
  matrix products: 384 us -> 197 us
  blocking collectives: 274 us -> 118 us
  other arithmetic: 122 us -> 149 us
    pallas_call x4 -> x8, Pallas kernels: 233 us -> 896 us  [the longest x2 337 us: reduce_near(): pl.pallas_call(reduce_body, out_shape=(jax.ShapeDtypeStruct((tokens, dept...]
    reduce_scatter x4 -> x0, waiting for transfers between devices: 637 us -> none  [the longest x2 542 us: scatter_all(): part = lax.psum_scatter(field, 'col', scatter_dimension=0, tiled=True)]
    dot_general x6 -> x0, matrix products: 186 us -> none  [the longest x1 45.2 us: local(): jnp.einsum('erf,edf->erd', grad_up, up_weight, preferred_element_type=jnp...]
    all_gather x2 -> x0, blocking collectives: 138 us -> none  [the longest x1 71.2 us: local(): index_all = lax.all_gather(expert_index, ('col', 'row'), axis=0, tiled=True)]
    all_gather x2 -> x0, waiting for transfers between devices: 93.8 us -> none  [gather_rows(): whole = lax.all_gather(part, ('col', 'row'), axis=0, tiled=True)]
    reduce_scatter x1, waiting for transfers between devices: 47.3 us -> 0.02 us  [local(): lax.psum_scatter(wide_dot(mixed_heads, output_full).astype(jnp.bfloat16),...]
    all_gather x1, waiting for transfers between devices: 27.1 us -> 0.01 us  [local(): lax.all_gather(value_weight, 'col', axis=0, tiled=True)]
    unnamed x22 -> x14, waiting for transfers between devices: 96.8 us -> 108 us
  transfers between devices with their start and end apart: 20 -> 13, of which waited for: 14 -> 7; matrix products, arithmetic and copies ran while one was open for 17% -> 12% of each run, Pallas kernels for 5% -> 10%
where the time goes in v2:
time: 1710 us; the launch traced here: 1700 us
  Pallas kernels  896 us (52%)
  waiting for transfers between devices  242 us (14%)
  matrix products  197 us (12%)
  other arithmetic  149 us (9%)
  blocking collectives  118 us (7%)
  local copies, waits for them, and re-layouts  75.2 us (4%)
  between operations  18 us (1%)
    pallas_call x2, Pallas kernels, reduce_near(): pl.pallas_call(reduce_body, out_shape=(jax.ShapeDtypeStruct((tokens, dept...  337 us
    pallas_call x2, Pallas kernels, gather_near(): pl.pallas_call(gather_body, out_shape=(jax.ShapeDtypeStruct((4, 2, 2, 2,...  324 us
    pallas_call x2, Pallas kernels, restore(): pl.pallas_call(functools.partial(restore_body, flipped), grid=(depth // C...  119 us
    pallas_call x2, Pallas kernels, project(): pl.pallas_call(functools.partial(project_body, flipped), grid=(depth // C...  116 us
    unnamed x14, waiting for transfers between devices  108 us
    all_gather x1, waiting for transfers between devices, local(): lax.all_gather(grad_hidden.astype(jnp.bfloat16), 'row', axis=0, tiled=True)  52.1 us
    unnamed x2, blocking collectives  42.5 us
  transfers between devices with their start and end apart: 13, of which 7 were waited for; matrix products, arithmetic and copies ran while one was open for 12% of the time, Pallas kernels for 10%

profile of v2, /device:TPU:0, one launch (start us, length us, event | category | flops | bytes accessed | tf_op | source)
XLA Modules:
  0.0 1704.7 jit_solution(6334446194673299531)
XLA Ops:
  12.5 13.4 all-gather
  29.7 13.9 all-reduce.9
  47.6 17.7 %all-gather.9.cloned.1.call-done = bf16[1024,2048]{1,0:T(8,128)(2,1)} async-done(((bf16[256,2048]{1,0:T(8,128)(2,1)}), bf16[1024,2048]{1,0:T(8,128)(2,1)}) %all-gather.9.cloned.1.call-update) | async-done | bytes 4194320 | tf_op jit(solution)/shard_map/all_gather | solution.py:653
  69.0 27.1 %all-gather.11.cloned.1.call-done = bf16[2048,512]{1,0:T(8,128)(2,1)} async-done(((bf16[256,512]{1,0:T(8,128)(2,1)}), bf16[2048,512]{1,0:T(8,128)(2,1)}) %all-gather.11.cloned.1.call-update) | async-done | bytes 2097168 | tf_op jit(solution)/shard_map/all_gather | solution.py:646
  101.4 24.9 %all-gather.13.cloned.1.call-done = bf16[2048,512]{1,0:T(8,128)(2,1)} async-done(((bf16[256,512]{1,0:T(8,128)(2,1)}), bf16[2048,512]{1,0:T(8,128)(2,1)}) %all-gather.13.cloned.1.call-update) | async-done | bytes 2097168 | tf_op jit(solution)/shard_map/all_gather | solution.py:647
  132.9 10.1 all-reduce.7
  169.1 23.2 %while.30 = (s32[]{:T(128)}, bf16[2,512,4,128]{3,1,2,0:T(8,128)(2,1)}, f32[2,4,512]{2,1,0:T(4,128)S(1)}, s32[2]{0:T(128)S(1)}, bf16[1024,4,128]{2,0,1:T(8,128)(2...) while((s32[]{:T(128)}, ...), condition=%wide.region_8.9_spmd.clone.clone, body=%wide.region_5.8_spmd.clone.sunk.clone | while | flops 1099430400 | bytes 31003272 | solution.py:705
  203.0 10.2 all-gather.1
  213.4 172.8 %shard_map.254 = (bf16[4,2,2,2,256,2048]{5,4,3,2,1,0:T(8,128)(2,1)}, s32[32,8,256]{2,1,0:T(8,128)}) custom-call(bf16[256,2048]{1,0:T(8,128)(2,1)} %own_ref.1, s32[8,256]{1,0:T(8,128)} %bitcast.219), custom_call_target="tpu_custom_call" | custom-call | tf_op jit(solution)/shard_map/pallas_call | solution.py:312
  386.2 15.5 all_gather.42
  408.6 150.9 %shard_map.255 = (bf16[4,2,2,2,256,2048]{5,4,3,2,1,0:T(8,128)(2,1)}, f32[32,8,256]{2,1,0:T(8,128)}) custom-call(bf16[256,2048]{1,0:T(8,128)(2,1)} %copy-done.24, f32[8,256]{1,0:T(8,128)} %bitcast.220), custom_call_target="tpu_custom_call" | custom-call | tf_op jit(solution)/shard_map/pallas_call | solution.py:312
  564.9 52.0 %shard_map.258 = (bf16[8,1280,2048]{2,1,0:T(8,128)(2,1)}, f32[8,1280,256]{2,1,0:T(8,128)}) custom-call(bf16[32,320,256]{2,1,0:T(8,128)(2,1)} %fusion.38.pick_ref, bf16[32,256,2048]{2,1,0:T(8,128)(2,1)} %bitcast.221, bf16[8,256,2048]{2,1,0:T(8,128)(2,1)} %refs_0_.3), custom_call_target="tpu_custom_call" | custom-call | flops 21474836480 | bytes 125829120 | tf_op jit(solution)/shard_map/pallas_call | solution.py:555
  616.8 63.7 %shard_map.256 = (bf16[8,1280,2048]{2,1,0:T(8,128)(2,1)}, f32[8,1280,256]{2,1,0:T(8,128)}, f32[8,1280,256]{2,1,0:T(8,128)}) custom-call(bf16[32,320,256]{2,1,0:T(8,128)(2,1)} %fusion.38.pick_ref, bf16[32,256,2048]{2,1,0:T(8,128)(2,1)} %bitcast.222, bf16[8,2048,256]{2,1,0:T(8,128)(2,1)} %refs_2_.1, bf16[8,2048,256]{2,1,0:T(8,128)(2,1)} %refs_3_.1), custom_call_target="tpu_custom_call" | custom-call | flops 32212254720 | bytes 125829120 | tf_op jit(solution)/shard_map/pallas_call | solution.py:555
  680.6 15.2 multiply_reduce_fusion.1
  700.7 15.8 multiply_convert_fusion.2
  724.5 12.0 copy.145
  736.4 9.9 fusion.88
  764.9 52.0 %shard_map.257 = bf16[32,256,2048]{2,1,0:T(8,128)(2,1)} custom-call(bf16[32,256,320]{2,1,0:T(8,128)(2,1)} %select_convert_fusion.spread_ref, bf16[8,1280,256]{2,1,0:T(8,128)(2,1)} %convert_element_type.203.refs_0_, bf16[8,256,2048]{2,1,0:T(8,128)(2,1)} %refs_0_.3), custom_call_target="tpu_custom_call" | custom-call | flops 21474836480 | bytes 62914560 | tf_op jit(solution)/shard_map/pallas_call | solution.py:599
  816.9 176.3 %shard_map.259 = (f32[256,2048]{1,0:T(8,128)}, f32[32,8,256]{2,1,0:T(8,128)}) custom-call(bf16[4,2,2,2,256,2048]{5,4,3,2,1,0:T(8,128)(2,1)} %bitcast.188, f32[32,8,256]{2,1,0:T(8,128)} %bitcast.199), custom_call_target="tpu_custom_call" | custom-call | tf_op jit(solution)/shard_map/pallas_call | solution.py:480
  993.2 66.9 %shard_map.260 = bf16[32,256,2048]{2,1,0:T(8,128)(2,1)} custom-call(bf16[32,256,320]{2,1,0:T(8,128)(2,1)} %get-tuple-element.342.spread_ref, bf16[8,1280,256]{2,1,0:T(8,128)(2,1)} %get-tuple-element.353.refs_0_, bf16[8,1280,256]{2,1,0:T(8,128)(2,1)} %get-tuple-element.352.refs_1_, bf16[8,2048,256]{2,1,0:T(8,128)(2,1)} %refs_2_.1, bf16[8,2048,256]{2,1,0:T(8,128)(2,1)} %refs_3_.1), custom_call_target="tpu_custom_call" | custom-call | flops 32212254720 | bytes 62914560 | tf_op jit(solution)/shard_map/pallas_call | solution.py:599
  1060.2 161.0 %shard_map.261 = (f32[256,2048]{1,0:T(8,128)}, f32[32,8,256]{2,1,0:T(8,128)}) custom-call(bf16[4,2,2,2,256,2048]{5,4,3,2,1,0:T(8,128)(2,1)} %bitcast.189, f32[32,8,256]{2,1,0:T(8,128)} %bitcast.200), custom_call_target="tpu_custom_call" | custom-call | tf_op jit(solution)/shard_map/pallas_call | solution.py:480
  1230.3 52.1 %all-gather.19.cloned.1.call-done = bf16[1024,2048]{1,0:T(8,128)(2,1)} async-done(((bf16[256,2048]{1,0:T(8,128)(2,1)}), bf16[1024,2048]{1,0:T(8,128)(2,1)}) %all-gather.19.cloned.1.call-update) | async-done | bytes 4194320 | tf_op jit(solution)/shard_map/all_gather | solution.py:832
  1288.6 50.3 %while.31 = (s32[]{:T(128)}, f32[1024,4,128]{0,2,1:T(8,128)S(1)}, f32[1024,4,128]{0,2,1:T(8,128)}, f32[2,512,4,128]{3,1,2,0:T(8,128)}, s32[2]{0:T(128)S(1)}, /*i...) while((s32[]{:T(128)}, f32[1024,4,128]{0,2,1:T(8,128)S(1)}, ...), condition=%wide.region_24.25_spmd.clone.clone, body=%wide.region_22.24_spmd.clone.sunk.clone | while | flops 2719218176 | bytes 180417440 | solution.py:869
  1371.7 8.9 all-reduce.11
  1425.8 8.5 fusion.45
  1444.9 24.6 %fusion.97 = f32[8,2048,256]{2,1,0:T(8,128)} fusion(bf16[8,1280,2048]{2,1,0:T(8,128)(2,1)} %get-tuple-element.143, bf16[8,1280,256]{2,1,0:T(8,128)(2,1)} %get-tuple-element.352.refs_1_), kind=kOutput, calls=%fused_computation.193 | convolution fusion | flops 10737418240 | bytes 63963136 | tf_op jit(solution)/shard_map/erd,erf->edf/dot_general | solution.py:813
  1470.5 25.6 %fusion.48 = f32[8,256,2048]{2,1,0:T(8,128)} fusion(bf16[8,1280,2048]{2,1,0:T(8,128)(2,1)} %get-tuple-element.144, f32[8,1280,256]{2,1,0:T(8,128)} %get-tuple-element.345, f32[8,1280]{1,0:T(8,128)S(1)} %copy-done.48), kind=kOutput, calls=%fused_computation.75 | convolution fusion | flops 10742661120 | bytes 69246976 | tf_op jit(solution)/shard_map/erf,erd->efd/dot_general | solution.py:816
  1496.1 24.4 %fusion.96 = f32[8,2048,256]{2,1,0:T(8,128)} fusion(bf16[8,1280,2048]{2,1,0:T(8,128)(2,1)} %get-tuple-element.143, bf16[8,1280,256]{2,1,0:T(8,128)(2,1)} %get-tuple-element.353.refs_0_), kind=kOutput, calls=%fused_computation.192 | convolution fusion | flops 10737418240 | bytes 63963136 | tf_op jit(solution)/shard_map/erd,erf->edf/dot_general | solution.py:810
  1526.1 8.8 reduce-scatter.13.cloned.1.call-done
  1536.7 104.9 %all-reduce.14.cloned.1.call-done = bf16[1028,2048]{1,0:T(8,128)(2,1)} async-done(((bf16[1028,2048]{1,0:T(8,128)(2,1)}), bf16[1028,2048]{1,0:T(8,128)(2,1)}) %all-reduce.14.cloned.1.call-update) | async-done | bytes 4210704
  1642.4 28.6 %all-reduce.8 = (bf16[2048]{0:T(1024)(128)(2,1)S(1)}, bf16[512]{0:T(512)(128)(2,1)S(1)}, bf16[512]{0:T(512)(128)(2,1)S(1)}, bf16[2048]{0:T(1024)(128)(2,1)S(1)}) all-reduce(bf16[2048]{0:T(1024)(128)(2,1)S(1)} %dynamic-slice_reduce_fusion, bf16[512]{0:T(512)(128)(2,1)S(1)} %get-tuple-element.287, ...), channel_id=4, replica_groups=mesh['row'=4,'col'=8] {'col'}, use_global_device_ids=true, to_apply=%region_32.33.clone | all-reduce | flops 5120 | bytes 20480
  1674.7 17.1 %all-reduce.10 = (bf16[256]{0:T(256)(128)(2,1)S(1)}, bf16[256,64]{0,1:T(8,128)(2,1)S(1)}) all-reduce(bf16[256]{0:T(256)(128)(2,1)S(1)} %dynamic-slice.11, bf16[256,64]{0,1:T(8,128)(2,1)} %reduce-scatter.17.cloned.1.call-done), channel_id=1, replica_groups=mesh['row'=4,'col'=8] {'row'}, use_global_device_ids=true, to_apply=%region_42.43 | all-reduce | flops 16640 | bytes 66560 | tf_op jit(solution)/shard_map/psum | solution.py:887
  (369 shorter events, 293.5 us)
Async XLA Ops:
  7.2 58.1 %all-gather.9.cloned.1.call-start = ((), (), s32[]{:S(2)}) async-start(), calls=%async_computation.6 | async-start | bytes 5242880 | tf_op jit(solution)/shard_map/all_gather | solution.py:653
  7.9 88.1 %all-gather.11.cloned.1.call-start = ((), (), s32[]{:S(2)}) async-start(), calls=%async_computation.7 | async-start | bytes 2359296 | tf_op jit(solution)/shard_map/all_gather | solution.py:646
  8.7 117.6 %all-gather.13.cloned.1.call-start = ((), (), s32[]{:S(2)}) async-start(), calls=%async_computation.8 | async-start | bytes 2359296 | tf_op jit(solution)/shard_map/all_gather | solution.py:647
  9.4 147.1 %all-gather.15.cloned.1.call-start = ((), (), s32[]{:S(2)}) async-start(), calls=%async_computation.9 | async-start | bytes 2359296 | tf_op jit(solution)/shard_map/all_gather | solution.py:648
  10.0 186.1 %all-gather.17.cloned.1.call-start = ((), (), s32[]{:S(2)}) async-start(), calls=%async_computation.10 | async-start | bytes 2359296 | tf_op jit(solution)/shard_map/all_gather | solution.py:649
  10.6 392.3 %reduce-scatter.7.cloned.1.call-start = ((), (), s32[]{:S(2)}) async-start(), calls=%async_computation.11 | async-start | bytes 5242880 | tf_op jit(solution)/shard_map/reduce_scatter | solution.py:708
  25.9 130.6 %copy-start.53 = (f32[8,1,256]{2,1,0:T(1,128)}, f32[8,1,256]{2,1,0:T(1,128)S(1)}, u32[]{:S(2)}) copy-start(f32[8,1,256]{2,1,0:T(1,128)S(1)} %convert_element_type.239) | copy-start | bytes 24580
  43.6 106.4 %copy-start.61 = (f32[512]{0:T(512)}, f32[512]{0:T(512)S(1)}, u32[]{:S(2)}) copy-start(f32[512]{0:T(512)S(1)} %convert_element_type.190) | copy-start | bytes 6148
  202.4 183.8 %copy-start.64 = (bf16[256,64]{0,1:T(8,128)(2,1)S(1)}, bf16[256,64]{0,1:T(8,128)(2,1)}, u32[]{:S(2)}) copy-start(bf16[256,64]{0,1:T(8,128)(2,1)} %param.30) | copy-start | bytes 98308
  202.4 200.5 %copy-start.15 = (bf16[256,2048]{1,0:T(8,128)(2,1)S(1)}, bf16[256,2048]{1,0:T(8,128)(2,1)}, u32[]{:S(2)}) copy-start(bf16[256,2048]{1,0:T(8,128)(2,1)} %param.19) | copy-start | bytes 3145732
  202.4 1079.9 %all-gather.19.cloned.1.call-start = ((), (), s32[]{:S(2)}) async-start(), calls=%async_computation.12 | async-start | bytes 5242880 | tf_op jit(solution)/shard_map/all_gather | solution.py:832
  213.3 194.0 %copy-start.49 = (f32[8,1,256]{2,1,0:T(1,128)}, f32[8,1,256]{2,1,0:T(1,128)S(1)}, u32[]{:S(2)}) copy-start(f32[8,1,256]{2,1,0:T(1,128)S(1)} %convert_element_type.240) | copy-start | bytes 24580
  213.4 194.6 %copy-start.63 = (s32[256,8]{0,1:T(8,128)S(1)}, s32[256,8]{0,1:T(8,128)}, u32[]{:S(2)}) copy-start(s32[256,8]{0,1:T(8,128)} %param.21) | copy-start | bytes 24580
  401.8 157.8 %copy-start.35 = (bf16[2048,64]{0,1:T(8,128)(2,1)}, bf16[2048,64]{0,1:T(8,128)(2,1)S(1)}, u32[]{:S(2)}) copy-start(bf16[2048,64]{0,1:T(8,128)(2,1)S(1)} %all_gather.42) | copy-start | bytes 786436
  405.1 155.8 %copy-start.74 = (f32[256]{0:T(256)}, f32[256]{0:T(256)S(1)}, u32[]{:S(2)}) copy-start(f32[256]{0:T(256)S(1)} %get-tuple-element.374) | copy-start | bytes 3076
  407.9 153.0 %copy-start.69 = (f32[256]{0:T(256)}, f32[256]{0:T(256)S(1)}, u32[]{:S(2)}) copy-start(f32[256]{0:T(256)S(1)} %fusion.76) | copy-start | bytes 3076
  1060.1 162.2 %copy-start.41 = (f32[256,64]{0,1:T(8,128)S(1)}, f32[256,64]{0,1:T(8,128)}, u32[]{:S(2)}) copy-start(f32[256,64]{0,1:T(8,128)} %copy-done.40) | copy-start | bytes 196612
  1060.1 162.3 %copy-start.68 = (f32[256]{0:T(256)S(1)}, f32[256]{0:T(256)}, u32[]{:S(2)}) copy-start(f32[256]{0:T(256)} %copy-done.67) | copy-start | bytes 3076
  1060.1 162.3 %copy-start.70 = (f32[256]{0:T(256)S(1)}, f32[256]{0:T(256)}, u32[]{:S(2)}) copy-start(f32[256]{0:T(256)} %copy-done.69) | copy-start | bytes 3076
  1060.1 162.4 %copy-start.16 = (bf16[256,2048]{1,0:T(8,128)(2,1)S(1)}, bf16[256,2048]{1,0:T(8,128)(2,1)}, u32[]{:S(2)}) copy-start(bf16[256,2048]{1,0:T(8,128)(2,1)} %param.19) | copy-start | bytes 3145732
  1060.1 162.3 %copy-start.26 = (bf16[256,2048]{1,0:T(8,128)(2,1)S(1)}, bf16[256,2048]{1,0:T(8,128)(2,1)}, u32[]{:S(2)}) copy-start(bf16[256,2048]{1,0:T(8,128)(2,1)} %reduce-scatter.7.cloned.1.call-done) | copy-start | bytes 3145732
  1060.1 162.3 %copy-start.36 = (bf16[2048,64]{0,1:T(8,128)(2,1)S(1)}, bf16[2048,64]{0,1:T(8,128)(2,1)}, u32[]{:S(2)}) copy-start(bf16[2048,64]{0,1:T(8,128)(2,1)} %copy-done.35) | copy-start | bytes 786436
  1060.1 162.3 %copy-start.50 = (f32[8,1,256]{2,1,0:T(1,128)S(1)}, f32[8,1,256]{2,1,0:T(1,128)}, u32[]{:S(2)}) copy-start(f32[8,1,256]{2,1,0:T(1,128)} %copy-done.49) | copy-start | bytes 24580
  1060.2 162.3 %copy-start.75 = (f32[256]{0:T(256)S(1)}, f32[256]{0:T(256)}, u32[]{:S(2)}) copy-start(f32[256]{0:T(256)} %copy-done.74) | copy-start | bytes 3076
  1229.0 291.6 %reduce-scatter.11.cloned.1.call-start = ((), (), s32[]{:S(2)}) async-start(), calls=%async_computation.14 | async-start | bytes 2359296 | tf_op jit(solution)/shard_map/reduce_scatter | solution.py:944
  1387.8 134.7 %reduce-scatter.9.cloned.1.call-start = ((), (), s32[]{:S(2)}) async-start(), calls=%async_computation.13 | async-start | bytes 2359296 | tf_op jit(solution)/shard_map/reduce_scatter | solution.py:941
  1395.4 128.9 %reduce-scatter.15.cloned.1.call-start = ((), (), s32[]{:S(2)}) async-start(), calls=%async_computation.16 | async-start | bytes 2359296 | tf_op jit(solution)/shard_map/reduce_scatter | solution.py:950
  1401.3 133.5 %reduce-scatter.13.cloned.1.call-start = ((), (), s32[]{:S(2)}) async-start(), calls=%async_computation.15 | async-start | bytes 2359296 | tf_op jit(solution)/shard_map/reduce_scatter | solution.py:947
  1409.7 232.0 %all-reduce.14.cloned.1.call-start = ((), (), s32[]{:S(2)}) async-start(), calls=%async_computation.18 | async-start | bytes 8454144
  1444.6 230.2 %reduce-scatter.17.cloned.1.call-start = ((), (), s32[]{:S(2)}) async-start(), calls=%async_computation.17 | async-start | bytes 294912 | tf_op jit(solution)/shard_map/reduce_scatter | solution.py:956
  1496.1 146.3 %copy-start.71 = (bf16[2048]{0:T(1024)(128)(2,1)S(1)}, bf16[2048]{0:T(1024)(128)(2,1)}, u32[]{:S(2)}) copy-start(bf16[2048]{0:T(1024)(128)(2,1)} %get-tuple-element.283) | copy-start | bytes 12292
  1520.5 174.3 %copy-start.27 = (f32[256,2048]{1,0:T(8,128)S(1)}, f32[256,2048]{1,0:T(8,128)}, u32[]{:S(2)}) copy-start(f32[256,2048]{1,0:T(8,128)} %get-tuple-element.341) | copy-start | bytes 6291460
  (75 other events, 835.9 us)
Sparse Core Ops, SparseCore 0:
  9.9 55.3 all-gather.8
  66.9 29.0 all-gather.10
  97.6 28.5 all-gather.12
  127.7 28.5 all-gather.14
  157.8 30.3 all-gather.16
  202.6 81.0 reduce-scatter.6
  1229.1 53.2 all-gather.18
  1387.9 35.8 reduce-scatter.10
  1426.7 34.4 reduce-scatter.8
  1463.5 34.4 reduce-scatter.14
  1500.4 34.4 reduce-scatter.12
  1538.4 103.1 all-reduce.13
  1644.0 30.7 reduce-scatter.16

commit v3 on v2

--- a/solution.py
+++ b/solution.py
@@ -12,6 +12,7 @@
 BLOCK = 512
 CHUNK = 256
 UNROLL = 4
+PACK_ROWS = 144
 
 
 EPS = 1e-05
@@ -200,133 +201,422 @@
 
 
 GSTEPS = 4
-
-
-def gather_body(own_ref, small_ref, all_ref, small_all, here_sem, small_here, small_send, small_recv, z_send, z_recv, g_send, g_recv, f_send, f_recv, p_send, p_recv):
+QUEUE = (2, 1, 3)
+ARRIVE = (1, 3, 2)
+
+
+def spread_out(own_ref, all_ref, sems):
     r, c, y, x, z, core, first, second = seat()
     pair, along_first, along_second, up = partners()
-    tokens = own_ref.shape[0]
-    step = tokens // GSTEPS
+    here_sem, z_send, z_recv, g_send, g_recv, f_send, f_recv, p_send, p_recv = sems
+    step = own_ref.shape[0] // GSTEPS
 
     def rows(q):
         return pl.ds(pl.multiple_of(q * step, step), step)
 
-    def place(zz, f, s, q):
-        yy, xx = row_of(core, f, s)
-        return all_ref.at[zz, core, yy, xx, rows(q)]
-
-    meet()
-    here = pltpu.make_async_copy(own_ref, all_ref.at[z, core, y, x], here_sem)
-    here.start()
-    small_local = pltpu.make_async_copy(small_ref, small_all.at[nth(0)[0]], small_here)
-    small_local.start()
-
-    def small(offset):
-        return small_copy(lambda spot: small_ref, small_all, small_send, small_recv, offset)
-
-    @pl.loop(1, RANKS)
-    def _(offset):
-        small(offset).start()
-
-    def z_copy(k, q):
-        return send(own_ref.at[rows(q)], place(z, first, second, q), z_send.at[k - 1, q], z_recv.at[k - 1, q], up[k - 1])
-
-    def g_copy(k, q, src):
-        zz = (z + 4 - k) % 4
-        return send(src, place(zz, first, second, q), g_send.at[k, q], g_recv.at[k, q], along_second)
-
-    def f_copy(k, s, q, src):
-        zz = (z + 4 - k) % 4
-        sec = second * (1 - s) + (1 - second) * s
-        return send(src, place(zz, first, sec, q), f_send.at[s, k, q], f_recv.at[s, k, q], along_first)
-
-    def p_copy(k, s, f, q, src):
-        zz = (z + 4 - k) % 4
+    def place(k, s, f, q):
         sec = second * (1 - s) + (1 - second) * s
         fir = first * (1 - f) + (1 - first) * f
-        return send(src, place(zz, fir, sec, q), p_send.at[f, s, k, q], p_recv.at[f, s, k, q], pair)
-
-    def out_of(k, s, f, q):
-        zz = (z + 4 - k) % 4
-        sec = second * (1 - s) + (1 - second) * s
-        fir = first * (1 - f) + (1 - first) * f
-        return place(zz, fir, sec, q)
-
-    @pl.loop(0, GSTEPS)
-    def _(q):
-        src = own_ref.at[rows(q)]
-        for k in (2, 1, 3):
-            z_copy(k, q).start()
-        g_copy(0, q, src).start()
-        f_copy(0, 0, q, src).start()
-        p_copy(0, 0, 0, q, src).start()
-
-    @pl.loop(0, GSTEPS)
-    def _(q):
-        for k in (1, 3, 2):
+        yy, xx = row_of(core, fir, sec)
+        return all_ref.at[(z + 4 - k) % 4, core, yy, xx, rows(q)]
+
+    def z_copy(k, q):
+        return send(
+            own_ref.at[rows(q)], place(0, 0, 0, q), z_send.at[k - 1, q], z_recv.at[k - 1, q], up[k - 1]
+        )
+
+    def g_copy(k, q, src):
+        return send(src, place(k, 0, 0, q), g_send.at[k, q], g_recv.at[k, q], along_second)
+
+    def f_copy(k, s, q, src):
+        return send(src, place(k, s, 0, q), f_send.at[s, k, q], f_recv.at[s, k, q], along_first)
+
+    def p_copy(k, s, f, q, src):
+        return send(src, place(k, s, f, q), p_send.at[f, s, k, q], p_recv.at[f, s, k, q], pair)
+
+    here = pltpu.make_async_copy(own_ref, all_ref.at[z, core, y, x], here_sem)
+
+    def begin():
+        here.start()
+
+        @pl.loop(0, GSTEPS)
+        def _(q):
+            src = own_ref.at[rows(q)]
+            for k in QUEUE:
+                z_copy(k, q).start()
+            g_copy(0, q, src).start()
+            f_copy(0, 0, q, src).start()
+            p_copy(0, 0, 0, q, src).start()
+
+    def forward(q):
+        for k in ARRIVE:
             z_copy(k, q).wait_recv()
-            src = out_of(k, 0, 0, q)
+            src = place(k, 0, 0, q)
             g_copy(k, q, src).start()
             f_copy(k, 0, q, src).start()
             p_copy(k, 0, 0, q, src).start()
-        for k in (0, 1, 3, 2):
-            src = out_of(k, 1, 0, q)
+        for k in (0, *ARRIVE):
+            src = place(k, 1, 0, q)
             g_copy(k, q, src).wait_recv()
             f_copy(k, 1, q, src).start()
             p_copy(k, 1, 0, q, src).start()
-        for k in (0, 1, 3, 2):
-            src = out_of(k, 0, 1, q)
+        for k in (0, *ARRIVE):
+            src = place(k, 0, 1, q)
             f_copy(k, 0, q, src).wait_recv()
             p_copy(k, 0, 1, q, src).start()
 
+    def finish():
+        @pl.loop(0, GSTEPS)
+        def _(q):
+            for k in (0, *ARRIVE):
+                src = place(k, 1, 1, q)
+                f_copy(k, 1, q, src).wait_recv()
+                p_copy(k, 1, 1, q, src).start()
+
+        here.wait()
+
+        @pl.loop(0, GSTEPS)
+        def _(q):
+            for k in range(4):
+                src = own_ref.at[rows(q)]
+                if k:
+                    z_copy(k, q).wait_send()
+                g_copy(k, q, src).wait_send()
+                for s in range(2):
+                    f_copy(k, s, q, src).wait_send()
+                    for f in range(2):
+                        p_copy(k, s, f, q, src).wait()
+
+    return begin, forward, finish
+
+
+def spread_sems():
+    dma = pltpu.SemaphoreType.DMA
+    shapes = [(3, GSTEPS), (4, GSTEPS), (2, 4, GSTEPS), (2, 2, 4, GSTEPS)]
+    return [dma(())] + [dma(shape) for shape in shapes for _ in range(2)]
+
+
+def small_out(small_ref, small_all, sems):
+    here_sem, small_send, small_recv = sems
+    local = pltpu.make_async_copy(small_ref, small_all.at[nth(0)[0]], here_sem)
+
+    def copy(offset):
+        return small_copy(lambda spot: small_ref, small_all, small_send, small_recv, offset)
+
+    def begin():
+        local.start()
+
+        @pl.loop(1, RANKS)
+        def _(offset):
+            copy(offset).start()
+
+    def finish():
+        local.wait()
+
+        @pl.loop(1, RANKS)
+        def _(offset):
+            copy(offset).wait()
+
+    return begin, finish
+
+
+def small_sems():
+    dma = pltpu.SemaphoreType.DMA
+    return [dma(()), dma((RANKS,)), dma((RANKS,))]
+
+
+def gather_body(own_ref, small_ref, all_ref, small_all, *sems):
+    begin, forward, finish = spread_out(own_ref, all_ref, sems[:9])
+    small_begin, small_finish = small_out(small_ref, small_all, sems[9:])
+    meet()
+    small_begin()
+    begin()
+
     @pl.loop(0, GSTEPS)
     def _(q):
-        for k in (0, 1, 3, 2):
-            src = out_of(k, 1, 1, q)
-            f_copy(k, 1, q, src).wait_recv()
-            p_copy(k, 1, 1, q, src).start()
-
-    here.wait()
-    small_local.wait()
-
-    @pl.loop(1, RANKS)
-    def _(offset):
-        small(offset).wait()
-
-    @pl.loop(0, GSTEPS)
-    def _(q):
-        for k in range(4):
-            src = own_ref.at[rows(q)]
-            if k:
-                z_copy(k, q).wait_send()
-            g_copy(k, q, src).wait_send()
-            for s in range(2):
-                f_copy(k, s, q, src).wait_send()
-                for f in range(2):
-                    p_copy(k, s, f, q, src).wait()
+        forward(q)
+
+    finish()
+    small_finish()
+
+
+ANYWHERE = pl.BlockSpec(memory_space=pl.ANY)
 
 
 def gather_near(own, small, collective_id):
     tokens, depth = own.shape
-    dma = pltpu.SemaphoreType.DMA
-    out, small_out = pl.pallas_call(
+    out, small_all = pl.pallas_call(
         gather_body,
         out_shape=(
             jax.ShapeDtypeStruct((4, 2, 2, 2, tokens, depth), own.dtype),
             jax.ShapeDtypeStruct((RANKS, *small.shape), small.dtype),
         ),
-        in_specs=[pl.BlockSpec(memory_space=pl.ANY)] * 2,
-        out_specs=[pl.BlockSpec(memory_space=pl.ANY)] * 2,
-        scratch_shapes=[
-            dma(()), dma(()), dma((RANKS,)), dma((RANKS,)),
-            dma((3, GSTEPS)), dma((3, GSTEPS)),
-            dma((4, GSTEPS)), dma((4, GSTEPS)),
-            dma((2, 4, GSTEPS)), dma((2, 4, GSTEPS)),
-            dma((2, 2, 4, GSTEPS)), dma((2, 2, 4, GSTEPS)),
-        ],
+        in_specs=[ANYWHERE] * 2,
+        out_specs=[ANYWHERE] * 2,
+        scratch_shapes=spread_sems() + small_sems(),
         compiler_params=pltpu.CompilerParams(collective_id=collective_id, has_side_effects=True),
     )(own, small)
-    return out.reshape(RANKS, tokens, depth), small_out
+    return out.reshape(RANKS, tokens, depth), small_all
+
+
+def start_body(x_ref, q_ref, k_ref, v_ref, o_ref, pack_ref, own_ref, small_ref,
+               x_all, q_all, k_all, v_all, o_all, pack_all, all_ref, small_all, *sems):
+    r, c, y, x, z, core, first, second = seat()
+    pair, along_first, along_second, up = partners()
+    begin, forward, finish = spread_out(own_ref, all_ref, sems[:9])
+    small_begin, small_finish = small_out(small_ref, small_all, sems[9:12])
+    here_sem, x_send, x_recv, w_send, w_recv, v_send, v_recv = sems[12:]
+    weights = [(q_ref, q_all), (k_ref, k_all), (v_ref, v_all), (o_ref, o_all), (pack_ref, pack_all)]
+
+    def block(index, col):
+        ref, whole = weights[index]
+        if index == 4:
+            return whole.at[col]
+        if index == 3:
+            width = ref.shape[1]
+            return whole.at[:, pl.ds(pl.multiple_of(col * width, width), width)]
+        height = ref.shape[0]
+        return whole.at[pl.ds(pl.multiple_of(col * height, height), height)]
+
+    def w_copy(index, k):
+        return send(
+            weights[index][0], block(index, c), w_send.at[index, k - 1], w_recv.at[index, k - 1], up[k - 1]
+        )
+
+    def pair_copy(index, k):
+        col = ((z + 4 - k) % 4) * 2 + core
+        src = weights[index][0] if k == 0 else block(index, col)
+        return send(src, block(index, col), v_send.at[index, k], v_recv.at[index, k], pair)
+
+    locals_ = [pltpu.make_async_copy(x_ref, x_all.at[r], here_sem.at[5])] + [
+        pltpu.make_async_copy(weights[i][0], block(i, c), here_sem.at[i]) for i in range(5)
+    ]
+    y1, x1 = row_of(core, first, 1 - second)
+    near_row = y1 * 2 + x1
+    x_first = send(x_ref, x_all.at[r], x_send.at[0], x_recv.at[0], along_first)
+    x_second = send(x_ref, x_all.at[r], x_send.at[1], x_recv.at[1], along_second)
+    x_relay = send(x_all.at[near_row], x_all.at[near_row], x_send.at[2], x_recv.at[2], along_first)
+
+    meet()
+    small_begin()
+    x_second.start()
+    x_first.start()
+    for index in (4, 0, 1, 2, 3):
+        for k in QUEUE:
+            w_copy(index, k).start()
+        pair_copy(index, 0).start()
+    begin()
+    for item in locals_:
+        item.start()
+    x_second.wait_recv()
+    x_relay.start()
+    for index in (4, 0, 1, 2, 3):
+        for k in ARRIVE:
+            w_copy(index, k).wait_recv()
+            pair_copy(index, k).start()
+
+    @pl.loop(0, GSTEPS)
+    def _(q):
+        forward(q)
+
+    finish()
+    small_finish()
+    for item in locals_:
+        item.wait()
+    x_first.wait()
+    x_second.wait_send()
+    x_relay.wait()
+    for index in range(5):
+        for k in range(4):
+            if k:
+                w_copy(index, k).wait_send()
+            pair_copy(index, k).wait()
+
+
+def start_near(x, weights, pack, own, small, collective_id):
+    tokens, depth = own.shape
+    dma = pltpu.SemaphoreType.DMA
+    height, width = weights[0].shape
+    shaped = lambda shape, like: jax.ShapeDtypeStruct(shape, like.dtype)
+    outs = pl.pallas_call(
+        start_body,
+        out_shape=(
+            shaped((4, *x.shape), x),
+            *[shaped((8 * height, width), w) for w in weights[:3]],
+            shaped((weights[3].shape[0], 8 * weights[3].shape[1]), weights[3]),
+            shaped((8, *pack.shape), pack),
+            shaped((4, 2, 2, 2, tokens, depth), own),
+            shaped((RANKS, *small.shape), small),
+        ),
+        in_specs=[ANYWHERE] * 8,
+        out_specs=[ANYWHERE] * 8,
+        scratch_shapes=spread_sems()
+        + small_sems()
+        + [dma((6,)), dma((3,)), dma((3,)), dma((5, 3)), dma((5, 3)), dma((5, 4)), dma((5, 4))],
+        compiler_params=pltpu.CompilerParams(collective_id=collective_id, has_side_effects=True),
+    )(x, *weights, pack, own, small)
+    x_all, q, k, v, o, pack_all, whole, small_all = outs
+    return x_all.reshape(-1, x.shape[1]), q, k, v, o, pack_all, whole.reshape(RANKS, tokens, depth), small_all
+
+
+def finish_body(field_ref, q_ref, k_ref, v_ref, o_ref, pack_ref,
+                out_ref, q_out, k_out, v_out, o_out, pack_all,
+                mine, first_in, second_in, total,
+                q_mine, k_mine, v_mine, o_mine, q_pair, k_pair, v_pair, o_pair, q_z, k_z, v_z, o_z,
+                q_sum, k_sum, v_sum, o_sum,
+                load_sem, f_send, f_recv, g_send, g_recv, w_load, p_send, p_recv, z_send, z_recv, out_sem,
+                *small):
+    r, c, y, x, z, core, first, second = seat()
+    pair, along_first, along_second, up = partners()
+    here_sem, small_send, small_recv = small
+    tokens, depth = out_ref.shape
+    other = 1 - core
+    grads = [q_ref, k_ref, v_ref, o_ref]
+    kept, pairs, zs = [q_mine, k_mine, v_mine, o_mine], [q_pair, k_pair, v_pair, o_pair], [q_z, k_z, v_z, o_z]
+    sums, outs = [q_sum, k_sum, v_sum, o_sum], [q_out, k_out, v_out, o_out]
+
+    def block(index, col):
+        ref = grads[index]
+        if index == 3:
+            width = ref.shape[1] // 8
+            return ref.at[:, pl.ds(pl.multiple_of(col * width, width), width)]
+        height = ref.shape[0] // 8
+        return ref.at[pl.ds(pl.multiple_of(col * height, height), height)]
+
+    def row(fir, sec):
+        yy, xx = row_of(core, fir, sec)
+        return yy * 2 + xx
+
+    local = pltpu.make_async_copy(pack_ref.at[c], pack_all.at[nth(0)[0]], here_sem)
+
+    def small_of(offset):
+        return small_copy(lambda spot: pack_ref.at[spot // 4], pack_all, small_send, small_recv, offset)
+
+    def load(fir, sec):
+        return pltpu.make_async_copy(field_ref.at[row(fir, sec)], mine.at[fir, sec], load_sem.at[fir, sec])
+
+    def f_copy(sec):
+        return send(field_ref.at[row(1 - first, sec)], first_in.at[sec], f_send.at[sec], f_recv.at[sec], along_first)
+
+    g_copy = send(mine.at[first, 1 - second], second_in, g_send, g_recv, along_second)
+
+    def w_load_copy(index, zz):
+        return pltpu.make_async_copy(block(index, zz * 2 + core), kept[index].at[zz], w_load.at[index, zz])
+
+    def w_give(index, zz):
+        return send(
+            block(index, zz * 2 + other), pairs[index].at[zz], p_send.at[index, zz], p_recv.at[index, zz], pair
+        )
+
+    def w_z(index, k):
+        return send(
+            kept[index].at[(z + k) % 4], zs[index].at[k - 1], z_send.at[index, k - 1], z_recv.at[index, k - 1], up[k - 1]
+        )
+
+    def add(ref, extras):
+        @pl.loop(0, ref.shape[0] // TILE)
+        def _(t):
+            here = pl.ds(pl.multiple_of(t * TILE, TILE), TILE)
+            value = ref[here].astype(jnp.float32)
+            for extra in extras:
+                value = value + extra[here].astype(jnp.float32)
+            ref[here] = value.astype(jnp.bfloat16)
+
+    def add_out(ref, extras, result):
+        @pl.loop(0, ref.shape[0] // TILE)
+        def _(t):
+            here = pl.ds(pl.multiple_of(t * TILE, TILE), TILE)
+            value = ref[here].astype(jnp.float32)
+            for extra in extras:
+                value = value + extra[here].astype(jnp.float32)
+            result[here] = value
+
+    meet()
+    f_copy(1 - second).start()
+    f_copy(second).start()
+    for index in range(4):
+        for k in (2, 1, 3, 0):
+            w_give(index, (z + k) % 4).start()
+            w_load_copy(index, (z + k) % 4).start()
+    load(first, 1 - second).start()
+    load(first, second).start()
+    local.start()
+
+    @pl.loop(1, RANKS)
+    def _(offset):
+        small_of(offset).start()
+
+    for index in range(4):
+        for k in (2, 1, 3):
+            zz = (z + k) % 4
+            w_load_copy(index, zz).wait()
+            w_give(index, zz).wait_recv()
+            add(kept[index].at[zz], [pairs[index].at[zz]])
+            w_z(index, k).start()
+    load(first, 1 - second).wait()
+    f_copy(1 - second).wait_recv()
+    add(mine.at[first, 1 - second], [first_in.at[1 - second]])
+    g_copy.start()
+    load(first, second).wait()
+    f_copy(second).wait_recv()
+    for index in range(4):
+        w_load_copy(index, z).wait()
+        w_give(index, z).wait_recv()
+    g_copy.wait_recv()
+    add_out(mine.at[first, second], [first_in.at[second], second_in], total)
+    pltpu.make_async_copy(total, out_ref, out_sem.at[4]).start()
+    for index in range(4):
+        for k in ARRIVE:
+            w_z(index, k).wait_recv()
+        add_out(
+            kept[index].at[z], [pairs[index].at[z]] + [zs[index].at[k] for k in range(3)], sums[index]
+        )
+        pltpu.make_async_copy(sums[index], outs[index], out_sem.at[index]).start()
+    for sec in range(2):
+        f_copy(sec).wait_send()
+    g_copy.wait_send()
+    for index in range(4):
+        for k in range(4):
+            w_give(index, (z + k) % 4).wait_send()
+            if k:
+                w_z(index, k).wait_send()
+        pltpu.make_async_copy(sums[index], outs[index], out_sem.at[index]).wait()
+    local.wait()
+
+    @pl.loop(1, RANKS)
+    def _(offset):
+        small_of(offset).wait()
+
+    pltpu.make_async_copy(total, out_ref, out_sem.at[4]).wait()
+
+
+def finish_near(field, grads, pack, collective_id):
+    rows_count, tokens, depth = field.shape
+    dma = pltpu.SemaphoreType.DMA
+    blocks = [(g.shape[0] // 8, g.shape[1]) for g in grads[:3]] + [(grads[3].shape[0], grads[3].shape[1] // 8)]
+    half = lambda *shape: pltpu.VMEM(shape, jnp.bfloat16)
+    return pl.pallas_call(
+        finish_body,
+        out_shape=(
+            jax.ShapeDtypeStruct((tokens, depth), jnp.float32),
+            *[jax.ShapeDtypeStruct(b, jnp.float32) for b in blocks],
+            jax.ShapeDtypeStruct((RANKS, *pack.shape[1:]), pack.dtype),
+        ),
+        in_specs=[ANYWHERE] * 6,
+        out_specs=[ANYWHERE] * 6,
+        scratch_shapes=[
+            half(2, 2, tokens, depth), half(2, tokens, depth), half(tokens, depth),
+            pltpu.VMEM((tokens, depth), jnp.float32),
+            *[half(4, *b) for b in blocks], *[half(4, *b) for b in blocks], *[half(3, *b) for b in blocks],
+            *[pltpu.VMEM(b, jnp.float32) for b in blocks],
+            dma((2, 2)), dma((2,)), dma((2,)), dma(()), dma(()),
+            dma((4, 4)), dma((4, 4)), dma((4, 4)), dma((4, 3)), dma((4, 3)), dma((5,)),
+        ]
+        + small_sems(),
+        compiler_params=pltpu.CompilerParams(
+            collective_id=collective_id, has_side_effects=True, vmem_limit_bytes=60 * 1024 * 1024
+        ),
+    )(field, *grads, pack)
 
 
 RSTEPS = 8
@@ -629,28 +919,57 @@
 ):
     tokens = layer_input.shape[0]
     rows_count = lax.axis_size("row")
-    (
-        attention_full,
-        query_scale_w,
-        key_scale_w,
-        query_full,
-        key_full,
-        value_full,
-        output_full,
-        feed_full,
-        router_full,
-    ) = (
-        lax.all_gather(attention_gain, "col", axis=0, tiled=True),
-        lax.all_gather(query_gain, "col", axis=0, tiled=True),
-        lax.all_gather(key_gain, "col", axis=0, tiled=True),
-        lax.all_gather(query_weight, "col", axis=0, tiled=True),
-        lax.all_gather(key_weight, "col", axis=0, tiled=True),
-        lax.all_gather(value_weight, "col", axis=0, tiled=True),
-        lax.all_gather(output_weight, "col", axis=1, tiled=True),
-        lax.all_gather(feed_gain, "col", axis=0, tiled=True),
-        lax.all_gather(router_weight, "col", axis=0, tiled=True),
-    )
-    sequence = lax.all_gather(layer_input, "row", axis=0, tiled=True)
+    near = rows_count == 4 and lax.axis_size("col") == 8
+    if near:
+        head_part = query_gain.shape[0]
+        slice_width = attention_gain.shape[0]
+        pack = jnp.concatenate(
+            [attention_gain, feed_gain, query_gain, key_gain, router_weight.reshape(-1)]
+        )
+        pack = jnp.pad(pack, (0, PACK_ROWS * 128 - pack.shape[0])).reshape(PACK_ROWS, 128)
+        (
+            sequence, query_full, key_full, value_full, output_full, pack_all, cotangent_all, index_all
+        ) = start_near(
+            layer_input,
+            [query_weight, key_weight, value_weight, output_weight],
+            pack,
+            cotangent,
+            expert_index.T,
+            1,
+        )
+        index_all = jnp.swapaxes(index_all, 1, 2)
+        pack_all = pack_all.reshape(8, -1)
+        ends = [slice_width, 2 * slice_width, 2 * slice_width + head_part, 2 * slice_width + 2 * head_part]
+        attention_full = pack_all[:, : ends[0]].reshape(-1)
+        feed_full = pack_all[:, ends[0] : ends[1]].reshape(-1)
+        query_scale_w = pack_all[:, ends[1] : ends[2]].reshape(-1)
+        key_scale_w = pack_all[:, ends[2] : ends[3]].reshape(-1)
+        router_full = pack_all[:, ends[3] : ends[3] + router_weight.size].reshape(
+            -1, router_weight.shape[1]
+        )
+    else:
+        (
+            attention_full,
+            query_scale_w,
+            key_scale_w,
+            query_full,
+            key_full,
+            value_full,
+            output_full,
+            feed_full,
+            router_full,
+        ) = (
+            lax.all_gather(attention_gain, "col", axis=0, tiled=True),
+            lax.all_gather(query_gain, "col", axis=0, tiled=True),
+            lax.all_gather(key_gain, "col", axis=0, tiled=True),
+            lax.all_gather(query_weight, "col", axis=0, tiled=True),
+            lax.all_gather(key_weight, "col", axis=0, tiled=True),
+            lax.all_gather(value_weight, "col", axis=0, tiled=True),
+            lax.all_gather(output_weight, "col", axis=1, tiled=True),
+            lax.all_gather(feed_gain, "col", axis=0, tiled=True),
+            lax.all_gather(router_weight, "col", axis=0, tiled=True),
+        )
+        sequence = lax.all_gather(layer_input, "row", axis=0, tiled=True)
     length = sequence.shape[0]
     model_width = sequence.shape[1]
     local_width = query_full.shape[1]
@@ -722,11 +1041,7 @@
     gate_hits = expert_index[:, :, None] == jnp.arange(experts, dtype=jnp.int32)
     gate_probs = jnp.sum(jnp.where(gate_hits, router_probs[:, None, :], 0.0), axis=-1)
 
-    near = rows_count == 4 and lax.axis_size("col") == 8
-    if near:
-        cotangent_all, index_all = gather_near(cotangent, expert_index.T, 1)
-        index_all = jnp.swapaxes(index_all, 1, 2)
-    else:
+    if not near:
         index_all = lax.all_gather(expert_index, ("col", "row"), axis=0, tiled=True)
     own = (index_all - lax.axis_index("col") * experts_local).reshape(ranks, tokens, -1)
     matches = own[..., None] == jnp.arange(experts_local, dtype=jnp.int32)
@@ -877,15 +1192,13 @@
     key_weighted = grad_key_normed * key_gain_f
     query_gain_term = jnp.sum(grad_query_normed * query_raw * query_rs, axis=0)
     key_gain_term = jnp.sum(grad_key_normed * key_raw * key_rs, axis=0)
-    query_inner, key_inner, feed_gain_total, router_total = (
+    query_inner, key_inner = (
         lax.psum(jnp.sum(query_weighted * query_raw, axis=-1).astype(jnp.bfloat16), "row").astype(
             jnp.float32
         ),
         lax.psum(jnp.sum(key_weighted * key_raw, axis=-1).astype(jnp.bfloat16), "row").astype(
             jnp.float32
         ),
-        lax.psum(feed_gain_term.astype(jnp.bfloat16), "row").astype(jnp.float32),
-        lax.psum(router_grad.astype(jnp.bfloat16), "row").astype(jnp.float32),
     )
     grad_query_raw = (
         query_rs * query_weighted - query_raw * query_rs**3 * (query_inner / model_width)[:, None]
@@ -906,57 +1219,95 @@
         attention_weighted * seq_float, axis=-1, keepdims=True
     )
     attention_gain_term = jnp.sum(grad_normed * seq_float * seq_scale, axis=0)
-    stacked = jnp.concatenate(
-        [
-            grad_seq_part.reshape(rows_count, tokens, model_width),
-            jnp.broadcast_to(attention_gain_term[None, None, :], (rows_count, 1, model_width)),
-        ],
-        axis=1,
-    ).reshape(rows_count * (tokens + 1), model_width)
-    summed = lax.psum_scatter(
-        stacked.astype(jnp.bfloat16), "row", scatter_dimension=0, tiled=True
-    ).astype(jnp.float32)
-    input_grad = grad_hidden + summed[:tokens]
-    attention_gain_total = summed[tokens]
-    (
-        grad_attention_gain,
-        grad_query_gain,
-        grad_key_gain,
-        grad_query_weight,
-        grad_key_weight,
-        grad_value_weight,
-        grad_output_weight,
-        grad_feed_gain,
-        grad_router_weight,
-    ) = (
-        lax.psum_scatter(
-            attention_gain_total.astype(jnp.bfloat16), "col", scatter_dimension=0, tiled=True
-        ).astype(jnp.float32),
-        lax.psum_scatter(
-            query_gain_term.astype(jnp.bfloat16), "col", scatter_dimension=0, tiled=True
-        ).astype(jnp.float32),
-        lax.psum_scatter(
-            key_gain_term.astype(jnp.bfloat16), "col", scatter_dimension=0, tiled=True
-        ).astype(jnp.float32),
-        lax.psum_scatter(
-            query_grad.astype(jnp.bfloat16), "col", scatter_dimension=0, tiled=True
-        ).astype(jnp.float32),
-        lax.psum_scatter(
-            key_grad.astype(jnp.bfloat16), "col", scatter_dimension=0, tiled=True
-        ).astype(jnp.float32),
-        lax.psum_scatter(
-            value_grad.astype(jnp.bfloat16), "col", scatter_dimension=0, tiled=True
-        ).astype(jnp.float32),
-        lax.psum_scatter(
-            output_grad.astype(jnp.bfloat16), "col", scatter_dimension=1, tiled=True
-        ).astype(jnp.float32),
-        lax.psum_scatter(
-            feed_gain_total.astype(jnp.bfloat16), "col", scatter_dimension=0, tiled=True
-        ).astype(jnp.float32),
-        lax.psum_scatter(
-            router_total.astype(jnp.bfloat16), "col", scatter_dimension=0, tiled=True
-        ).astype(jnp.float32),
-    )
+    if near:
+        cols = lax.axis_size("col")
+        pack = jnp.concatenate(
+            [
+                attention_gain_term.reshape(cols, -1),
+                feed_gain_term.reshape(cols, -1),
+                query_gain_term.reshape(cols, -1),
+                key_gain_term.reshape(cols, -1),
+                router_grad.reshape(cols, -1),
+            ],
+            axis=1,
+        )
+        pack = jnp.pad(pack, ((0, 0), (0, PACK_ROWS * 128 - pack.shape[1])))
+        pack = pack.astype(jnp.bfloat16).reshape(cols, PACK_ROWS, 128)
+        (
+            summed, grad_query_weight, grad_key_weight, grad_value_weight, grad_output_weight, packs
+        ) = finish_near(
+            grad_seq_part.astype(jnp.bfloat16).reshape(rows_count, tokens, model_width),
+            [grad.astype(jnp.bfloat16) for grad in (query_grad, key_grad, value_grad, output_grad)],
+            pack,
+            4,
+        )
+        input_grad = grad_hidden + summed
+        packs = packs.reshape(cols, rows_count, -1).astype(jnp.float32)
+        whole = jnp.sum(packs, axis=(0, 1))
+        heads_sum = jnp.sum(
+            lax.dynamic_index_in_dim(packs, lax.axis_index("row"), 1, keepdims=False), axis=0
+        )
+        grad_attention_gain = whole[: ends[0]]
+        grad_feed_gain = whole[ends[0] : ends[1]]
+        grad_query_gain = heads_sum[ends[1] : ends[2]]
+        grad_key_gain = heads_sum[ends[2] : ends[3]]
+        grad_router_weight = whole[ends[3] : ends[3] + router_weight.size].reshape(router_weight.shape)
+    else:
+        stacked = jnp.concatenate(
+            [
+                grad_seq_part.reshape(rows_count, tokens, model_width),
+                jnp.broadcast_to(attention_gain_term[None, None, :], (rows_count, 1, model_width)),
+            ],
+            axis=1,
+        ).reshape(rows_count * (tokens + 1), model_width)
+        summed = lax.psum_scatter(
+            stacked.astype(jnp.bfloat16), "row", scatter_dimension=0, tiled=True
+        ).astype(jnp.float32)
+        input_grad = grad_hidden + summed[:tokens]
+        attention_gain_total = summed[tokens]
+        feed_gain_total, router_total = (
+            lax.psum(feed_gain_term.astype(jnp.bfloat16), "row").astype(jnp.float32),
+            lax.psum(router_grad.astype(jnp.bfloat16), "row").astype(jnp.float32),
+        )
+        (
+            grad_attention_gain,
+            grad_query_gain,
+            grad_key_gain,
+            grad_query_weight,
+            grad_key_weight,
+            grad_value_weight,
+            grad_output_weight,
+            grad_feed_gain,
+            grad_router_weight,
+        ) = (
+            lax.psum_scatter(
+                attention_gain_total.astype(jnp.bfloat16), "col", scatter_dimension=0, tiled=True
+            ).astype(jnp.float32),
+            lax.psum_scatter(
+                query_gain_term.astype(jnp.bfloat16), "col", scatter_dimension=0, tiled=True
+            ).astype(jnp.float32),
+            lax.psum_scatter(
+                key_gain_term.astype(jnp.bfloat16), "col", scatter_dimension=0, tiled=True
+            ).astype(jnp.float32),
+            lax.psum_scatter(
+                query_grad.astype(jnp.bfloat16), "col", scatter_dimension=0, tiled=True
+            ).astype(jnp.float32),
+            lax.psum_scatter(
+                key_grad.astype(jnp.bfloat16), "col", scatter_dimension=0, tiled=True
+            ).astype(jnp.float32),
+            lax.psum_scatter(
+                value_grad.astype(jnp.bfloat16), "col", scatter_dimension=0, tiled=True
+            ).astype(jnp.float32),
+            lax.psum_scatter(
+                output_grad.astype(jnp.bfloat16), "col", scatter_dimension=1, tiled=True
+            ).astype(jnp.float32),
+            lax.psum_scatter(
+                feed_gain_total.astype(jnp.bfloat16), "col", scatter_dimension=0, tiled=True
+            ).astype(jnp.float32),
+            lax.psum_scatter(
+                router_total.astype(jnp.bfloat16), "col", scatter_dimension=0, tiled=True
+            ).astype(jnp.float32),
+        )
     return (
         layer_output,
         input_grad,

time: 1710 us -> 1630 us (0.953)
  Pallas kernels: 896 us -> 1110 us
  waiting for transfers between devices: 242 us -> 59 us
  blocking collectives: 118 us -> 18.2 us
  matrix products: 197 us -> 178 us
    pallas_call x0 -> x2, Pallas kernels: none -> 386 us  [the longest x1 267 us: start_near(): pl.pallas_call(start_body, out_shape=(shaped((4, *x.shape), x), *[shaped(...]
    pallas_call x2 -> x1, Pallas kernels: 324 us -> 155 us  [gather_near(): pl.pallas_call(gather_body, out_shape=(jax.ShapeDtypeStruct((4, 2, 2, 2,...]
    unnamed x14 -> x2, waiting for transfers between devices: 108 us -> 0.03 us
    all_gather x5 -> x0, waiting for transfers between devices: 69.6 us -> none  [the longest x1 27.1 us: local(): lax.all_gather(query_weight, 'col', axis=0, tiled=True)]
    reduce_scatter x1, waiting for transfers between devices: 0.02 us -> 58.4 us  [local(): lax.psum_scatter(wide_dot(mixed_heads, output_full).astype(jnp.bfloat16),...]
    all_gather x1, waiting for transfers between devices: 52.1 us -> 0.57 us  [local(): lax.all_gather(grad_hidden.astype(jnp.bfloat16), 'row', axis=0, tiled=True)]
    unnamed x2 -> x0, blocking collectives: 42.5 us -> none
    all_gather x3 -> x0, blocking collectives: 39.2 us -> none  [the longest x1 15.5 us: local(): lax.all_gather(router_weight, 'col', axis=0, tiled=True)]
  transfers between devices with their start and end apart: 13 -> 2, of which waited for: 7 -> 2; matrix products, arithmetic and copies ran while one was open for 12% -> 4% of each run, Pallas kernels for 10% -> 0%
where the time goes in v3:
time: 1630 us; the launch traced here: 1620 us
  Pallas kernels  1110 us (68%)
  matrix products  178 us (11%)
  other arithmetic  148 us (9%)
  local copies, waits for them, and re-layouts  83.3 us (5%)
  waiting for transfers between devices  59 us (4%)
  blocking collectives  18.2 us (1%)
    pallas_call x2, Pallas kernels, reduce_near(): pl.pallas_call(reduce_body, out_shape=(jax.ShapeDtypeStruct((tokens, dept...  336 us
    pallas_call x1, Pallas kernels, start_near(): pl.pallas_call(start_body, out_shape=(shaped((4, *x.shape), x), *[shaped(...  267 us
    pallas_call x1, Pallas kernels, gather_near(): pl.pallas_call(gather_body, out_shape=(jax.ShapeDtypeStruct((4, 2, 2, 2,...  155 us
    pallas_call x1, Pallas kernels, finish_near(): pl.pallas_call(finish_body, out_shape=(jax.ShapeDtypeStruct((tokens, dept...  119 us
    pallas_call x2, Pallas kernels, restore(): pl.pallas_call(functools.partial(restore_body, flipped), grid=(depth // C...  119 us
    pallas_call x2, Pallas kernels, project(): pl.pallas_call(functools.partial(project_body, flipped), grid=(depth // C...  116 us
    reduce_scatter x1, waiting for transfers between devices, local(): lax.psum_scatter(wide_dot(mixed_heads, output_full).astype(jnp.bfloat16),...  58.4 us
  transfers between devices with their start and end apart: 2, of which 2 were waited for; matrix products, arithmetic and copies ran while one was open for 4% of the time, Pallas kernels for 0%

profile of v3, /device:TPU:0, one launch (start us, length us, event | category | flops | bytes accessed | tf_op | source)
XLA Modules:
  0.0 1620.7 jit_solution(14485970819134004082)
XLA Ops:
  11.6 266.7 %shard_map.254 = (bf16[4,256,2048]{2,1,0:T(8,128)(2,1)}, bf16[2048,512]{1,0:T(8,128)(2,1)}, bf16[2048,512]{1,0:T(8,128)(2,1)}, bf16[2048,512]{1,0:T(8,128)(2,1)}...) custom-call(bf16[256,2048]{1,0:T(8,128)(2,1)} %x_ref.1, ...), custom_call_target="tpu_custom_call" | custom-call | tf_op jit(solution)/shard_map/pallas_call | solution.py:441
  291.9 9.3 all-reduce.2
  323.4 6.1 fusion.55
  329.5 23.3 %while.30 = (s32[]{:T(128)}, bf16[2,512,4,128]{3,1,2,0:T(8,128)(2,1)}, f32[2,4,512]{2,1,0:T(4,128)S(1)}, s32[2]{0:T(128)S(1)}, bf16[1024,4,128]{2,0,1:T(8,128)(2...) while((s32[]{:T(128)}, ...), condition=%wide.region_8.9_spmd.clone.clone, body=%wide.region_5.8_spmd.clone.sunk.clone | while | flops 1099430400 | bytes 31003272 | solution.py:1024
  364.6 5.3 fusion.41
  369.9 58.4 %reduce-scatter.2.cloned.1.call-done = bf16[256,2048]{1,0:T(8,128)(2,1)} async-done(((bf16[1024,2048]{1,0:T(8,128)(2,1)}), bf16[256,2048]{1,0:T(8,128)(2,1)}) %reduce-scatter.2.cloned.1.call-update) | async-done | bytes 1048592 | tf_op jit(solution)/shard_map/reduce_scatter | solution.py:1027
  433.0 154.6 %shard_map.255 = (bf16[4,2,2,2,256,2048]{5,4,3,2,1,0:T(8,128)(2,1)}, f32[32,8,256]{2,1,0:T(8,128)}) custom-call(bf16[256,2048]{1,0:T(8,128)(2,1)} %copy-done.27, f32[8,256]{1,0:T(8,128)} %bitcast.271), custom_call_target="tpu_custom_call" | custom-call | tf_op jit(solution)/shard_map/pallas_call | solution.py:348
  593.0 51.9 %shard_map.258 = (bf16[8,1280,2048]{2,1,0:T(8,128)(2,1)}, f32[8,1280,256]{2,1,0:T(8,128)}) custom-call(bf16[32,320,256]{2,1,0:T(8,128)(2,1)} %fusion.38.pick_ref, bf16[32,256,2048]{2,1,0:T(8,128)(2,1)} %bitcast.272, bf16[8,256,2048]{2,1,0:T(8,128)(2,1)} %refs_0_.3), custom_call_target="tpu_custom_call" | custom-call | flops 21474836480 | bytes 125829120 | tf_op jit(solution)/shard_map/pallas_call | solution.py:845
  644.9 63.6 %shard_map.256 = (bf16[8,1280,2048]{2,1,0:T(8,128)(2,1)}, f32[8,1280,256]{2,1,0:T(8,128)}, f32[8,1280,256]{2,1,0:T(8,128)}) custom-call(bf16[32,320,256]{2,1,0:T(8,128)(2,1)} %fusion.38.pick_ref, bf16[32,256,2048]{2,1,0:T(8,128)(2,1)} %bitcast.273, bf16[8,2048,256]{2,1,0:T(8,128)(2,1)} %refs_2_.1, bf16[8,2048,256]{2,1,0:T(8,128)(2,1)} %refs_3_.1), custom_call_target="tpu_custom_call" | custom-call | flops 32212254720 | bytes 125829120 | tf_op jit(solution)/shard_map/pallas_call | solution.py:845
  708.5 15.2 multiply_reduce_fusion.1
  728.7 14.9 multiply_convert_fusion.2
  743.6 5.0 eq.74
  748.6 12.0 copy.155
  760.6 9.9 fusion.83
  773.3 8.1 copy.156
  781.4 6.9 convert_element_type.215.refs_0_
  788.3 24.3 %fusion.92 = f32[8,2048,256]{2,1,0:T(8,128)} fusion(bf16[8,1280,2048]{2,1,0:T(8,128)(2,1)} %get-tuple-element.167, bf16[8,1280,256]{2,1,0:T(8,128)(2,1)} %get-tuple-element.424.refs_1_), kind=kOutput, calls=%fused_computation.201 | convolution fusion | flops 10737418240 | bytes 63963136 | tf_op jit(solution)/shard_map/erd,erf->edf/dot_general | solution.py:1128
  812.6 7.7 select_convert_fusion.spread_ref
  820.3 52.0 %shard_map.257 = bf16[32,256,2048]{2,1,0:T(8,128)(2,1)} custom-call(bf16[32,256,320]{2,1,0:T(8,128)(2,1)} %select_convert_fusion.spread_ref, bf16[8,1280,256]{2,1,0:T(8,128)(2,1)} %convert_element_type.215.refs_0_, bf16[8,256,2048]{2,1,0:T(8,128)(2,1)} %refs_0_.3), custom_call_target="tpu_custom_call" | custom-call | flops 21474836480 | bytes 62914560 | tf_op jit(solution)/shard_map/pallas_call | solution.py:889
  872.3 174.2 %shard_map.259 = (f32[256,2048]{1,0:T(8,128)}, f32[32,8,256]{2,1,0:T(8,128)}) custom-call(bf16[4,2,2,2,256,2048]{5,4,3,2,1,0:T(8,128)(2,1)} %bitcast.233, f32[32,8,256]{2,1,0:T(8,128)} %bitcast.245), custom_call_target="tpu_custom_call" | custom-call | tf_op jit(solution)/shard_map/pallas_call | solution.py:770
  1046.5 66.9 %shard_map.260 = bf16[32,256,2048]{2,1,0:T(8,128)(2,1)} custom-call(bf16[32,256,320]{2,1,0:T(8,128)(2,1)} %get-tuple-element.414.spread_ref, bf16[8,1280,256]{2,1,0:T(8,128)(2,1)} %get-tuple-element.425.refs_0_, bf16[8,1280,256]{2,1,0:T(8,128)(2,1)} %get-tuple-element.424.refs_1_, bf16[8,2048,256]{2,1,0:T(8,128)(2,1)} %refs_2_.1, bf16[8,2048,256]{2,1,0:T(8,128)(2,1)} %refs_3_.1), custom_call_target="tpu_custom_call" | custom-call | flops 32212254720 | bytes 62914560 | tf_op jit(solution)/shard_map/pallas_call | solution.py:889
  1113.5 161.3 %shard_map.261 = (f32[256,2048]{1,0:T(8,128)}, f32[32,8,256]{2,1,0:T(8,128)}) custom-call(bf16[4,2,2,2,256,2048]{5,4,3,2,1,0:T(8,128)(2,1)} %bitcast.234, f32[32,8,256]{2,1,0:T(8,128)} %bitcast.246), custom_call_target="tpu_custom_call" | custom-call | tf_op jit(solution)/shard_map/pallas_call | solution.py:770
  1284.6 24.6 %fusion.91 = f32[8,2048,256]{2,1,0:T(8,128)} fusion(bf16[8,1280,2048]{2,1,0:T(8,128)(2,1)} %get-tuple-element.167, bf16[8,1280,256]{2,1,0:T(8,128)(2,1)} %get-tuple-element.425.refs_0_), kind=kOutput, calls=%fused_computation.200 | convolution fusion | flops 10737418240 | bytes 63963136 | tf_op jit(solution)/shard_map/erd,erf->edf/dot_general | solution.py:1125
  1309.2 26.2 %fusion.50 = f32[8,256,2048]{2,1,0:T(8,128)} fusion(bf16[8,1280,2048]{2,1,0:T(8,128)(2,1)} %get-tuple-element.168, f32[8,1280,256]{2,1,0:T(8,128)} %get-tuple-element.417, f32[8,1280]{1,0:T(8,128)S(1)} %copy-done.61), kind=kOutput, calls=%fused_computation.78 | convolution fusion | flops 10742661120 | bytes 69246976 | tf_op jit(solution)/shard_map/erf,erd->efd/dot_general | solution.py:1131
  1336.0 6.5 convolution_convert_fusion.6
  1342.5 50.7 %while.31 = (s32[]{:T(128)}, f32[1024,4,128]{0,2,1:T(8,128)S(1)}, f32[1024,4,128]{0,2,1:T(8,128)}, f32[2,512,4,128]{3,1,2,0:T(8,128)}, s32[2]{0:T(128)S(1)}, /*i...) while((s32[]{:T(128)}, f32[1024,4,128]{0,2,1:T(8,128)S(1)}, ...), condition=%wide.region_24.25_spmd.clone.clone, body=%wide.region_22.24_spmd.clone.sunk.clone | while | flops 2719218176 | bytes 180417440 | solution.py:1184
  1387.6 5.2 bitcast_add_fusion.9
  1425.6 8.9 all-reduce.3
  1444.6 5.7 fusion.89
  1456.4 9.4 fusion.49
  1466.8 6.1 convolution_convert_fusion.2.v_ref
  1480.4 119.0 %shard_map.262 = (f32[256,2048]{1,0:T(8,128)}, f32[256,512]{1,0:T(8,128)}, f32[256,512]{1,0:T(8,128)}, f32[256,512]{1,0:T(8,128)}, f32[512,256]{1,0:T(8,128)}, /*index=5*/bf16[32,144,128]{2,1,0:T(8,128)(2,1)}) custom-call(bf16[4,256,2048]{2,1,0:T(8,128)(2,1)} %bitcast.236, bf16[2048,512]{1,0:T(8,128)(2,1)} %convolution_convert_fusion.4.q_ref, ...), custom_call_target="tpu_custom_call" | custom-call | tf_op jit(solution)/shard_map/pallas_call | solution.py:598
  (362 shorter events, 210.4 us)
Async XLA Ops:
  7.2 421.2 %reduce-scatter.2.cloned.1.call-start = ((), (), s32[]{:S(2)}) async-start(), calls=%async_computation.1 | async-start | bytes 5242880 | tf_op jit(solution)/shard_map/reduce_scatter | solution.py:1027
  283.8 80.1 %copy-start.66 = (f32[1,2,4,128]{3,1,2,0:T(2,128)}, f32[1,2,4,128]{3,1,2,0:T(2,128)S(1)}, u32[]{:S(2)}) copy-start(f32[1,2,4,128]{3,1,2,0:T(2,128)S(1)} %copy.180) | copy-start | bytes 12292
  283.8 80.8 %copy-start.58 = (f32[1,2,8,128]{3,1,2,0:T(2,128)}, f32[1,2,8,128]{3,1,2,0:T(2,128)S(1)}, u32[]{:S(2)}) copy-start(f32[1,2,8,128]{3,1,2,0:T(2,128)S(1)} %copy.182) | copy-start | bytes 24580
  288.0 13.9 copy-start.22
  291.9 11.5 copy-start.75
  352.8 8.4 copy-start.4
  352.8 8.4 copy-start.11
  352.8 8.4 copy-start.12
  352.8 8.4 copy-start.64
  352.8 8.4 copy-start.94
  361.3 974.8 %all-gather.2.cloned.1.call-start = ((), (), s32[]{:S(2)}) async-start(), calls=%async_computation.2 | async-start | bytes 5242880 | tf_op jit(solution)/shard_map/all_gather | solution.py:1147
  363.2 67.4 %copy-start.62 = (f32[1,2,8,128]{3,1,2,0:T(2,128)}, f32[1,2,8,128]{3,1,2,0:T(2,128)S(1)}, u32[]{:S(2)}) copy-start(f32[1,2,8,128]{3,1,2,0:T(2,128)S(1)} %copy.184) | copy-start | bytes 24580
  363.8 67.4 %copy-start.38 = (bf16[2048,64]{1,0:T(8,128)(2,1)}, bf16[2048,64]{1,0:T(8,128)(2,1)S(1)}, u32[]{:S(2)}) copy-start(bf16[2048,64]{1,0:T(8,128)(2,1)S(1)} %reshape.354) | copy-start | bytes 786436
  364.6 63.8 %copy-start.17 = (bf16[256,2048]{1,0:T(8,128)(2,1)S(1)}, bf16[256,2048]{1,0:T(8,128)(2,1)}, u32[]{:S(2)}) copy-start(bf16[256,2048]{1,0:T(8,128)(2,1)} %x_ref.1) | copy-start | bytes 3145732
  432.3 160.7 %copy-start.79 = (f32[256]{0:T(256)}, f32[256]{0:T(256)S(1)}, u32[]{:S(2)}) copy-start(f32[256]{0:T(256)S(1)} %fusion.78) | copy-start | bytes 3076
  728.7 15.0 copy-start.60
  1113.5 162.5 %copy-start.49 = (f32[256,64]{0,1:T(8,128)S(1)}, f32[256,64]{0,1:T(8,128)}, u32[]{:S(2)}) copy-start(f32[256,64]{0,1:T(8,128)} %copy-done.48) | copy-start | bytes 196612
  1113.5 162.5 %copy-start.78 = (f32[256]{0:T(256)S(1)}, f32[256]{0:T(256)}, u32[]{:S(2)}) copy-start(f32[256]{0:T(256)} %copy-done.77) | copy-start | bytes 3076
  1113.5 162.5 %copy-start.80 = (f32[256]{0:T(256)S(1)}, f32[256]{0:T(256)}, u32[]{:S(2)}) copy-start(f32[256]{0:T(256)} %copy-done.79) | copy-start | bytes 3076
  1113.5 162.6 %copy-start.28 = (bf16[256,2048]{1,0:T(8,128)(2,1)S(1)}, bf16[256,2048]{1,0:T(8,128)(2,1)}, u32[]{:S(2)}) copy-start(bf16[256,2048]{1,0:T(8,128)(2,1)} %copy-done.27) | copy-start | bytes 3145732
  1113.5 162.9 %copy-start.26 = (bf16[256,2048]{1,0:T(8,128)(2,1)S(1)}, bf16[256,2048]{1,0:T(8,128)(2,1)}, u32[]{:S(2)}) copy-start(bf16[256,2048]{1,0:T(8,128)(2,1)} %reduce-scatter.2.cloned.1.call-done) | copy-start | bytes 3145732
  1113.5 162.9 %copy-start.63 = (f32[1,2,8,128]{3,1,2,0:T(2,128)S(1)}, f32[1,2,8,128]{3,1,2,0:T(2,128)}, u32[]{:S(2)}) copy-start(f32[1,2,8,128]{3,1,2,0:T(2,128)} %copy-done.62) | copy-start | bytes 24580
  1113.5 162.9 %copy-start.85 = (f32[256]{0:T(256)S(1)}, f32[256]{0:T(256)}, u32[]{:S(2)}) copy-start(f32[256]{0:T(256)} %copy-done.84) | copy-start | bytes 3076
  1284.6 24.6 %copy-start.61 = (f32[8,1280]{1,0:T(8,128)S(1)}, f32[8,1280]{1,0:T(8,128)}, u32[]{:S(2)}) copy-start(f32[8,1280]{1,0:T(8,128)} %copy-done.60) | copy-start | bytes 122884
  1335.4 7.1 copy-start.3
  1335.4 7.1 copy-start.5
  1335.4 7.1 copy-start.65
  1415.8 7.1 copy-start.69
  1415.9 7.1 copy-start.76
  1423.6 11.0 copy-start.83
  1456.4 9.6 copy-start.50
  1456.4 9.6 copy-start.81
  (74 other events, 240.0 us)
Sparse Core Ops, SparseCore 0:
  361.4 66.9 reduce-scatter.1
  1282.7 53.3 all-gather.1

commit v4 on v3

--- a/solution.py
+++ b/solution.py
@@ -325,38 +325,7 @@
     return [dma(()), dma((RANKS,)), dma((RANKS,))]
 
 
-def gather_body(own_ref, small_ref, all_ref, small_all, *sems):
-    begin, forward, finish = spread_out(own_ref, all_ref, sems[:9])
-    small_begin, small_finish = small_out(small_ref, small_all, sems[9:])
-    meet()
-    small_begin()
-    begin()
-
-    @pl.loop(0, GSTEPS)
-    def _(q):
-        forward(q)
-
-    finish()
-    small_finish()
-
-
 ANYWHERE = pl.BlockSpec(memory_space=pl.ANY)
-
-
-def gather_near(own, small, collective_id):
-    tokens, depth = own.shape
-    out, small_all = pl.pallas_call(
-        gather_body,
-        out_shape=(
-            jax.ShapeDtypeStruct((4, 2, 2, 2, tokens, depth), own.dtype),
-            jax.ShapeDtypeStruct((RANKS, *small.shape), small.dtype),
-        ),
-        in_specs=[ANYWHERE] * 2,
-        out_specs=[ANYWHERE] * 2,
-        scratch_shapes=spread_sems() + small_sems(),
-        compiler_params=pltpu.CompilerParams(collective_id=collective_id, has_side_effects=True),
-    )(own, small)
-    return out.reshape(RANKS, tokens, depth), small_all
 
 
 def start_body(x_ref, q_ref, k_ref, v_ref, o_ref, pack_ref, own_ref, small_ref,
@@ -401,24 +370,24 @@
     small_begin()
     x_second.start()
     x_first.start()
+    begin()
     for index in (4, 0, 1, 2, 3):
         for k in QUEUE:
             w_copy(index, k).start()
         pair_copy(index, 0).start()
-    begin()
     for item in locals_:
         item.start()
     x_second.wait_recv()
     x_relay.start()
+
+    @pl.loop(0, GSTEPS)
+    def _(q):
+        forward(q)
+
     for index in (4, 0, 1, 2, 3):
         for k in ARRIVE:
             w_copy(index, k).wait_recv()
             pair_copy(index, k).start()
-
-    @pl.loop(0, GSTEPS)
-    def _(q):
-        forward(q)
-
     finish()
     small_finish()
     for item in locals_:
@@ -796,12 +765,8 @@
     )(part.reshape(4, 2, 2, 2, tokens, depth), small)
 
 
-def project_body(flipped, pick_ref, field_ref, *refs):
-    count = len(flipped)
-    weights, (rows_ref, *outs), sums = refs[:count], refs[count:2*count+1], refs[2*count+1:]
-    k = pl.program_id(0)
-    ranks = pick_ref.shape[0]
-    groups = rows_ref.shape[0]
+def fill_rows(pick_ref, field_ref, rows_ref):
+    ranks, groups = pick_ref.shape[0], rows_ref.shape[0]
 
     @pl.loop(0, ranks // 2, unroll=UNROLL)
     def _(i):
@@ -809,54 +774,162 @@
             wide_dot(pick_ref[2 * i + side], field_ref[2 * i + side]).reshape(groups, SLOTS, CHUNK)
             for side in range(2)
         ]
-        rows_ref[:, pl.ds(pl.multiple_of(i * 2 * SLOTS, 2 * SLOTS), 2 * SLOTS)] = jnp.concatenate(parts, axis=1).astype(jnp.bfloat16)
-
-    def project(e, first):
-        rows = rows_ref[e]
-        for weight, flip, total in zip(weights, flipped, sums):
-            term = outer_cols(rows, weight[e]) if flip else wide_dot(rows, weight[e])
-            if first: total[e] = term
-            else: total[e] += term
+        here = pl.ds(pl.multiple_of(i * 2 * SLOTS, 2 * SLOTS), 2 * SLOTS)
+        rows_ref[:, here] = jnp.concatenate(parts, axis=1).astype(jnp.bfloat16)
+
+
+def add_products(k, rows_ref, pairs):
+    groups = rows_ref.shape[0]
+
+    def products(e, first):
+        for product, total in pairs:
+            term = product(rows_ref[e], e)
+            if first:
+                total[e] = term
+            else:
+                total[e] += term
 
     @pl.when(k == 0)
     def _():
         @pl.loop(0, groups)
         def _(e):
-            project(e, True)
+            products(e, True)
 
     @pl.when(k > 0)
     def _():
         @pl.loop(0, groups)
         def _(e):
-            project(e, False)
-
-    @pl.when(k == pl.num_programs(0) - 1)
+            products(e, False)
+
+
+def grads_in_body(pick_ref, field_ref, down_ref, own_ref, small_ref,
+                  rows_ref, plain_ref, all_ref, small_all, total, *sems):
+    begin, forward, finish = spread_out(own_ref, all_ref, sems[:9])
+    small_begin, small_finish = small_out(small_ref, small_all, sems[9:])
+    k, last = pl.program_id(0), pl.num_programs(0) - 1
+
+    @pl.when(k == 0)
     def _():
-        for out, total in zip(outs, sums):
-            pltpu.sync_copy(total, out)
-
-def project(pick, field, weights, flipped):
+        meet()
+        small_begin()
+        begin()
+
+    fill_rows(pick_ref, field_ref, rows_ref)
+    add_products(k, rows_ref, [(lambda rows, e: outer_cols(rows, down_ref[e]), total)])
+
+    @pl.when(k % 2 == 1)
+    def _():
+        forward(k // 2)
+
+    @pl.when(k == last)
+    def _():
+        pltpu.sync_copy(total, plain_ref)
+        finish()
+        small_finish()
+
+
+def grads_in(pick, field, down, own, small, collective_id):
     ranks, width, tokens = pick.shape
     groups, depth = width // SLOTS, field.shape[-1]
-    length = ranks * SLOTS
-    inner = weights[0].shape[1] if flipped[0] else weights[0].shape[2]
-    wspecs = [pl.BlockSpec((groups, inner, CHUNK), lambda k: (0, 0, k)) if f else pl.BlockSpec((groups, CHUNK, inner), lambda k: (0, k, 0)) for f in flipped]
-    flops = 2 * groups * length * depth * (tokens + inner * len(weights))
-    return pl.pallas_call(
-        functools.partial(project_body, flipped),
-        grid=(depth // CHUNK,),
+    length, inner = ranks * SLOTS, down.shape[1]
+    steps = depth // CHUNK
+    rows, plain, whole, small_all = pl.pallas_call(
+        grads_in_body,
+        grid=(steps,),
         in_specs=[
             pl.BlockSpec((ranks, width, tokens), lambda k: (0, 0, 0), pipeline_mode=pl.Buffered(1)),
             pl.BlockSpec((ranks, tokens, CHUNK), lambda k: (0, 0, k)),
-            *wspecs,
+            pl.BlockSpec((groups, inner, CHUNK), lambda k: (0, 0, k)),
+            ANYWHERE,
+            ANYWHERE,
         ],
-        out_specs=[pl.BlockSpec((groups, length, CHUNK), lambda k: (0, 0, k))] + [pl.BlockSpec(memory_space=pl.ANY)] * len(weights),
-        out_shape=[jax.ShapeDtypeStruct((groups, length, depth), jnp.bfloat16)]
-        + [jax.ShapeDtypeStruct((groups, length, inner), jnp.float32)] * len(weights),
-        scratch_shapes=[pltpu.VMEM((groups, length, inner), jnp.float32)] * len(weights),
+        out_specs=[pl.BlockSpec((groups, length, CHUNK), lambda k: (0, 0, k))] + [ANYWHERE] * 3,
+        out_shape=[
+            jax.ShapeDtypeStruct((groups, length, depth), jnp.bfloat16),
+            jax.ShapeDtypeStruct((groups, length, inner), jnp.float32),
+            jax.ShapeDtypeStruct((4, 2, 2, 2, *own.shape), own.dtype),
+            jax.ShapeDtypeStruct((RANKS, *small.shape), small.dtype),
+        ],
+        scratch_shapes=[pltpu.VMEM((groups, length, inner), jnp.float32)] + spread_sems() + small_sems(),
+        compiler_params=pltpu.CompilerParams(
+            collective_id=collective_id, has_side_effects=True, vmem_limit_bytes=62 * 1024 * 1024
+        ),
+    )(pick, field, down, own, small)
+    return rows, plain, whole.reshape(RANKS, *own.shape), small_all
+
+
+def feed_in_body(steps, pick_ref, field_ref, gate_ref, up_ref, plain_ref, probs_ref,
+                 rows_ref, act_ref, weighted_ref, grad_gate_ref, grad_up_ref, gates_ref, gate_sum, up_sum):
+    k = pl.program_id(0)
+
+    @pl.when(k < steps)
+    def _():
+        fill_rows(pick_ref, field_ref, rows_ref)
+        add_products(
+            k,
+            rows_ref,
+            [
+                (lambda rows, e: wide_dot(rows, gate_ref[e]), gate_sum),
+                (lambda rows, e: wide_dot(rows, up_ref[e]), up_sum),
+            ],
+        )
+
+    @pl.when(k >= steps)
+    def _():
+        e = k - steps
+        length = act_ref.shape[1]
+
+        @pl.loop(0, length // 128)
+        def _(t):
+            here = pl.ds(pl.multiple_of(t * 128, 128), 128)
+            gate_val, up_val = gate_sum[e, here], up_sum[e, here]
+            plain, probs = plain_ref[0, here], probs_ref[0, here]
+            sigmoid_val = jax.nn.sigmoid(gate_val)
+            silu_val = gate_val * sigmoid_val
+            activated = silu_val * up_val
+            grad_act = plain * probs
+            grad_up_ref[0, here] = (grad_act * silu_val).astype(jnp.bfloat16)
+            grad_gate_ref[0, here] = (
+                grad_act * up_val * (sigmoid_val * (1.0 + gate_val * (1.0 - sigmoid_val)))
+            ).astype(jnp.bfloat16)
+            gates_ref[0, here] = jnp.sum(activated * plain, axis=-1, keepdims=True)
+            weighted_ref[0, here] = (activated * probs).astype(jnp.bfloat16)
+            act_ref[0, here] = activated.astype(jnp.bfloat16)
+
+
+def feed_in(pick, field, gate, up, plain, probs):
+    ranks, width, tokens = pick.shape
+    groups, depth = width // SLOTS, field.shape[-1]
+    length, inner = ranks * SLOTS, gate.shape[2]
+    steps = depth // CHUNK
+    held = lambda k: jnp.minimum(k, steps - 1)
+    late = lambda k: (jnp.maximum(k - steps, 0), 0, 0)
+    wide = pl.BlockSpec((1, length, inner), late)
+    thin = pl.BlockSpec((1, length, 1), late)
+    low = jax.ShapeDtypeStruct((groups, length, inner), jnp.bfloat16)
+    return pl.pallas_call(
+        functools.partial(feed_in_body, steps),
+        grid=(steps + groups,),
+        in_specs=[
+            pl.BlockSpec((ranks, width, tokens), lambda k: (0, 0, 0), pipeline_mode=pl.Buffered(1)),
+            pl.BlockSpec((ranks, tokens, CHUNK), lambda k: (0, 0, held(k))),
+            pl.BlockSpec((groups, CHUNK, inner), lambda k: (0, held(k), 0)),
+            pl.BlockSpec((groups, CHUNK, inner), lambda k: (0, held(k), 0)),
+            wide,
+            thin,
+        ],
+        out_specs=[pl.BlockSpec((groups, length, CHUNK), lambda k: (0, 0, held(k))), wide, wide, wide, wide, thin],
+        out_shape=[
+            jax.ShapeDtypeStruct((groups, length, depth), jnp.bfloat16),
+            low, low, low, low,
+            jax.ShapeDtypeStruct((groups, length, 1), jnp.float32),
+        ],
+        scratch_shapes=[pltpu.VMEM((groups, length, inner), jnp.float32)] * 2,
         compiler_params=pltpu.CompilerParams(vmem_limit_bytes=63 * 1024 * 1024),
-        cost_estimate=pl.CostEstimate(flops=flops, bytes_accessed=120 << 20, transcendentals=0),
-    )(pick, field.reshape(ranks, tokens, depth), *weights)
+        cost_estimate=pl.CostEstimate(
+            flops=2 * groups * length * depth * (tokens + 2 * inner), bytes_accessed=120 << 20, transcendentals=0
+        ),
+    )(pick, field, gate, up, plain, probs)
 
 
 def restore_body(flipped, spread_ref, *refs):
@@ -1054,19 +1127,39 @@
     places = jnp.arange(SLOTS, dtype=jnp.float32)
     slot_t = jnp.swapaxes(slot, 1, 2)
     width = experts_local * SLOTS
-    pick = (slot_t[:, :, None, :] == places[None, None, :, None]).astype(jnp.bfloat16)
-    pick = pick.reshape(ranks, width, tokens)
-    spread = slot[:, :, :, None] == places
-    spread_plain = spread.astype(jnp.bfloat16).reshape(ranks, tokens, width)
+    picked = slot_t[:, :, None, :] == places[None, None, :, None]
+    pick = picked.astype(jnp.bfloat16).reshape(ranks, width, tokens)
+    lanes = jnp.arange(width, dtype=jnp.int32)
+    widen = (lanes[None, :] // SLOTS == jnp.arange(experts_local)[:, None]).astype(jnp.bfloat16)
+    spread = jnp.einsum(
+        "ste,ew->stw", slot.astype(jnp.bfloat16), widen, preferred_element_type=jnp.float32
+    ) == (lanes % SLOTS).astype(jnp.float32)
+    spread_plain = spread.astype(jnp.bfloat16)
+
+    def weigh(probs_all):
+        probs_own = jnp.sum(
+            jnp.where(matches, probs_all.reshape(ranks, tokens, -1, 1), 0.0), axis=2
+        )
+        probs_wide = jnp.einsum(
+            "ste,ew->stw", probs_own.astype(jnp.bfloat16), widen, preferred_element_type=jnp.float32
+        )
+        spread_probs = jnp.where(spread, probs_wide, 0.0).astype(jnp.bfloat16)
+        probs_t = jnp.swapaxes(probs_own, 1, 2)
+        row_probs = jnp.sum(jnp.where(picked, probs_t[:, :, None, :], 0.0), axis=-1)
+        row_probs = jnp.swapaxes(row_probs, 0, 1).reshape(experts_local, ranks * SLOTS, 1)
+        return spread_probs, row_probs
+
     if near:
-        expert_grads, plain_act = project(pick, cotangent_all, [down_weight], (True,))
-        feed_all, probs_all = gather_near(feed_normed, gate_probs.T, 2)
-        probs_all = jnp.swapaxes(probs_all, 1, 2)
-        expert_rows, gate_val, up_val = project(
-            pick, feed_all, [gate_weight, up_weight], (False, False)
+        expert_grads, plain_act, feed_all, probs_all = grads_in(
+            pick, cotangent_all, down_weight, feed_normed, gate_probs.T, 2
+        )
+        spread_probs, row_probs = weigh(jnp.swapaxes(probs_all, 1, 2))
+        expert_rows, activated, weighted_act, grad_gate, grad_up, row_gates = feed_in(
+            pick, feed_all, gate_weight, up_weight, plain_act, row_probs
         )
     else:
         probs_all = lax.all_gather(gate_probs, ("col", "row"), axis=0, tiled=True)
+        spread_probs, row_probs = weigh(probs_all)
         expert_grads = gather_rows(pick, cotangent)
         expert_rows = gather_rows(pick, feed_normed)
         gate_val = jnp.einsum(
@@ -1078,27 +1171,20 @@
         plain_act = jnp.einsum(
             "erd,efd->erf", expert_grads, down_weight, preferred_element_type=jnp.float32
         )
-    probs_own = jnp.sum(
-        jnp.where(matches, probs_all.reshape(ranks, tokens, -1, 1), 0.0), axis=2
-    )
-    weighted = jnp.where(spread, probs_own[..., None], 0.0)
-    spread_probs = weighted.astype(jnp.bfloat16).reshape(ranks, tokens, width)
-    row_probs = jnp.sum(weighted, axis=1)
-    row_probs = jnp.swapaxes(row_probs, 0, 1).reshape(experts_local, ranks * SLOTS, 1)
-    sigmoid_val = jax.nn.sigmoid(gate_val)
-    silu_val = gate_val * sigmoid_val
-    activated = silu_val * up_val
-    grad_act = plain_act * row_probs
-    grad_up = (grad_act * silu_val).astype(jnp.bfloat16)
-    grad_gate = (
-        grad_act * up_val * sigmoid_val * (1.0 + gate_val * (1.0 - sigmoid_val))
-    ).astype(jnp.bfloat16)
-    row_gates = jnp.sum(activated * plain_act, axis=-1).reshape(experts_local, ranks, 1, SLOTS)
-    weighted_act = (activated * row_probs).astype(jnp.bfloat16)
-    activated = activated.astype(jnp.bfloat16)
-    own_gates = jnp.sum(jnp.where(spread, jnp.transpose(row_gates, (1, 2, 0, 3)), 0.0), axis=-1)
+        sigmoid_val = jax.nn.sigmoid(gate_val)
+        silu_val = gate_val * sigmoid_val
+        activated = silu_val * up_val
+        grad_act = plain_act * row_probs
+        grad_up = (grad_act * silu_val).astype(jnp.bfloat16)
+        grad_gate = (
+            grad_act * up_val * sigmoid_val * (1.0 + gate_val * (1.0 - sigmoid_val))
+        ).astype(jnp.bfloat16)
+        row_gates = jnp.sum(activated * plain_act, axis=-1)
+        weighted_act = (activated * row_probs).astype(jnp.bfloat16)
+        activated = activated.astype(jnp.bfloat16)
+    row_gates = jnp.swapaxes(row_gates.reshape(experts_local, ranks, SLOTS), 0, 1)
+    own_gates = jnp.sum(jnp.where(picked, row_gates[..., None], 0.0), axis=2)
     if near:
-        own_gates = jnp.swapaxes(own_gates, 1, 2)
         grad_feed_part = restore(
             spread_plain, [grad_gate, grad_up], [gate_weight, up_weight], (True, True)
         )
@@ -1109,7 +1195,9 @@
         mixture = reduce_near(mixture_part, own_gates, 3)[0]
     else:
         own_gates = lax.psum_scatter(
-            own_gates.reshape(-1, rows_count, tokens, experts_local), "row", scatter_dimension=1
+            jnp.swapaxes(own_gates, 1, 2).reshape(-1, rows_count, tokens, experts_local),
+            "row",
+            scatter_dimension=1,
         )
         grad_probs = lax.all_to_all(own_gates, "col", split_axis=0, concat_axis=2, tiled=True)[0]
         back_rows = (

time: 1630 us -> 1450 us (0.89)
  Pallas kernels: 1110 us -> 1010 us
  other arithmetic: 148 us -> 97.1 us
  local copies, waits for them, and re-layouts: 83.3 us -> 59 us
  waiting for transfers between devices: 59 us -> 41.1 us
    pallas_call x1, Pallas kernels: 267 us -> 203 us  [start_near(): pl.pallas_call(start_body, out_shape=(shaped((4, *x.shape), x), *[shaped(...]
    convert_element_type x5 -> x1, other arithmetic: 43.1 us -> 3.68 us  [local(): pick = picked.astype(jnp.bfloat16).reshape(ranks, width, tokens)]
    pallas_call x3 -> x2, Pallas kernels: 270 us -> 237 us  [the longest x1 163 us: grads_in(): pl.pallas_call(grads_in_body, grid=(steps,), in_specs=[pl.BlockSpec((rank...]
    reduce_scatter x1, waiting for transfers between devices: 58.4 us -> 38.5 us  [local(): lax.psum_scatter(wide_dot(mixed_heads, output_full).astype(jnp.bfloat16),...]
    eq x4 -> x2, local copies, waits for them, and re-layouts: 17.1 us -> 0.09 us  [local(): picked = slot_t[:, :, None, :] == places[None, None, :, None]]
  transfers between devices with their start and end apart: 2 -> 2, of which waited for: 2 -> 2; matrix products, arithmetic and copies ran while one was open for 4% -> 5% of each run, Pallas kernels for 0% -> 0%
where the time goes in v4:
time: 1450 us; the launch traced here: 1440 us
  Pallas kernels  1010 us (70%)
  matrix products  188 us (13%)
  other arithmetic  97.1 us (7%)
  local copies, waits for them, and re-layouts  59 us (4%)
  waiting for transfers between devices  41.1 us (3%)
  blocking collectives  17.5 us (1%)
  between operations  15.1 us (1%)
    pallas_call x2, Pallas kernels, reduce_near(): pl.pallas_call(reduce_body, out_shape=(jax.ShapeDtypeStruct((tokens, dept...  337 us
    pallas_call x1, Pallas kernels, start_near(): pl.pallas_call(start_body, out_shape=(shaped((4, *x.shape), x), *[shaped(...  203 us
    pallas_call x1, Pallas kernels, grads_in(): pl.pallas_call(grads_in_body, grid=(steps,), in_specs=[pl.BlockSpec((rank...  163 us
    pallas_call x2, Pallas kernels, restore(): pl.pallas_call(functools.partial(restore_body, flipped), grid=(depth // C...  119 us
    pallas_call x1, Pallas kernels, finish_near(): pl.pallas_call(finish_body, out_shape=(jax.ShapeDtypeStruct((tokens, dept...  119 us
    pallas_call x1, Pallas kernels, feed_in(): pl.pallas_call(functools.partial(feed_in_body, steps), grid=(steps + grou...  73.8 us
    reduce_scatter x1, waiting for transfers between devices, local(): lax.psum_scatter(wide_dot(mixed_heads, output_full).astype(jnp.bfloat16),...  38.5 us
  transfers between devices with their start and end apart: 2, of which 2 were waited for; matrix products, arithmetic and copies ran while one was open for 5% of the time, Pallas kernels for 0%

profile of v4, /device:TPU:0, one launch (start us, length us, event | category | flops | bytes accessed | tf_op | source)
XLA Modules:
  0.0 1440.8 jit_solution(10576060945542884003)
XLA Ops:
  11.6 203.4 %shard_map.254 = (bf16[4,256,2048]{2,1,0:T(8,128)(2,1)}, bf16[2048,512]{1,0:T(8,128)(2,1)}, bf16[2048,512]{1,0:T(8,128)(2,1)}, bf16[2048,512]{1,0:T(8,128)(2,1)}...) custom-call(bf16[256,2048]{1,0:T(8,128)(2,1)} %x_ref.1, ...), custom_call_target="tpu_custom_call" | custom-call | tf_op jit(solution)/shard_map/pallas_call | solution.py:410
  228.7 8.6 all-reduce.2
  259.4 6.1 fusion.52
  265.6 23.1 %while.30 = (s32[]{:T(128)}, bf16[2,512,4,128]{3,1,2,0:T(8,128)(2,1)}, f32[2,4,512]{2,1,0:T(4,128)S(1)}, s32[2]{0:T(128)S(1)}, bf16[1024,4,128]{2,0,1:T(8,128)(2...) while((s32[]{:T(128)}, ...), condition=%wide.region_8.9_spmd.clone.clone, body=%wide.region_5.8_spmd.clone.sunk.clone | while | flops 1099430400 | bytes 31003272 | solution.py:1097
  292.7 4.4 convolution_convert_fusion
  305.3 5.2 fusion.40
  310.5 5.4 fusion.100
  315.9 38.5 %reduce-scatter.2.cloned.1.call-done = bf16[256,2048]{1,0:T(8,128)(2,1)} async-done(((bf16[1024,2048]{1,0:T(8,128)(2,1)}), bf16[256,2048]{1,0:T(8,128)(2,1)}) %reduce-scatter.2.cloned.1.call-update) | async-done | bytes 1048592 | tf_op jit(solution)/shard_map/reduce_scatter | solution.py:1100
  358.5 163.4 %shard_map.255 = (bf16[8,1280,2048]{2,1,0:T(8,128)(2,1)}, f32[8,1280,256]{2,1,0:T(8,128)}, bf16[4,2,2,2,256,2048]{5,4,3,2,1,0:T(8,128)(2,1)}, f32[32,8,256]{2,1,0:T(8,128)}) custom-call(bf16[32,320,256]{2,1,0:T(8,128)(2,1)} %fusion.37.pick_ref, bf16[32,256,2048]{2,1,0:T(8,128)(2,1)} %bitcast.240, bf16[8,256,2048]{2,1,0:T(8,128)(2,1)} %refs_1_.1, ...), custom_call_target="tpu_custom_call" | custom-call | tf_op jit(solution)/shard_map/pallas_call | solution.py:836
  527.9 6.5 select_convert_fusion.spread_ref
  534.4 73.8 %shard_map.256 = (bf16[8,1280,2048]{2,1,0:T(8,128)(2,1)}, bf16[8,1280,256]{2,1,0:T(8,128)(2,1)}, bf16[8,1280,256]{2,1,0:T(8,128)(2,1)}, bf16[8,1280,256]{2,1,0:T...) custom-call(bf16[32,320,256]{2,1,0:T(8,128)(2,1)} %fusion.37.pick_ref, ...), custom_call_target="tpu_custom_call" | custom-call | flops 32212254720 | bytes 125829120 | tf_op jit(solution)/shard_map/pallas_call | solution.py:910
  608.2 3.9 reduce.3
  615.2 24.3 %fusion.105 = f32[8,2048,256]{2,1,0:T(8,128)} fusion(bf16[8,1280,2048]{2,1,0:T(8,128)(2,1)} %get-tuple-element.172, bf16[8,1280,256]{2,1,0:T(8,128)(2,1)} %get-tuple-element.159.refs_1_), kind=kOutput, calls=%fused_computation.212 | convolution fusion | flops 10737418240 | bytes 63963136 | tf_op jit(solution)/shard_map/erd,erf->edf/dot_general | solution.py:1216
  639.5 52.0 %shard_map.257 = bf16[32,256,2048]{2,1,0:T(8,128)(2,1)} custom-call(bf16[32,256,320]{2,1,0:T(8,128)(2,1)} %select_convert_fusion.spread_ref, bf16[8,1280,256]{2,1,0:T(8,128)(2,1)} %get-tuple-element.155.refs_0_, bf16[8,256,2048]{2,1,0:T(8,128)(2,1)} %refs_1_.1), custom_call_target="tpu_custom_call" | custom-call | flops 21474836480 | bytes 62914560 | tf_op jit(solution)/shard_map/pallas_call | solution.py:962
  691.5 176.4 %shard_map.258 = (f32[256,2048]{1,0:T(8,128)}, f32[32,8,256]{2,1,0:T(8,128)}) custom-call(bf16[4,2,2,2,256,2048]{5,4,3,2,1,0:T(8,128)(2,1)} %bitcast.242, f32[32,8,256]{2,1,0:T(8,128)} %select_reduce_fusion.small_ref), custom_call_target="tpu_custom_call" | custom-call | tf_op jit(solution)/shard_map/pallas_call | solution.py:739
  868.0 66.9 %shard_map.259 = bf16[32,256,2048]{2,1,0:T(8,128)(2,1)} custom-call(bf16[32,256,320]{2,1,0:T(8,128)(2,1)} %get-tuple-element.423.spread_ref, bf16[8,1280,256]{2,1,0:T(8,128)(2,1)} %get-tuple-element.158.refs_0_, bf16[8,1280,256]{2,1,0:T(8,128)(2,1)} %get-tuple-element.159.refs_1_, bf16[8,2048,256]{2,1,0:T(8,128)(2,1)} %refs_2_.1, bf16[8,2048,256]{2,1,0:T(8,128)(2,1)} %refs_3_.1), custom_call_target="tpu_custom_call" | custom-call | flops 32212254720 | bytes 62914560 | tf_op jit(solution)/shard_map/pallas_call | solution.py:962
  934.9 160.2 %shard_map.260 = (f32[256,2048]{1,0:T(8,128)}, f32[32,8,256]{2,1,0:T(8,128)}) custom-call(bf16[4,2,2,2,256,2048]{5,4,3,2,1,0:T(8,128)(2,1)} %bitcast.241, f32[32,8,256]{2,1,0:T(8,128)} %select_reduce_fusion.small_ref), custom_call_target="tpu_custom_call" | custom-call | tf_op jit(solution)/shard_map/pallas_call | solution.py:739
  1104.8 24.8 %fusion.104 = f32[8,2048,256]{2,1,0:T(8,128)} fusion(bf16[8,1280,2048]{2,1,0:T(8,128)(2,1)} %get-tuple-element.172, bf16[8,1280,256]{2,1,0:T(8,128)(2,1)} %get-tuple-element.158.refs_0_), kind=kOutput, calls=%fused_computation.211 | convolution fusion | flops 10737418240 | bytes 63963136 | tf_op jit(solution)/shard_map/erd,erf->edf/dot_general | solution.py:1213
  1129.6 24.1 %fusion.106 = f32[8,256,2048]{2,1,0:T(8,128)} fusion(bf16[8,1280,256]{2,1,0:T(8,128)(2,1)} %get-tuple-element.173, bf16[8,1280,2048]{2,1,0:T(8,128)(2,1)} %get-tuple-element.174), kind=kOutput, calls=%fused_computation.213 | convolution fusion | flops 10737418240 | bytes 63963136 | tf_op jit(solution)/shard_map/erf,erd->efd/dot_general | solution.py:1219
  1156.3 6.2 convolution_convert_fusion.6
  1162.5 50.6 %while.31 = (s32[]{:T(128)}, f32[1024,4,128]{0,2,1:T(8,128)S(1)}, f32[1024,4,128]{0,2,1:T(8,128)}, f32[2,512,4,128]{3,1,2,0:T(8,128)}, s32[2]{0:T(128)S(1)}, /*i...) while((s32[]{:T(128)}, f32[1024,4,128]{0,2,1:T(8,128)S(1)}, ...), condition=%wide.region_23.24_spmd.clone.clone, body=%wide.region_21.23_spmd.clone.sunk.clone | while | flops 2719218176 | bytes 180417440 | solution.py:1272
  1183.3 4.0 bitcast_add_fusion.9
  1207.9 5.2 bitcast_add_fusion.9
  1216.2 4.1 copy.134
  1222.6 3.9 broadcast_multiply_fusion
  1246.0 8.9 all-reduce.3
  1259.6 3.9 convolution_convert_fusion.3.k_ref
  1265.0 5.7 fusion.102
  1270.7 3.8 convolution_convert_fusion.4.q_ref
  1276.8 9.4 fusion.48
  1287.2 6.1 convolution_convert_fusion.2.v_ref
  1300.9 118.8 %shard_map.261 = (f32[256,2048]{1,0:T(8,128)}, f32[256,512]{1,0:T(8,128)}, f32[256,512]{1,0:T(8,128)}, f32[256,512]{1,0:T(8,128)}, f32[512,256]{1,0:T(8,128)}, /*index=5*/bf16[32,144,128]{2,1,0:T(8,128)(2,1)}) custom-call(bf16[4,256,2048]{2,1,0:T(8,128)(2,1)} %bitcast.243, bf16[2048,512]{1,0:T(8,128)(2,1)} %convolution_convert_fusion.4.q_ref, ...), custom_call_target="tpu_custom_call" | custom-call | tf_op jit(solution)/shard_map/pallas_call | solution.py:567
  (331 shorter events, 189.2 us)
Async XLA Ops:
  7.2 347.3 %reduce-scatter.2.cloned.1.call-start = ((), (), s32[]{:S(2)}) async-start(), calls=%async_computation.1 | async-start | bytes 5242880 | tf_op jit(solution)/shard_map/reduce_scatter | solution.py:1100
  220.5 84.2 %copy-start.59 = (f32[1,2,4,128]{3,1,2,0:T(2,128)}, f32[1,2,4,128]{3,1,2,0:T(2,128)S(1)}, u32[]{:S(2)}) copy-start(f32[1,2,4,128]{3,1,2,0:T(2,128)S(1)} %copy.155) | copy-start | bytes 12292
  220.6 84.7 %copy-start.55 = (f32[1,2,8,128]{3,1,2,0:T(2,128)}, f32[1,2,8,128]{3,1,2,0:T(2,128)S(1)}, u32[]{:S(2)}) copy-start(f32[1,2,8,128]{3,1,2,0:T(2,128)S(1)} %copy.157) | copy-start | bytes 24580
  224.8 13.2 copy-start.22
  228.7 10.8 copy-start.68
  237.9 6.3 copy-start.63
  249.3 7.1 copy-start.40
  288.7 8.4 copy-start.4
  288.7 8.4 copy-start.11
  288.7 8.4 copy-start.12
  288.7 8.4 copy-start.57
  288.7 8.4 copy-start.81
  297.1 859.2 %all-gather.2.cloned.1.call-start = ((), (), s32[]{:S(2)}) async-start(), calls=%async_computation.2 | async-start | bytes 5242880 | tf_op jit(solution)/shard_map/all_gather | solution.py:1235
  310.5 43.9 %copy-start.17 = (bf16[256,2048]{1,0:T(8,128)(2,1)S(1)}, bf16[256,2048]{1,0:T(8,128)(2,1)}, u32[]{:S(2)}) copy-start(bf16[256,2048]{1,0:T(8,128)(2,1)} %x_ref.1) | copy-start | bytes 3145732
  934.9 161.4 %copy-start.26 = (bf16[256,2048]{1,0:T(8,128)(2,1)S(1)}, bf16[256,2048]{1,0:T(8,128)(2,1)}, u32[]{:S(2)}) copy-start(bf16[256,2048]{1,0:T(8,128)(2,1)} %copy-done.25) | copy-start | bytes 3145732
  934.9 161.7 %copy-start.28 = (bf16[256,2048]{1,0:T(8,128)(2,1)S(1)}, bf16[256,2048]{1,0:T(8,128)(2,1)}, u32[]{:S(2)}) copy-start(bf16[256,2048]{1,0:T(8,128)(2,1)} %reduce-scatter.2.cloned.1.call-done) | copy-start | bytes 3145732
  1153.7 8.8 copy-start.3
  1153.7 8.8 copy-start.5
  1153.7 8.8 copy-start.58
  1153.7 8.8 copy-start.82
  1176.2 6.1 copy-start.1
  1200.8 6.1 copy-start.1
  1236.1 7.2 copy-start.62
  1236.2 7.2 copy-start.69
  1238.1 5.2 copy-start.44
  1243.9 11.0 copy-start.72
  1270.7 5.7 copy-start.9
  1276.8 9.6 copy-start.47
  1276.8 9.6 copy-start.70
  1287.2 6.1 copy-start.10
  1287.2 6.3 copy-start.16
  1287.2 6.3 copy-start.73
  (61 other events, 172.6 us)
Sparse Core Ops, SparseCore 0:
  297.2 57.2 reduce-scatter.1
  1102.9 53.3 all-gather.1

commit v5 on v4

--- a/solution.py
+++ b/solution.py
@@ -428,16 +428,18 @@
     return x_all.reshape(-1, x.shape[1]), q, k, v, o, pack_all, whole.reshape(RANKS, tokens, depth), small_all
 
 
-def finish_body(field_ref, q_ref, k_ref, v_ref, o_ref, pack_ref,
-                out_ref, q_out, k_out, v_out, o_out, pack_all,
+def finish_body(part_ref, field_ref, q_ref, k_ref, v_ref, o_ref, pack_ref,
+                mixture_ref, out_ref, q_out, k_out, v_out, o_out, pack_all,
                 mine, first_in, second_in, total,
                 q_mine, k_mine, v_mine, o_mine, q_pair, k_pair, v_pair, o_pair, q_z, k_z, v_z, o_z,
                 q_sum, k_sum, v_sum, o_sum,
                 load_sem, f_send, f_recv, g_send, g_recv, w_load, p_send, p_recv, z_send, z_recv, out_sem,
-                *small):
+                *rest):
     r, c, y, x, z, core, first, second = seat()
     pair, along_first, along_second, up = partners()
-    here_sem, small_send, small_recv = small
+    small_begin, small_finish = small_each(pack_ref, pack_all, rest[:3], lambda spot: spot // 4)
+    begin, tick, finish = shrink(part_ref, *rest[3:9], rest[9:18])
+    mixture = rest[8]
     tokens, depth = out_ref.shape
     other = 1 - core
     grads = [q_ref, k_ref, v_ref, o_ref]
@@ -455,11 +457,6 @@
     def row(fir, sec):
         yy, xx = row_of(core, fir, sec)
         return yy * 2 + xx
-
-    local = pltpu.make_async_copy(pack_ref.at[c], pack_all.at[nth(0)[0]], here_sem)
-
-    def small_of(offset):
-        return small_copy(lambda spot: pack_ref.at[spot // 4], pack_all, small_send, small_recv, offset)
 
     def load(fir, sec):
         return pltpu.make_async_copy(field_ref.at[row(fir, sec)], mine.at[fir, sec], load_sem.at[fir, sec])
@@ -501,46 +498,56 @@
             result[here] = value
 
     meet()
-    f_copy(1 - second).start()
-    f_copy(second).start()
     for index in range(4):
         for k in (2, 1, 3, 0):
             w_give(index, (z + k) % 4).start()
             w_load_copy(index, (z + k) % 4).start()
+    begin()
+    f_copy(1 - second).start()
+    f_copy(second).start()
     load(first, 1 - second).start()
     load(first, second).start()
-    local.start()
-
-    @pl.loop(1, RANKS)
-    def _(offset):
-        small_of(offset).start()
-
+    small_begin()
     for index in range(4):
-        for k in (2, 1, 3):
+        for k in QUEUE:
             zz = (z + k) % 4
             w_load_copy(index, zz).wait()
             w_give(index, zz).wait_recv()
             add(kept[index].at[zz], [pairs[index].at[zz]])
             w_z(index, k).start()
-    load(first, 1 - second).wait()
-    f_copy(1 - second).wait_recv()
-    add(mine.at[first, 1 - second], [first_in.at[1 - second]])
-    g_copy.start()
-    load(first, second).wait()
-    f_copy(second).wait_recv()
+
+    @pl.loop(0, RSTEPS)
+    def _(i):
+        tick(i)
+
+        @pl.when(i == 2)
+        def _():
+            load(first, 1 - second).wait()
+            f_copy(1 - second).wait_recv()
+            add(mine.at[first, 1 - second], [first_in.at[1 - second]])
+            g_copy.start()
+
     for index in range(4):
         w_load_copy(index, z).wait()
         w_give(index, z).wait_recv()
-    g_copy.wait_recv()
-    add_out(mine.at[first, second], [first_in.at[second], second_in], total)
-    pltpu.make_async_copy(total, out_ref, out_sem.at[4]).start()
-    for index in range(4):
         for k in ARRIVE:
             w_z(index, k).wait_recv()
         add_out(
             kept[index].at[z], [pairs[index].at[z]] + [zs[index].at[k] for k in range(3)], sums[index]
         )
         pltpu.make_async_copy(sums[index], outs[index], out_sem.at[index]).start()
+    load(first, second).wait()
+    f_copy(second).wait_recv()
+    g_copy.wait_recv()
+    add_out(mine.at[first, second], [first_in.at[second], second_in], total)
+    pltpu.make_async_copy(total, out_ref, out_sem.at[4]).start()
+
+    @pl.loop(RSTEPS, TICKS)
+    def _(i):
+        tick(i)
+
+    pltpu.make_async_copy(mixture, mixture_ref, out_sem.at[5]).start()
+    finish()
     for sec in range(2):
         f_copy(sec).wait_send()
     g_copy.wait_send()
@@ -550,16 +557,12 @@
             if k:
                 w_z(index, k).wait_send()
         pltpu.make_async_copy(sums[index], outs[index], out_sem.at[index]).wait()
-    local.wait()
-
-    @pl.loop(1, RANKS)
-    def _(offset):
-        small_of(offset).wait()
-
+    small_finish()
     pltpu.make_async_copy(total, out_ref, out_sem.at[4]).wait()
-
-
-def finish_near(field, grads, pack, collective_id):
+    pltpu.make_async_copy(mixture, mixture_ref, out_sem.at[5]).wait()
+
+
+def finish_near(part, field, grads, pack, collective_id):
     rows_count, tokens, depth = field.shape
     dma = pltpu.SemaphoreType.DMA
     blocks = [(g.shape[0] // 8, g.shape[1]) for g in grads[:3]] + [(grads[3].shape[0], grads[3].shape[1] // 8)]
@@ -568,201 +571,270 @@
         finish_body,
         out_shape=(
             jax.ShapeDtypeStruct((tokens, depth), jnp.float32),
+            jax.ShapeDtypeStruct((tokens, depth), jnp.float32),
             *[jax.ShapeDtypeStruct(b, jnp.float32) for b in blocks],
             jax.ShapeDtypeStruct((RANKS, *pack.shape[1:]), pack.dtype),
         ),
-        in_specs=[ANYWHERE] * 6,
-        out_specs=[ANYWHERE] * 6,
+        in_specs=[ANYWHERE] * 7,
+        out_specs=[ANYWHERE] * 7,
         scratch_shapes=[
             half(2, 2, tokens, depth), half(2, tokens, depth), half(tokens, depth),
             pltpu.VMEM((tokens, depth), jnp.float32),
             *[half(4, *b) for b in blocks], *[half(4, *b) for b in blocks], *[half(3, *b) for b in blocks],
             *[pltpu.VMEM(b, jnp.float32) for b in blocks],
             dma((2, 2)), dma((2,)), dma((2,)), dma(()), dma(()),
-            dma((4, 4)), dma((4, 4)), dma((4, 4)), dma((4, 3)), dma((4, 3)), dma((5,)),
+            dma((4, 4)), dma((4, 4)), dma((4, 4)), dma((4, 3)), dma((4, 3)), dma((6,)),
         ]
-        + small_sems(),
+        + small_sems()
+        + shrink_scratch(tokens, depth),
         compiler_params=pltpu.CompilerParams(
-            collective_id=collective_id, has_side_effects=True, vmem_limit_bytes=60 * 1024 * 1024
+            collective_id=collective_id, has_side_effects=True, vmem_limit_bytes=63 * 1024 * 1024
         ),
-    )(field, *grads, pack)
+    )(part.reshape(4, 2, 2, 2, tokens, depth), field, *grads, pack)
 
 
 RSTEPS = 8
 TILE = 16
-
-
-def reduce_body(part_ref, small_ref, out_ref, small_all, mine, pair_in, first_in, second_in, z_in, total,
-                load_sem, p_send, p_recv, f_send, f_recv, g_send, g_recv, z_send, z_recv, out_sem,
-                small_here, small_send, small_recv):
+LAGS = (0, 1, 2, 4)
+TICKS = RSTEPS + LAGS[3]
+
+
+def shrink(part_ref, sums, near_own, first_in, second_in, z_in, total, sems):
     r, c, y, x, z, core, first, second = seat()
     pair, along_first, along_second, up = partners()
-    tokens, depth = out_ref.shape
+    load_sem, p_send, p_recv, f_send, f_recv, g_send, g_recv, z_send, z_recv = sems
+    tokens = total.shape[0]
     step = tokens // RSTEPS
     other = 1 - core
 
     def rows(q):
         return pl.ds(pl.multiple_of(q * step, step), step)
 
-    meet()
-
-    small_local = pltpu.make_async_copy(small_ref.at[nth(0)[0]], small_all.at[nth(0)[0]], small_here)
-    small_local.start()
-
-    def small(offset):
-        return small_copy(lambda spot: small_ref.at[spot], small_all, small_send, small_recv, offset)
-
-    @pl.loop(1, RANKS)
-    def _(offset):
-        small(offset).start()
-
-    def load(f, s, q):
-        yy, xx = row_of(core, f, s)
-        return pltpu.make_async_copy(part_ref.at[:, core, yy, xx, rows(q)], mine.at[f, s, :, rows(q)], load_sem.at[f, s, q])
-
-    def give(f, s, q):
-        yy, xx = row_of(other, f, s)
-        return send(part_ref.at[:, other, yy, xx, rows(q)], pair_in.at[f, s, :, rows(q)],
-                    p_send.at[f, s, q], p_recv.at[f, s, q], pair)
-
-    def f_copy(s, q):
-        return send(mine.at[1 - first, s, :, rows(q)], first_in.at[s, :, rows(q)], f_send.at[s, q], f_recv.at[s, q], along_first)
+    def spot(kind):
+        fir = (1 - first) if kind < 2 else first
+        sec = (1 - second) if kind in (0, 2) else second
+        return fir, sec
+
+    def load(kind, q):
+        yy, xx = row_of(core, *spot(kind))
+        return pltpu.make_async_copy(
+            part_ref.at[:, core, yy, xx, rows(q)], near_own.at[q % 2, kind], load_sem.at[kind, q % 2]
+        )
+
+    def give(fir, sec, q):
+        yy, xx = row_of(other, fir, sec)
+        return send(
+            part_ref.at[:, other, yy, xx, rows(q)],
+            sums.at[fir, sec, :, rows(q)],
+            p_send.at[fir, sec, q],
+            p_recv.at[fir, sec, q],
+            pair,
+        )
+
+    def f_copy(sec, q):
+        return send(
+            sums.at[1 - first, sec, :, rows(q)],
+            first_in.at[sec, :, rows(q)],
+            f_send.at[sec, q],
+            f_recv.at[sec, q],
+            along_first,
+        )
 
     def g_copy(q):
-        return send(mine.at[first, 1 - second, :, rows(q)], second_in.at[:, rows(q)], g_send.at[q], g_recv.at[q], along_second)
+        return send(
+            sums.at[first, 1 - second, :, rows(q)], second_in.at[:, rows(q)], g_send.at[q], g_recv.at[q], along_second
+        )
 
     def z_copy(k, q):
-        return send(mine.at[first, second, (z + k) % 4, rows(q)], z_in.at[k - 1, rows(q)],
-                    z_send.at[k - 1, q], z_recv.at[k - 1, q], up[k - 1])
-
-    def order(me_first, me_second):
-        return [(1 - me_first, 1 - me_second), (1 - me_first, me_second), (me_first, 1 - me_second), (me_first, me_second)]
-
-    @pl.loop(0, RSTEPS)
-    def _(q):
-        for f, s in order(second, first):
-            give(f, s, q).start()
-        for f, s in order(first, second):
-            load(f, s, q).start()
-
-    def add_into(f, s, q, extra):
+        return send(
+            sums.at[first, second, (z + k) % 4, rows(q)],
+            z_in.at[k - 1, rows(q)],
+            z_send.at[k - 1, q],
+            z_recv.at[k - 1, q],
+            up[k - 1],
+        )
+
+    def begin():
+        @pl.loop(0, RSTEPS)
+        def _(q):
+            for fir, sec in ((1 - second, 1 - first), (1 - second, first), (second, 1 - first), (second, first)):
+                give(fir, sec, q).start()
+
+        for kind in range(4):
+            load(kind, 0).start()
+
+    def add(kind, q, extra):
+        fir, sec = spot(kind)
+
+        @pl.when(q + 1 < RSTEPS)
+        def _():
+            load(kind, q + 1).start()
+
+        load(kind, q).wait()
+        give(fir, sec, q).wait_recv()
+
         @pl.loop(0, 4 * (step // TILE))
         def _(t):
             zz, at = t // (step // TILE), t % (step // TILE)
             here = pl.ds(pl.multiple_of(q * step + at * TILE, TILE), TILE)
-            value = mine[f, s, zz, here].astype(jnp.float32) + pair_in[f, s, zz, here].astype(jnp.float32)
+            near = pl.ds(pl.multiple_of(at * TILE, TILE), TILE)
+            value = sums[fir, sec, zz, here].astype(jnp.float32)
+            value = value + near_own[q % 2, kind, zz, near].astype(jnp.float32)
             for ref in extra:
                 value = value + ref[zz, here].astype(jnp.float32)
-            mine[f, s, zz, here] = value.astype(jnp.bfloat16)
+            sums[fir, sec, zz, here] = value.astype(jnp.bfloat16)
 
     def stage_first(q):
-        for s in (1 - second, second):
-            load(1 - first, s, q).wait()
-            give(1 - first, s, q).wait_recv()
-            add_into(1 - first, s, q, [])
-            f_copy(s, q).start()
+        for kind, sec in ((0, 1 - second), (1, second)):
+            add(kind, q, [])
+            f_copy(sec, q).start()
 
     def stage_second(q):
-        load(first, 1 - second, q).wait()
-        give(first, 1 - second, q).wait_recv()
         f_copy(1 - second, q).wait_recv()
-        add_into(first, 1 - second, q, [first_in.at[1 - second]])
+        add(2, q, [first_in.at[1 - second]])
         g_copy(q).start()
 
     def stage_z(q):
-        load(first, second, q).wait()
-        give(first, second, q).wait_recv()
         f_copy(second, q).wait_recv()
         g_copy(q).wait_recv()
-        add_into(first, second, q, [first_in.at[second], second_in])
-        for k in (2, 1, 3):
+        add(3, q, [first_in.at[second], second_in])
+        for k in QUEUE:
             z_copy(k, q).start()
 
     def stage_out(q):
-        for k in (1, 3, 2):
+        for k in ARRIVE:
             z_copy(k, q).wait_recv()
 
         @pl.loop(0, step // TILE)
         def _(t):
             here = pl.ds(pl.multiple_of(q * step + t * TILE, TILE), TILE)
-            value = mine[first, second, z, here].astype(jnp.float32)
+            value = sums[first, second, z, here].astype(jnp.float32)
             for k in range(3):
                 value = value + z_in[k, here].astype(jnp.float32)
             total[here] = value
 
-    LAG1, LAG2, LAG3 = 1, 2, 4
-
-    @pl.loop(0, RSTEPS + LAG3)
-    def _(q):
-        @pl.when(q < RSTEPS)
-        def _():
-            stage_first(q)
-
-        @pl.when((q >= LAG1) & (q < RSTEPS + LAG1))
-        def _():
-            stage_second(q - LAG1)
-
-        @pl.when((q >= LAG2) & (q < RSTEPS + LAG2))
-        def _():
-            stage_z(q - LAG2)
-
-        @pl.when(q >= LAG3)
-        def _():
-            stage_out(q - LAG3)
-
-    done = pltpu.make_async_copy(total, out_ref, out_sem)
-    done.start()
-
-    @pl.loop(0, RSTEPS)
-    def _(q):
-        for f in range(2):
-            for s in range(2):
-                give(f, s, q).wait_send()
-        for s in range(2):
-            f_copy(s, q).wait_send()
-        g_copy(q).wait_send()
-        for k in (1, 2, 3):
-            z_copy(k, q).wait_send()
-
-    small_local.wait()
-
-    @pl.loop(1, RANKS)
-    def _(offset):
-        small(offset).wait()
-
-    done.wait()
-
-
-def reduce_near(part, small, collective_id):
+    def tick(i):
+        for stage, lag in zip((stage_first, stage_second, stage_z, stage_out), LAGS):
+
+            @pl.when((i >= lag) & (i < RSTEPS + lag))
+            def _(stage=stage, lag=lag):
+                stage(i - lag)
+
+    def finish():
+        @pl.loop(0, RSTEPS)
+        def _(q):
+            for fir in range(2):
+                for sec in range(2):
+                    give(fir, sec, q).wait_send()
+            for sec in range(2):
+                f_copy(sec, q).wait_send()
+            g_copy(q).wait_send()
+            for k in QUEUE:
+                z_copy(k, q).wait_send()
+
+    return begin, tick, finish
+
+
+def shrink_scratch(tokens, depth):
+    dma = pltpu.SemaphoreType.DMA
+    low = lambda *shape: pltpu.VMEM((*shape, depth), jnp.bfloat16)
+    buffers = [
+        low(2, 2, 4, tokens), low(2, 4, 4, tokens // RSTEPS), low(2, 4, tokens), low(4, tokens), low(3, tokens),
+        pltpu.VMEM((tokens, depth), jnp.float32),
+    ]
+    shapes = [(2, 2, RSTEPS), (2, RSTEPS), (RSTEPS,), (3, RSTEPS)]
+    return buffers + [dma((4, 2))] + [dma(shape) for shape in shapes for _ in range(2)]
+
+
+def small_each(small_ref, small_all, sems, pick):
+    here_sem, small_send, small_recv = sems
+    local = pltpu.make_async_copy(small_ref.at[pick(nth(0)[0])], small_all.at[nth(0)[0]], here_sem)
+
+    def copy(offset):
+        return small_copy(lambda spot: small_ref.at[pick(spot)], small_all, small_send, small_recv, offset)
+
+    def begin():
+        local.start()
+
+        @pl.loop(1, RANKS)
+        def _(offset):
+            copy(offset).start()
+
+    def finish():
+        local.wait()
+
+        @pl.loop(1, RANKS)
+        def _(offset):
+            copy(offset).wait()
+
+    return begin, finish
+
+
+SPACING = 5
+
+
+def feed_back_body(part_ref, small_ref, rows_ref, gate_ref, up_ref, act_ref, grads_ref,
+                   out_ref, small_all, gate_out, up_out, down_out, *scratch):
+    begin, tick, finish = shrink(part_ref, *scratch[:6], scratch[6:15])
+    total, out_sem = scratch[5], scratch[15]
+    small_begin, small_finish = small_each(small_ref, small_all, scratch[16:], lambda spot: spot)
+    e, k = pl.program_id(0), pl.program_id(1)
+    step = e * pl.num_programs(1) + k
+    last = pl.num_programs(0) * pl.num_programs(1) - 1
+
+    @pl.when(step == 0)
+    def _():
+        meet()
+        small_begin()
+        begin()
+
+    rows = rows_ref[0]
+    gate_out[0] = inner_rows(rows, gate_ref[0])
+    up_out[0] = inner_rows(rows, up_ref[0])
+    down_out[0] = inner_rows(act_ref[0], grads_ref[0])
+
+    @pl.when((step % SPACING == 0) & (step // SPACING < TICKS))
+    def _():
+        tick(step // SPACING)
+
+    @pl.when(step == last)
+    def _():
+        done = pltpu.make_async_copy(total, out_ref, out_sem)
+        done.start()
+        finish()
+        small_finish()
+        done.wait()
+
+
+def feed_back(part, small, rows, grad_gate, grad_up, act, grads, collective_id):
     tokens, depth = part.shape[0] // RANKS, part.shape[1]
+    groups, length, inner = grad_gate.shape
     dma = pltpu.SemaphoreType.DMA
+    slab = pl.BlockSpec((1, length, CHUNK), lambda e, k: (e, 0, k))
+    held = pl.BlockSpec((1, length, inner), lambda e, k: (e, 0, 0))
     return pl.pallas_call(
-        reduce_body,
+        feed_back_body,
+        grid=(groups, depth // CHUNK),
+        in_specs=[ANYWHERE, ANYWHERE, slab, held, held, held, slab],
+        out_specs=[
+            ANYWHERE,
+            ANYWHERE,
+            pl.BlockSpec((1, CHUNK, inner), lambda e, k: (e, k, 0)),
+            pl.BlockSpec((1, CHUNK, inner), lambda e, k: (e, k, 0)),
+            pl.BlockSpec((1, inner, CHUNK), lambda e, k: (e, 0, k)),
+        ],
         out_shape=(
             jax.ShapeDtypeStruct((tokens, depth), jnp.float32),
             jax.ShapeDtypeStruct(small.shape, small.dtype),
+            jax.ShapeDtypeStruct((groups, depth, inner), jnp.float32),
+            jax.ShapeDtypeStruct((groups, depth, inner), jnp.float32),
+            jax.ShapeDtypeStruct((groups, inner, depth), jnp.float32),
         ),
-        in_specs=[pl.BlockSpec(memory_space=pl.ANY)] * 2,
-        out_specs=[pl.BlockSpec(memory_space=pl.ANY)] * 2,
-        scratch_shapes=[
-            pltpu.VMEM((2, 2, 4, tokens, depth), jnp.bfloat16),
-            pltpu.VMEM((2, 2, 4, tokens, depth), jnp.bfloat16),
-            pltpu.VMEM((2, 4, tokens, depth), jnp.bfloat16),
-            pltpu.VMEM((4, tokens, depth), jnp.bfloat16),
-            pltpu.VMEM((3, tokens, depth), jnp.bfloat16),
-            pltpu.VMEM((tokens, depth), jnp.float32),
-            dma((2, 2, RSTEPS)),
-            dma((2, 2, RSTEPS)), dma((2, 2, RSTEPS)),
-            dma((2, RSTEPS)), dma((2, RSTEPS)),
-            dma((RSTEPS,)), dma((RSTEPS,)),
-            dma((3, RSTEPS)), dma((3, RSTEPS)),
-            dma(()),
-            dma(()), dma((RANKS,)), dma((RANKS,)),
-        ],
+        scratch_shapes=shrink_scratch(tokens, depth) + [dma(())] + small_sems(),
         compiler_params=pltpu.CompilerParams(
-            collective_id=collective_id, has_side_effects=True, vmem_limit_bytes=60 * 1024 * 1024
+            collective_id=collective_id, has_side_effects=True, vmem_limit_bytes=63 * 1024 * 1024
         ),
-    )(part.reshape(4, 2, 2, 2, tokens, depth), small)
+    )(part.reshape(4, 2, 2, 2, tokens, depth), small, rows, grad_gate, grad_up, act, grads)
 
 
 def fill_rows(pick_ref, field_ref, rows_ref):
@@ -1188,11 +1260,13 @@
         grad_feed_part = restore(
             spread_plain, [grad_gate, grad_up], [gate_weight, up_weight], (True, True)
         )
-        grad_feed, gates_in = reduce_near(grad_feed_part, own_gates, 3)
+        grad_feed, gates_in, grad_gate_weight, grad_up_weight, grad_down_weight = feed_back(
+            grad_feed_part, own_gates, expert_rows, grad_gate, grad_up, weighted_act, expert_grads, 3
+        )
+        activated = lax.optimization_barrier((activated, grad_feed))[0]
         gates_in = jnp.sum(gates_in.reshape(-1, rows_count, experts_local, tokens), axis=1)
         grad_probs = gates_in.reshape(experts, tokens).T
         mixture_part = restore(spread_probs, [activated], [down_weight], (False,))
-        mixture = reduce_near(mixture_part, own_gates, 3)[0]
     else:
         own_gates = lax.psum_scatter(
             jnp.swapaxes(own_gates, 1, 2).reshape(-1, rows_count, tokens, experts_local),
@@ -1209,16 +1283,15 @@
             "erf,efd->erd", activated, down_weight, preferred_element_type=jnp.float32
         ).astype(jnp.bfloat16)
         mixture = return_rows(spread_probs, out_rows).astype(jnp.float32)
-    layer_output = hidden + mixture
-    grad_gate_weight = jnp.einsum(
-        "erd,erf->edf", expert_rows, grad_gate, preferred_element_type=jnp.float32
-    )
-    grad_up_weight = jnp.einsum(
-        "erd,erf->edf", expert_rows, grad_up, preferred_element_type=jnp.float32
-    )
-    grad_down_weight = jnp.einsum(
-        "erf,erd->efd", weighted_act, expert_grads, preferred_element_type=jnp.float32
-    )
+        grad_gate_weight = jnp.einsum(
+            "erd,erf->edf", expert_rows, grad_gate, preferred_element_type=jnp.float32
+        )
+        grad_up_weight = jnp.einsum(
+            "erd,erf->edf", expert_rows, grad_up, preferred_element_type=jnp.float32
+        )
+        grad_down_weight = jnp.einsum(
+            "erf,erd->efd", weighted_act, expert_grads, preferred_element_type=jnp.float32
+        )
     grad_out = cotangent.astype(jnp.float32)
     grad_logits = (
         router_probs * (grad_probs - jnp.sum(router_probs * grad_probs, axis=-1, keepdims=True))
@@ -1322,8 +1395,9 @@
         pack = jnp.pad(pack, ((0, 0), (0, PACK_ROWS * 128 - pack.shape[1])))
         pack = pack.astype(jnp.bfloat16).reshape(cols, PACK_ROWS, 128)
         (
-            summed, grad_query_weight, grad_key_weight, grad_value_weight, grad_output_weight, packs
+            mixture, summed, grad_query_weight, grad_key_weight, grad_value_weight, grad_output_weight, packs
         ) = finish_near(
+            mixture_part,
             grad_seq_part.astype(jnp.bfloat16).reshape(rows_count, tokens, model_width),
             [grad.astype(jnp.bfloat16) for grad in (query_grad, key_grad, value_grad, output_grad)],
             pack,
@@ -1396,6 +1470,7 @@
                 router_total.astype(jnp.bfloat16), "col", scatter_dimension=0, tiled=True
             ).astype(jnp.float32),
         )
+    layer_output = hidden + mixture
     return (
         layer_output,
         input_grad,

time: 1450 us -> 1370 us (0.945)
  matrix products: 188 us -> 114 us
  Pallas kernels: 1010 us -> 966 us
  local copies, waits for them, and re-layouts: 59 us -> 93.8 us
    pallas_call x2 -> x1, Pallas kernels: 337 us -> 190 us  [feed_back(): pl.pallas_call(feed_back_body, grid=(groups, depth // CHUNK), in_specs=[A...]
    pallas_call x1, Pallas kernels: 119 us -> 217 us  [finish_near(): pl.pallas_call(finish_body, out_shape=(jax.ShapeDtypeStruct((tokens, dept...]
    dot_general x3 -> x0, matrix products: 73.2 us -> none  [the longest x1 24.8 us: local(): jnp.einsum('erd,erf->edf', expert_rows, grad_gate, preferred_element_type...]
    unnamed x165 -> x198, local copies, waits for them, and re-layouts: 17.8 us -> 50.4 us
  transfers between devices with their start and end apart: 2 -> 2, of which waited for: 2 -> 1; matrix products, arithmetic and copies ran while one was open for 5% -> 2% of each run, Pallas kernels for 0% -> 4%
where the time goes in v5:
time: 1370 us; the launch traced here: 1360 us
  Pallas kernels  966 us (71%)
  matrix products  114 us (8%)
  other arithmetic  98.2 us (7%)
  local copies, waits for them, and re-layouts  93.8 us (7%)
  waiting for transfers between devices  46.2 us (3%)
  blocking collectives  18 us (1%)
  between operations  15.1 us (1%)
    pallas_call x1, Pallas kernels, finish_near(): pl.pallas_call(finish_body, out_shape=(jax.ShapeDtypeStruct((tokens, dept...  217 us
    pallas_call x1, Pallas kernels, start_near(): pl.pallas_call(start_body, out_shape=(shaped((4, *x.shape), x), *[shaped(...  203 us
    pallas_call x1, Pallas kernels, feed_back(): pl.pallas_call(feed_back_body, grid=(groups, depth // CHUNK), in_specs=[A...  190 us
    pallas_call x1, Pallas kernels, grads_in(): pl.pallas_call(grads_in_body, grid=(steps,), in_specs=[pl.BlockSpec((rank...  163 us
    pallas_call x2, Pallas kernels, restore(): pl.pallas_call(functools.partial(restore_body, flipped), grid=(depth // C...  119 us
    pallas_call x1, Pallas kernels, feed_in(): pl.pallas_call(functools.partial(feed_in_body, steps), grid=(steps + grou...  73.3 us
    unnamed x198, local copies, waits for them, and re-layouts  50.4 us
    reduce_scatter x1, waiting for transfers between devices, local(): lax.psum_scatter(wide_dot(mixed_heads, output_full).astype(jnp.bfloat16),...  46.1 us
  transfers between devices with their start and end apart: 2, of which 1 were waited for; matrix products, arithmetic and copies ran while one was open for 2% of the time, Pallas kernels for 4%

profile of v5, /device:TPU:0, one launch (start us, length us, event | category | flops | bytes accessed | tf_op | source)
XLA Modules:
  0.0 1359.6 jit_solution(110569697025865633)
XLA Ops:
  11.6 203.4 %shard_map.254 = (bf16[4,256,2048]{2,1,0:T(8,128)(2,1)}, bf16[2048,512]{1,0:T(8,128)(2,1)}, bf16[2048,512]{1,0:T(8,128)(2,1)}, bf16[2048,512]{1,0:T(8,128)(2,1)}...) custom-call(bf16[256,2048]{1,0:T(8,128)(2,1)} %x_ref.1, ...), custom_call_target="tpu_custom_call" | custom-call | tf_op jit(solution)/shard_map/pallas_call | solution.py:410
  229.2 8.6 all-reduce.2
  259.9 6.1 fusion.52
  266.1 23.1 %while.30 = (s32[]{:T(128)}, bf16[2,512,4,128]{3,1,2,0:T(8,128)(2,1)}, f32[2,4,512]{2,1,0:T(4,128)S(1)}, s32[2]{0:T(128)S(1)}, bf16[1024,4,128]{2,0,1:T(8,128)(2...) while((s32[]{:T(128)}, ...), condition=%wide.region_8.9_spmd.clone.clone, body=%wide.region_5.8_spmd.clone.sunk.clone | while | flops 1099430400 | bytes 31003272 | solution.py:1169
  293.1 4.4 convolution_convert_fusion
  303.4 5.4 fusion.101
  308.8 46.1 %reduce-scatter.2.cloned.1.call-done = bf16[256,2048]{1,0:T(8,128)(2,1)} async-done(((bf16[1024,2048]{1,0:T(8,128)(2,1)}), bf16[256,2048]{1,0:T(8,128)(2,1)}) %reduce-scatter.2.cloned.1.call-update) | async-done | bytes 1048592 | tf_op jit(solution)/shard_map/reduce_scatter | solution.py:1172
  358.4 163.4 %shard_map.255 = (bf16[8,1280,2048]{2,1,0:T(8,128)(2,1)}, f32[8,1280,256]{2,1,0:T(8,128)}, bf16[4,2,2,2,256,2048]{5,4,3,2,1,0:T(8,128)(2,1)}, f32[32,8,256]{2,1,0:T(8,128)}) custom-call(bf16[32,320,256]{2,1,0:T(8,128)(2,1)} %fusion.37.pick_ref, bf16[32,256,2048]{2,1,0:T(8,128)(2,1)} %bitcast.234, bf16[8,256,2048]{2,1,0:T(8,128)(2,1)} %refs_1_.1, ...), custom_call_target="tpu_custom_call" | custom-call | tf_op jit(solution)/shard_map/pallas_call | solution.py:908
  528.5 73.3 %shard_map.256 = (bf16[8,1280,2048]{2,1,0:T(8,128)(2,1)}, bf16[8,1280,256]{2,1,0:T(8,128)(2,1)}, bf16[8,1280,256]{2,1,0:T(8,128)(2,1)}, bf16[8,1280,256]{2,1,0:T...) custom-call(bf16[32,320,256]{2,1,0:T(8,128)(2,1)} %fusion.37.pick_ref, ...), custom_call_target="tpu_custom_call" | custom-call | flops 32212254720 | bytes 125829120 | tf_op jit(solution)/shard_map/pallas_call | solution.py:982
  601.9 3.9 reduce.3
  608.9 67.4 %shard_map.257 = bf16[32,256,2048]{2,1,0:T(8,128)(2,1)} custom-call(bf16[32,256,320]{2,1,0:T(8,128)(2,1)} %get-tuple-element.436.spread_ref, bf16[8,1280,256]{2,1,0:T(8,128)(2,1)} %get-tuple-element.160.refs_0_.gate_ref, bf16[8,1280,256]{2,1,0:T(8,128)(2,1)} %get-tuple-element.161.refs_1_.up_ref, bf16[8,2048,256]{2,1,0:T(8,128)(2,1)} %refs_2_.1, ...), custom_call_target="tpu_custom_call" | custom-call | flops 32212254720 | bytes 62914560 | tf_op jit(solution)/shard_map/pallas_call | solution.py:1034
  676.3 189.8 %shard_map.258 = (f32[256,2048]{1,0:T(8,128)}, f32[32,8,256]{2,1,0:T(8,128)}, f32[8,2048,256]{2,1,0:T(8,128)}, f32[8,2048,256]{2,1,0:T(8,128)}, f32[8,256,2048]{2,1,0:T(8,128)}) custom-call(bf16[4,2,2,2,256,2048]{5,4,3,2,1,0:T(8,128)(2,1)} %bitcast.236, f32[32,8,256]{2,1,0:T(8,128)} %select_reduce_fusion.small_ref, ...), custom_call_target="tpu_custom_call" | custom-call | tf_op jit(solution)/shard_map/pallas_call | solution.py:815
  874.7 5.4 fusion.40
  885.9 4.6 select_convert_fusion.spread_ref
  890.5 51.9 %shard_map.259 = bf16[32,256,2048]{2,1,0:T(8,128)(2,1)} custom-call(bf16[32,256,320]{2,1,0:T(8,128)(2,1)} %select_convert_fusion.spread_ref, bf16[8,1280,256]{2,1,0:T(8,128)(2,1)} %get-tuple-element.167.refs_0_, bf16[8,256,2048]{2,1,0:T(8,128)(2,1)} %refs_1_.1), custom_call_target="tpu_custom_call" | custom-call | flops 21474836480 | bytes 62914560 | tf_op jit(solution)/shard_map/pallas_call | solution.py:1034
  942.5 6.3 convolution_convert_fusion.6
  948.8 50.6 %while.31 = (s32[]{:T(128)}, f32[1024,4,128]{0,2,1:T(8,128)S(1)}, f32[1024,4,128]{0,2,1:T(8,128)}, f32[2,512,4,128]{3,1,2,0:T(8,128)}, s32[2]{0:T(128)S(1)}, /*i...) while((s32[]{:T(128)}, f32[1024,4,128]{0,2,1:T(8,128)S(1)}, ...), condition=%wide.region_23.24_spmd.clone.clone, body=%wide.region_21.23_spmd.clone.sunk.clone | while | flops 2719218176 | bytes 180417440 | solution.py:1345
  962.5 3.8 bitcast_add_fusion.8
  969.6 4.0 bitcast_add_fusion.9
  994.2 5.3 bitcast_add_fusion.9
  1002.5 4.2 copy.125
  1008.5 3.8 broadcast_multiply_fusion
  1031.7 9.3 all-reduce.3
  1045.8 3.8 convolution_convert_fusion.3.k_ref
  1051.2 5.8 fusion.102
  1057.0 3.8 convolution_convert_fusion.4.q_ref
  1063.0 9.4 fusion.48
  1073.5 6.1 convolution_convert_fusion.2.v_ref
  1087.1 216.7 %shard_map.260 = (f32[256,2048]{1,0:T(8,128)}, f32[256,2048]{1,0:T(8,128)}, f32[256,512]{1,0:T(8,128)}, f32[256,512]{1,0:T(8,128)}, f32[256,512]{1,0:T(8,128)}, ...) custom-call(bf16[4,2,2,2,256,2048]{5,4,3,2,1,0:T(8,128)(2,1)} %bitcast.235, bf16[4,256,2048]{2,1,0:T(8,128)(2,1)} %bitcast.241, ...), custom_call_target="tpu_custom_call" | custom-call | tf_op jit(solution)/shard_map/pallas_call | solution.py:570
  1320.1 13.2 copy.197
  1335.4 8.5 copy.198
  1346.4 6.2 copy.199
  (363 shorter events, 192.1 us)
Async XLA Ops:
  7.2 347.7 %reduce-scatter.2.cloned.1.call-start = ((), (), s32[]{:S(2)}) async-start(), calls=%async_computation.1 | async-start | bytes 5242880 | tf_op jit(solution)/shard_map/reduce_scatter | solution.py:1172
  225.2 13.2 copy-start.26
  229.2 10.8 copy-start.75
  238.4 6.3 copy-start.70
  249.8 7.1 copy-start.41
  289.1 8.4 copy-start.4
  289.1 8.4 copy-start.11
  289.1 8.4 copy-start.12
  289.1 8.4 copy-start.63
  289.1 8.4 copy-start.88
  297.5 644.9 %all-gather.2.cloned.1.call-start = ((), (), s32[]{:S(2)}) async-start(), calls=%async_computation.2 | async-start | bytes 5242880 | tf_op jit(solution)/shard_map/all_gather | solution.py:1308
  303.4 51.5 %copy-start.14 = (bf16[256,2048]{1,0:T(8,128)(2,1)S(1)}, bf16[256,2048]{1,0:T(8,128)(2,1)}, u32[]{:S(2)}) copy-start(bf16[256,2048]{1,0:T(8,128)(2,1)} %x_ref.1) | copy-start | bytes 3145732
  874.7 11.2 copy-start.44
  942.4 6.4 copy-start.3
  942.4 6.4 copy-start.5
  942.4 6.4 copy-start.64
  942.4 6.4 copy-start.89
  1021.9 7.1 copy-start.69
  1022.0 7.1 copy-start.76
  1029.7 11.4 copy-start.80
  1063.0 9.6 copy-start.52
  1063.0 9.6 copy-start.78
  1073.5 6.3 copy-start.19
  1073.5 6.3 copy-start.81
  1314.9 18.4 %slice-start.4 = ((s8[16777216]{0:T(1024)(128)(4,1)}), s8[4194304]{0:T(1024)(128)(4,1)S(1)}, s32[]{:S(2)}) async-start(s8[16777216]{0:T(1024)(128)(4,1)} %bitcast.239), calls=%async_computation.7 | async-start | bytes 8388608
  1320.0 13.2 slice-start.5
  1320.0 13.8 %slice-start.6 = ((s8[16777216]{0:T(1024)(128)(4,1)}), s8[4194304]{0:T(1024)(128)(4,1)S(1)}, s32[]{:S(2)}) async-start(s8[16777216]{0:T(1024)(128)(4,1)} %bitcast.239), calls=%async_computation.9 | async-start | bytes 8388608
  1320.0 15.3 %slice-start.7 = ((s8[16777216]{0:T(1024)(128)(4,1)}), s8[4194304]{0:T(1024)(128)(4,1)S(1)}, s32[]{:S(2)}) async-start(s8[16777216]{0:T(1024)(128)(4,1)} %bitcast.239), calls=%async_computation.10 | async-start | bytes 8388608
  1320.0 23.8 %slice-start = ((s8[16777216]{0:T(1024)(128)(4,1)}), s8[4194304]{0:T(1024)(128)(4,1)S(1)}, s32[]{:S(2)}) async-start(s8[16777216]{0:T(1024)(128)(4,1)} %bitcast.237), calls=%async_computation.3 | async-start | bytes 8388608
  1320.1 23.8 %slice-start.1 = ((s8[16777216]{0:T(1024)(128)(4,1)}), s8[4194304]{0:T(1024)(128)(4,1)S(1)}, s32[]{:S(2)}) async-start(s8[16777216]{0:T(1024)(128)(4,1)} %bitcast.237), calls=%async_computation.4 | async-start | bytes 8388608
  1335.4 9.9 slice-start.2
  1335.4 11.1 slice-start.3
  (76 other events, 227.0 us)
Sparse Core Ops, SparseCore 0:
  297.6 57.2 reduce-scatter.1
  873.2 51.9 all-gather.1

commit v6 on v5

--- a/solution.py
+++ b/solution.py
@@ -44,22 +44,9 @@
     half_size = HD // 2
     freqs = THETA ** (-(jnp.arange(half_size, dtype=jnp.float32) * 2.0) / HD)
     angles = jnp.arange(length, dtype=jnp.float32)[:, None] * freqs[None, :]
-    cosine = jnp.concatenate([jnp.cos(angles), jnp.cos(angles)], axis=-1)[:, None, :]
-    sine_table = jnp.concatenate([jnp.sin(angles), jnp.sin(angles)], axis=-1)[:, None, :]
+    cosine = jnp.concatenate([jnp.cos(angles), jnp.cos(angles)], axis=-1)
+    sine_table = jnp.concatenate([-jnp.sin(angles), jnp.sin(angles)], axis=-1)
     return (cosine, sine_table)
-
-
-def rotate(field, cosine, sine_table):
-    half_size = field.shape[-1] // 2
-    turned = jnp.concatenate([-field[..., half_size:], field[..., :half_size]], axis=-1)
-    return field * cosine + turned * sine_table
-
-
-def unrotate(gradient, cosine, sine_table):
-    half_size = gradient.shape[-1] // 2
-    moved = gradient * sine_table
-    back_turned = jnp.concatenate([moved[..., half_size:], -moved[..., :half_size]], axis=-1)
-    return gradient * cosine + back_turned
 
 
 def dispatch_body(pick_ref, field_ref, rows_ref):
@@ -789,9 +776,9 @@
         begin()
 
     rows = rows_ref[0]
-    gate_out[0] = inner_rows(rows, gate_ref[0])
-    up_out[0] = inner_rows(rows, up_ref[0])
-    down_out[0] = inner_rows(act_ref[0], grads_ref[0])
+    gate_out[0] = inner_rows(rows, gate_ref[0]).astype(jnp.bfloat16)
+    up_out[0] = inner_rows(rows, up_ref[0]).astype(jnp.bfloat16)
+    down_out[0] = inner_rows(act_ref[0], grads_ref[0]).astype(jnp.bfloat16)
 
     @pl.when((step % SPACING == 0) & (step // SPACING < TICKS))
     def _():
@@ -826,9 +813,9 @@
         out_shape=(
             jax.ShapeDtypeStruct((tokens, depth), jnp.float32),
             jax.ShapeDtypeStruct(small.shape, small.dtype),
-            jax.ShapeDtypeStruct((groups, depth, inner), jnp.float32),
-            jax.ShapeDtypeStruct((groups, depth, inner), jnp.float32),
-            jax.ShapeDtypeStruct((groups, inner, depth), jnp.float32),
+            jax.ShapeDtypeStruct((groups, depth, inner), jnp.bfloat16),
+            jax.ShapeDtypeStruct((groups, depth, inner), jnp.bfloat16),
+            jax.ShapeDtypeStruct((groups, inner, depth), jnp.bfloat16),
         ),
         scratch_shapes=shrink_scratch(tokens, depth) + [dma(())] + small_sems(),
         compiler_params=pltpu.CompilerParams(
@@ -1004,9 +991,7 @@
     )(pick, field, gate, up, plain, probs)
 
 
-def restore_body(flipped, spread_ref, *refs):
-    count = len(flipped)
-    lefts, weights, field_ref, rows = refs[:count], refs[count:2*count], refs[2*count], refs[2*count+1]
+def fill_field(flipped, spread_ref, lefts, weights, field_ref, rows):
     groups = rows.shape[0]
     ranks = spread_ref.shape[0]
 
@@ -1018,31 +1003,293 @@
             total = term if total is None else total + term
         rows[e] = total
 
-    @pl.loop(0, ranks, unroll=2*UNROLL)
+    @pl.loop(0, ranks, unroll=2 * UNROLL)
     def _(s):
-        part = rows[:, pl.ds(pl.multiple_of(s * SLOTS, SLOTS), SLOTS)].reshape(groups * SLOTS, CHUNK).astype(jnp.bfloat16)
+        part = rows[:, pl.ds(pl.multiple_of(s * SLOTS, SLOTS), SLOTS)]
+        part = part.reshape(groups * SLOTS, CHUNK).astype(jnp.bfloat16)
         field_ref[s] = wide_dot(spread_ref[s], part).astype(jnp.bfloat16)
 
-def restore(spread, lefts, weights, flipped):
+
+def restore_body(flipped, spread_ref, *refs):
+    count = len(flipped)
+    fill_field(flipped, spread_ref, refs[:count], refs[count : 2 * count], *refs[2 * count :])
+
+
+def restore_specs(spread, lefts, weights, flipped):
     ranks, tokens, width = spread.shape
     groups = width // SLOTS
-    length = ranks * SLOTS
-    inner = lefts[0].shape[2]
+    length, inner = ranks * SLOTS, lefts[0].shape[2]
     depth = weights[0].shape[1] if flipped[0] else weights[0].shape[2]
-    wspecs = [pl.BlockSpec((groups, CHUNK, inner), lambda k: (0, k, 0)) if f else pl.BlockSpec((groups, inner, CHUNK), lambda k: (0, 0, k)) for f in flipped]
-    flops = 2 * groups * length * depth * (tokens + inner * len(weights))
+    once = pl.Buffered(1)
+    in_specs = (
+        [pl.BlockSpec((ranks, tokens, width), lambda k: (0, 0, 0), pipeline_mode=once)]
+        + [pl.BlockSpec((groups, length, inner), lambda k: (0, 0, 0), pipeline_mode=once)] * len(lefts)
+        + [
+            pl.BlockSpec((groups, CHUNK, inner), lambda k: (0, k, 0))
+            if flip
+            else pl.BlockSpec((groups, inner, CHUNK), lambda k: (0, 0, k))
+            for flip in flipped
+        ]
+    )
+    out_spec = pl.BlockSpec((ranks, tokens, CHUNK), lambda k: (0, 0, k))
+    out_shape = jax.ShapeDtypeStruct((ranks, tokens, depth), jnp.bfloat16)
+    return depth // CHUNK, in_specs, out_spec, out_shape, pltpu.VMEM((groups, length, CHUNK), jnp.float32)
+
+
+def restore(spread, lefts, weights, flipped):
+    steps, in_specs, out_spec, out_shape, rows = restore_specs(spread, lefts, weights, flipped)
     field = pl.pallas_call(
         functools.partial(restore_body, flipped),
-        grid=(depth // CHUNK,),
-        in_specs=[pl.BlockSpec((ranks, tokens, width), lambda k: (0, 0, 0), pipeline_mode=pl.Buffered(1))]
-        + [pl.BlockSpec((groups, length, inner), lambda k: (0, 0, 0), pipeline_mode=pl.Buffered(1))] * len(lefts) + wspecs,
-        out_specs=pl.BlockSpec((ranks, tokens, CHUNK), lambda k: (0, 0, k)),
-        out_shape=jax.ShapeDtypeStruct((ranks, tokens, depth), jnp.bfloat16),
-        scratch_shapes=[pltpu.VMEM((groups, length, CHUNK), jnp.float32)],
+        grid=(steps,),
+        in_specs=in_specs,
+        out_specs=out_spec,
+        out_shape=out_shape,
+        scratch_shapes=[rows],
         compiler_params=pltpu.CompilerParams(vmem_limit_bytes=63 * 1024 * 1024),
-        cost_estimate=pl.CostEstimate(flops=flops, bytes_accessed=60 << 20, transcendentals=0),
     )(spread, *lefts, *weights)
-    return field.reshape(ranks * tokens, depth)
+    return field.reshape(-1, field.shape[2])
+
+
+PARTS = 4
+
+
+def restore_out_body(spread_ref, left_ref, weight_ref, own_ref, field_ref, all_ref, rows,
+                     here_sem, f_send, f_recv, g_send, g_recv, h_send, h_recv):
+    r, c, y, x, z, core, first, second = seat()
+    pair, along_first, along_second, up = partners()
+    y1, x1 = row_of(core, first, 1 - second)
+    near_row = y1 * 2 + x1
+    step = own_ref.shape[0] // PARTS
+    k = pl.program_id(0)
+    here = pltpu.make_async_copy(own_ref, all_ref.at[r], here_sem)
+
+    def part(ref, q):
+        return ref.at[pl.ds(q * step, step)]
+
+    def f_copy(q):
+        return send(part(own_ref, q), part(all_ref.at[r], q), f_send.at[q], f_recv.at[q], along_first)
+
+    def g_copy(q):
+        return send(part(own_ref, q), part(all_ref.at[r], q), g_send.at[q], g_recv.at[q], along_second)
+
+    def h_copy(q):
+        there = part(all_ref.at[near_row], q)
+        return send(there, there, h_send.at[q], h_recv.at[q], along_first)
+
+    @pl.when(k == 0)
+    def _():
+        meet()
+        here.start()
+        for q in range(PARTS):
+            g_copy(q).start()
+            f_copy(q).start()
+
+    fill_field((False,), spread_ref, [left_ref], [weight_ref], field_ref, rows)
+
+    @pl.when(k == 1)
+    def _():
+        for q in range(PARTS):
+            g_copy(q).wait_recv()
+            h_copy(q).start()
+
+    @pl.when(k == pl.num_programs(0) - 1)
+    def _():
+        here.wait()
+        for q in range(PARTS):
+            g_copy(q).wait_send()
+            f_copy(q).wait()
+            h_copy(q).wait()
+
+
+def restore_out(spread, left, weight, own, collective_id):
+    steps, in_specs, out_spec, out_shape, rows = restore_specs(spread, [left], [weight], (False,))
+    dma = pltpu.SemaphoreType.DMA
+    field, whole = pl.pallas_call(
+        restore_out_body,
+        grid=(steps,),
+        in_specs=in_specs + [ANYWHERE],
+        out_specs=[out_spec, ANYWHERE],
+        out_shape=[out_shape, jax.ShapeDtypeStruct((4, *own.shape), own.dtype)],
+        scratch_shapes=[rows, dma(())] + [dma((PARTS,))] * 6,
+        compiler_params=pltpu.CompilerParams(
+            collective_id=collective_id, has_side_effects=True, vmem_limit_bytes=63 * 1024 * 1024
+        ),
+    )(spread, left, weight, own)
+    return field.reshape(-1, field.shape[2]), whole.reshape(-1, own.shape[1])
+
+
+def branch_body(mixed_ref, weight_ref, out_ref, away, near, first_in, second_in,
+                f_send, f_recv, g_send, g_recv):
+    r, c, y, x, z, core, first, second = seat()
+    pair, along_first, along_second, up = partners()
+    tokens, depth = out_ref.shape
+    width = depth // PARTS
+
+    def columns(j):
+        return pl.ds(j * width, width)
+
+    def product(fir, sec, j):
+        yy, xx = row_of(core, fir, sec)
+        rows = pl.ds(pl.multiple_of((yy * 2 + xx) * tokens, tokens), tokens)
+        return wide_dot(mixed_ref[rows], weight_ref[:, columns(j)])
+
+    def f_copy(sec, j):
+        return send(
+            away.at[sec, :, columns(j)], first_in.at[sec, :, columns(j)], f_send.at[sec, j], f_recv.at[sec, j], along_first
+        )
+
+    def g_copy(j):
+        return send(near.at[:, columns(j)], second_in.at[:, columns(j)], g_send.at[j], g_recv.at[j], along_second)
+
+    meet()
+    for j in range(PARTS):
+        away[1 - second, :, columns(j)] = product(1 - first, 1 - second, j).astype(jnp.bfloat16)
+        f_copy(1 - second, j).start()
+    for j in range(PARTS):
+        away[second, :, columns(j)] = product(1 - first, second, j).astype(jnp.bfloat16)
+        f_copy(second, j).start()
+    for j in range(PARTS):
+        value = product(first, 1 - second, j)
+        f_copy(1 - second, j).wait_recv()
+        value = value + first_in[1 - second, :, columns(j)].astype(jnp.float32)
+        near[:, columns(j)] = value.astype(jnp.bfloat16)
+        g_copy(j).start()
+    for j in range(PARTS):
+        out_ref[:, columns(j)] = product(first, second, j)
+    for j in range(PARTS):
+        f_copy(second, j).wait_recv()
+        g_copy(j).wait_recv()
+        out_ref[:, columns(j)] += first_in[second, :, columns(j)].astype(jnp.float32) + second_in[
+            :, columns(j)
+        ].astype(jnp.float32)
+    for j in range(PARTS):
+        g_copy(j).wait_send()
+        for sec in range(2):
+            f_copy(sec, j).wait_send()
+
+
+def branch_near(mixed, weight, collective_id):
+    tokens, depth = mixed.shape[0] // 4, weight.shape[1]
+    dma = pltpu.SemaphoreType.DMA
+    inside = pl.BlockSpec(memory_space=pltpu.VMEM)
+    low = lambda *shape: pltpu.VMEM((*shape, tokens, depth), jnp.bfloat16)
+    return pl.pallas_call(
+        branch_body,
+        in_specs=[inside] * 2,
+        out_specs=inside,
+        out_shape=jax.ShapeDtypeStruct((tokens, depth), jnp.float32),
+        scratch_shapes=[
+            low(2), low(), low(2), low(), dma((2, PARTS)), dma((2, PARTS)), dma((PARTS,)), dma((PARTS,))
+        ],
+        compiler_params=pltpu.CompilerParams(
+            collective_id=collective_id, has_side_effects=True, vmem_limit_bytes=40 * 1024 * 1024
+        ),
+    )(mixed, weight)
+
+
+def causal_scores(query_rows, key_rows):
+    scores = outer_cols(query_rows, key_rows) * HD ** (-0.5)
+    count, length = scores.shape
+    position = lax.broadcasted_iota(jnp.int32, scores.shape, 0) + (length - count)
+    return jnp.where(position >= lax.broadcasted_iota(jnp.int32, scores.shape, 1), scores, MASKED)
+
+
+def attend_body(q_raw, k_raw, v_ref, q_rs, k_rs, q_gain, k_gain, cos_ref, sin_ref,
+                mixed_ref, q_out, k_out, lse_ref):
+    length = v_ref.shape[0]
+    block = min(256, length)
+    for raw, scale, gain, out in ((q_raw, q_rs, q_gain, q_out), (k_raw, k_rs, k_gain, k_out)):
+        normed = raw[...] * scale[...] * gain[...]
+        turned = normed * cos_ref[...] + pltpu.roll(normed, HD // 2, 1) * sin_ref[...]
+        out[...] = turned.astype(jnp.bfloat16)
+    for start in range(0, length, block):
+        here, seen = pl.ds(start, block), pl.ds(0, start + block)
+        scores = causal_scores(q_out[here], k_out[seen])
+        row_top = jnp.max(scores, axis=-1, keepdims=True)
+        exponent = jnp.exp(scores - row_top)
+        row_total = jnp.sum(exponent, axis=-1, keepdims=True)
+        weights = (exponent / row_total).astype(jnp.bfloat16)
+        mixed_ref[here] = wide_dot(weights, v_ref[seen]).astype(jnp.bfloat16)
+        lse_ref[0, here] = row_top + jnp.log(row_total)
+
+
+def attend(q_raw, k_raw, values, q_rs, k_rs, q_gain, k_gain, cosine, sine):
+    length, width = q_raw.shape
+    heads = width // HD
+    slab = pl.BlockSpec((length, HD), lambda h: (0, h))
+    thin = pl.BlockSpec((length, 1), lambda h: (0, 0))
+    line = pl.BlockSpec((1, HD), lambda h: (0, h))
+    table = pl.BlockSpec((length, HD), lambda h: (0, 0))
+    low = jax.ShapeDtypeStruct((length, width), jnp.bfloat16)
+    return pl.pallas_call(
+        attend_body,
+        grid=(heads,),
+        in_specs=[slab, slab, slab, thin, thin, line, line, table, table],
+        out_specs=[slab, slab, slab, pl.BlockSpec((1, length, 1), lambda h: (h, 0, 0))],
+        out_shape=[low, low, low, jax.ShapeDtypeStruct((heads, length, 1), jnp.float32)],
+        cost_estimate=pl.CostEstimate(
+            flops=4 * heads * length * length * HD, bytes_accessed=8 << 20, transcendentals=heads * length * length
+        ),
+    )(q_raw, k_raw, values, q_rs, k_rs, q_gain[None], k_gain[None], cosine, sine)
+
+
+def attend_back_body(q_ref, k_ref, v_ref, grad_ref, lse_ref, q_raw, k_raw, q_rs, k_rs, q_gain, k_gain, cos_ref, sin_ref,
+                     v_grad, q_grad, k_grad, q_term, k_term, q_inner, k_inner, dq, dk, dv):
+    length = v_ref.shape[0]
+    block = min(256, length)
+    dk[...] = jnp.zeros_like(dk)
+    dv[...] = jnp.zeros_like(dv)
+    for start in range(0, length, block):
+        here, seen = pl.ds(start, block), pl.ds(0, start + block)
+        query_rows, key_rows, grads = q_ref[here], k_ref[seen], grad_ref[here]
+        probs = jnp.exp(causal_scores(query_rows, key_rows) - lse_ref[0, here])
+        dv[seen] += inner_rows(probs.astype(jnp.bfloat16), grads)
+        weights = outer_cols(grads, v_ref[seen])
+        delta = jnp.sum(probs * weights, axis=-1, keepdims=True)
+        scores = (probs * (weights - delta)).astype(jnp.bfloat16)
+        dq[here] = wide_dot(scores, key_rows) * HD ** (-0.5)
+        dk[seen] += inner_rows(scores, query_rows) * HD ** (-0.5)
+    v_grad[...] = dv[...].astype(jnp.bfloat16)
+    for raw, scale, gain, grad, out, term, inner in (
+        (q_raw, q_rs, q_gain, dq, q_grad, q_term, q_inner),
+        (k_raw, k_rs, k_gain, dk, k_grad, k_term, k_inner),
+    ):
+        field, value = raw[...], grad[...]
+        normed = value * cos_ref[...] + pltpu.roll(value * sin_ref[...], HD // 2, 1)
+        weighted = normed * gain[...]
+        out[...] = weighted
+        term[...] = jnp.sum(normed * field * scale[...], axis=0, keepdims=True)
+        inner[0] = jnp.sum(weighted * field, axis=-1, keepdims=True)
+
+
+def attend_back(queries, keys, values, grads, lse, q_raw, k_raw, q_rs, k_rs, q_gain, k_gain, cosine, sine):
+    length, width = q_raw.shape
+    heads = width // HD
+    slab = pl.BlockSpec((length, HD), lambda h: (0, h))
+    thin = pl.BlockSpec((length, 1), lambda h: (0, 0))
+    line = pl.BlockSpec((1, HD), lambda h: (0, h))
+    table = pl.BlockSpec((length, HD), lambda h: (0, 0))
+    column = pl.BlockSpec((1, length, 1), lambda h: (h, 0, 0))
+    wide = jax.ShapeDtypeStruct((length, width), jnp.float32)
+    return pl.pallas_call(
+        attend_back_body,
+        grid=(heads,),
+        in_specs=[slab] * 4 + [column, slab, slab, thin, thin, line, line, table, table],
+        out_specs=[slab, slab, slab, line, line, column, column],
+        out_shape=[
+            jax.ShapeDtypeStruct((length, width), jnp.bfloat16),
+            wide,
+            wide,
+            jax.ShapeDtypeStruct((1, width), jnp.float32),
+            jax.ShapeDtypeStruct((1, width), jnp.float32),
+            jax.ShapeDtypeStruct((heads, length, 1), jnp.float32),
+            jax.ShapeDtypeStruct((heads, length, 1), jnp.float32),
+        ],
+        scratch_shapes=[pltpu.VMEM((length, HD), jnp.float32)] * 3,
+        cost_estimate=pl.CostEstimate(
+            flops=10 * heads * length * length * HD, bytes_accessed=16 << 20, transcendentals=heads * length * length
+        ),
+    )(queries, keys, values, grads, lse, q_raw, k_raw, q_rs, k_rs, q_gain[None], k_gain[None], cosine, sine)
 
 
 def local(
@@ -1118,14 +1365,13 @@
     length = sequence.shape[0]
     model_width = sequence.shape[1]
     local_width = query_full.shape[1]
-    local_heads = local_width // HD
     seq_float = sequence.astype(jnp.float32)
     seq_scale = rms_scale(seq_float)
     attention_float = attention_full.astype(jnp.float32)
     normed = (seq_float * seq_scale * attention_float).astype(jnp.bfloat16)
     query_raw = wide_dot(normed, query_full)
     key_raw = wide_dot(normed, key_full)
-    value_heads = wide_dot(normed, value_full).astype(jnp.bfloat16).reshape(length, local_heads, HD)
+    values = wide_dot(normed, value_full).astype(jnp.bfloat16)
     query_total, key_total = lax.psum(
         (jnp.sum(query_raw * query_raw, axis=-1), jnp.sum(key_raw * key_raw, axis=-1)), "row"
     )
@@ -1134,44 +1380,15 @@
     query_gain_f = query_scale_w.astype(jnp.float32)
     key_gain_f = key_scale_w.astype(jnp.float32)
     cosine, sine_table = rope_tables(length)
-    queries = rotate(
-        (query_raw * query_rs * query_gain_f).reshape(length, local_heads, HD), cosine, sine_table
-    ).astype(jnp.bfloat16)
-    keys_rotated = rotate(
-        (key_raw * key_rs * key_gain_f).reshape(length, local_heads, HD), cosine, sine_table
-    ).astype(jnp.bfloat16)
-    block_rows = min(512, length)
-    starts = jnp.arange(length // block_rows, dtype=jnp.int32) * block_rows
-    key_position = jnp.arange(length, dtype=jnp.int32)
-    score_scale = HD ** (-0.5)
-
-    def block_scores(offset):
-        query_rows = lax.dynamic_slice_in_dim(queries, offset, block_rows, 0)
-        scores = (
-            jnp.einsum("qhd,khd->hqk", query_rows, keys_rotated, preferred_element_type=jnp.float32)
-            * score_scale
-        )
-        query_position = offset + jnp.arange(block_rows, dtype=jnp.int32)
-        allowed = query_position[:, None] >= key_position[None, :]
-        return (query_rows, jnp.where(allowed[None, :, :], scores, MASKED))
-
-    def forward_block(offset):
-        query_rows, scores = block_scores(offset)
-        row_top = jnp.max(scores, axis=-1, keepdims=True)
-        exponent = jnp.exp(scores - row_top)
-        row_total = jnp.sum(exponent, axis=-1, keepdims=True)
-        weights = (exponent / row_total).astype(jnp.bfloat16)
-        mixed_block = jnp.einsum(
-            "hqk,khd->qhd", weights, value_heads, preferred_element_type=jnp.float32
-        )
-        return (mixed_block, (row_top + jnp.log(row_total))[..., 0])
-
-    mixed_blocks, lse_blocks = lax.map(forward_block, starts)
-    mixed_heads = mixed_blocks.reshape(length, local_width).astype(jnp.bfloat16)
-    lse_all = jnp.moveaxis(lse_blocks, 0, 1).reshape(local_heads, length)
-    branch = lax.psum_scatter(
-        wide_dot(mixed_heads, output_full).astype(jnp.bfloat16), "row", scatter_dimension=0, tiled=True
-    ).astype(jnp.float32)
+    mixed_heads, queries, keys_rotated, lse_all = attend(
+        query_raw, key_raw, values, query_rs, key_rs, query_gain_f, key_gain_f, cosine, sine_table
+    )
+    if near:
+        branch = branch_near(mixed_heads, output_full, 5)
+    else:
+        branch = lax.psum_scatter(
+            wide_dot(mixed_heads, output_full).astype(jnp.bfloat16), "row", scatter_dimension=0, tiled=True
+        ).astype(jnp.float32)
     hidden = layer_input.astype(jnp.float32) + branch
     feed_scale = rms_scale(hidden)
     feed_float = feed_full.astype(jnp.float32)
@@ -1263,10 +1480,11 @@
         grad_feed, gates_in, grad_gate_weight, grad_up_weight, grad_down_weight = feed_back(
             grad_feed_part, own_gates, expert_rows, grad_gate, grad_up, weighted_act, expert_grads, 3
         )
-        activated = lax.optimization_barrier((activated, grad_feed))[0]
+        grad_gate_weight = grad_gate_weight.astype(jnp.float32)
+        grad_up_weight = grad_up_weight.astype(jnp.float32)
+        grad_down_weight = grad_down_weight.astype(jnp.float32)
         gates_in = jnp.sum(gates_in.reshape(-1, rows_count, experts_local, tokens), axis=1)
         grad_probs = gates_in.reshape(experts, tokens).T
-        mixture_part = restore(spread_probs, [activated], [down_weight], (False,))
     else:
         own_gates = lax.psum_scatter(
             jnp.swapaxes(own_gates, 1, 2).reshape(-1, rows_count, tokens, experts_local),
@@ -1305,61 +1523,24 @@
         + feed_scale * feed_weighted
         - hidden * feed_scale**3 * jnp.mean(feed_weighted * hidden, axis=-1, keepdims=True)
     )
-    grad_branch = lax.all_gather(grad_hidden.astype(jnp.bfloat16), "row", axis=0, tiled=True)
+    if near:
+        mixture_part, grad_branch = restore_out(
+            spread_probs, activated, down_weight, grad_hidden.astype(jnp.bfloat16), 6
+        )
+    else:
+        grad_branch = lax.all_gather(grad_hidden.astype(jnp.bfloat16), "row", axis=0, tiled=True)
     output_grad = inner_rows(mixed_heads, grad_branch)
-    grad_mixed = (
-        outer_cols(grad_branch, output_full).astype(jnp.bfloat16).reshape(length, local_heads, HD)
+    grad_mixed = outer_cols(grad_branch, output_full).astype(jnp.bfloat16)
+    (
+        grad_value_low, query_weighted, key_weighted, query_gain_term, key_gain_term, query_inner, key_inner
+    ) = attend_back(
+        queries, keys_rotated, values, grad_mixed, lse_all, query_raw, key_raw, query_rs, key_rs,
+        query_gain_f, key_gain_f, cosine, sine_table,
     )
-
-    def backward_block(carry, offset):
-        grad_keys, grad_values = carry
-        query_rows, scores = block_scores(offset)
-        lse_rows = lax.dynamic_slice_in_dim(lse_all, offset, block_rows, 1)
-        probs_block = jnp.exp(scores - lse_rows[:, :, None])
-        weights_low = probs_block.astype(jnp.bfloat16)
-        grad_rows_out = lax.dynamic_slice_in_dim(grad_mixed, offset, block_rows, 0)
-        grad_weights = jnp.einsum(
-            "qhd,khd->hqk", grad_rows_out, value_heads, preferred_element_type=jnp.float32
-        )
-        grad_values = grad_values + jnp.einsum(
-            "hqk,qhd->khd", weights_low, grad_rows_out, preferred_element_type=jnp.float32
-        )
-        delta_rows = jnp.sum(probs_block * grad_weights, axis=-1, keepdims=True)
-        grad_scores = (probs_block * (grad_weights - delta_rows)).astype(jnp.bfloat16)
-        grad_query_block = (
-            jnp.einsum(
-                "hqk,khd->qhd", grad_scores, keys_rotated, preferred_element_type=jnp.float32
-            )
-            * score_scale
-        )
-        grad_keys = (
-            grad_keys
-            + jnp.einsum(
-                "hqk,qhd->khd", grad_scores, query_rows, preferred_element_type=jnp.float32
-            )
-            * score_scale
-        )
-        return ((grad_keys, grad_values), grad_query_block)
-
-    zero_heads = jnp.zeros((length, local_heads, HD), jnp.float32)
-    (grad_keys, grad_values), grad_query_blocks = lax.scan(
-        backward_block, (zero_heads, zero_heads), starts
-    )
-    grad_queries = grad_query_blocks.reshape(length, local_heads, HD)
-    grad_query_normed = unrotate(grad_queries, cosine, sine_table).reshape(length, local_width)
-    grad_key_normed = unrotate(grad_keys, cosine, sine_table).reshape(length, local_width)
-    grad_value_low = grad_values.reshape(length, local_width).astype(jnp.bfloat16)
-    query_weighted = grad_query_normed * query_gain_f
-    key_weighted = grad_key_normed * key_gain_f
-    query_gain_term = jnp.sum(grad_query_normed * query_raw * query_rs, axis=0)
-    key_gain_term = jnp.sum(grad_key_normed * key_raw * key_rs, axis=0)
+    query_gain_term, key_gain_term = query_gain_term.reshape(-1), key_gain_term.reshape(-1)
     query_inner, key_inner = (
-        lax.psum(jnp.sum(query_weighted * query_raw, axis=-1).astype(jnp.bfloat16), "row").astype(
-            jnp.float32
-        ),
-        lax.psum(jnp.sum(key_weighted * key_raw, axis=-1).astype(jnp.bfloat16), "row").astype(
-            jnp.float32
-        ),
+        lax.psum(jnp.sum(query_inner, axis=(0, 2)), "row"),
+        lax.psum(jnp.sum(key_inner, axis=(0, 2)), "row"),
     )
     grad_query_raw = (
         query_rs * query_weighted - query_raw * query_rs**3 * (query_inner / model_width)[:, None]

time: 1370 us -> 1280 us (0.934)
  Pallas kernels: 966 us -> 1070 us
  local copies, waits for them, and re-layouts: 93.8 us -> 33.2 us
  matrix products: 114 us -> 67.6 us
  waiting for transfers between devices: 46.2 us -> 0 us
  other arithmetic: 98.2 us -> 80.3 us
    pallas_call x2 -> x5, Pallas kernels: 119 us -> 222 us  [the longest x1 71.5 us: restore_out(): pl.pallas_call(restore_out_body, grid=(steps,), in_specs=in_specs + [ANYW...]
    reduce_scatter x1 -> x0, waiting for transfers between devices: 46.1 us -> none  [local(): lax.psum_scatter(wide_dot(mixed_heads, output_full).astype(jnp.bfloat16),...]
    dot_general x14 -> x0, matrix products: 44.5 us -> none  [the longest x2 9.32 us: backward_block(): jnp.einsum('hqk,qhd->khd', weights_low, grad_rows_out, preferred_element_...]
    unnamed x198 -> x120, local copies, waits for them, and re-layouts: 50.4 us -> 11.5 us
    convert_element_type x4 -> x3, other arithmetic: 15.4 us -> 33.9 us  [the longest x1 11.8 us: local(): grad_down_weight = grad_down_weight.astype(jnp.float32)]
  transfers between devices with their start and end apart: 2 -> 0, of which waited for: 1 -> 0; matrix products, arithmetic and copies ran while one was open for 2% -> 0% of each run, Pallas kernels for 4% -> 0%
where the time goes in v6:
time: 1280 us; the launch traced here: 1270 us
  Pallas kernels  1070 us (84%)
  other arithmetic  80.3 us (6%)
  matrix products  67.6 us (5%)
  local copies, waits for them, and re-layouts  33.2 us (3%)
  blocking collectives  17.5 us (1%)
    pallas_call x1, Pallas kernels, finish_near(): pl.pallas_call(finish_body, out_shape=(jax.ShapeDtypeStruct((tokens, dept...  217 us
    pallas_call x1, Pallas kernels, start_near(): pl.pallas_call(start_body, out_shape=(shaped((4, *x.shape), x), *[shaped(...  203 us
    pallas_call x1, Pallas kernels, feed_back(): pl.pallas_call(feed_back_body, grid=(groups, depth // CHUNK), in_specs=[A...  188 us
    pallas_call x1, Pallas kernels, grads_in(): pl.pallas_call(grads_in_body, grid=(steps,), in_specs=[pl.BlockSpec((rank...  162 us
    pallas_call x1, Pallas kernels, feed_in(): pl.pallas_call(functools.partial(feed_in_body, steps), grid=(steps + grou...  73.3 us
    pallas_call x1, Pallas kernels, restore_out(): pl.pallas_call(restore_out_body, grid=(steps,), in_specs=in_specs + [ANYW...  71.5 us
    pallas_call x1, Pallas kernels, restore(): pl.pallas_call(functools.partial(restore_body, flipped), grid=(steps,), i...  66.9 us
    pallas_call x1, Pallas kernels, branch_near(): pl.pallas_call(branch_body, in_specs=[inside] * 2, out_specs=inside, out_...  46 us

profile of v6, /device:TPU:0, one launch (start us, length us, event | category | flops | bytes accessed | tf_op | source)
XLA Modules:
  0.0 1267.3 jit_solution(18142078876341165196)
XLA Ops:
  5.0 203.4 %shard_map.254 = (bf16[4,256,2048]{2,1,0:T(8,128)(2,1)}, bf16[2048,512]{1,0:T(8,128)(2,1)}, bf16[2048,512]{1,0:T(8,128)(2,1)}, bf16[2048,512]{1,0:T(8,128)(2,1)}...) custom-call(bf16[256,2048]{1,0:T(8,128)(2,1)} %x_ref.1, ...), custom_call_target="tpu_custom_call" | custom-call | tf_op jit(solution)/shard_map/pallas_call | solution.py:397
  208.5 3.2 fusion.1
  217.0 3.8 multiply_reduce_fusion.4
  220.7 8.4 all-reduce.3
  236.7 5.5 convolution_convert_fusion.6.v_ref
  246.9 16.2 %shard_map.255 = (bf16[1024,512]{1,0:T(8,128)(2,1)}, bf16[1024,512]{1,0:T(8,128)(2,1)}, bf16[1024,512]{1,0:T(8,128)(2,1)}, f32[4,1024,1]{2,1,0:T(8,128)}) custom-call(f32[1024,512]{1,0:T(8,128)} %copy.86.q_raw, f32[1024,512]{1,0:T(8,128)} %copy.87.k_raw, bf16[1024,512]{1,0:T(8,128)(2,1)} %convolution_convert_fusion.6.v_ref, f32[1024,1]{1,0:T(8,128)} %copy.88.q_rs, ...), custom_call_target="tpu_custom_call" | custom-call | flops 2147483648 | bytes 8388608 | tf_op jit(solution)/shard_map/pallas_call | solution.py:1224
  264.4 46.0 %shard_map.256 = f32[256,2048]{1,0:T(8,128)S(1)} custom-call(bf16[1024,512]{1,0:T(8,128)(2,1)S(1)} %copy-done.1, bf16[512,2048]{1,0:T(8,128)(2,1)S(1)} %copy-done), custom_call_target="tpu_custom_call" | custom-call | tf_op jit(solution)/shard_map/pallas_call | solution.py:1176
  315.4 3.7 fusion.pick_ref
  319.1 162.4 %shard_map.257 = (bf16[8,1280,2048]{2,1,0:T(8,128)(2,1)}, f32[8,1280,256]{2,1,0:T(8,128)}, bf16[4,2,2,2,256,2048]{5,4,3,2,1,0:T(8,128)(2,1)}, f32[32,8,256]{2,1,0:T(8,128)}) custom-call(bf16[32,320,256]{2,1,0:T(8,128)(2,1)} %fusion.pick_ref, bf16[32,256,2048]{2,1,0:T(8,128)(2,1)} %bitcast.127, bf16[8,256,2048]{2,1,0:T(8,128)(2,1)} %weight_ref.1, ...), custom_call_target="tpu_custom_call" | custom-call | tf_op jit(solution)/shard_map/pallas_call | solution.py:895
  487.4 73.3 %shard_map.258 = (bf16[8,1280,2048]{2,1,0:T(8,128)(2,1)}, bf16[8,1280,256]{2,1,0:T(8,128)(2,1)}, bf16[8,1280,256]{2,1,0:T(8,128)(2,1)}, bf16[8,1280,256]{2,1,0:T...) custom-call(bf16[32,320,256]{2,1,0:T(8,128)(2,1)} %fusion.pick_ref, bf16[32,256,2048]{2,1,0:T(8,128)(2,1)} %bitcast.155, ...), custom_call_target="tpu_custom_call" | custom-call | flops 32212254720 | bytes 125829120 | tf_op jit(solution)/shard_map/pallas_call | solution.py:969
  560.8 3.9 reduce.3
  567.9 5.2 fusion.49
  573.1 66.9 %shard_map.259 = bf16[32,256,2048]{2,1,0:T(8,128)(2,1)} custom-call(bf16[32,256,320]{2,1,0:T(8,128)(2,1)} %get-tuple-element.180.spread_ref, bf16[8,1280,256]{2,1,0:T(8,128)(2,1)} %get-tuple-element.70.refs_0_.gate_ref, bf16[8,1280,256]{2,1,0:T(8,128)(2,1)} %get-tuple-element.71.refs_1_.up_ref, bf16[8,2048,256]{2,1,0:T(8,128)(2,1)} %refs_2_.1, ...), custom_call_target="tpu_custom_call" | custom-call | tf_op jit(solution)/shard_map/pallas_call | solution.py:1041
  639.9 188.3 %shard_map.260 = (f32[256,2048]{1,0:T(8,128)}, f32[32,8,256]{2,1,0:T(8,128)}, bf16[8,2048,256]{2,1,0:T(8,128)(2,1)}, bf16[8,2048,256]{2,1,0:T(8,128)(2,1)}, bf16[8,256,2048]{2,1,0:T(8,128)(2,1)}) custom-call(bf16[4,2,2,2,256,2048]{5,4,3,2,1,0:T(8,128)(2,1)} %bitcast.126, f32[32,8,256]{2,1,0:T(8,128)} %select_reduce_fusion.small_ref, ...), custom_call_target="tpu_custom_call" | custom-call | tf_op jit(solution)/shard_map/pallas_call | solution.py:802
  838.8 4.6 select_convert_fusion.spread_ref
  843.4 71.5 %shard_map.261 = (bf16[32,256,2048]{2,1,0:T(8,128)(2,1)}, bf16[4,256,2048]{2,1,0:T(8,128)(2,1)}) custom-call(bf16[32,256,320]{2,1,0:T(8,128)(2,1)} %select_convert_fusion.spread_ref, bf16[8,1280,256]{2,1,0:T(8,128)(2,1)} %get-tuple-element.69.left_ref, bf16[8,256,2048]{2,1,0:T(8,128)(2,1)} %weight_ref.1, bf16[256,2048]{1,0:T(8,128)(2,1)} %get-tuple-element.150.own_ref), custom_call_target="tpu_custom_call" | custom-call | tf_op jit(solution)/shard_map/pallas_call | solution.py:1107
  914.9 6.2 convolution_convert_fusion.5.grad_ref
  921.1 21.8 %shard_map.262 = (bf16[1024,512]{1,0:T(8,128)(2,1)}, f32[1024,512]{1,0:T(8,128)}, f32[1024,512]{1,0:T(8,128)}, f32[1,512]{1,0:T(1,128)}, f32[1,512]{1,0:T(1,128)...) custom-call(bf16[1024,512]{1,0:T(8,128)(2,1)} %get-tuple-element.79.q_ref, bf16[1024,512]{1,0:T(8,128)(2,1)} %get-tuple-element.80.k_ref, ...), custom_call_target="tpu_custom_call" | custom-call | flops 5368709120 | bytes 16777216 | tf_op jit(solution)/shard_map/pallas_call | solution.py:1274
  946.8 9.1 all-reduce.2
  962.3 5.8 fusion.50
  968.1 9.0 fusion.9
  978.2 6.0 convolution_convert_fusion.o_ref
  984.3 3.8 convolution_convert_fusion.1.v_ref
  988.0 3.8 convolution_convert_fusion.2.k_ref
  991.8 3.8 convolution_convert_fusion.3.q_ref
  995.6 3.6 fusion.6
  999.3 217.1 %shard_map.263 = (f32[256,2048]{1,0:T(8,128)}, f32[256,2048]{1,0:T(8,128)}, f32[256,512]{1,0:T(8,128)}, f32[256,512]{1,0:T(8,128)}, f32[256,512]{1,0:T(8,128)}, ...) custom-call(bf16[4,2,2,2,256,2048]{5,4,3,2,1,0:T(8,128)(2,1)} %bitcast.128, bf16[4,256,2048]{2,1,0:T(8,128)(2,1)} %bitcast.131, ...), custom_call_target="tpu_custom_call" | custom-call | tf_op jit(solution)/shard_map/pallas_call | solution.py:557
  1216.4 4.0 add.115
  1225.3 3.2 add.114
  1230.1 11.1 convert_element_type.190
  1241.1 11.1 convert_element_type.191
  1252.2 11.8 convert_element_type.192
  (194 shorter events, 68.2 us)
Async XLA Ops:
  208.5 4.4 copy-start.3
  229.8 6.9 copy-start.38
  229.8 6.9 copy-start.40
  246.9 16.2 %copy-start = (bf16[512,2048]{1,0:T(8,128)(2,1)S(1)}, bf16[512,2048]{1,0:T(8,128)(2,1)}, u32[]{:S(2)}) copy-start(bf16[512,2048]{1,0:T(8,128)(2,1)} %get-tuple-element.63.weight_ref) | copy-start | bytes 6291460
  246.9 63.5 %copy-start.15 = (bf16[256,2048]{1,0:T(8,128)(2,1)S(1)}, bf16[256,2048]{1,0:T(8,128)(2,1)}, u32[]{:S(2)}) copy-start(bf16[256,2048]{1,0:T(8,128)(2,1)} %x_ref.1) | copy-start | bytes 3145732
  312.3 6.8 copy-start.9
  482.8 4.6 copy-start.18
  560.7 7.1 copy-start.51
  828.2 5.2 copy-start.7
  943.0 12.9 %copy-start.11 = (f32[1024,512]{1,0:T(8,128)S(1)}, f32[1024,512]{1,0:T(8,128)}, u32[]{:S(2)}) copy-start(f32[1024,512]{1,0:T(8,128)} %copy.87.k_raw) | copy-start | bytes 6291460
  943.0 12.9 %copy-start.41 = (f32[1024]{0:T(1024)S(1)}, f32[1024]{0:T(1024)}, u32[]{:S(2)}) copy-start(f32[1024]{0:T(1024)} %copy-done.40) | copy-start | bytes 12292
  943.0 12.9 %copy-start.44 = (f32[1024]{0:T(1024)S(1)}, f32[1024]{0:T(1024)}, u32[]{:S(2)}) copy-start(f32[1024]{0:T(1024)} %get-tuple-element.164) | copy-start | bytes 12292
  962.2 5.8 copy-start.27
  962.2 5.8 copy-start.4
  962.2 5.8 copy-start.22
  962.2 5.8 copy-start.23
  962.2 5.8 copy-start.35
  962.3 5.8 copy-start.37
  968.1 9.0 copy-start.46
  968.1 9.1 copy-start.45
  968.1 10.1 copy-start.2
  978.2 6.0 copy-start.14
  978.2 6.0 copy-start.24
  988.0 3.8 copy-start.28
  988.0 7.5 slice-start
  991.8 3.8 copy-start.5
  991.8 3.8 slice-start.1
  1216.3 4.0 copy-start.12
  1220.3 5.0 copy-start.8
  1252.2 11.8 copy-start.32
  1252.2 12.6 copy-start.31
  1252.2 13.4 %copy-start.30 = (f32[256,512]{1,0:T(8,128)S(1)}, f32[256,512]{1,0:T(8,128)}, u32[]{:S(2)}) copy-start(f32[256,512]{1,0:T(8,128)} %get-tuple-element.214) | copy-start | bytes 1572868
  (22 other events, 49.8 us)

commit v7 on v6

--- a/solution.py
+++ b/solution.py
@@ -195,7 +195,7 @@
 def spread_out(own_ref, all_ref, sems):
     r, c, y, x, z, core, first, second = seat()
     pair, along_first, along_second, up = partners()
-    here_sem, z_send, z_recv, g_send, g_recv, f_send, f_recv, p_send, p_recv = sems
+    here_sem, u_send, u_recv, d_send, d_recv, g_send, g_recv, f_send, f_recv, p_send, p_recv = sems
     step = own_ref.shape[0] // GSTEPS
 
     def rows(q):
@@ -207,10 +207,28 @@
         yy, xx = row_of(core, fir, sec)
         return all_ref.at[(z + 4 - k) % 4, core, yy, xx, rows(q)]
 
-    def z_copy(k, q):
-        return send(
-            own_ref.at[rows(q)], place(0, 0, 0, q), z_send.at[k - 1, q], z_recv.at[k - 1, q], up[k - 1]
-        )
+    above, below = (r, ((z + 1) % 4) * 2 + core), (r, ((z + 3) % 4) * 2 + core)
+
+    def source(k, q):
+        return own_ref.at[rows(q)] if k == 0 else place(k, 0, 0, q)
+
+    def up_copy(d, q):
+        return send(source(d, q), place(d, 0, 0, q), u_send.at[d, q], u_recv.at[d, q], above)
+
+    def down_copy(d, q):
+        k = (4 - d) % 4
+        return send(source(k, q), place(k, 0, 0, q), d_send.at[d, q], d_recv.at[d, q], below)
+
+    def came_up(d, q):
+        there = place(d, 0, 0, q)
+        return send(there, there, u_send.at[d - 1, q], u_recv.at[d - 1, q], above)
+
+    def came_down(d, q):
+        there = place(4 - d, 0, 0, q)
+        return send(there, there, d_send.at[d - 1, q], d_recv.at[d - 1, q], below)
+
+    bottom, top = 1 - jnp.minimum(z, 1), z // 3
+    arrived = [bottom * (3 - i) + top * (1 + i) + (1 - bottom - top) * ARRIVE[i] for i in range(3)]
 
     def g_copy(k, q, src):
         return send(src, place(k, 0, 0, q), g_send.at[k, q], g_recv.at[k, q], along_second)
@@ -229,25 +247,56 @@
         @pl.loop(0, GSTEPS)
         def _(q):
             src = own_ref.at[rows(q)]
-            for k in QUEUE:
-                z_copy(k, q).start()
+
+            @pl.when(z < 3)
+            def _():
+                up_copy(0, q).start()
+
+            @pl.when(z > 0)
+            def _():
+                down_copy(0, q).start()
+
             g_copy(0, q, src).start()
             f_copy(0, 0, q, src).start()
             p_copy(0, 0, 0, q, src).start()
 
     def forward(q):
-        for k in ARRIVE:
-            z_copy(k, q).wait_recv()
+        def pass_on(k):
             src = place(k, 0, 0, q)
             g_copy(k, q, src).start()
             f_copy(k, 0, q, src).start()
             p_copy(k, 0, 0, q, src).start()
-        for k in (0, *ARRIVE):
+
+        for d in (1, 2, 3):
+
+            @pl.when(z >= d)
+            def _():
+                came_up(d, q).wait_recv()
+                if d < 3:
+
+                    @pl.when(z < 3)
+                    def _():
+                        up_copy(d, q).start()
+
+                pass_on(d)
+
+            @pl.when(z + d <= 3)
+            def _():
+                came_down(d, q).wait_recv()
+                if d < 3:
+
+                    @pl.when(z > 0)
+                    def _():
+                        down_copy(d, q).start()
+
+                pass_on(4 - d)
+
+        for k in (0, *arrived):
             src = place(k, 1, 0, q)
             g_copy(k, q, src).wait_recv()
             f_copy(k, 1, q, src).start()
             p_copy(k, 1, 0, q, src).start()
-        for k in (0, *ARRIVE):
+        for k in (0, *arrived):
             src = place(k, 0, 1, q)
             f_copy(k, 0, q, src).wait_recv()
             p_copy(k, 0, 1, q, src).start()
@@ -255,7 +304,7 @@
     def finish():
         @pl.loop(0, GSTEPS)
         def _(q):
-            for k in (0, *ARRIVE):
+            for k in (0, *arrived):
                 src = place(k, 1, 1, q)
                 f_copy(k, 1, q, src).wait_recv()
                 p_copy(k, 1, 1, q, src).start()
@@ -264,10 +313,18 @@
 
         @pl.loop(0, GSTEPS)
         def _(q):
+            for d in range(3):
+
+                @pl.when((z < 3) & (z >= d))
+                def _():
+                    up_copy(d, q).wait_send()
+
+                @pl.when((z > 0) & (z + d <= 3))
+                def _():
+                    down_copy(d, q).wait_send()
+
             for k in range(4):
                 src = own_ref.at[rows(q)]
-                if k:
-                    z_copy(k, q).wait_send()
                 g_copy(k, q, src).wait_send()
                 for s in range(2):
                     f_copy(k, s, q, src).wait_send()
@@ -279,7 +336,7 @@
 
 def spread_sems():
     dma = pltpu.SemaphoreType.DMA
-    shapes = [(3, GSTEPS), (4, GSTEPS), (2, 4, GSTEPS), (2, 2, 4, GSTEPS)]
+    shapes = [(3, GSTEPS), (3, GSTEPS), (4, GSTEPS), (2, 4, GSTEPS), (2, 2, 4, GSTEPS)]
     return [dma(())] + [dma(shape) for shape in shapes for _ in range(2)]
 
 
@@ -319,9 +376,9 @@
                x_all, q_all, k_all, v_all, o_all, pack_all, all_ref, small_all, *sems):
     r, c, y, x, z, core, first, second = seat()
     pair, along_first, along_second, up = partners()
-    begin, forward, finish = spread_out(own_ref, all_ref, sems[:9])
-    small_begin, small_finish = small_out(small_ref, small_all, sems[9:12])
-    here_sem, x_send, x_recv, w_send, w_recv, v_send, v_recv = sems[12:]
+    begin, forward, finish = spread_out(own_ref, all_ref, sems[:11])
+    small_begin, small_finish = small_out(small_ref, small_all, sems[11:14])
+    here_sem, x_send, x_recv, w_send, w_recv, v_send, v_recv = sems[14:]
     weights = [(q_ref, q_all), (k_ref, k_all), (v_ref, v_all), (o_ref, o_all), (pack_ref, pack_all)]
 
     def block(index, col):
@@ -503,7 +560,7 @@
             add(kept[index].at[zz], [pairs[index].at[zz]])
             w_z(index, k).start()
 
-    @pl.loop(0, RSTEPS)
+    @pl.loop(0, RSTEPS + LAGS[2])
     def _(i):
         tick(i)
 
@@ -529,7 +586,7 @@
     add_out(mine.at[first, second], [first_in.at[second], second_in], total)
     pltpu.make_async_copy(total, out_ref, out_sem.at[4]).start()
 
-    @pl.loop(RSTEPS, TICKS)
+    @pl.loop(RSTEPS + LAGS[2], TICKS)
     def _(i):
         tick(i)
 
@@ -757,9 +814,6 @@
     return begin, finish
 
 
-SPACING = 5
-
-
 def feed_back_body(part_ref, small_ref, rows_ref, gate_ref, up_ref, act_ref, grads_ref,
                    out_ref, small_all, gate_out, up_out, down_out, *scratch):
     begin, tick, finish = shrink(part_ref, *scratch[:6], scratch[6:15])
@@ -780,12 +834,16 @@
     up_out[0] = inner_rows(rows, up_ref[0]).astype(jnp.bfloat16)
     down_out[0] = inner_rows(act_ref[0], grads_ref[0]).astype(jnp.bfloat16)
 
-    @pl.when((step % SPACING == 0) & (step // SPACING < TICKS))
+    @pl.when(k == 0)
     def _():
-        tick(step // SPACING)
+        tick(e)
 
     @pl.when(step == last)
     def _():
+        @pl.loop(RSTEPS, TICKS)
+        def _(i):
+            tick(i)
+
         done = pltpu.make_async_copy(total, out_ref, out_sem)
         done.start()
         finish()
@@ -796,6 +854,7 @@
 def feed_back(part, small, rows, grad_gate, grad_up, act, grads, collective_id):
     tokens, depth = part.shape[0] // RANKS, part.shape[1]
     groups, length, inner = grad_gate.shape
+    assert groups == RSTEPS
     dma = pltpu.SemaphoreType.DMA
     slab = pl.BlockSpec((1, length, CHUNK), lambda e, k: (e, 0, k))
     held = pl.BlockSpec((1, length, inner), lambda e, k: (e, 0, 0))
@@ -824,6 +883,24 @@
     )(part.reshape(4, 2, 2, 2, tokens, depth), small, rows, grad_gate, grad_up, act, grads)
 
 
+def widen_body(*refs):
+    half = len(refs) // 2
+    for low, wide in zip(refs[:half], refs[half:]):
+        wide[...] = low[...].astype(jnp.float32)
+
+
+def widen_all(*arrays):
+    specs = [pl.BlockSpec((1, *array.shape[1:]), lambda e: (e, 0, 0)) for array in arrays]
+    return pl.pallas_call(
+        widen_body,
+        grid=(arrays[0].shape[0],),
+        in_specs=specs,
+        out_specs=specs,
+        out_shape=[jax.ShapeDtypeStruct(array.shape, jnp.float32) for array in arrays],
+        compiler_params=pltpu.CompilerParams(vmem_limit_bytes=40 * 1024 * 1024),
+    )(*arrays)
+
+
 def fill_rows(pick_ref, field_ref, rows_ref):
     ranks, groups = pick_ref.shape[0], rows_ref.shape[0]
 
@@ -863,8 +940,8 @@
 
 def grads_in_body(pick_ref, field_ref, down_ref, own_ref, small_ref,
                   rows_ref, plain_ref, all_ref, small_all, total, *sems):
-    begin, forward, finish = spread_out(own_ref, all_ref, sems[:9])
-    small_begin, small_finish = small_out(small_ref, small_all, sems[9:])
+    begin, forward, finish = spread_out(own_ref, all_ref, sems[:11])
+    small_begin, small_finish = small_out(small_ref, small_all, sems[11:])
     k, last = pl.program_id(0), pl.num_programs(0) - 1
 
     @pl.when(k == 0)
@@ -1086,9 +1163,10 @@
 
     fill_field((False,), spread_ref, [left_ref], [weight_ref], field_ref, rows)
 
-    @pl.when(k == 1)
-    def _():
-        for q in range(PARTS):
+    for q in range(PARTS):
+
+        @pl.when(k == q + 1)
+        def _():
             g_copy(q).wait_recv()
             h_copy(q).start()
 
@@ -1480,9 +1558,9 @@
         grad_feed, gates_in, grad_gate_weight, grad_up_weight, grad_down_weight = feed_back(
             grad_feed_part, own_gates, expert_rows, grad_gate, grad_up, weighted_act, expert_grads, 3
         )
-        grad_gate_weight = grad_gate_weight.astype(jnp.float32)
-        grad_up_weight = grad_up_weight.astype(jnp.float32)
-        grad_down_weight = grad_down_weight.astype(jnp.float32)
+        grad_gate_weight, grad_up_weight, grad_down_weight = widen_all(
+            grad_gate_weight, grad_up_weight, grad_down_weight
+        )
         gates_in = jnp.sum(gates_in.reshape(-1, rows_count, experts_local, tokens), axis=1)
         grad_probs = gates_in.reshape(experts, tokens).T
     else:

time: 1280 us -> 1270 us (level)
  other arithmetic: 80.3 us -> 45.4 us
  Pallas kernels: 1070 us -> 1090 us
    pallas_call x1, Pallas kernels: 203 us -> 251 us  [start_near(): pl.pallas_call(start_body, out_shape=(shaped((4, *x.shape), x), *[shaped(...]
    convert_element_type x3 -> x0, other arithmetic: 33.9 us -> none  [the longest x1 11.8 us: local(): grad_down_weight = grad_down_weight.astype(jnp.float32)]
    pallas_call x1, Pallas kernels: 188 us -> 160 us  [feed_back(): pl.pallas_call(feed_back_body, grid=(groups, depth // CHUNK), in_specs=[A...]
    pallas_call x0 -> x1, Pallas kernels: none -> 22 us  [widen_all(): pl.pallas_call(widen_body, grid=(arrays[0].shape[0],), in_specs=specs, ou...]
    pallas_call x1, Pallas kernels: 71.5 us -> 57.7 us  [restore_out(): pl.pallas_call(restore_out_body, grid=(steps,), in_specs=in_specs + [ANYW...]
where the time goes in v7:
time: 1270 us; the launch traced here: 1260 us
  Pallas kernels  1090 us (86%)
  matrix products  66.1 us (5%)
  other arithmetic  45.4 us (4%)
  local copies, waits for them, and re-layouts  37.7 us (3%)
  blocking collectives  18.4 us (1%)
    pallas_call x1, Pallas kernels, start_near(): pl.pallas_call(start_body, out_shape=(shaped((4, *x.shape), x), *[shaped(...  251 us
    pallas_call x1, Pallas kernels, finish_near(): pl.pallas_call(finish_body, out_shape=(jax.ShapeDtypeStruct((tokens, dept...  217 us
    pallas_call x1, Pallas kernels, grads_in(): pl.pallas_call(grads_in_body, grid=(steps,), in_specs=[pl.BlockSpec((rank...  165 us
    pallas_call x1, Pallas kernels, feed_back(): pl.pallas_call(feed_back_body, grid=(groups, depth // CHUNK), in_specs=[A...  160 us
    pallas_call x1, Pallas kernels, feed_in(): pl.pallas_call(functools.partial(feed_in_body, steps), grid=(steps + grou...  73.6 us
    pallas_call x1, Pallas kernels, restore(): pl.pallas_call(functools.partial(restore_body, flipped), grid=(steps,), i...  66.9 us
    pallas_call x1, Pallas kernels, restore_out(): pl.pallas_call(restore_out_body, grid=(steps,), in_specs=in_specs + [ANYW...  57.7 us
    pallas_call x1, Pallas kernels, branch_near(): pl.pallas_call(branch_body, in_specs=[inside] * 2, out_specs=inside, out_...  38.5 us

profile of v7, /device:TPU:0, one launch (start us, length us, event | category | flops | bytes accessed | tf_op | source)
XLA Modules:
  0.0 1259.7 jit_solution(10386434019003066062)
XLA Ops:
  5.0 251.2 %shard_map.254 = (bf16[4,256,2048]{2,1,0:T(8,128)(2,1)}, bf16[2048,512]{1,0:T(8,128)(2,1)}, bf16[2048,512]{1,0:T(8,128)(2,1)}, bf16[2048,512]{1,0:T(8,128)(2,1)}...) custom-call(bf16[256,2048]{1,0:T(8,128)(2,1)} %x_ref.1, ...), custom_call_target="tpu_custom_call" | custom-call | tf_op jit(solution)/shard_map/pallas_call | solution.py:454
  256.2 3.2 fusion.1
  264.7 3.8 multiply_reduce_fusion.4
  268.4 9.3 all-reduce.3
  285.3 5.6 convolution_convert_fusion.6.v_ref
  295.5 16.2 %shard_map.255 = (bf16[1024,512]{1,0:T(8,128)(2,1)}, bf16[1024,512]{1,0:T(8,128)(2,1)}, bf16[1024,512]{1,0:T(8,128)(2,1)}, f32[4,1024,1]{2,1,0:T(8,128)}) custom-call(f32[1024,512]{1,0:T(8,128)} %copy.86.q_raw, f32[1024,512]{1,0:T(8,128)} %copy.87.k_raw, bf16[1024,512]{1,0:T(8,128)(2,1)} %convolution_convert_fusion.6.v_ref, f32[1024,1]{1,0:T(8,128)} %copy.88.q_rs, ...), custom_call_target="tpu_custom_call" | custom-call | flops 2147483648 | bytes 8388608 | tf_op jit(solution)/shard_map/pallas_call | solution.py:1302
  312.9 38.5 %shard_map.256 = f32[256,2048]{1,0:T(8,128)S(1)} custom-call(bf16[1024,512]{1,0:T(8,128)(2,1)S(1)} %copy-done.2, bf16[512,2048]{1,0:T(8,128)(2,1)S(1)} %copy-done.1), custom_call_target="tpu_custom_call" | custom-call | tf_op jit(solution)/shard_map/pallas_call | solution.py:1254
  356.5 3.7 fusion.pick_ref
  360.2 164.8 %shard_map.257 = (bf16[8,1280,2048]{2,1,0:T(8,128)(2,1)}, f32[8,1280,256]{2,1,0:T(8,128)}, bf16[4,2,2,2,256,2048]{5,4,3,2,1,0:T(8,128)(2,1)}, f32[32,8,256]{2,1,0:T(8,128)}) custom-call(bf16[32,320,256]{2,1,0:T(8,128)(2,1)} %fusion.pick_ref, bf16[32,256,2048]{2,1,0:T(8,128)(2,1)} %bitcast.127, bf16[8,256,2048]{2,1,0:T(8,128)(2,1)} %weight_ref.1, ...), custom_call_target="tpu_custom_call" | custom-call | tf_op jit(solution)/shard_map/pallas_call | solution.py:972
  527.8 3.1 reshape.270.probs_ref
  530.9 73.6 %shard_map.258 = (bf16[8,1280,2048]{2,1,0:T(8,128)(2,1)}, bf16[8,1280,256]{2,1,0:T(8,128)(2,1)}, bf16[8,1280,256]{2,1,0:T(8,128)(2,1)}, bf16[8,1280,256]{2,1,0:T...) custom-call(bf16[32,320,256]{2,1,0:T(8,128)(2,1)} %fusion.pick_ref, bf16[32,256,2048]{2,1,0:T(8,128)(2,1)} %bitcast.155, ...), custom_call_target="tpu_custom_call" | custom-call | flops 32212254720 | bytes 125829120 | tf_op jit(solution)/shard_map/pallas_call | solution.py:1046
  604.5 3.9 reduce.3
  611.6 5.3 fusion.49
  616.9 66.9 %shard_map.259 = bf16[32,256,2048]{2,1,0:T(8,128)(2,1)} custom-call(bf16[32,256,320]{2,1,0:T(8,128)(2,1)} %get-tuple-element.186.spread_ref, bf16[8,1280,256]{2,1,0:T(8,128)(2,1)} %get-tuple-element.73.refs_0_.gate_ref, bf16[8,1280,256]{2,1,0:T(8,128)(2,1)} %get-tuple-element.74.refs_1_.up_ref, bf16[8,2048,256]{2,1,0:T(8,128)(2,1)} %refs_2_.1, ...), custom_call_target="tpu_custom_call" | custom-call | tf_op jit(solution)/shard_map/pallas_call | solution.py:1118
  683.9 160.3 %shard_map.260 = (f32[256,2048]{1,0:T(8,128)}, f32[32,8,256]{2,1,0:T(8,128)}, bf16[8,2048,256]{2,1,0:T(8,128)(2,1)}, bf16[8,2048,256]{2,1,0:T(8,128)(2,1)}, bf16[8,256,2048]{2,1,0:T(8,128)(2,1)}) custom-call(bf16[4,2,2,2,256,2048]{5,4,3,2,1,0:T(8,128)(2,1)} %bitcast.126, f32[32,8,256]{2,1,0:T(8,128)} %select_reduce_fusion.small_ref, ...), custom_call_target="tpu_custom_call" | custom-call | tf_op jit(solution)/shard_map/pallas_call | solution.py:861
  844.2 3.4 copy-done
  847.6 22.0 %shard_map.264 = (f32[8,2048,256]{2,1,0:T(8,128)}, f32[8,2048,256]{2,1,0:T(8,128)}, f32[8,256,2048]{2,1,0:T(8,128)}) custom-call(bf16[8,2048,256]{2,1,0:T(8,128)(2,1)S(1)} %copy-done, bf16[8,2048,256]{2,1,0:T(8,128)(2,1)} %get-tuple-element.101.refs_1_, bf16[8,256,2048]{2,1,0:T(8,128)(2,1)} %get-tuple-element.102.refs_2_), custom_call_target="tpu_custom_call" | custom-call | tf_op jit(solution)/shard_map/pallas_call | solution.py:894
  877.8 4.5 select_convert_fusion.spread_ref
  882.3 57.7 %shard_map.261 = (bf16[32,256,2048]{2,1,0:T(8,128)(2,1)}, bf16[4,256,2048]{2,1,0:T(8,128)(2,1)}) custom-call(bf16[32,256,320]{2,1,0:T(8,128)(2,1)} %select_convert_fusion.spread_ref, bf16[8,1280,256]{2,1,0:T(8,128)(2,1)} %get-tuple-element.72.left_ref, bf16[8,256,2048]{2,1,0:T(8,128)(2,1)} %weight_ref.1, bf16[256,2048]{1,0:T(8,128)(2,1)} %get-tuple-element.156.own_ref), custom_call_target="tpu_custom_call" | custom-call | tf_op jit(solution)/shard_map/pallas_call | solution.py:1185
  940.0 6.2 convolution_convert_fusion.5.grad_ref
  946.2 21.8 %shard_map.262 = (bf16[1024,512]{1,0:T(8,128)(2,1)}, f32[1024,512]{1,0:T(8,128)}, f32[1024,512]{1,0:T(8,128)}, f32[1,512]{1,0:T(1,128)}, f32[1,512]{1,0:T(1,128)...) custom-call(bf16[1024,512]{1,0:T(8,128)(2,1)} %get-tuple-element.82.q_ref, bf16[1024,512]{1,0:T(8,128)(2,1)} %get-tuple-element.83.k_ref, ...), custom_call_target="tpu_custom_call" | custom-call | flops 5368709120 | bytes 16777216 | tf_op jit(solution)/shard_map/pallas_call | solution.py:1352
  971.9 9.1 all-reduce.2
  987.4 5.6 fusion.50
  993.0 8.8 fusion.9
  1003.0 6.0 convolution_convert_fusion.o_ref
  1009.0 3.8 convolution_convert_fusion.1.v_ref
  1012.8 3.8 convolution_convert_fusion.2.k_ref
  1016.5 3.8 convolution_convert_fusion.3.q_ref
  1020.3 3.8 fusion.6
  1024.1 217.1 %shard_map.263 = (f32[256,2048]{1,0:T(8,128)}, f32[256,2048]{1,0:T(8,128)}, f32[256,512]{1,0:T(8,128)}, f32[256,512]{1,0:T(8,128)}, f32[256,512]{1,0:T(8,128)}, ...) custom-call(bf16[4,2,2,2,256,2048]{5,4,3,2,1,0:T(8,128)(2,1)} %bitcast.128, bf16[4,256,2048]{2,1,0:T(8,128)(2,1)} %bitcast.131, ...), custom_call_target="tpu_custom_call" | custom-call | tf_op jit(solution)/shard_map/pallas_call | solution.py:614
  1241.3 4.0 add.115
  1250.3 3.2 add.114
  (196 shorter events, 63.9 us)
Async XLA Ops:
  256.2 4.4 copy-start.4
  278.4 6.9 copy-start.40
  278.4 6.9 copy-start.42
  295.5 16.2 %copy-start.1 = (bf16[512,2048]{1,0:T(8,128)(2,1)S(1)}, bf16[512,2048]{1,0:T(8,128)(2,1)}, u32[]{:S(2)}) copy-start(bf16[512,2048]{1,0:T(8,128)(2,1)} %get-tuple-element.66.weight_ref) | copy-start | bytes 6291460
  295.5 55.9 %copy-start.17 = (bf16[256,2048]{1,0:T(8,128)(2,1)S(1)}, bf16[256,2048]{1,0:T(8,128)(2,1)}, u32[]{:S(2)}) copy-start(bf16[256,2048]{1,0:T(8,128)(2,1)} %x_ref.1) | copy-start | bytes 3145732
  353.4 6.8 copy-start.10
  526.3 4.6 copy-start.20
  604.5 7.1 copy-start.53
  847.6 22.0 %copy-start.35 = (f32[32,8,256]{2,1,0:T(8,128)S(1)}, f32[32,8,256]{2,1,0:T(8,128)}, u32[]{:S(2)}) copy-start(f32[32,8,256]{2,1,0:T(8,128)} %get-tuple-element.80) | copy-start | bytes 786436
  847.6 22.1 %copy-start.11 = (bf16[256,2048]{1,0:T(8,128)(2,1)S(1)}, bf16[256,2048]{1,0:T(8,128)(2,1)}, u32[]{:S(2)}) copy-start(bf16[256,2048]{1,0:T(8,128)(2,1)} %copy-done.10) | copy-start | bytes 3145732
  968.1 12.9 %copy-start.13 = (f32[1024,512]{1,0:T(8,128)S(1)}, f32[1024,512]{1,0:T(8,128)}, u32[]{:S(2)}) copy-start(f32[1024,512]{1,0:T(8,128)} %copy.87.k_raw) | copy-start | bytes 6291460
  968.1 12.9 %copy-start.43 = (f32[1024]{0:T(1024)S(1)}, f32[1024]{0:T(1024)}, u32[]{:S(2)}) copy-start(f32[1024]{0:T(1024)} %copy-done.42) | copy-start | bytes 12292
  968.1 12.9 %copy-start.46 = (f32[1024]{0:T(1024)S(1)}, f32[1024]{0:T(1024)}, u32[]{:S(2)}) copy-start(f32[1024]{0:T(1024)} %get-tuple-element.170) | copy-start | bytes 12292
  987.3 5.6 copy-start.29
  987.3 5.6 copy-start.5
  987.3 5.6 copy-start.24
  987.3 5.6 copy-start.25
  987.3 5.6 copy-start.37
  987.3 5.6 copy-start.39
  993.0 8.9 copy-start.48
  993.0 9.0 copy-start.47
  993.0 9.9 copy-start.3
  1003.0 6.0 copy-start.16
  1003.0 6.0 copy-start.26
  1009.0 3.8 copy-start.28
  1012.8 7.5 slice-start
  1016.5 3.8 copy-start.6
  1016.5 3.8 slice-start.1
  1241.2 4.0 copy-start.14
  1245.2 5.0 copy-start.9
  1253.4 4.2 copy-start.32
  1253.4 5.0 copy-start.31
  (24 other events, 57.3 us)

commit v8 on v7

--- a/solution.py
+++ b/solution.py
@@ -260,7 +260,7 @@
             f_copy(0, 0, q, src).start()
             p_copy(0, 0, 0, q, src).start()
 
-    def forward(q):
+    def along_z(q):
         def pass_on(k):
             src = place(k, 0, 0, q)
             g_copy(k, q, src).start()
@@ -290,6 +290,15 @@
                         down_copy(d, q).start()
 
                 pass_on(4 - d)
+
+    def forward(q):
+        @pl.when(q == 0)
+        def _():
+            along_z(q)
+
+        @pl.when(q + 1 < GSTEPS)
+        def _():
+            along_z(q + 1)
 
         for k in (0, *arrived):
             src = place(k, 1, 0, q)
@@ -373,13 +382,13 @@
 
 
 def start_body(x_ref, q_ref, k_ref, v_ref, o_ref, pack_ref, own_ref, small_ref,
-               x_all, q_all, k_all, v_all, o_all, pack_all, all_ref, small_all, *sems):
+               x_all, qkv_all, o_all, pack_all, all_ref, small_all, *sems):
     r, c, y, x, z, core, first, second = seat()
     pair, along_first, along_second, up = partners()
     begin, forward, finish = spread_out(own_ref, all_ref, sems[:11])
     small_begin, small_finish = small_out(small_ref, small_all, sems[11:14])
     here_sem, x_send, x_recv, w_send, w_recv, v_send, v_recv = sems[14:]
-    weights = [(q_ref, q_all), (k_ref, k_all), (v_ref, v_all), (o_ref, o_all), (pack_ref, pack_all)]
+    weights = [(q_ref, qkv_all), (k_ref, qkv_all), (v_ref, qkv_all), (o_ref, o_all), (pack_ref, pack_all)]
 
     def block(index, col):
         ref, whole = weights[index]
@@ -388,8 +397,8 @@
         if index == 3:
             width = ref.shape[1]
             return whole.at[:, pl.ds(pl.multiple_of(col * width, width), width)]
-        height = ref.shape[0]
-        return whole.at[pl.ds(pl.multiple_of(col * height, height), height)]
+        height, width = ref.shape
+        return whole.at[pl.ds(pl.multiple_of(col * height, height), height), pl.ds(index * width, width)]
 
     def w_copy(index, k):
         return send(
@@ -415,18 +424,16 @@
     x_second.start()
     x_first.start()
     begin()
-    for index in (4, 0, 1, 2, 3):
-        for k in QUEUE:
-            w_copy(index, k).start()
-        pair_copy(index, 0).start()
     for item in locals_:
         item.start()
     x_second.wait_recv()
     x_relay.start()
-
-    @pl.loop(0, GSTEPS)
-    def _(q):
+    for q, group in enumerate(((4, 0), (1,), (2, 3), ())):
         forward(q)
+        for index in group:
+            for k in QUEUE:
+                w_copy(index, k).start()
+            pair_copy(index, 0).start()
 
     for index in (4, 0, 1, 2, 3):
         for k in ARRIVE:
@@ -455,28 +462,27 @@
         start_body,
         out_shape=(
             shaped((4, *x.shape), x),
-            *[shaped((8 * height, width), w) for w in weights[:3]],
+            shaped((8 * height, 3 * width), weights[0]),
             shaped((weights[3].shape[0], 8 * weights[3].shape[1]), weights[3]),
             shaped((8, *pack.shape), pack),
             shaped((4, 2, 2, 2, tokens, depth), own),
             shaped((RANKS, *small.shape), small),
         ),
         in_specs=[ANYWHERE] * 8,
-        out_specs=[ANYWHERE] * 8,
+        out_specs=[ANYWHERE] * 6,
         scratch_shapes=spread_sems()
         + small_sems()
         + [dma((6,)), dma((3,)), dma((3,)), dma((5, 3)), dma((5, 3)), dma((5, 4)), dma((5, 4))],
         compiler_params=pltpu.CompilerParams(collective_id=collective_id, has_side_effects=True),
     )(x, *weights, pack, own, small)
-    x_all, q, k, v, o, pack_all, whole, small_all = outs
-    return x_all.reshape(-1, x.shape[1]), q, k, v, o, pack_all, whole.reshape(RANKS, tokens, depth), small_all
-
-
-def finish_body(part_ref, field_ref, q_ref, k_ref, v_ref, o_ref, pack_ref,
+    x_all, qkv, o, pack_all, whole, small_all = outs
+    return x_all.reshape(-1, x.shape[1]), qkv, o, pack_all, whole.reshape(RANKS, tokens, depth), small_all
+
+
+def finish_body(part_ref, field_ref, qkv_ref, o_ref, pack_ref,
                 mixture_ref, out_ref, q_out, k_out, v_out, o_out, pack_all,
                 mine, first_in, second_in, total,
-                q_mine, k_mine, v_mine, o_mine, q_pair, k_pair, v_pair, o_pair, q_z, k_z, v_z, o_z,
-                q_sum, k_sum, v_sum, o_sum,
+                qkv_mine, o_mine, qkv_pair, o_pair, qkv_z, o_z, qkv_sum, o_sum,
                 load_sem, f_send, f_recv, g_send, g_recv, w_load, p_send, p_recv, z_send, z_recv, out_sem,
                 *rest):
     r, c, y, x, z, core, first, second = seat()
@@ -486,13 +492,20 @@
     mixture = rest[8]
     tokens, depth = out_ref.shape
     other = 1 - core
-    grads = [q_ref, k_ref, v_ref, o_ref]
-    kept, pairs, zs = [q_mine, k_mine, v_mine, o_mine], [q_pair, k_pair, v_pair, o_pair], [q_z, k_z, v_z, o_z]
-    sums, outs = [q_sum, k_sum, v_sum, o_sum], [q_out, k_out, v_out, o_out]
+    grads, kept, pairs = [qkv_ref, o_ref], [qkv_mine, o_mine], [qkv_pair, o_pair]
+    zs, sums = [qkv_z, o_z], [qkv_sum, o_sum]
+    width = q_out.shape[1]
+    results = [
+        [
+            pltpu.make_async_copy(qkv_sum.at[:, pl.ds(i * width, width)], out, out_sem.at[i])
+            for i, out in enumerate((q_out, k_out, v_out))
+        ],
+        [pltpu.make_async_copy(o_sum, o_out, out_sem.at[3])],
+    ]
 
     def block(index, col):
         ref = grads[index]
-        if index == 3:
+        if index == 1:
             width = ref.shape[1] // 8
             return ref.at[:, pl.ds(pl.multiple_of(col * width, width), width)]
         height = ref.shape[0] // 8
@@ -542,7 +555,7 @@
             result[here] = value
 
     meet()
-    for index in range(4):
+    for index in range(2):
         for k in (2, 1, 3, 0):
             w_give(index, (z + k) % 4).start()
             w_load_copy(index, (z + k) % 4).start()
@@ -552,7 +565,7 @@
     load(first, 1 - second).start()
     load(first, second).start()
     small_begin()
-    for index in range(4):
+    for index in range(2):
         for k in QUEUE:
             zz = (z + k) % 4
             w_load_copy(index, zz).wait()
@@ -571,7 +584,7 @@
             add(mine.at[first, 1 - second], [first_in.at[1 - second]])
             g_copy.start()
 
-    for index in range(4):
+    for index in range(2):
         w_load_copy(index, z).wait()
         w_give(index, z).wait_recv()
         for k in ARRIVE:
@@ -579,7 +592,8 @@
         add_out(
             kept[index].at[z], [pairs[index].at[z]] + [zs[index].at[k] for k in range(3)], sums[index]
         )
-        pltpu.make_async_copy(sums[index], outs[index], out_sem.at[index]).start()
+        for result in results[index]:
+            result.start()
     load(first, second).wait()
     f_copy(second).wait_recv()
     g_copy.wait_recv()
@@ -595,12 +609,13 @@
     for sec in range(2):
         f_copy(sec).wait_send()
     g_copy.wait_send()
-    for index in range(4):
+    for index in range(2):
         for k in range(4):
             w_give(index, (z + k) % 4).wait_send()
             if k:
                 w_z(index, k).wait_send()
-        pltpu.make_async_copy(sums[index], outs[index], out_sem.at[index]).wait()
+        for result in results[index]:
+            result.wait()
     small_finish()
     pltpu.make_async_copy(total, out_ref, out_sem.at[4]).wait()
     pltpu.make_async_copy(mixture, mixture_ref, out_sem.at[5]).wait()
@@ -609,17 +624,18 @@
 def finish_near(part, field, grads, pack, collective_id):
     rows_count, tokens, depth = field.shape
     dma = pltpu.SemaphoreType.DMA
-    blocks = [(g.shape[0] // 8, g.shape[1]) for g in grads[:3]] + [(grads[3].shape[0], grads[3].shape[1] // 8)]
+    blocks = [(grads[0].shape[0] // 8, grads[0].shape[1]), (grads[1].shape[0], grads[1].shape[1] // 8)]
+    results = [(blocks[0][0], blocks[0][1] // 3)] * 3 + [blocks[1]]
     half = lambda *shape: pltpu.VMEM(shape, jnp.bfloat16)
     return pl.pallas_call(
         finish_body,
         out_shape=(
             jax.ShapeDtypeStruct((tokens, depth), jnp.float32),
             jax.ShapeDtypeStruct((tokens, depth), jnp.float32),
-            *[jax.ShapeDtypeStruct(b, jnp.float32) for b in blocks],
+            *[jax.ShapeDtypeStruct(b, jnp.float32) for b in results],
             jax.ShapeDtypeStruct((RANKS, *pack.shape[1:]), pack.dtype),
         ),
-        in_specs=[ANYWHERE] * 7,
+        in_specs=[ANYWHERE] * 5,
         out_specs=[ANYWHERE] * 7,
         scratch_shapes=[
             half(2, 2, tokens, depth), half(2, tokens, depth), half(tokens, depth),
@@ -627,7 +643,7 @@
             *[half(4, *b) for b in blocks], *[half(4, *b) for b in blocks], *[half(3, *b) for b in blocks],
             *[pltpu.VMEM(b, jnp.float32) for b in blocks],
             dma((2, 2)), dma((2,)), dma((2,)), dma(()), dma(()),
-            dma((4, 4)), dma((4, 4)), dma((4, 4)), dma((4, 3)), dma((4, 3)), dma((6,)),
+            dma((2, 4)), dma((2, 4)), dma((2, 4)), dma((2, 3)), dma((2, 3)), dma((6,)),
         ]
         + small_sems()
         + shrink_scratch(tokens, depth),
@@ -1273,9 +1289,10 @@
 
 
 def attend_body(q_raw, k_raw, v_ref, q_rs, k_rs, q_gain, k_gain, cos_ref, sin_ref,
-                mixed_ref, q_out, k_out, lse_ref):
+                mixed_ref, q_out, k_out, v_out, lse_ref):
     length = v_ref.shape[0]
     block = min(256, length)
+    v_out[...] = v_ref[...].astype(jnp.bfloat16)
     for raw, scale, gain, out in ((q_raw, q_rs, q_gain, q_out), (k_raw, k_rs, k_gain, k_out)):
         normed = raw[...] * scale[...] * gain[...]
         turned = normed * cos_ref[...] + pltpu.roll(normed, HD // 2, 1) * sin_ref[...]
@@ -1287,12 +1304,16 @@
         exponent = jnp.exp(scores - row_top)
         row_total = jnp.sum(exponent, axis=-1, keepdims=True)
         weights = (exponent / row_total).astype(jnp.bfloat16)
-        mixed_ref[here] = wide_dot(weights, v_ref[seen]).astype(jnp.bfloat16)
+        mixed_ref[here] = wide_dot(weights, v_out[seen]).astype(jnp.bfloat16)
         lse_ref[0, here] = row_top + jnp.log(row_total)
 
 
-def attend(q_raw, k_raw, values, q_rs, k_rs, q_gain, k_gain, cosine, sine):
-    length, width = q_raw.shape
+def three_slabs(length, heads):
+    return [pl.BlockSpec((length, HD), lambda h, at=at: (0, at * heads + h)) for at in range(3)]
+
+
+def attend(raw, q_rs, k_rs, q_gain, k_gain, cosine, sine):
+    length, width = raw.shape[0], raw.shape[1] // 3
     heads = width // HD
     slab = pl.BlockSpec((length, HD), lambda h: (0, h))
     thin = pl.BlockSpec((length, 1), lambda h: (0, 0))
@@ -1302,13 +1323,13 @@
     return pl.pallas_call(
         attend_body,
         grid=(heads,),
-        in_specs=[slab, slab, slab, thin, thin, line, line, table, table],
-        out_specs=[slab, slab, slab, pl.BlockSpec((1, length, 1), lambda h: (h, 0, 0))],
-        out_shape=[low, low, low, jax.ShapeDtypeStruct((heads, length, 1), jnp.float32)],
+        in_specs=three_slabs(length, heads) + [thin, thin, line, line, table, table],
+        out_specs=[slab, slab, slab, slab, pl.BlockSpec((1, length, 1), lambda h: (h, 0, 0))],
+        out_shape=[low, low, low, low, jax.ShapeDtypeStruct((heads, length, 1), jnp.float32)],
         cost_estimate=pl.CostEstimate(
             flops=4 * heads * length * length * HD, bytes_accessed=8 << 20, transcendentals=heads * length * length
         ),
-    )(q_raw, k_raw, values, q_rs, k_rs, q_gain[None], k_gain[None], cosine, sine)
+    )(raw, raw, raw, q_rs, k_rs, q_gain[None], k_gain[None], cosine, sine)
 
 
 def attend_back_body(q_ref, k_ref, v_ref, grad_ref, lse_ref, q_raw, k_raw, q_rs, k_rs, q_gain, k_gain, cos_ref, sin_ref,
@@ -1340,8 +1361,8 @@
         inner[0] = jnp.sum(weighted * field, axis=-1, keepdims=True)
 
 
-def attend_back(queries, keys, values, grads, lse, q_raw, k_raw, q_rs, k_rs, q_gain, k_gain, cosine, sine):
-    length, width = q_raw.shape
+def attend_back(queries, keys, values, grads, lse, raw, q_rs, k_rs, q_gain, k_gain, cosine, sine):
+    length, width = raw.shape[0], raw.shape[1] // 3
     heads = width // HD
     slab = pl.BlockSpec((length, HD), lambda h: (0, h))
     thin = pl.BlockSpec((length, 1), lambda h: (0, 0))
@@ -1352,7 +1373,7 @@
     return pl.pallas_call(
         attend_back_body,
         grid=(heads,),
-        in_specs=[slab] * 4 + [column, slab, slab, thin, thin, line, line, table, table],
+        in_specs=[slab] * 4 + [column] + three_slabs(length, heads)[:2] + [thin, thin, line, line, table, table],
         out_specs=[slab, slab, slab, line, line, column, column],
         out_shape=[
             jax.ShapeDtypeStruct((length, width), jnp.bfloat16),
@@ -1367,7 +1388,7 @@
         cost_estimate=pl.CostEstimate(
             flops=10 * heads * length * length * HD, bytes_accessed=16 << 20, transcendentals=heads * length * length
         ),
-    )(queries, keys, values, grads, lse, q_raw, k_raw, q_rs, k_rs, q_gain[None], k_gain[None], cosine, sine)
+    )(queries, keys, values, grads, lse, raw, raw, q_rs, k_rs, q_gain[None], k_gain[None], cosine, sine)
 
 
 def local(
@@ -1398,7 +1419,7 @@
         )
         pack = jnp.pad(pack, (0, PACK_ROWS * 128 - pack.shape[0])).reshape(PACK_ROWS, 128)
         (
-            sequence, query_full, key_full, value_full, output_full, pack_all, cotangent_all, index_all
+            sequence, qkv_full, output_full, pack_all, cotangent_all, index_all
         ) = start_near(
             layer_input,
             [query_weight, key_weight, value_weight, output_weight],
@@ -1439,17 +1460,17 @@
             lax.all_gather(feed_gain, "col", axis=0, tiled=True),
             lax.all_gather(router_weight, "col", axis=0, tiled=True),
         )
+        qkv_full = jnp.concatenate([query_full, key_full, value_full], axis=1)
         sequence = lax.all_gather(layer_input, "row", axis=0, tiled=True)
     length = sequence.shape[0]
     model_width = sequence.shape[1]
-    local_width = query_full.shape[1]
+    local_width = qkv_full.shape[1] // 3
     seq_float = sequence.astype(jnp.float32)
     seq_scale = rms_scale(seq_float)
     attention_float = attention_full.astype(jnp.float32)
     normed = (seq_float * seq_scale * attention_float).astype(jnp.bfloat16)
-    query_raw = wide_dot(normed, query_full)
-    key_raw = wide_dot(normed, key_full)
-    values = wide_dot(normed, value_full).astype(jnp.bfloat16)
+    raw = wide_dot(normed, qkv_full)
+    query_raw, key_raw = raw[:, :local_width], raw[:, local_width : 2 * local_width]
     query_total, key_total = lax.psum(
         (jnp.sum(query_raw * query_raw, axis=-1), jnp.sum(key_raw * key_raw, axis=-1)), "row"
     )
@@ -1458,8 +1479,8 @@
     query_gain_f = query_scale_w.astype(jnp.float32)
     key_gain_f = key_scale_w.astype(jnp.float32)
     cosine, sine_table = rope_tables(length)
-    mixed_heads, queries, keys_rotated, lse_all = attend(
-        query_raw, key_raw, values, query_rs, key_rs, query_gain_f, key_gain_f, cosine, sine_table
+    mixed_heads, queries, keys_rotated, values, lse_all = attend(
+        raw, query_rs, key_rs, query_gain_f, key_gain_f, cosine, sine_table
     )
     if near:
         branch = branch_near(mixed_heads, output_full, 5)
@@ -1612,7 +1633,7 @@
     (
         grad_value_low, query_weighted, key_weighted, query_gain_term, key_gain_term, query_inner, key_inner
     ) = attend_back(
-        queries, keys_rotated, values, grad_mixed, lse_all, query_raw, key_raw, query_rs, key_rs,
+        queries, keys_rotated, values, grad_mixed, lse_all, raw, query_rs, key_rs,
         query_gain_f, key_gain_f, cosine, sine_table,
     )
     query_gain_term, key_gain_term = query_gain_term.reshape(-1), key_gain_term.reshape(-1)
@@ -1626,14 +1647,9 @@
     grad_key_raw = (
         key_rs * key_weighted - key_raw * key_rs**3 * (key_inner / model_width)[:, None]
     ).astype(jnp.bfloat16)
-    query_grad = inner_rows(normed, grad_query_raw)
-    key_grad = inner_rows(normed, grad_key_raw)
-    value_grad = inner_rows(normed, grad_value_low)
-    grad_normed = (
-        outer_cols(grad_query_raw, query_full)
-        + outer_cols(grad_key_raw, key_full)
-        + outer_cols(grad_value_low, value_full)
-    )
+    raw_grads = jnp.concatenate([grad_query_raw, grad_key_raw, grad_value_low], axis=1)
+    qkv_grad = inner_rows(normed, raw_grads)
+    grad_normed = outer_cols(raw_grads, qkv_full)
     attention_weighted = grad_normed * attention_float
     grad_seq_part = seq_scale * attention_weighted - seq_float * seq_scale**3 * jnp.mean(
         attention_weighted * seq_float, axis=-1, keepdims=True
@@ -1658,7 +1674,7 @@
         ) = finish_near(
             mixture_part,
             grad_seq_part.astype(jnp.bfloat16).reshape(rows_count, tokens, model_width),
-            [grad.astype(jnp.bfloat16) for grad in (query_grad, key_grad, value_grad, output_grad)],
+            [grad.astype(jnp.bfloat16) for grad in (qkv_grad, output_grad)],
             pack,
             4,
         )
@@ -1686,6 +1702,7 @@
         ).astype(jnp.float32)
         input_grad = grad_hidden + summed[:tokens]
         attention_gain_total = summed[tokens]
+        query_grad, key_grad, value_grad = jnp.split(qkv_grad, 3, axis=1)
         feed_gain_total, router_total = (
             lax.psum(feed_gain_term.astype(jnp.bfloat16), "row").astype(jnp.float32),
             lax.psum(router_grad.astype(jnp.bfloat16), "row").astype(jnp.float32),

time: 1270 us -> 1220 us (0.961)
  Pallas kernels: 1090 us -> 1050 us
    pallas_call x2, Pallas kernels: 267 us -> 232 us  [the longest x1 215 us: start_near(): pl.pallas_call(start_body, out_shape=(shaped((4, *x.shape), x), shaped((8...]
    dot_general x5 -> x3, matrix products: 25.5 us -> 21.1 us  [outer_cols(): lax.dot_general(left, right, (((1,), (1,)), ((), ())), preferred_element_...]
where the time goes in v8:
time: 1220 us; the launch traced here: 1210 us
  Pallas kernels  1050 us (86%)
  matrix products  54.5 us (4%)
  other arithmetic  46.7 us (4%)
  local copies, waits for them, and re-layouts  39.1 us (3%)
  blocking collectives  18.6 us (2%)
    pallas_call x1, Pallas kernels, finish_near(): pl.pallas_call(finish_body, out_shape=(jax.ShapeDtypeStruct((tokens, dept...  216 us
    pallas_call x1, Pallas kernels, start_near(): pl.pallas_call(start_body, out_shape=(shaped((4, *x.shape), x), shaped((8...  215 us
    pallas_call x1, Pallas kernels, feed_back(): pl.pallas_call(feed_back_body, grid=(groups, depth // CHUNK), in_specs=[A...  161 us
    pallas_call x1, Pallas kernels, grads_in(): pl.pallas_call(grads_in_body, grid=(steps,), in_specs=[pl.BlockSpec((rank...  161 us
    pallas_call x1, Pallas kernels, feed_in(): pl.pallas_call(functools.partial(feed_in_body, steps), grid=(steps + grou...  73.2 us
    pallas_call x1, Pallas kernels, restore(): pl.pallas_call(functools.partial(restore_body, flipped), grid=(steps,), i...  66.9 us
    pallas_call x1, Pallas kernels, restore_out(): pl.pallas_call(restore_out_body, grid=(steps,), in_specs=in_specs + [ANYW...  57.2 us
    pallas_call x1, Pallas kernels, branch_near(): pl.pallas_call(branch_body, in_specs=[inside] * 2, out_specs=inside, out_...  41.9 us

profile of v8, /device:TPU:0, one launch (start us, length us, event | category | flops | bytes accessed | tf_op | source)
XLA Modules:
  0.0 1214.1 jit_solution(861632597193325967)
XLA Ops:
  1.6 2.8 concatenate.16
  5.0 215.4 %shard_map.254 = (bf16[4,256,2048]{2,1,0:T(8,128)(2,1)}, bf16[2048,1536]{1,0:T(8,128)(2,1)}, bf16[512,2048]{1,0:T(8,128)(2,1)}, bf16[8,144,128]{2,1,0:T(8,128)(2...) custom-call(bf16[256,2048]{1,0:T(8,128)(2,1)} %x_ref.1, bf16[256,512]{1,0:T(8,128)(2,1)} %q_ref.1, ...), custom_call_target="tpu_custom_call" | custom-call | tf_op jit(solution)/shard_map/pallas_call | solution.py:461
  220.4 3.2 fusion.1
  225.8 3.2 copy-done.41
  229.0 6.7 fusion.53.q_raw.k_raw.v_ref
  238.6 9.2 all-reduce.3
  255.1 16.6 %shard_map.255 = (bf16[1024,512]{1,0:T(8,128)(2,1)}, bf16[1024,512]{1,0:T(8,128)(2,1)}, bf16[1024,512]{1,0:T(8,128)(2,1)}, bf16[1024,512]{1,0:T(8,128)(2,1)}, f32[4,1024,1]{2,1,0:T(8,128)}) custom-call(f32[1024,1536]{1,0:T(8,128)} %copy-done.4, f32[1024,1536]{1,0:T(8,128)} %copy-done.4, f32[1024,1536]{1,0:T(8,128)} %copy-done.4, f32[1024,1]{1,0:T(8,128)} %copy.68.q_rs, ...), custom_call_target="tpu_custom_call" | custom-call | flops 2147483648 | bytes 8388608 | tf_op jit(solution)/shard_map/pallas_call | solution.py:1323
  273.0 41.9 %shard_map.256 = f32[256,2048]{1,0:T(8,128)S(1)} custom-call(bf16[1024,512]{1,0:T(8,128)(2,1)S(1)} %copy-done.2, bf16[512,2048]{1,0:T(8,128)(2,1)S(1)} %copy-done.1), custom_call_target="tpu_custom_call" | custom-call | tf_op jit(solution)/shard_map/pallas_call | solution.py:1270
  319.9 3.7 fusion.pick_ref
  323.6 160.7 %shard_map.257 = (bf16[8,1280,2048]{2,1,0:T(8,128)(2,1)}, f32[8,1280,256]{2,1,0:T(8,128)}, bf16[4,2,2,2,256,2048]{5,4,3,2,1,0:T(8,128)(2,1)}, f32[32,8,256]{2,1,0:T(8,128)}) custom-call(bf16[32,320,256]{2,1,0:T(8,128)(2,1)} %fusion.pick_ref, bf16[32,256,2048]{2,1,0:T(8,128)(2,1)} %bitcast.113, bf16[8,256,2048]{2,1,0:T(8,128)(2,1)} %weight_ref.1, ...), custom_call_target="tpu_custom_call" | custom-call | tf_op jit(solution)/shard_map/pallas_call | solution.py:988
  487.8 3.1 reshape.270.probs_ref
  490.9 73.2 %shard_map.258 = (bf16[8,1280,2048]{2,1,0:T(8,128)(2,1)}, bf16[8,1280,256]{2,1,0:T(8,128)(2,1)}, bf16[8,1280,256]{2,1,0:T(8,128)(2,1)}, bf16[8,1280,256]{2,1,0:T...) custom-call(bf16[32,320,256]{2,1,0:T(8,128)(2,1)} %fusion.pick_ref, bf16[32,256,2048]{2,1,0:T(8,128)(2,1)} %bitcast.141, ...), custom_call_target="tpu_custom_call" | custom-call | flops 32212254720 | bytes 125829120 | tf_op jit(solution)/shard_map/pallas_call | solution.py:1062
  564.1 3.9 reduce.3
  568.3 2.9 select_reduce_fusion.small_ref
  571.2 5.2 fusion.52
  576.5 66.9 %shard_map.259 = bf16[32,256,2048]{2,1,0:T(8,128)(2,1)} custom-call(bf16[32,256,320]{2,1,0:T(8,128)(2,1)} %get-tuple-element.184.spread_ref, bf16[8,1280,256]{2,1,0:T(8,128)(2,1)} %get-tuple-element.70.refs_0_.gate_ref, bf16[8,1280,256]{2,1,0:T(8,128)(2,1)} %get-tuple-element.71.refs_1_.up_ref, bf16[8,2048,256]{2,1,0:T(8,128)(2,1)} %refs_2_.1, ...), custom_call_target="tpu_custom_call" | custom-call | tf_op jit(solution)/shard_map/pallas_call | solution.py:1134
  643.4 161.4 %shard_map.260 = (f32[256,2048]{1,0:T(8,128)}, f32[32,8,256]{2,1,0:T(8,128)}, bf16[8,2048,256]{2,1,0:T(8,128)(2,1)}, bf16[8,2048,256]{2,1,0:T(8,128)(2,1)}, bf16[8,256,2048]{2,1,0:T(8,128)(2,1)}) custom-call(bf16[4,2,2,2,256,2048]{5,4,3,2,1,0:T(8,128)(2,1)} %bitcast.112, f32[32,8,256]{2,1,0:T(8,128)} %select_reduce_fusion.small_ref, ...), custom_call_target="tpu_custom_call" | custom-call | tf_op jit(solution)/shard_map/pallas_call | solution.py:877
  804.8 3.4 copy-done
  808.1 22.0 %shard_map.264 = (f32[8,2048,256]{2,1,0:T(8,128)}, f32[8,2048,256]{2,1,0:T(8,128)}, f32[8,256,2048]{2,1,0:T(8,128)}) custom-call(bf16[8,2048,256]{2,1,0:T(8,128)(2,1)S(1)} %copy-done, bf16[8,2048,256]{2,1,0:T(8,128)(2,1)} %get-tuple-element.99.refs_1_, bf16[8,256,2048]{2,1,0:T(8,128)(2,1)} %get-tuple-element.100.refs_2_), custom_call_target="tpu_custom_call" | custom-call | tf_op jit(solution)/shard_map/pallas_call | solution.py:910
  838.4 4.5 select_convert_fusion.spread_ref
  842.8 57.2 %shard_map.261 = (bf16[32,256,2048]{2,1,0:T(8,128)(2,1)}, bf16[4,256,2048]{2,1,0:T(8,128)(2,1)}) custom-call(bf16[32,256,320]{2,1,0:T(8,128)(2,1)} %select_convert_fusion.spread_ref, bf16[8,1280,256]{2,1,0:T(8,128)(2,1)} %get-tuple-element.69.left_ref, bf16[8,256,2048]{2,1,0:T(8,128)(2,1)} %weight_ref.1, bf16[256,2048]{1,0:T(8,128)(2,1)} %get-tuple-element.156.own_ref), custom_call_target="tpu_custom_call" | custom-call | tf_op jit(solution)/shard_map/pallas_call | solution.py:1201
  900.0 6.2 convolution_convert_fusion.3.grad_ref
  906.3 21.9 %shard_map.262 = (bf16[1024,512]{1,0:T(8,128)(2,1)}, f32[1024,512]{1,0:T(8,128)}, f32[1024,512]{1,0:T(8,128)}, f32[1,512]{1,0:T(1,128)}, f32[1,512]{1,0:T(1,128)...) custom-call(bf16[1024,512]{1,0:T(8,128)(2,1)} %get-tuple-element.79.q_ref, bf16[1024,512]{1,0:T(8,128)(2,1)} %get-tuple-element.80.k_ref, ...), custom_call_target="tpu_custom_call" | custom-call | flops 5368709120 | bytes 16777216 | tf_op jit(solution)/shard_map/pallas_call | solution.py:1373
  931.9 9.4 all-reduce.2
  941.4 3.8 subtract_convert_fusion.1
  945.8 12.4 %fusion.9 = (bf16[2048]{0:T(1024)(128)(2,1)S(1)}, f32[1024]{0:T(1024)S(1)}, f32[1024,2048]{1,0:T(8,128)}) fusion(bf16[4,256,2048]{2,1,0:T(8,128)(2,1)S(1)} %copy-done.9, f32[1024]{0:T(1024)S(1)} %bitcast.134, f32[2048]{0:T(1024)S(1)} %bitcast.131, bf16[2048,1536]{1,0:T(8,128)(2,1)} %get-tuple-element.61, bf16[1024,512]{1,0:T(8,128)(2,1)S(1)} %copy-done.42, ...), kind=kOutput, calls=%fused_computation.19 | convolution fusion | flops 6466565120 | bytes 22040576 | tf_op jit(solution)/shard_map/dot_general | solution.py:34
  959.3 6.0 convolution_convert_fusion.1.o_ref
  965.4 9.4 convolution_convert_fusion.qkv_ref
  974.8 3.5 fusion.6
  978.3 216.2 %shard_map.263 = (f32[256,2048]{1,0:T(8,128)}, f32[256,2048]{1,0:T(8,128)}, f32[256,512]{1,0:T(8,128)}, f32[256,512]{1,0:T(8,128)}, f32[256,512]{1,0:T(8,128)}, ...) custom-call(bf16[4,2,2,2,256,2048]{5,4,3,2,1,0:T(8,128)(2,1)} %bitcast.114, bf16[4,256,2048]{2,1,0:T(8,128)(2,1)} %bitcast.115, ...), custom_call_target="tpu_custom_call" | custom-call | tf_op jit(solution)/shard_map/pallas_call | solution.py:630
  1194.5 4.0 add.107
  1203.6 3.2 add.106
  (170 shorter events, 49.2 us)
Async XLA Ops:
  220.4 4.4 copy-start.8
  224.7 4.3 copy-start.41
  225.8 9.9 copy-start.14
  248.4 6.7 copy-start.32
  248.4 6.7 copy-start.34
  255.1 16.7 %copy-start.1 = (bf16[512,2048]{1,0:T(8,128)(2,1)S(1)}, bf16[512,2048]{1,0:T(8,128)(2,1)}, u32[]{:S(2)}) copy-start(bf16[512,2048]{1,0:T(8,128)(2,1)} %get-tuple-element.63.weight_ref) | copy-start | bytes 6291460
  255.1 59.8 %copy-start.16 = (bf16[256,2048]{1,0:T(8,128)(2,1)S(1)}, bf16[256,2048]{1,0:T(8,128)(2,1)}, u32[]{:S(2)}) copy-start(bf16[256,2048]{1,0:T(8,128)(2,1)} %x_ref.1) | copy-start | bytes 3145732
  316.9 6.8 copy-start.11
  564.1 7.1 copy-start.44
  808.1 22.0 %copy-start.27 = (f32[32,8,256]{2,1,0:T(8,128)S(1)}, f32[32,8,256]{2,1,0:T(8,128)}, u32[]{:S(2)}) copy-start(f32[32,8,256]{2,1,0:T(8,128)} %get-tuple-element.77) | copy-start | bytes 786436
  808.1 22.1 %copy-start.12 = (bf16[256,2048]{1,0:T(8,128)(2,1)S(1)}, bf16[256,2048]{1,0:T(8,128)(2,1)}, u32[]{:S(2)}) copy-start(bf16[256,2048]{1,0:T(8,128)(2,1)} %copy-done.11) | copy-start | bytes 3145732
  928.1 13.2 %copy-start.21 = (f32[1024,512]{1,0:T(8,128)S(1)}, f32[1024,512]{1,0:T(8,128)}, u32[]{:S(2)}) copy-start(f32[1024,512]{1,0:T(8,128)} %get-tuple-element.84) | copy-start | bytes 6291460
  928.1 13.2 %copy-start.33 = (f32[1024]{0:T(1024)S(1)}, f32[1024]{0:T(1024)}, u32[]{:S(2)}) copy-start(f32[1024]{0:T(1024)} %copy-done.32) | copy-start | bytes 12292
  928.1 13.2 %copy-start.35 = (f32[1024]{0:T(1024)S(1)}, f32[1024]{0:T(1024)}, u32[]{:S(2)}) copy-start(f32[1024]{0:T(1024)} %copy-done.34) | copy-start | bytes 12292
  928.1 13.2 %copy-start.37 = (f32[1024]{0:T(1024)S(1)}, f32[1024]{0:T(1024)}, u32[]{:S(2)}) copy-start(f32[1024]{0:T(1024)} %get-tuple-element.174) | copy-start | bytes 12292
  928.2 13.2 %copy-start.38 = (f32[1024]{0:T(1024)S(1)}, f32[1024]{0:T(1024)}, u32[]{:S(2)}) copy-start(f32[1024]{0:T(1024)} %get-tuple-element.189) | copy-start | bytes 12292
  941.4 4.1 copy-start.9
  941.4 4.1 copy-start.29
  941.4 4.4 copy-start.42
  945.2 12.9 %copy-start.22 = (bf16[1024,512]{1,0:T(8,128)(2,1)}, bf16[1024,512]{1,0:T(8,128)(2,1)S(1)}, u32[]{:S(2)}) copy-start(bf16[1024,512]{1,0:T(8,128)(2,1)S(1)} %get-tuple-element.163) | copy-start | bytes 3145732
  945.8 12.4 %copy-start.40 = (f32[1,512]{1,0:T(1,128)S(1)}, f32[1,512]{1,0:T(1,128)}, u32[]{:S(2)}) copy-start(f32[1,512]{1,0:T(1,128)} %get-tuple-element.89) | copy-start | bytes 6148
  945.8 12.5 %copy-start.39 = (f32[1,512]{1,0:T(1,128)S(1)}, f32[1,512]{1,0:T(1,128)}, u32[]{:S(2)}) copy-start(f32[1,512]{1,0:T(1,128)} %get-tuple-element.90) | copy-start | bytes 6148
  945.8 13.5 %copy-start.3 = (bf16[1024,512]{1,0:T(8,128)(2,1)S(1)}, bf16[1024,512]{1,0:T(8,128)(2,1)}, u32[]{:S(2)}) copy-start(bf16[1024,512]{1,0:T(8,128)(2,1)} %get-tuple-element.62.mixed_ref) | copy-start | bytes 3145732
  959.3 6.1 copy-start.15
  959.3 6.1 copy-start.23
  959.3 6.1 copy-start.43
  959.3 15.4 %slice-start = ((s8[8388608]{0:T(1024)(128)(4,1)}), s8[4194304]{0:T(1024)(128)(4,1)S(1)}, s32[]{:S(2)}) async-start(s8[8388608]{0:T(1024)(128)(4,1)} %bitcast.116), calls=%async_computation | async-start | bytes 8388608
  965.4 9.4 copy-start.10
  965.4 9.4 slice-start.1
  1194.5 9.1 copy-start.7
  1206.8 5.3 copy-start.25
  1206.8 6.1 copy-start.24
  (15 other events, 37.3 us)

commit v9 on v8

--- a/solution.py
+++ b/solution.py
@@ -291,7 +291,7 @@
 
                 pass_on(4 - d)
 
-    def forward(q):
+    def forward(q, between=None):
         @pl.when(q == 0)
         def _():
             along_z(q)
@@ -299,6 +299,9 @@
         @pl.when(q + 1 < GSTEPS)
         def _():
             along_z(q + 1)
+
+        if between is not None:
+            between()
 
         for k in (0, *arrived):
             src = place(k, 1, 0, q)
@@ -428,12 +431,14 @@
         item.start()
     x_second.wait_recv()
     x_relay.start()
-    for q, group in enumerate(((4, 0), (1,), (2, 3), ())):
-        forward(q)
+    def weights_out(group):
         for index in group:
             for k in QUEUE:
                 w_copy(index, k).start()
             pair_copy(index, 0).start()
+
+    for q, group in enumerate(((4, 0), (1, 2), (3,), ())):
+        forward(q, functools.partial(weights_out, group))
 
     for index in (4, 0, 1, 2, 3):
         for k in ARRIVE:
@@ -531,10 +536,34 @@
             block(index, zz * 2 + other), pairs[index].at[zz], p_send.at[index, zz], p_recv.at[index, zz], pair
         )
 
-    def w_z(index, k):
+    above, below = (r, ((z + 1) % 4) * 2 + core), (r, ((z + 3) % 4) * 2 + core)
+
+    def up_copy(index, dest):
         return send(
-            kept[index].at[(z + k) % 4], zs[index].at[k - 1], z_send.at[index, k - 1], z_recv.at[index, k - 1], up[k - 1]
-        )
+            kept[index].at[dest], zs[index].at[dest], z_send.at[index, dest], z_recv.at[index, dest], above
+        )
+
+    def down_copy(index, dest, slot):
+        return send(kept[index].at[dest], zs[index].at[slot], z_send.at[index, dest], z_recv.at[index, slot], below)
+
+    def chain(stage):
+        @pl.when(z == stage)
+        def _():
+            for index in range(2):
+                for dest in range(3, stage, -1):
+                    if stage > 0:
+                        up_copy(index, dest).wait_recv()
+                        add(kept[index].at[dest], [zs[index].at[dest]])
+                    up_copy(index, dest).start()
+
+        @pl.when(z == 3 - stage)
+        def _():
+            for index in range(2):
+                for dest in range(3 - stage):
+                    if stage > 0:
+                        down_copy(index, dest, dest).wait_recv()
+                        add(kept[index].at[dest], [zs[index].at[dest]])
+                    down_copy(index, dest, 4 if dest == 2 - stage else dest).start()
 
     def add(ref, extras):
         @pl.loop(0, ref.shape[0] // TILE)
@@ -566,18 +595,26 @@
     load(first, second).start()
     small_begin()
     for index in range(2):
-        for k in QUEUE:
+        for k in (2, 1, 3, 0):
             zz = (z + k) % 4
             w_load_copy(index, zz).wait()
             w_give(index, zz).wait_recv()
             add(kept[index].at[zz], [pairs[index].at[zz]])
-            w_z(index, k).start()
+    chain(0)
 
     @pl.loop(0, RSTEPS + LAGS[2])
     def _(i):
         tick(i)
 
         @pl.when(i == 2)
+        def _():
+            chain(1)
+
+        @pl.when(i == 4)
+        def _():
+            chain(2)
+
+        @pl.when(i == 1)
         def _():
             load(first, 1 - second).wait()
             f_copy(1 - second).wait_recv()
@@ -585,13 +622,22 @@
             g_copy.start()
 
     for index in range(2):
-        w_load_copy(index, z).wait()
-        w_give(index, z).wait_recv()
-        for k in ARRIVE:
-            w_z(index, k).wait_recv()
-        add_out(
-            kept[index].at[z], [pairs[index].at[z]] + [zs[index].at[k] for k in range(3)], sums[index]
-        )
+        @pl.when(z == 0)
+        def _():
+            down_copy(index, 0, 4).wait_recv()
+            add_out(kept[index].at[z], [zs[index].at[4]], sums[index])
+
+        @pl.when(z == 3)
+        def _():
+            up_copy(index, 3).wait_recv()
+            add_out(kept[index].at[z], [zs[index].at[3]], sums[index])
+
+        @pl.when((z > 0) & (z < 3))
+        def _():
+            up_copy(index, z).wait_recv()
+            down_copy(index, z, 4).wait_recv()
+            add_out(kept[index].at[z], [zs[index].at[z], zs[index].at[4]], sums[index])
+
         for result in results[index]:
             result.start()
     load(first, second).wait()
@@ -613,7 +659,7 @@
         for k in range(4):
             w_give(index, (z + k) % 4).wait_send()
             if k:
-                w_z(index, k).wait_send()
+                up_copy(index, (z + k) % 4).wait_send()
         for result in results[index]:
             result.wait()
     small_finish()
@@ -640,10 +686,10 @@
         scratch_shapes=[
             half(2, 2, tokens, depth), half(2, tokens, depth), half(tokens, depth),
             pltpu.VMEM((tokens, depth), jnp.float32),
-            *[half(4, *b) for b in blocks], *[half(4, *b) for b in blocks], *[half(3, *b) for b in blocks],
+            *[half(4, *b) for b in blocks], *[half(4, *b) for b in blocks], *[half(5, *b) for b in blocks],
             *[pltpu.VMEM(b, jnp.float32) for b in blocks],
             dma((2, 2)), dma((2,)), dma((2,)), dma(()), dma(()),
-            dma((2, 4)), dma((2, 4)), dma((2, 4)), dma((2, 3)), dma((2, 3)), dma((6,)),
+            dma((2, 4)), dma((2, 4)), dma((2, 4)), dma((2, 4)), dma((2, 5)), dma((6,)),
         ]
         + small_sems()
         + shrink_scratch(tokens, depth),

time: 1220 us -> 1200 us (0.984)
  Pallas kernels: 1050 us -> 1030 us
    pallas_call x1, Pallas kernels: 215 us -> 202 us  [start_near(): pl.pallas_call(start_body, out_shape=(shaped((4, *x.shape), x), shaped((8...]
where the time goes in v9:
time: 1200 us; the launch traced here: 1190 us
  Pallas kernels  1030 us (86%)
  matrix products  54.5 us (5%)
  other arithmetic  46.7 us (4%)
  local copies, waits for them, and re-layouts  39.1 us (3%)
  blocking collectives  18.5 us (2%)
    pallas_call x1, Pallas kernels, finish_near(): pl.pallas_call(finish_body, out_shape=(jax.ShapeDtypeStruct((tokens, dept...  206 us
    pallas_call x1, Pallas kernels, start_near(): pl.pallas_call(start_body, out_shape=(shaped((4, *x.shape), x), shaped((8...  202 us
    pallas_call x1, Pallas kernels, grads_in(): pl.pallas_call(grads_in_body, grid=(steps,), in_specs=[pl.BlockSpec((rank...  163 us
    pallas_call x1, Pallas kernels, feed_back(): pl.pallas_call(feed_back_body, grid=(groups, depth // CHUNK), in_specs=[A...  160 us
    pallas_call x1, Pallas kernels, feed_in(): pl.pallas_call(functools.partial(feed_in_body, steps), grid=(steps + grou...  73.2 us
    pallas_call x1, Pallas kernels, restore(): pl.pallas_call(functools.partial(restore_body, flipped), grid=(steps,), i...  66.9 us
    pallas_call x1, Pallas kernels, restore_out(): pl.pallas_call(restore_out_body, grid=(steps,), in_specs=in_specs + [ANYW...  57.6 us
    pallas_call x1, Pallas kernels, branch_near(): pl.pallas_call(branch_body, in_specs=[inside] * 2, out_specs=inside, out_...  38.2 us

profile of v9, /device:TPU:0, one launch (start us, length us, event | category | flops | bytes accessed | tf_op | source)
XLA Modules:
  0.0 1188.8 jit_solution(6754400457697146256)
XLA Ops:
  1.6 2.8 concatenate.16
  5.0 202.5 %shard_map.254 = (bf16[4,256,2048]{2,1,0:T(8,128)(2,1)}, bf16[2048,1536]{1,0:T(8,128)(2,1)}, bf16[512,2048]{1,0:T(8,128)(2,1)}, bf16[8,144,128]{2,1,0:T(8,128)(2...) custom-call(bf16[256,2048]{1,0:T(8,128)(2,1)} %x_ref.1, bf16[256,512]{1,0:T(8,128)(2,1)} %q_ref.1, ...), custom_call_target="tpu_custom_call" | custom-call | tf_op jit(solution)/shard_map/pallas_call | solution.py:466
  207.5 3.2 fusion.1
  212.9 3.2 copy-done.41
  216.2 6.7 fusion.53.q_raw.k_raw.v_ref
  225.7 9.4 all-reduce.3
  242.5 16.6 %shard_map.255 = (bf16[1024,512]{1,0:T(8,128)(2,1)}, bf16[1024,512]{1,0:T(8,128)(2,1)}, bf16[1024,512]{1,0:T(8,128)(2,1)}, bf16[1024,512]{1,0:T(8,128)(2,1)}, f32[4,1024,1]{2,1,0:T(8,128)}) custom-call(f32[1024,1536]{1,0:T(8,128)} %copy-done.4, f32[1024,1536]{1,0:T(8,128)} %copy-done.4, f32[1024,1536]{1,0:T(8,128)} %copy-done.4, f32[1024,1]{1,0:T(8,128)} %copy.68.q_rs, ...), custom_call_target="tpu_custom_call" | custom-call | flops 2147483648 | bytes 8388608 | tf_op jit(solution)/shard_map/pallas_call | solution.py:1369
  260.3 38.2 %shard_map.256 = f32[256,2048]{1,0:T(8,128)S(1)} custom-call(bf16[1024,512]{1,0:T(8,128)(2,1)S(1)} %copy-done.2, bf16[512,2048]{1,0:T(8,128)(2,1)S(1)} %copy-done.1), custom_call_target="tpu_custom_call" | custom-call | tf_op jit(solution)/shard_map/pallas_call | solution.py:1316
  303.5 3.7 fusion.pick_ref
  307.2 162.5 %shard_map.257 = (bf16[8,1280,2048]{2,1,0:T(8,128)(2,1)}, f32[8,1280,256]{2,1,0:T(8,128)}, bf16[4,2,2,2,256,2048]{5,4,3,2,1,0:T(8,128)(2,1)}, f32[32,8,256]{2,1,0:T(8,128)}) custom-call(bf16[32,320,256]{2,1,0:T(8,128)(2,1)} %fusion.pick_ref, bf16[32,256,2048]{2,1,0:T(8,128)(2,1)} %bitcast.113, bf16[8,256,2048]{2,1,0:T(8,128)(2,1)} %weight_ref.1, ...), custom_call_target="tpu_custom_call" | custom-call | tf_op jit(solution)/shard_map/pallas_call | solution.py:1034
  473.2 3.1 reshape.270.probs_ref
  476.3 73.2 %shard_map.258 = (bf16[8,1280,2048]{2,1,0:T(8,128)(2,1)}, bf16[8,1280,256]{2,1,0:T(8,128)(2,1)}, bf16[8,1280,256]{2,1,0:T(8,128)(2,1)}, bf16[8,1280,256]{2,1,0:T...) custom-call(bf16[32,320,256]{2,1,0:T(8,128)(2,1)} %fusion.pick_ref, bf16[32,256,2048]{2,1,0:T(8,128)(2,1)} %bitcast.141, ...), custom_call_target="tpu_custom_call" | custom-call | flops 32212254720 | bytes 125829120 | tf_op jit(solution)/shard_map/pallas_call | solution.py:1108
  549.5 3.9 reduce.3
  553.7 2.9 select_reduce_fusion.small_ref
  556.6 5.2 fusion.52
  561.9 66.9 %shard_map.259 = bf16[32,256,2048]{2,1,0:T(8,128)(2,1)} custom-call(bf16[32,256,320]{2,1,0:T(8,128)(2,1)} %get-tuple-element.184.spread_ref, bf16[8,1280,256]{2,1,0:T(8,128)(2,1)} %get-tuple-element.70.refs_0_.gate_ref, bf16[8,1280,256]{2,1,0:T(8,128)(2,1)} %get-tuple-element.71.refs_1_.up_ref, bf16[8,2048,256]{2,1,0:T(8,128)(2,1)} %refs_2_.1, ...), custom_call_target="tpu_custom_call" | custom-call | tf_op jit(solution)/shard_map/pallas_call | solution.py:1180
  628.8 160.5 %shard_map.260 = (f32[256,2048]{1,0:T(8,128)}, f32[32,8,256]{2,1,0:T(8,128)}, bf16[8,2048,256]{2,1,0:T(8,128)(2,1)}, bf16[8,2048,256]{2,1,0:T(8,128)(2,1)}, bf16[8,256,2048]{2,1,0:T(8,128)(2,1)}) custom-call(bf16[4,2,2,2,256,2048]{5,4,3,2,1,0:T(8,128)(2,1)} %bitcast.112, f32[32,8,256]{2,1,0:T(8,128)} %select_reduce_fusion.small_ref, ...), custom_call_target="tpu_custom_call" | custom-call | tf_op jit(solution)/shard_map/pallas_call | solution.py:923
  789.3 3.4 copy-done
  792.7 22.0 %shard_map.264 = (f32[8,2048,256]{2,1,0:T(8,128)}, f32[8,2048,256]{2,1,0:T(8,128)}, f32[8,256,2048]{2,1,0:T(8,128)}) custom-call(bf16[8,2048,256]{2,1,0:T(8,128)(2,1)S(1)} %copy-done, bf16[8,2048,256]{2,1,0:T(8,128)(2,1)} %get-tuple-element.99.refs_1_, bf16[8,256,2048]{2,1,0:T(8,128)(2,1)} %get-tuple-element.100.refs_2_), custom_call_target="tpu_custom_call" | custom-call | tf_op jit(solution)/shard_map/pallas_call | solution.py:956
  822.9 4.5 select_convert_fusion.spread_ref
  827.4 57.6 %shard_map.261 = (bf16[32,256,2048]{2,1,0:T(8,128)(2,1)}, bf16[4,256,2048]{2,1,0:T(8,128)(2,1)}) custom-call(bf16[32,256,320]{2,1,0:T(8,128)(2,1)} %select_convert_fusion.spread_ref, bf16[8,1280,256]{2,1,0:T(8,128)(2,1)} %get-tuple-element.69.left_ref, bf16[8,256,2048]{2,1,0:T(8,128)(2,1)} %weight_ref.1, bf16[256,2048]{1,0:T(8,128)(2,1)} %get-tuple-element.156.own_ref), custom_call_target="tpu_custom_call" | custom-call | tf_op jit(solution)/shard_map/pallas_call | solution.py:1247
  885.0 6.2 convolution_convert_fusion.3.grad_ref
  891.2 21.9 %shard_map.262 = (bf16[1024,512]{1,0:T(8,128)(2,1)}, f32[1024,512]{1,0:T(8,128)}, f32[1024,512]{1,0:T(8,128)}, f32[1,512]{1,0:T(1,128)}, f32[1,512]{1,0:T(1,128)...) custom-call(bf16[1024,512]{1,0:T(8,128)(2,1)} %get-tuple-element.79.q_ref, bf16[1024,512]{1,0:T(8,128)(2,1)} %get-tuple-element.80.k_ref, ...), custom_call_target="tpu_custom_call" | custom-call | flops 5368709120 | bytes 16777216 | tf_op jit(solution)/shard_map/pallas_call | solution.py:1419
  916.9 9.1 all-reduce.2
  926.1 3.8 subtract_convert_fusion.1
  930.5 12.4 %fusion.9 = (bf16[2048]{0:T(1024)(128)(2,1)S(1)}, f32[1024]{0:T(1024)S(1)}, f32[1024,2048]{1,0:T(8,128)}) fusion(bf16[4,256,2048]{2,1,0:T(8,128)(2,1)S(1)} %copy-done.9, f32[1024]{0:T(1024)S(1)} %bitcast.134, f32[2048]{0:T(1024)S(1)} %bitcast.131, bf16[2048,1536]{1,0:T(8,128)(2,1)} %get-tuple-element.61, bf16[1024,512]{1,0:T(8,128)(2,1)S(1)} %copy-done.42, ...), kind=kOutput, calls=%fused_computation.19 | convolution fusion | flops 6466565120 | bytes 22040576 | tf_op jit(solution)/shard_map/dot_general | solution.py:34
  944.0 6.0 convolution_convert_fusion.1.o_ref
  950.0 9.4 convolution_convert_fusion.qkv_ref
  959.4 3.5 fusion.6
  963.0 206.2 %shard_map.263 = (f32[256,2048]{1,0:T(8,128)}, f32[256,2048]{1,0:T(8,128)}, f32[256,512]{1,0:T(8,128)}, f32[256,512]{1,0:T(8,128)}, f32[256,512]{1,0:T(8,128)}, ...) custom-call(bf16[4,2,2,2,256,2048]{5,4,3,2,1,0:T(8,128)(2,1)} %bitcast.114, bf16[4,256,2048]{2,1,0:T(8,128)(2,1)} %bitcast.115, ...), custom_call_target="tpu_custom_call" | custom-call | tf_op jit(solution)/shard_map/pallas_call | solution.py:676
  1169.2 4.0 add.107
  1178.3 3.2 add.106
  (170 shorter events, 49.2 us)
Async XLA Ops:
  207.5 4.4 copy-start.8
  211.9 4.3 copy-start.41
  212.9 9.9 copy-start.14
  235.7 6.7 copy-start.32
  235.7 6.7 copy-start.34
  242.4 16.7 %copy-start.1 = (bf16[512,2048]{1,0:T(8,128)(2,1)S(1)}, bf16[512,2048]{1,0:T(8,128)(2,1)}, u32[]{:S(2)}) copy-start(bf16[512,2048]{1,0:T(8,128)(2,1)} %get-tuple-element.63.weight_ref) | copy-start | bytes 6291460
  242.4 56.1 %copy-start.16 = (bf16[256,2048]{1,0:T(8,128)(2,1)S(1)}, bf16[256,2048]{1,0:T(8,128)(2,1)}, u32[]{:S(2)}) copy-start(bf16[256,2048]{1,0:T(8,128)(2,1)} %x_ref.1) | copy-start | bytes 3145732
  300.5 6.8 copy-start.11
  549.5 7.1 copy-start.44
  792.7 22.0 %copy-start.27 = (f32[32,8,256]{2,1,0:T(8,128)S(1)}, f32[32,8,256]{2,1,0:T(8,128)}, u32[]{:S(2)}) copy-start(f32[32,8,256]{2,1,0:T(8,128)} %get-tuple-element.77) | copy-start | bytes 786436
  792.7 22.1 %copy-start.12 = (bf16[256,2048]{1,0:T(8,128)(2,1)S(1)}, bf16[256,2048]{1,0:T(8,128)(2,1)}, u32[]{:S(2)}) copy-start(bf16[256,2048]{1,0:T(8,128)(2,1)} %copy-done.11) | copy-start | bytes 3145732
  913.1 13.0 %copy-start.21 = (f32[1024,512]{1,0:T(8,128)S(1)}, f32[1024,512]{1,0:T(8,128)}, u32[]{:S(2)}) copy-start(f32[1024,512]{1,0:T(8,128)} %get-tuple-element.84) | copy-start | bytes 6291460
  913.1 13.0 %copy-start.33 = (f32[1024]{0:T(1024)S(1)}, f32[1024]{0:T(1024)}, u32[]{:S(2)}) copy-start(f32[1024]{0:T(1024)} %copy-done.32) | copy-start | bytes 12292
  913.1 13.0 %copy-start.35 = (f32[1024]{0:T(1024)S(1)}, f32[1024]{0:T(1024)}, u32[]{:S(2)}) copy-start(f32[1024]{0:T(1024)} %copy-done.34) | copy-start | bytes 12292
  913.1 13.0 %copy-start.37 = (f32[1024]{0:T(1024)S(1)}, f32[1024]{0:T(1024)}, u32[]{:S(2)}) copy-start(f32[1024]{0:T(1024)} %get-tuple-element.174) | copy-start | bytes 12292
  913.1 13.0 %copy-start.38 = (f32[1024]{0:T(1024)S(1)}, f32[1024]{0:T(1024)}, u32[]{:S(2)}) copy-start(f32[1024]{0:T(1024)} %get-tuple-element.189) | copy-start | bytes 12292
  926.1 4.1 copy-start.9
  926.1 4.1 copy-start.29
  926.1 4.4 copy-start.42
  929.9 12.9 %copy-start.22 = (bf16[1024,512]{1,0:T(8,128)(2,1)}, bf16[1024,512]{1,0:T(8,128)(2,1)S(1)}, u32[]{:S(2)}) copy-start(bf16[1024,512]{1,0:T(8,128)(2,1)S(1)} %get-tuple-element.163) | copy-start | bytes 3145732
  930.5 12.4 %copy-start.40 = (f32[1,512]{1,0:T(1,128)S(1)}, f32[1,512]{1,0:T(1,128)}, u32[]{:S(2)}) copy-start(f32[1,512]{1,0:T(1,128)} %get-tuple-element.89) | copy-start | bytes 6148
  930.5 12.5 %copy-start.39 = (f32[1,512]{1,0:T(1,128)S(1)}, f32[1,512]{1,0:T(1,128)}, u32[]{:S(2)}) copy-start(f32[1,512]{1,0:T(1,128)} %get-tuple-element.90) | copy-start | bytes 6148
  930.5 13.5 %copy-start.3 = (bf16[1024,512]{1,0:T(8,128)(2,1)S(1)}, bf16[1024,512]{1,0:T(8,128)(2,1)}, u32[]{:S(2)}) copy-start(bf16[1024,512]{1,0:T(8,128)(2,1)} %get-tuple-element.62.mixed_ref) | copy-start | bytes 3145732
  944.0 6.1 copy-start.15
  944.0 6.1 copy-start.23
  944.0 6.1 copy-start.43
  944.0 15.4 %slice-start = ((s8[8388608]{0:T(1024)(128)(4,1)}), s8[4194304]{0:T(1024)(128)(4,1)S(1)}, s32[]{:S(2)}) async-start(s8[8388608]{0:T(1024)(128)(4,1)} %bitcast.116), calls=%async_computation | async-start | bytes 8388608
  950.0 9.4 copy-start.10
  950.0 9.4 slice-start.1
  1169.2 9.1 copy-start.7
  1181.5 5.3 copy-start.25
  1181.5 6.1 copy-start.24
  (15 other events, 37.3 us)

commit v10 on v9

--- a/solution.py
+++ b/solution.py
@@ -187,7 +187,7 @@
     )
 
 
-GSTEPS = 4
+GSTEPS = 8
 QUEUE = (2, 1, 3)
 ARRIVE = (1, 3, 2)
 
@@ -437,8 +437,16 @@
                 w_copy(index, k).start()
             pair_copy(index, 0).start()
 
-    for q, group in enumerate(((4, 0), (1, 2), (3,), ())):
-        forward(q, functools.partial(weights_out, group))
+    @pl.loop(0, GSTEPS)
+    def _(q):
+        def between():
+            for at, group in enumerate(((4,), (0,), (1,), (2,), (3,))):
+
+                @pl.when(q == at)
+                def _(group=group):
+                    weights_out(group)
+
+        forward(q, between)
 
     for index in (4, 0, 1, 2, 3):
         for k in ARRIVE:
@@ -606,15 +614,15 @@
     def _(i):
         tick(i)
 
-        @pl.when(i == 2)
+        @pl.when(i == 4)
         def _():
             chain(1)
 
-        @pl.when(i == 4)
+        @pl.when(i == 8)
         def _():
             chain(2)
 
-        @pl.when(i == 1)
+        @pl.when(i == 2)
         def _():
             load(first, 1 - second).wait()
             f_copy(1 - second).wait_recv()
@@ -699,9 +707,9 @@
     )(part.reshape(4, 2, 2, 2, tokens, depth), field, *grads, pack)
 
 
-RSTEPS = 8
+RSTEPS = 16
 TILE = 16
-LAGS = (0, 1, 2, 4)
+LAGS = (0, 1, 3, 6)
 TICKS = RSTEPS + LAGS[3]
 
 
@@ -896,9 +904,11 @@
     up_out[0] = inner_rows(rows, up_ref[0]).astype(jnp.bfloat16)
     down_out[0] = inner_rows(act_ref[0], grads_ref[0]).astype(jnp.bfloat16)
 
-    @pl.when(k == 0)
-    def _():
-        tick(e)
+    for half in range(2):
+
+        @pl.when(k == half * (pl.num_programs(1) // 2))
+        def _():
+            tick(2 * e + half)
 
     @pl.when(step == last)
     def _():
@@ -916,7 +926,7 @@
 def feed_back(part, small, rows, grad_gate, grad_up, act, grads, collective_id):
     tokens, depth = part.shape[0] // RANKS, part.shape[1]
     groups, length, inner = grad_gate.shape
-    assert groups == RSTEPS
+    assert 2 * groups == RSTEPS
     dma = pltpu.SemaphoreType.DMA
     slab = pl.BlockSpec((1, length, CHUNK), lambda e, k: (e, 0, k))
     held = pl.BlockSpec((1, length, inner), lambda e, k: (e, 0, 0))
@@ -1015,9 +1025,7 @@
     fill_rows(pick_ref, field_ref, rows_ref)
     add_products(k, rows_ref, [(lambda rows, e: outer_cols(rows, down_ref[e]), total)])
 
-    @pl.when(k % 2 == 1)
-    def _():
-        forward(k // 2)
+    forward(k)
 
     @pl.when(k == last)
     def _():
@@ -1031,6 +1039,7 @@
     groups, depth = width // SLOTS, field.shape[-1]
     length, inner = ranks * SLOTS, down.shape[1]
     steps = depth // CHUNK
+    assert steps == GSTEPS
     rows, plain, whole, small_all = pl.pallas_call(
         grads_in_body,
         grid=(steps,),

time: 1200 us -> 1250 us (1.042)
  Pallas kernels: 1030 us -> 1080 us
    pallas_call x1, Pallas kernels: 202 us -> 234 us  [start_near(): pl.pallas_call(start_body, out_shape=(shaped((4, *x.shape), x), shaped((8...]
    pallas_call x1, Pallas kernels: 206 us -> 225 us  [finish_near(): pl.pallas_call(finish_body, out_shape=(jax.ShapeDtypeStruct((tokens, dept...]
where the time goes in v10:
time: 1250 us; the launch traced here: 1240 us
  Pallas kernels  1080 us (86%)
  matrix products  54.5 us (4%)
  other arithmetic  46.7 us (4%)
  local copies, waits for them, and re-layouts  39.1 us (3%)
  blocking collectives  18.7 us (1%)
    pallas_call x1, Pallas kernels, start_near(): pl.pallas_call(start_body, out_shape=(shaped((4, *x.shape), x), shaped((8...  234 us
    pallas_call x1, Pallas kernels, finish_near(): pl.pallas_call(finish_body, out_shape=(jax.ShapeDtypeStruct((tokens, dept...  225 us
    pallas_call x1, Pallas kernels, grads_in(): pl.pallas_call(grads_in_body, grid=(steps,), in_specs=[pl.BlockSpec((rank...  163 us
    pallas_call x1, Pallas kernels, feed_back(): pl.pallas_call(feed_back_body, grid=(groups, depth // CHUNK), in_specs=[A...  163 us
    pallas_call x1, Pallas kernels, feed_in(): pl.pallas_call(functools.partial(feed_in_body, steps), grid=(steps + grou...  73.2 us
    pallas_call x1, Pallas kernels, restore(): pl.pallas_call(functools.partial(restore_body, flipped), grid=(steps,), i...  66.9 us
    pallas_call x1, Pallas kernels, restore_out(): pl.pallas_call(restore_out_body, grid=(steps,), in_specs=in_specs + [ANYW...  56.6 us
    pallas_call x1, Pallas kernels, branch_near(): pl.pallas_call(branch_body, in_specs=[inside] * 2, out_specs=inside, out_...  38.9 us

profile of v10, /device:TPU:0, one launch (start us, length us, event | category | flops | bytes accessed | tf_op | source)
XLA Modules:
  0.0 1242.2 jit_solution(3276432988739561824)
XLA Ops:
  1.6 2.8 concatenate.16
  5.0 234.0 %shard_map.254 = (bf16[4,256,2048]{2,1,0:T(8,128)(2,1)}, bf16[2048,1536]{1,0:T(8,128)(2,1)}, bf16[512,2048]{1,0:T(8,128)(2,1)}, bf16[8,144,128]{2,1,0:T(8,128)(2...) custom-call(bf16[256,2048]{1,0:T(8,128)(2,1)} %x_ref.1, bf16[256,512]{1,0:T(8,128)(2,1)} %q_ref.1, ...), custom_call_target="tpu_custom_call" | custom-call | tf_op jit(solution)/shard_map/pallas_call | solution.py:474
  239.0 3.2 fusion.1
  244.4 3.2 copy-done.41
  247.7 6.7 fusion.53.q_raw.k_raw.v_ref
  257.2 9.6 all-reduce.3
  274.2 16.6 %shard_map.255 = (bf16[1024,512]{1,0:T(8,128)(2,1)}, bf16[1024,512]{1,0:T(8,128)(2,1)}, bf16[1024,512]{1,0:T(8,128)(2,1)}, bf16[1024,512]{1,0:T(8,128)(2,1)}, f32[4,1024,1]{2,1,0:T(8,128)}) custom-call(f32[1024,1536]{1,0:T(8,128)} %copy-done.4, f32[1024,1536]{1,0:T(8,128)} %copy-done.4, f32[1024,1536]{1,0:T(8,128)} %copy-done.4, f32[1024,1]{1,0:T(8,128)} %copy.68.q_rs, ...), custom_call_target="tpu_custom_call" | custom-call | flops 2147483648 | bytes 8388608 | tf_op jit(solution)/shard_map/pallas_call | solution.py:1378
  292.1 38.9 %shard_map.256 = f32[256,2048]{1,0:T(8,128)S(1)} custom-call(bf16[1024,512]{1,0:T(8,128)(2,1)S(1)} %copy-done.2, bf16[512,2048]{1,0:T(8,128)(2,1)S(1)} %copy-done.1), custom_call_target="tpu_custom_call" | custom-call | tf_op jit(solution)/shard_map/pallas_call | solution.py:1325
  336.0 3.7 fusion.pick_ref
  339.7 163.4 %shard_map.257 = (bf16[8,1280,2048]{2,1,0:T(8,128)(2,1)}, f32[8,1280,256]{2,1,0:T(8,128)}, bf16[4,2,2,2,256,2048]{5,4,3,2,1,0:T(8,128)(2,1)}, f32[32,8,256]{2,1,0:T(8,128)}) custom-call(bf16[32,320,256]{2,1,0:T(8,128)(2,1)} %fusion.pick_ref, bf16[32,256,2048]{2,1,0:T(8,128)(2,1)} %bitcast.113, bf16[8,256,2048]{2,1,0:T(8,128)(2,1)} %weight_ref.1, ...), custom_call_target="tpu_custom_call" | custom-call | tf_op jit(solution)/shard_map/pallas_call | solution.py:1043
  506.5 3.1 reshape.270.probs_ref
  509.6 73.2 %shard_map.258 = (bf16[8,1280,2048]{2,1,0:T(8,128)(2,1)}, bf16[8,1280,256]{2,1,0:T(8,128)(2,1)}, bf16[8,1280,256]{2,1,0:T(8,128)(2,1)}, bf16[8,1280,256]{2,1,0:T...) custom-call(bf16[32,320,256]{2,1,0:T(8,128)(2,1)} %fusion.pick_ref, bf16[32,256,2048]{2,1,0:T(8,128)(2,1)} %bitcast.141, ...), custom_call_target="tpu_custom_call" | custom-call | flops 32212254720 | bytes 125829120 | tf_op jit(solution)/shard_map/pallas_call | solution.py:1117
  582.8 3.9 reduce.3
  587.0 2.9 select_reduce_fusion.small_ref
  589.9 5.2 fusion.52
  595.1 66.9 %shard_map.259 = bf16[32,256,2048]{2,1,0:T(8,128)(2,1)} custom-call(bf16[32,256,320]{2,1,0:T(8,128)(2,1)} %get-tuple-element.184.spread_ref, bf16[8,1280,256]{2,1,0:T(8,128)(2,1)} %get-tuple-element.70.refs_0_.gate_ref, bf16[8,1280,256]{2,1,0:T(8,128)(2,1)} %get-tuple-element.71.refs_1_.up_ref, bf16[8,2048,256]{2,1,0:T(8,128)(2,1)} %refs_2_.1, ...), custom_call_target="tpu_custom_call" | custom-call | tf_op jit(solution)/shard_map/pallas_call | solution.py:1189
  662.1 162.8 %shard_map.260 = (f32[256,2048]{1,0:T(8,128)}, f32[32,8,256]{2,1,0:T(8,128)}, bf16[8,2048,256]{2,1,0:T(8,128)(2,1)}, bf16[8,2048,256]{2,1,0:T(8,128)(2,1)}, bf16[8,256,2048]{2,1,0:T(8,128)(2,1)}) custom-call(bf16[4,2,2,2,256,2048]{5,4,3,2,1,0:T(8,128)(2,1)} %bitcast.112, f32[32,8,256]{2,1,0:T(8,128)} %select_reduce_fusion.small_ref, ...), custom_call_target="tpu_custom_call" | custom-call | tf_op jit(solution)/shard_map/pallas_call | solution.py:933
  824.9 3.4 copy-done
  828.2 21.8 %shard_map.264 = (f32[8,2048,256]{2,1,0:T(8,128)}, f32[8,2048,256]{2,1,0:T(8,128)}, f32[8,256,2048]{2,1,0:T(8,128)}) custom-call(bf16[8,2048,256]{2,1,0:T(8,128)(2,1)S(1)} %copy-done, bf16[8,2048,256]{2,1,0:T(8,128)(2,1)} %get-tuple-element.99.refs_1_, bf16[8,256,2048]{2,1,0:T(8,128)(2,1)} %get-tuple-element.100.refs_2_), custom_call_target="tpu_custom_call" | custom-call | tf_op jit(solution)/shard_map/pallas_call | solution.py:966
  858.3 4.5 select_convert_fusion.spread_ref
  862.8 56.6 %shard_map.261 = (bf16[32,256,2048]{2,1,0:T(8,128)(2,1)}, bf16[4,256,2048]{2,1,0:T(8,128)(2,1)}) custom-call(bf16[32,256,320]{2,1,0:T(8,128)(2,1)} %select_convert_fusion.spread_ref, bf16[8,1280,256]{2,1,0:T(8,128)(2,1)} %get-tuple-element.69.left_ref, bf16[8,256,2048]{2,1,0:T(8,128)(2,1)} %weight_ref.1, bf16[256,2048]{1,0:T(8,128)(2,1)} %get-tuple-element.156.own_ref), custom_call_target="tpu_custom_call" | custom-call | tf_op jit(solution)/shard_map/pallas_call | solution.py:1256
  919.4 6.2 convolution_convert_fusion.3.grad_ref
  925.6 21.9 %shard_map.262 = (bf16[1024,512]{1,0:T(8,128)(2,1)}, f32[1024,512]{1,0:T(8,128)}, f32[1024,512]{1,0:T(8,128)}, f32[1,512]{1,0:T(1,128)}, f32[1,512]{1,0:T(1,128)...) custom-call(bf16[1024,512]{1,0:T(8,128)(2,1)} %get-tuple-element.79.q_ref, bf16[1024,512]{1,0:T(8,128)(2,1)} %get-tuple-element.80.k_ref, ...), custom_call_target="tpu_custom_call" | custom-call | flops 5368709120 | bytes 16777216 | tf_op jit(solution)/shard_map/pallas_call | solution.py:1428
  951.3 9.1 all-reduce.2
  960.5 3.8 subtract_convert_fusion.1
  964.9 12.4 fusion.9
  978.4 6.0 convolution_convert_fusion.1.o_ref
  984.5 9.4 convolution_convert_fusion.qkv_ref
  993.9 3.5 fusion.6
  997.4 225.2 %shard_map.263 = (f32[256,2048]{1,0:T(8,128)}, f32[256,2048]{1,0:T(8,128)}, f32[256,512]{1,0:T(8,128)}, f32[256,512]{1,0:T(8,128)}, f32[256,512]{1,0:T(8,128)}, ...) custom-call(bf16[4,2,2,2,256,2048]{5,4,3,2,1,0:T(8,128)(2,1)} %bitcast.114, bf16[4,256,2048]{2,1,0:T(8,128)(2,1)} %bitcast.115, ...), custom_call_target="tpu_custom_call" | custom-call | tf_op jit(solution)/shard_map/pallas_call | solution.py:684
  1222.6 4.0 add.107
  1231.7 3.2 add.106
  (170 shorter events, 49.2 us)
Async XLA Ops:
  239.0 4.4 copy-start.8
  243.4 4.3 copy-start.41
  244.4 9.9 copy-start.14
  267.5 6.7 copy-start.32
  267.5 6.7 copy-start.34
  274.2 16.7 %copy-start.1 = (bf16[512,2048]{1,0:T(8,128)(2,1)S(1)}, bf16[512,2048]{1,0:T(8,128)(2,1)}, u32[]{:S(2)}) copy-start(bf16[512,2048]{1,0:T(8,128)(2,1)} %get-tuple-element.63.weight_ref) | copy-start | bytes 6291460
  274.2 56.8 %copy-start.16 = (bf16[256,2048]{1,0:T(8,128)(2,1)S(1)}, bf16[256,2048]{1,0:T(8,128)(2,1)}, u32[]{:S(2)}) copy-start(bf16[256,2048]{1,0:T(8,128)(2,1)} %x_ref.1) | copy-start | bytes 3145732
  332.9 6.8 copy-start.11
  582.8 7.1 copy-start.44
  828.2 21.8 %copy-start.27 = (f32[32,8,256]{2,1,0:T(8,128)S(1)}, f32[32,8,256]{2,1,0:T(8,128)}, u32[]{:S(2)}) copy-start(f32[32,8,256]{2,1,0:T(8,128)} %get-tuple-element.77) | copy-start | bytes 786436
  828.2 21.9 %copy-start.12 = (bf16[256,2048]{1,0:T(8,128)(2,1)S(1)}, bf16[256,2048]{1,0:T(8,128)(2,1)}, u32[]{:S(2)}) copy-start(bf16[256,2048]{1,0:T(8,128)(2,1)} %copy-done.11) | copy-start | bytes 3145732
  947.5 13.0 %copy-start.21 = (f32[1024,512]{1,0:T(8,128)S(1)}, f32[1024,512]{1,0:T(8,128)}, u32[]{:S(2)}) copy-start(f32[1024,512]{1,0:T(8,128)} %get-tuple-element.84) | copy-start | bytes 6291460
  947.5 13.0 %copy-start.33 = (f32[1024]{0:T(1024)S(1)}, f32[1024]{0:T(1024)}, u32[]{:S(2)}) copy-start(f32[1024]{0:T(1024)} %copy-done.32) | copy-start | bytes 12292
  947.5 13.0 %copy-start.35 = (f32[1024]{0:T(1024)S(1)}, f32[1024]{0:T(1024)}, u32[]{:S(2)}) copy-start(f32[1024]{0:T(1024)} %copy-done.34) | copy-start | bytes 12292
  947.5 13.0 %copy-start.37 = (f32[1024]{0:T(1024)S(1)}, f32[1024]{0:T(1024)}, u32[]{:S(2)}) copy-start(f32[1024]{0:T(1024)} %get-tuple-element.174) | copy-start | bytes 12292
  947.5 13.0 %copy-start.38 = (f32[1024]{0:T(1024)S(1)}, f32[1024]{0:T(1024)}, u32[]{:S(2)}) copy-start(f32[1024]{0:T(1024)} %get-tuple-element.189) | copy-start | bytes 12292
  960.5 4.1 copy-start.9
  960.5 4.1 copy-start.29
  960.5 4.4 copy-start.42
  964.3 12.9 %copy-start.22 = (bf16[1024,512]{1,0:T(8,128)(2,1)}, bf16[1024,512]{1,0:T(8,128)(2,1)S(1)}, u32[]{:S(2)}) copy-start(bf16[1024,512]{1,0:T(8,128)(2,1)S(1)} %get-tuple-element.163) | copy-start | bytes 3145732
  964.9 12.4 copy-start.40
  964.9 12.5 %copy-start.39 = (f32[1,512]{1,0:T(1,128)S(1)}, f32[1,512]{1,0:T(1,128)}, u32[]{:S(2)}) copy-start(f32[1,512]{1,0:T(1,128)} %get-tuple-element.90) | copy-start | bytes 6148
  964.9 13.5 %copy-start.3 = (bf16[1024,512]{1,0:T(8,128)(2,1)S(1)}, bf16[1024,512]{1,0:T(8,128)(2,1)}, u32[]{:S(2)}) copy-start(bf16[1024,512]{1,0:T(8,128)(2,1)} %get-tuple-element.62.mixed_ref) | copy-start | bytes 3145732
  978.4 6.1 copy-start.15
  978.4 6.1 copy-start.23
  978.4 6.1 copy-start.43
  978.4 15.4 %slice-start = ((s8[8388608]{0:T(1024)(128)(4,1)}), s8[4194304]{0:T(1024)(128)(4,1)S(1)}, s32[]{:S(2)}) async-start(s8[8388608]{0:T(1024)(128)(4,1)} %bitcast.116), calls=%async_computation | async-start | bytes 8388608
  984.4 9.4 copy-start.10
  984.5 9.4 slice-start.1
  1222.6 9.1 copy-start.7
  1234.9 5.3 copy-start.25
  1234.9 6.1 copy-start.24
  (15 other events, 37.3 us)

commit v11 on v9

--- a/solution.py
+++ b/solution.py
@@ -943,24 +943,6 @@
             collective_id=collective_id, has_side_effects=True, vmem_limit_bytes=63 * 1024 * 1024
         ),
     )(part.reshape(4, 2, 2, 2, tokens, depth), small, rows, grad_gate, grad_up, act, grads)
-
-
-def widen_body(*refs):
-    half = len(refs) // 2
-    for low, wide in zip(refs[:half], refs[half:]):
-        wide[...] = low[...].astype(jnp.float32)
-
-
-def widen_all(*arrays):
-    specs = [pl.BlockSpec((1, *array.shape[1:]), lambda e: (e, 0, 0)) for array in arrays]
-    return pl.pallas_call(
-        widen_body,
-        grid=(arrays[0].shape[0],),
-        in_specs=specs,
-        out_specs=specs,
-        out_shape=[jax.ShapeDtypeStruct(array.shape, jnp.float32) for array in arrays],
-        compiler_params=pltpu.CompilerParams(vmem_limit_bytes=40 * 1024 * 1024),
-    )(*arrays)
 
 
 def fill_rows(pick_ref, field_ref, rows_ref):
@@ -1378,8 +1360,12 @@
     )(raw, raw, raw, q_rs, k_rs, q_gain[None], k_gain[None], cosine, sine)
 
 
-def attend_back_body(q_ref, k_ref, v_ref, grad_ref, lse_ref, q_raw, k_raw, q_rs, k_rs, q_gain, k_gain, cos_ref, sin_ref,
-                     v_grad, q_grad, k_grad, q_term, k_term, q_inner, k_inner, dq, dk, dv):
+def attend_back_body(count, *refs):
+    (q_ref, k_ref, v_ref, grad_ref, lse_ref, q_raw, k_raw, q_rs, k_rs, q_gain, k_gain, cos_ref, sin_ref) = refs[:13]
+    v_grad, q_grad, k_grad, q_term, k_term, q_inner, k_inner = refs[13 + count : 20 + count]
+    dq, dk, dv = refs[20 + 2 * count :]
+    for low, wide in zip(refs[13 : 13 + count], refs[20 + count : 20 + 2 * count]):
+        wide[...] = low[...].astype(jnp.float32)
     length = v_ref.shape[0]
     block = min(256, length)
     dk[...] = jnp.zeros_like(dk)
@@ -1407,7 +1393,7 @@
         inner[0] = jnp.sum(weighted * field, axis=-1, keepdims=True)
 
 
-def attend_back(queries, keys, values, grads, lse, raw, q_rs, k_rs, q_gain, k_gain, cosine, sine):
+def attend_back(lows, queries, keys, values, grads, lse, raw, q_rs, k_rs, q_gain, k_gain, cosine, sine):
     length, width = raw.shape[0], raw.shape[1] // 3
     heads = width // HD
     slab = pl.BlockSpec((length, HD), lambda h: (0, h))
@@ -1416,11 +1402,14 @@
     table = pl.BlockSpec((length, HD), lambda h: (0, 0))
     column = pl.BlockSpec((1, length, 1), lambda h: (h, 0, 0))
     wide = jax.ShapeDtypeStruct((length, width), jnp.float32)
-    return pl.pallas_call(
-        attend_back_body,
+    slices = [
+        pl.BlockSpec((low.shape[0] // heads, *low.shape[1:]), lambda h: (h, 0, 0)) for low in lows
+    ]
+    outs = pl.pallas_call(
+        functools.partial(attend_back_body, len(lows)),
         grid=(heads,),
-        in_specs=[slab] * 4 + [column] + three_slabs(length, heads)[:2] + [thin, thin, line, line, table, table],
-        out_specs=[slab, slab, slab, line, line, column, column],
+        in_specs=[slab] * 4 + [column] + three_slabs(length, heads)[:2] + [thin, thin, line, line, table, table] + slices,
+        out_specs=[slab, slab, slab, line, line, column, column] + slices,
         out_shape=[
             jax.ShapeDtypeStruct((length, width), jnp.bfloat16),
             wide,
@@ -1429,12 +1418,15 @@
             jax.ShapeDtypeStruct((1, width), jnp.float32),
             jax.ShapeDtypeStruct((heads, length, 1), jnp.float32),
             jax.ShapeDtypeStruct((heads, length, 1), jnp.float32),
-        ],
+        ]
+        + [jax.ShapeDtypeStruct(low.shape, jnp.float32) for low in lows],
+        compiler_params=pltpu.CompilerParams(vmem_limit_bytes=60 * 1024 * 1024),
         scratch_shapes=[pltpu.VMEM((length, HD), jnp.float32)] * 3,
         cost_estimate=pl.CostEstimate(
             flops=10 * heads * length * length * HD, bytes_accessed=16 << 20, transcendentals=heads * length * length
         ),
-    )(queries, keys, values, grads, lse, raw, raw, q_rs, k_rs, q_gain[None], k_gain[None], cosine, sine)
+    )(queries, keys, values, grads, lse, raw, raw, q_rs, k_rs, q_gain[None], k_gain[None], cosine, sine, *lows)
+    return outs[:7], outs[7:]
 
 
 def local(
@@ -1625,9 +1617,7 @@
         grad_feed, gates_in, grad_gate_weight, grad_up_weight, grad_down_weight = feed_back(
             grad_feed_part, own_gates, expert_rows, grad_gate, grad_up, weighted_act, expert_grads, 3
         )
-        grad_gate_weight, grad_up_weight, grad_down_weight = widen_all(
-            grad_gate_weight, grad_up_weight, grad_down_weight
-        )
+        expert_terms = [grad_gate_weight, grad_up_weight, grad_down_weight]
         gates_in = jnp.sum(gates_in.reshape(-1, rows_count, experts_local, tokens), axis=1)
         grad_probs = gates_in.reshape(experts, tokens).T
     else:
@@ -1678,11 +1668,14 @@
     grad_mixed = outer_cols(grad_branch, output_full).astype(jnp.bfloat16)
     (
         grad_value_low, query_weighted, key_weighted, query_gain_term, key_gain_term, query_inner, key_inner
-    ) = attend_back(
+    ), widened = attend_back(
+        expert_terms if near else [],
         queries, keys_rotated, values, grad_mixed, lse_all, raw, query_rs, key_rs,
         query_gain_f, key_gain_f, cosine, sine_table,
     )
     query_gain_term, key_gain_term = query_gain_term.reshape(-1), key_gain_term.reshape(-1)
+    if near:
+        grad_gate_weight, grad_up_weight, grad_down_weight = widened
     query_inner, key_inner = (
         lax.psum(jnp.sum(query_inner, axis=(0, 2)), "row"),
         lax.psum(jnp.sum(key_inner, axis=(0, 2)), "row"),

time: 1200 us -> 1190 us (level)
    pallas_call x2 -> x1, Pallas kernels: 43.8 us -> 35.9 us  [attend_back(): pl.pallas_call(functools.partial(attend_back_body, len(lows)), grid=(head...]
where the time goes in v11:
time: 1190 us; the launch traced here: 1180 us
  Pallas kernels  1020 us (86%)
  matrix products  55.1 us (5%)
  other arithmetic  47.6 us (4%)
  local copies, waits for them, and re-layouts  34.7 us (3%)
  blocking collectives  18.7 us (2%)
    pallas_call x1, Pallas kernels, finish_near(): pl.pallas_call(finish_body, out_shape=(jax.ShapeDtypeStruct((tokens, dept...  206 us
    pallas_call x1, Pallas kernels, start_near(): pl.pallas_call(start_body, out_shape=(shaped((4, *x.shape), x), shaped((8...  202 us
    pallas_call x1, Pallas kernels, grads_in(): pl.pallas_call(grads_in_body, grid=(steps,), in_specs=[pl.BlockSpec((rank...  163 us
    pallas_call x1, Pallas kernels, feed_back(): pl.pallas_call(feed_back_body, grid=(groups, depth // CHUNK), in_specs=[A...  161 us
    pallas_call x1, Pallas kernels, feed_in(): pl.pallas_call(functools.partial(feed_in_body, steps), grid=(steps + grou...  73.2 us
    pallas_call x1, Pallas kernels, restore(): pl.pallas_call(functools.partial(restore_body, flipped), grid=(steps,), i...  66.9 us
    pallas_call x1, Pallas kernels, restore_out(): pl.pallas_call(restore_out_body, grid=(steps,), in_specs=in_specs + [ANYW...  57.6 us
    pallas_call x1, Pallas kernels, branch_near(): pl.pallas_call(branch_body, in_specs=[inside] * 2, out_specs=inside, out_...  38.2 us

profile of v11, /device:TPU:0, one launch (start us, length us, event | category | flops | bytes accessed | tf_op | source)
XLA Modules:
  0.0 1178.3 jit_solution(15531049236510873704)
XLA Ops:
  1.6 2.8 concatenate.16
  5.0 202.5 %shard_map.254 = (bf16[4,256,2048]{2,1,0:T(8,128)(2,1)}, bf16[2048,1536]{1,0:T(8,128)(2,1)}, bf16[512,2048]{1,0:T(8,128)(2,1)}, bf16[8,144,128]{2,1,0:T(8,128)(2...) custom-call(bf16[256,2048]{1,0:T(8,128)(2,1)} %x_ref.1, bf16[256,512]{1,0:T(8,128)(2,1)} %q_ref.1, ...), custom_call_target="tpu_custom_call" | custom-call | tf_op jit(solution)/shard_map/pallas_call | solution.py:466
  207.5 3.2 fusion.1
  212.9 3.2 copy-done.40
  216.2 6.7 fusion.53.q_raw.k_raw.v_ref.refs_5_.refs_6_
  222.8 2.6 copy-done.3
  225.7 9.4 all-reduce.3
  242.5 16.7 %shard_map.255 = (bf16[1024,512]{1,0:T(8,128)(2,1)}, bf16[1024,512]{1,0:T(8,128)(2,1)}, bf16[1024,512]{1,0:T(8,128)(2,1)}, bf16[1024,512]{1,0:T(8,128)(2,1)}, f32[4,1024,1]{2,1,0:T(8,128)}) custom-call(f32[1024,1536]{1,0:T(8,128)} %copy-done.3, f32[1024,1536]{1,0:T(8,128)} %copy-done.3, f32[1024,1536]{1,0:T(8,128)} %copy-done.3, ...), custom_call_target="tpu_custom_call" | custom-call | flops 2147483648 | bytes 8388608 | tf_op jit(solution)/shard_map/pallas_call | solution.py:1351
  260.5 38.2 %shard_map.256 = f32[256,2048]{1,0:T(8,128)S(1)} custom-call(bf16[1024,512]{1,0:T(8,128)(2,1)S(1)} %copy-done.1, bf16[512,2048]{1,0:T(8,128)(2,1)S(1)} %copy-done), custom_call_target="tpu_custom_call" | custom-call | tf_op jit(solution)/shard_map/pallas_call | solution.py:1298
  304.2 3.7 fusion.pick_ref
  307.9 162.6 %shard_map.257 = (bf16[8,1280,2048]{2,1,0:T(8,128)(2,1)}, f32[8,1280,256]{2,1,0:T(8,128)}, bf16[4,2,2,2,256,2048]{5,4,3,2,1,0:T(8,128)(2,1)}, f32[32,8,256]{2,1,0:T(8,128)}) custom-call(bf16[32,320,256]{2,1,0:T(8,128)(2,1)} %fusion.pick_ref, bf16[32,256,2048]{2,1,0:T(8,128)(2,1)} %bitcast.114, bf16[8,256,2048]{2,1,0:T(8,128)(2,1)} %weight_ref.1, ...), custom_call_target="tpu_custom_call" | custom-call | tf_op jit(solution)/shard_map/pallas_call | solution.py:1016
  474.0 3.1 reshape.270.probs_ref
  477.1 73.2 %shard_map.258 = (bf16[8,1280,2048]{2,1,0:T(8,128)(2,1)}, bf16[8,1280,256]{2,1,0:T(8,128)(2,1)}, bf16[8,1280,256]{2,1,0:T(8,128)(2,1)}, bf16[8,1280,256]{2,1,0:T...) custom-call(bf16[32,320,256]{2,1,0:T(8,128)(2,1)} %fusion.pick_ref, bf16[32,256,2048]{2,1,0:T(8,128)(2,1)} %bitcast.141, ...), custom_call_target="tpu_custom_call" | custom-call | flops 32212254720 | bytes 125829120 | tf_op jit(solution)/shard_map/pallas_call | solution.py:1090
  550.3 3.9 reduce.3
  554.4 2.9 select_reduce_fusion.small_ref
  557.4 5.2 fusion.52
  562.5 66.9 %shard_map.259 = bf16[32,256,2048]{2,1,0:T(8,128)(2,1)} custom-call(bf16[32,256,320]{2,1,0:T(8,128)(2,1)} %get-tuple-element.184.spread_ref, bf16[8,1280,256]{2,1,0:T(8,128)(2,1)} %get-tuple-element.70.refs_0_.gate_ref, bf16[8,1280,256]{2,1,0:T(8,128)(2,1)} %get-tuple-element.71.refs_1_.up_ref, bf16[8,2048,256]{2,1,0:T(8,128)(2,1)} %refs_2_.1, ...), custom_call_target="tpu_custom_call" | custom-call | tf_op jit(solution)/shard_map/pallas_call | solution.py:1162
  629.4 160.6 %shard_map.260 = (f32[256,2048]{1,0:T(8,128)}, f32[32,8,256]{2,1,0:T(8,128)}, bf16[8,2048,256]{2,1,0:T(8,128)(2,1)}, bf16[8,2048,256]{2,1,0:T(8,128)(2,1)}, bf16[8,256,2048]{2,1,0:T(8,128)(2,1)}) custom-call(bf16[4,2,2,2,256,2048]{5,4,3,2,1,0:T(8,128)(2,1)} %bitcast.112, f32[32,8,256]{2,1,0:T(8,128)} %select_reduce_fusion.small_ref, ...), custom_call_target="tpu_custom_call" | custom-call | tf_op jit(solution)/shard_map/pallas_call | solution.py:923
  791.2 3.0 multiply_reduce_fusion
  797.0 4.6 select_convert_fusion.spread_ref
  801.6 57.6 %shard_map.261 = (bf16[32,256,2048]{2,1,0:T(8,128)(2,1)}, bf16[4,256,2048]{2,1,0:T(8,128)(2,1)}) custom-call(bf16[32,256,320]{2,1,0:T(8,128)(2,1)} %select_convert_fusion.spread_ref, bf16[8,1280,256]{2,1,0:T(8,128)(2,1)} %get-tuple-element.69.left_ref, bf16[8,256,2048]{2,1,0:T(8,128)(2,1)} %weight_ref.1, bf16[256,2048]{1,0:T(8,128)(2,1)} %get-tuple-element.156.own_ref), custom_call_target="tpu_custom_call" | custom-call | tf_op jit(solution)/shard_map/pallas_call | solution.py:1229
  859.3 6.2 convolution_convert_fusion.3.refs_3_
  865.5 35.9 %shard_map.262 = (bf16[1024,512]{1,0:T(8,128)(2,1)}, f32[1024,512]{1,0:T(8,128)}, f32[1024,512]{1,0:T(8,128)}, f32[1,512]{1,0:T(1,128)}, f32[1,512]{1,0:T(1,128)...) custom-call(bf16[1024,512]{1,0:T(8,128)(2,1)} %get-tuple-element.79., ...), custom_call_target="tpu_custom_call" | custom-call | flops 5368709120 | bytes 16777216 | tf_op jit(solution)/shard_map/pallas_call | solution.py:1408
  905.2 9.3 all-reduce.2
  914.6 3.6 subtract_convert_fusion.1
  919.0 12.3 %fusion.9 = (bf16[2048]{0:T(1024)(128)(2,1)S(1)}, f32[1024]{0:T(1024)S(1)}, f32[1024,2048]{1,0:T(8,128)}) fusion(bf16[4,256,2048]{2,1,0:T(8,128)(2,1)S(1)} %copy-done.8, f32[1024]{0:T(1024)S(1)} %bitcast.134, f32[2048]{0:T(1024)S(1)} %bitcast.131, bf16[2048,1536]{1,0:T(8,128)(2,1)} %get-tuple-element.61, bf16[1024,512]{1,0:T(8,128)(2,1)S(1)} %copy-done.42, ...), kind=kOutput, calls=%fused_computation.19 | convolution fusion | flops 6466565120 | bytes 22040576 | tf_op jit(solution)/shard_map/dot_general | solution.py:34
  933.5 11.6 convolution_convert_fusion.qkv_ref
  945.2 3.6 fusion.6
  948.8 3.8 convolution_convert_fusion.1.o_ref
  952.5 206.2 %shard_map.263 = (f32[256,2048]{1,0:T(8,128)}, f32[256,2048]{1,0:T(8,128)}, f32[256,512]{1,0:T(8,128)}, f32[256,512]{1,0:T(8,128)}, f32[256,512]{1,0:T(8,128)}, ...) custom-call(bf16[4,2,2,2,256,2048]{5,4,3,2,1,0:T(8,128)(2,1)} %bitcast.113, bf16[4,256,2048]{2,1,0:T(8,128)(2,1)} %bitcast.115, ...), custom_call_target="tpu_custom_call" | custom-call | tf_op jit(solution)/shard_map/pallas_call | solution.py:676
  1158.7 4.0 add.107
  1167.8 3.2 add.106
  (167 shorter events, 44.3 us)
Async XLA Ops:
  207.5 4.4 copy-start.7
  211.9 4.3 copy-start.40
  212.9 9.9 copy-start.13
  235.7 6.8 copy-start.31
  235.7 6.8 copy-start.33
  242.5 16.7 %copy-start = (bf16[512,2048]{1,0:T(8,128)(2,1)S(1)}, bf16[512,2048]{1,0:T(8,128)(2,1)}, u32[]{:S(2)}) copy-start(bf16[512,2048]{1,0:T(8,128)(2,1)} %get-tuple-element.63.weight_ref) | copy-start | bytes 6291460
  242.5 56.2 %copy-start.14 = (bf16[256,2048]{1,0:T(8,128)(2,1)S(1)}, bf16[256,2048]{1,0:T(8,128)(2,1)}, u32[]{:S(2)}) copy-start(bf16[256,2048]{1,0:T(8,128)(2,1)} %x_ref.1) | copy-start | bytes 3145732
  300.6 7.3 copy-start.10
  307.9 162.6 %copy-start.18 = (s32[32,256,8]{1,2,0:T(8,128)S(1)}, s32[32,256,8]{1,2,0:T(8,128)}, u32[]{:S(2)}) copy-start(s32[32,256,8]{1,2,0:T(8,128)} %copy-done.17) | copy-start | bytes 786436
  550.3 7.1 copy-start.43
  790.0 4.3 copy-start.5
  790.0 4.3 copy-start.15
  901.4 13.2 %copy-start.21 = (f32[1024,512]{1,0:T(8,128)S(1)}, f32[1024,512]{1,0:T(8,128)}, u32[]{:S(2)}) copy-start(f32[1024,512]{1,0:T(8,128)} %get-tuple-element.87) | copy-start | bytes 6291460
  901.4 13.2 %copy-start.32 = (f32[1024]{0:T(1024)S(1)}, f32[1024]{0:T(1024)}, u32[]{:S(2)}) copy-start(f32[1024]{0:T(1024)} %copy-done.31) | copy-start | bytes 12292
  901.4 13.2 %copy-start.34 = (f32[1024]{0:T(1024)S(1)}, f32[1024]{0:T(1024)}, u32[]{:S(2)}) copy-start(f32[1024]{0:T(1024)} %copy-done.33) | copy-start | bytes 12292
  901.4 13.2 %copy-start.36 = (f32[1024]{0:T(1024)S(1)}, f32[1024]{0:T(1024)}, u32[]{:S(2)}) copy-start(f32[1024]{0:T(1024)} %get-tuple-element.174) | copy-start | bytes 12292
  901.4 13.2 %copy-start.37 = (f32[1024]{0:T(1024)S(1)}, f32[1024]{0:T(1024)}, u32[]{:S(2)}) copy-start(f32[1024]{0:T(1024)} %get-tuple-element.189) | copy-start | bytes 12292
  914.6 4.1 copy-start.8
  914.6 4.1 copy-start.28
  914.6 4.1 copy-start.30
  914.6 4.4 copy-start.42
  918.2 13.2 %copy-start.22 = (bf16[1024,512]{1,0:T(8,128)(2,1)}, bf16[1024,512]{1,0:T(8,128)(2,1)S(1)}, u32[]{:S(2)}) copy-start(bf16[1024,512]{1,0:T(8,128)(2,1)S(1)} %get-tuple-element.163) | copy-start | bytes 3145732
  919.0 12.4 %copy-start.39 = (f32[1,512]{1,0:T(1,128)S(1)}, f32[1,512]{1,0:T(1,128)}, u32[]{:S(2)}) copy-start(f32[1,512]{1,0:T(1,128)} %get-tuple-element.92) | copy-start | bytes 6148
  919.0 12.5 %copy-start.38 = (f32[1,512]{1,0:T(1,128)S(1)}, f32[1,512]{1,0:T(1,128)}, u32[]{:S(2)}) copy-start(f32[1,512]{1,0:T(1,128)} %get-tuple-element.93) | copy-start | bytes 6148
  919.0 12.6 %copy-start.11 = (bf16[256,2048]{1,0:T(8,128)(2,1)S(1)}, bf16[256,2048]{1,0:T(8,128)(2,1)}, u32[]{:S(2)}) copy-start(bf16[256,2048]{1,0:T(8,128)(2,1)} %copy-done.10) | copy-start | bytes 3145732
  933.5 11.6 slice-start
  933.5 11.6 copy-start.9
  933.5 11.6 slice-start.1
  1158.7 4.1 copy-start.12
  1158.7 9.1 copy-start.6
  1171.0 5.3 copy-start.25
  1171.0 6.1 copy-start.24
  (14 other events, 30.4 us)
